TPU v7x, 32 devices: a whole 2x2x4 slice. The times are simulated.
32 devices in a mesh: dp: 8 (over z, x), mp: 4 (over y, core).
Axes of the slice: x: 2, y: 2, z: 4, core: 2. Of those that a mesh axis runs over, the one named last changes fastest.
Arguments:
- encoder_in: bfloat16 [7296, 768], P('dp'), may hold values from -6 to 6
- decoder_in: bfloat16 [1024, 768], P('dp'), may hold values from -6 to 6
- decoder_cotangent: float32 [1024, 768], P('dp'), may hold values from -6 to 6
- counts: int32 [8, 2], P('dp'), may hold values from 0 to 4, as said below
- prefix_len: int32 [32], P('dp'), may hold values from 1 to 32
- suffix_len: int32 [32], P('dp'), may hold values from 1 to 32
- project_in: float32 [3, 3, 768, 768], P(None, None, 'dp', 'mp'), may hold values from -0.21875 to 0.21875
- project_in_rows: float32 [3, 3, 768], replicated, may hold values from 6e-10 to 2.4e-09
- project_in_cols: float32 [3, 3, 768], replicated, may hold values from 6e-10 to 2.4e-09
- project_in_moment: float32 [3, 3, 768, 768], P(None, None, 'dp', 'mp'), may hold values from -3 to 3
- project_in_average: float32 [3, 3, 768, 768], P(None, None, 'dp', 'mp'), may hold values from -0.21875 to 0.21875
- project_out: float32 [3, 768, 768], P(None, 'mp', 'dp'), may hold values from -0.625 to 0.625
- project_out_rows: float32 [3, 768], replicated, may hold values from 6e-10 to 2.4e-09
- project_out_cols: float32 [3, 768], replicated, may hold values from 6e-10 to 2.4e-09
- project_out_moment: float32 [3, 768, 768], P(None, 'mp', 'dp'), may hold values from -3 to 3
- project_out_average: float32 [3, 768, 768], P(None, 'mp', 'dp'), may hold values from -0.625 to 0.625
- expand: float32 [2, 768, 3072], P(None, 'dp', 'mp'), may hold values from -0.21875 to 0.21875
- expand_rows: float32 [2, 768], replicated, may hold values from 5e-11 to 2e-10
- expand_cols: float32 [2, 3072], replicated, may hold values from 5e-11 to 2e-10
- expand_moment: float32 [2, 768, 3072], P(None, 'dp', 'mp'), may hold values from -3 to 3
- expand_average: float32 [2, 768, 3072], P(None, 'dp', 'mp'), may hold values from -0.21875 to 0.21875
- contract: float32 [2, 3072, 768], P(None, 'mp', 'dp'), may hold values from -0.109375 to 0.109375
- contract_rows: float32 [2, 3072], replicated, may hold values from 6e-10 to 2.4e-09
- contract_cols: float32 [2, 768], replicated, may hold values from 6e-10 to 2.4e-09
- contract_moment: float32 [2, 3072, 768], P(None, 'mp', 'dp'), may hold values from -3 to 3
- contract_average: float32 [2, 3072, 768], P(None, 'mp', 'dp'), may hold values from -0.109375 to 0.109375
- norm_gains: float32 [5, 768], P(None, 'dp'), may hold values from 0.35 to 1.95
- norm_gains_square: float32 [5, 768], P(None, 'dp'), may hold values from 6e-10 to 2.4e-09
- norm_gains_moment: float32 [5, 768], P(None, 'dp'), may hold values from -3 to 3
- norm_gains_average: float32 [5, 768], P(None, 'dp'), may hold values from 0.5 to 1.5
Outputs:
- decoder_out: float32 [1024, 768], P('dp')
- encoder_in_grad: float32 [7296, 768], P('dp')
- decoder_in_grad: float32 [1024, 768], P('dp')
- grad_norm: float32 [], replicated
- project_in_grad: float32 [3, 3, 768, 768], P(None, None, 'dp', 'mp')
- project_in_rows_new: float32 [3, 3, 768], replicated
- project_in_cols_new: float32 [3, 3, 768], replicated
- project_in_moment_new: float32 [3, 3, 768, 768], P(None, None, 'dp', 'mp')
- project_in_new: float32 [3, 3, 768, 768], P(None, None, 'dp', 'mp')
- project_in_average_new: float32 [3, 3, 768, 768], P(None, None, 'dp', 'mp')
- project_in_low: bfloat16 [3, 3, 768, 768], P(None, None, 'dp', 'mp')
- project_out_grad: float32 [3, 768, 768], P(None, 'mp', 'dp')
- project_out_rows_new: float32 [3, 768], replicated
- project_out_cols_new: float32 [3, 768], replicated
- project_out_moment_new: float32 [3, 768, 768], P(None, 'mp', 'dp')
- project_out_new: float32 [3, 768, 768], P(None, 'mp', 'dp')
- project_out_average_new: float32 [3, 768, 768], P(None, 'mp', 'dp')
- project_out_low: bfloat16 [3, 768, 768], P(None, 'mp', 'dp')
- expand_grad: float32 [2, 768, 3072], P(None, 'dp', 'mp')
- expand_rows_new: float32 [2, 768], replicated
- expand_cols_new: float32 [2, 3072], replicated
- expand_moment_new: float32 [2, 768, 3072], P(None, 'dp', 'mp')
- expand_new: float32 [2, 768, 3072], P(None, 'dp', 'mp')
- expand_average_new: float32 [2, 768, 3072], P(None, 'dp', 'mp')
- expand_low: bfloat16 [2, 768, 3072], P(None, 'dp', 'mp')
- contract_grad: float32 [2, 3072, 768], P(None, 'mp', 'dp')
- contract_rows_new: float32 [2, 3072], replicated
- contract_cols_new: float32 [2, 768], replicated
- contract_moment_new: float32 [2, 3072, 768], P(None, 'mp', 'dp')
- contract_new: float32 [2, 3072, 768], P(None, 'mp', 'dp')
- contract_average_new: float32 [2, 3072, 768], P(None, 'mp', 'dp')
- contract_low: bfloat16 [2, 3072, 768], P(None, 'mp', 'dp')
- norm_gains_grad: float32 [5, 768], P(None, 'dp')
- norm_gains_square_new: float32 [5, 768], P(None, 'dp')
- norm_gains_moment_new: float32 [5, 768], P(None, 'dp')
- norm_gains_new: float32 [5, 768], P(None, 'dp')
- norm_gains_average_new: float32 [5, 768], P(None, 'dp')
- norm_gains_low: bfloat16 [5, 768], P(None, 'dp')
Inputs may be any that keep to these rules, and one draw needn't show every extreme that they name: Per group the image-text pairs take the first slots and the text-only pairs the next ones; the two counts of a group sum to at least half of 4, to at most 4, and to exactly 4 in at least one group.
All inputs are finite; a program needn't handle non-finite values.
Results may differ from a plain program's by a relative error of at most 0.0233.
Values may be sent and summed in bfloat16 or wider, within the bound.
No kernel may reach another device: no remote copies, remote signals or barrier semaphores. Data moves between devices by JAX's collectives and lax.ppermute only.
A program may use at most 128 MiB of HBM per device.

v0:
```python
import jax
import jax.numpy as jnp
from jax import lax
from jax.sharding import PartitionSpec as P

D = 768
HEAD_DIM = 64
FF = 3072
PATCHES = 196
SUFFIX = 32
ENC_LEN = 228


EPS_NORM = 1e-06
EPS_STAT = 1e-30
DECAY = 0.99
MOMENTUM = 0.9
AVERAGE = 0.6
RATE_MATRIX = 0.004
RATE_GAIN = 0.05
MASKED = -1000000000.0


def rmsnorm(inputs, gain):
    return inputs * lax.rsqrt(jnp.mean(inputs * inputs, -1, keepdims=True) + EPS_NORM) * gain


def gelu_tanh(values):
    return jax.nn.gelu(values, approximate=True)


def build_masks(count_row, prefix_row, suffix_row, pairs):
    slots = jnp.arange(pairs)
    images = slots < count_row[0]
    active = slots < count_row[0] + count_row[1]
    place = jnp.arange(ENC_LEN)
    key_ok = jnp.where(
        place[None, :] < PATCHES, images[:, None], place[None, :] - PATCHES < prefix_row[:, None]
    )
    steps = jnp.arange(SUFFIX)
    causal = (steps[None, None, :] <= steps[None, :, None]) & (
        steps[None, None, :] < suffix_row[:, None, None]
    )
    live = active[:, None] & (steps[None, :] < suffix_row[:, None])
    return (key_ok[:, None, None, :], causal[:, None], live.reshape(-1))


def attend(queries, keys_all, values_all, allowed):
    scores = jnp.einsum(
        "pqhd,pkhd->phqk", queries, keys_all, preferred_element_type=jnp.float32
    ) * HEAD_DIM ** (-0.5)
    scores = jnp.where(allowed, scores, MASKED)
    highest = jnp.max(scores, -1, keepdims=True)
    expons = jnp.exp(scores - highest)
    totals = jnp.sum(expons, -1, keepdims=True)
    probs = (expons / totals).astype(jnp.bfloat16)
    mixed = jnp.einsum(
        "phqk,pkhd->pqhd", probs, values_all, preferred_element_type=jnp.float32
    ).astype(jnp.bfloat16)
    return (mixed, highest + jnp.log(totals))


def attend_back(queries, keys_all, values_all, allowed, logsum, grad_mixed):
    scale = HEAD_DIM ** (-0.5)
    scores = (
        jnp.einsum("pqhd,pkhd->phqk", queries, keys_all, preferred_element_type=jnp.float32) * scale
    )
    scores = jnp.where(allowed, scores, MASKED)
    probs = jnp.exp(scores - logsum)
    grad_probs = jnp.einsum(
        "pqhd,pkhd->phqk", grad_mixed, values_all, preferred_element_type=jnp.float32
    )
    grad_scores = (probs * (grad_probs - jnp.sum(grad_probs * probs, -1, keepdims=True))).astype(
        jnp.bfloat16
    )
    grad_query = (
        jnp.einsum("phqk,pkhd->pqhd", grad_scores, keys_all, preferred_element_type=jnp.float32)
        * scale
    ).astype(jnp.bfloat16)
    grad_key = (
        jnp.einsum("phqk,pqhd->pkhd", grad_scores, queries, preferred_element_type=jnp.float32)
        * scale
    ).astype(jnp.bfloat16)
    grad_value = jnp.einsum(
        "phqk,pqhd->pkhd",
        probs.astype(jnp.bfloat16),
        grad_mixed,
        preferred_element_type=jnp.float32,
    ).astype(jnp.bfloat16)
    return (grad_query, grad_key, grad_value)


def spread(gradient, row_index, col_index, full_rows, full_cols):
    square = gradient * gradient
    row_part = jnp.sum(square, -1)
    col_part = jnp.sum(square, -2)
    row_full = lax.dynamic_update_slice_in_dim(
        jnp.zeros(row_part.shape[:-1] + (full_rows,), jnp.float32),
        row_part,
        row_index * row_part.shape[-1],
        row_part.ndim - 1,
    )
    col_full = lax.dynamic_update_slice_in_dim(
        jnp.zeros(col_part.shape[:-1] + (full_cols,), jnp.float32),
        col_part,
        col_index * col_part.shape[-1],
        col_part.ndim - 1,
    )
    return (row_full, col_full)


def update_matrix(
    gradient, weight, rows_old, cols_old, moment, average, row_sum, col_sum, row_index, col_index
):
    full_rows = rows_old.shape[-1]
    full_cols = cols_old.shape[-1]
    rows_new = DECAY * rows_old + (1.0 - DECAY) * (row_sum / full_cols + EPS_STAT)
    cols_new = DECAY * cols_old + (1.0 - DECAY) * (col_sum / full_rows + EPS_STAT)
    row_local = lax.dynamic_slice_in_dim(
        rows_new, row_index * gradient.shape[-2], gradient.shape[-2], rows_new.ndim - 1
    )
    col_local = lax.dynamic_slice_in_dim(
        cols_new, col_index * gradient.shape[-1], gradient.shape[-1], cols_new.ndim - 1
    )
    second = (
        row_local[..., :, None] * col_local[..., None, :] / jnp.mean(rows_new, -1)[..., None, None]
    )
    stepped = gradient * lax.rsqrt(second)
    moment_new = MOMENTUM * moment + stepped
    weight_new = weight - RATE_MATRIX * (MOMENTUM * moment_new + stepped)
    average_new = AVERAGE * average + (1.0 - AVERAGE) * weight_new
    return (
        gradient,
        rows_new,
        cols_new,
        moment_new,
        weight_new,
        average_new,
        weight_new.astype(jnp.bfloat16),
    )


def on_device(
    encoder_in,
    decoder_in,
    decoder_cotangent,
    counts,
    prefix_len,
    suffix_len,
    project_in,
    project_in_rows,
    project_in_cols,
    project_in_moment,
    project_in_average,
    project_out,
    project_out_rows,
    project_out_cols,
    project_out_moment,
    project_out_average,
    expand,
    expand_rows,
    expand_cols,
    expand_moment,
    expand_average,
    contract,
    contract_rows,
    contract_cols,
    contract_moment,
    contract_average,
    norm_gains,
    norm_gains_square,
    norm_gains_moment,
    norm_gains_average,
):
    weight_in, weight_out, weight_up, weight_down, weight_gain = (
        lax.all_gather(project_in.astype(jnp.bfloat16), "dp", axis=2, tiled=True),
        lax.all_gather(project_out.astype(jnp.bfloat16), "dp", axis=2, tiled=True),
        lax.all_gather(expand.astype(jnp.bfloat16), "dp", axis=1, tiled=True),
        lax.all_gather(contract.astype(jnp.bfloat16), "dp", axis=2, tiled=True),
        lax.all_gather(norm_gains.astype(jnp.bfloat16), "dp", axis=1, tiled=True),
    )
    gain_rows = weight_gain.astype(jnp.float32)
    local_heads = weight_in.shape[-1] // HEAD_DIM
    pairs = prefix_len.shape[0]
    key_ok, causal, live = build_masks(counts[0], prefix_len, suffix_len, pairs)

    def heads_total(partial_value):
        return lax.psum(partial_value, "mp")

    def inputs_total(partial_value):
        return lax.psum(partial_value, "mp")

    def split_heads(flat, length):
        return flat.reshape(pairs, length, local_heads, HEAD_DIM)

    def attn_forward(query_in, key_in, layer_index, allowed, query_len, key_len):
        queries = jnp.dot(
            query_in, weight_in[layer_index, 0], preferred_element_type=jnp.float32
        ).astype(jnp.bfloat16)
        keys_all = jnp.dot(
            key_in, weight_in[layer_index, 1], preferred_element_type=jnp.float32
        ).astype(jnp.bfloat16)
        values_all = jnp.dot(
            key_in, weight_in[layer_index, 2], preferred_element_type=jnp.float32
        ).astype(jnp.bfloat16)
        mixed, logsum = attend(
            split_heads(queries, query_len),
            split_heads(keys_all, key_len),
            split_heads(values_all, key_len),
            allowed,
        )
        flat = mixed.reshape(pairs * query_len, local_heads * HEAD_DIM)
        branch = heads_total(
            jnp.dot(flat, weight_out[layer_index], preferred_element_type=jnp.float32)
        )
        return (branch, (queries, keys_all, values_all, flat, logsum))

    def attn_backward(query_in, key_in, layer_index, allowed, query_len, key_len, stored, grad_out):
        queries, keys_all, values_all, flat, logsum = stored
        grad_low = grad_out.astype(jnp.bfloat16)
        grad_proj_out = jnp.einsum("tm,td->md", flat, grad_low, preferred_element_type=jnp.float32)
        grad_mixed = jnp.einsum(
            "td,md->tm", grad_low, weight_out[layer_index], preferred_element_type=jnp.float32
        ).astype(jnp.bfloat16)
        grad_query, grad_key, grad_value = attend_back(
            split_heads(queries, query_len),
            split_heads(keys_all, key_len),
            split_heads(values_all, key_len),
            allowed,
            logsum,
            split_heads(grad_mixed, query_len),
        )
        grad_query = grad_query.reshape(pairs * query_len, -1)
        grad_key = grad_key.reshape(pairs * key_len, -1)
        grad_value = grad_value.reshape(pairs * key_len, -1)
        grad_proj_in = jnp.stack(
            [
                jnp.einsum("td,tm->dm", query_in, grad_query, preferred_element_type=jnp.float32),
                jnp.einsum("td,tm->dm", key_in, grad_key, preferred_element_type=jnp.float32),
                jnp.einsum("td,tm->dm", key_in, grad_value, preferred_element_type=jnp.float32),
            ]
        )
        back_query = jnp.einsum(
            "tm,dm->td", grad_query, weight_in[layer_index, 0], preferred_element_type=jnp.float32
        )
        back_key = jnp.einsum(
            "tm,dm->td", grad_key, weight_in[layer_index, 1], preferred_element_type=jnp.float32
        ) + jnp.einsum(
            "tm,dm->td", grad_value, weight_in[layer_index, 2], preferred_element_type=jnp.float32
        )
        return (grad_proj_in, grad_proj_out, back_query, back_key)

    def mlp_forward(inputs, gain_row, layer_index):
        normed, norm_pull = jax.vjp(rmsnorm, inputs, gain_row)
        normed_low = normed.astype(jnp.bfloat16)
        upper = jnp.dot(normed_low, weight_up[layer_index], preferred_element_type=jnp.float32)
        active, gelu_pull = jax.vjp(gelu_tanh, upper)
        active_low = active.astype(jnp.bfloat16)
        branch = heads_total(
            jnp.dot(active_low, weight_down[layer_index], preferred_element_type=jnp.float32)
        )
        return (branch, (norm_pull, normed_low, gelu_pull, active_low))

    def mlp_backward(layer_index, stored, grad_out):
        norm_pull, normed_low, gelu_pull, active_low = stored
        grad_low = grad_out.astype(jnp.bfloat16)
        grad_down = jnp.einsum(
            "tf,td->fd", active_low, grad_low, preferred_element_type=jnp.float32
        )
        grad_active = jnp.einsum(
            "td,fd->tf", grad_low, weight_down[layer_index], preferred_element_type=jnp.float32
        )
        grad_upper = gelu_pull(grad_active)[0].astype(jnp.bfloat16)
        grad_up = jnp.einsum(
            "td,tf->df", normed_low, grad_upper, preferred_element_type=jnp.float32
        )
        back = inputs_total(
            jnp.einsum(
                "tf,df->td", grad_upper, weight_up[layer_index], preferred_element_type=jnp.float32
            )
        )
        grad_input, grad_gain = norm_pull(back)
        return (grad_up, grad_down, grad_input, grad_gain)

    enc_x = encoder_in.astype(jnp.float32)
    dec_x = decoder_in.astype(jnp.float32)
    normed, pull_enc_attn = jax.vjp(rmsnorm, enc_x, gain_rows[0])
    normed_enc = normed.astype(jnp.bfloat16)
    branch, kept_enc_attn = attn_forward(normed_enc, normed_enc, 0, key_ok, ENC_LEN, ENC_LEN)
    enc_mid = enc_x + branch
    branch, kept_enc_mlp = mlp_forward(enc_mid, gain_rows[1], 0)
    memory = (enc_mid + branch).astype(jnp.bfloat16)
    normed, pull_dec_self = jax.vjp(rmsnorm, dec_x, gain_rows[2])
    normed_self = normed.astype(jnp.bfloat16)
    branch, kept_dec_self = attn_forward(normed_self, normed_self, 1, causal, SUFFIX, SUFFIX)
    dec_one = dec_x + branch
    normed, pull_dec_cross = jax.vjp(rmsnorm, dec_one, gain_rows[3])
    normed_cross = normed.astype(jnp.bfloat16)
    branch, kept_dec_cross = attn_forward(normed_cross, memory, 2, key_ok, SUFFIX, ENC_LEN)
    dec_two = dec_one + branch
    branch, kept_dec_mlp = mlp_forward(dec_two, gain_rows[4], 1)
    decoder_out = dec_two + branch
    gradient = jnp.where(live[:, None], decoder_cotangent, jnp.float32(0.0))
    up_dec, down_dec, grad_input, gain_four = mlp_backward(1, kept_dec_mlp, gradient)
    gradient = gradient + grad_input
    in_cross, out_cross, back_query, back_memory = attn_backward(
        normed_cross, memory, 2, key_ok, SUFFIX, ENC_LEN, kept_dec_cross, gradient
    )
    back_query, back_memory = (
        lax.psum(back_query.astype(jnp.bfloat16), "mp").astype(jnp.float32),
        lax.psum(back_memory.astype(jnp.bfloat16), "mp").astype(jnp.float32),
    )
    grad_input, gain_three = pull_dec_cross(back_query)
    gradient = gradient + grad_input
    in_self, out_self, back_query, back_key = attn_backward(
        normed_self, normed_self, 1, causal, SUFFIX, SUFFIX, kept_dec_self, gradient
    )
    grad_input, gain_two = pull_dec_self(inputs_total(back_query + back_key))
    decoder_in_grad = gradient + grad_input
    gradient = back_memory
    up_enc, down_enc, grad_input, gain_one = mlp_backward(0, kept_enc_mlp, gradient)
    gradient = gradient + grad_input
    in_enc, out_enc, back_query, back_key = attn_backward(
        normed_enc, normed_enc, 0, key_ok, ENC_LEN, ENC_LEN, kept_enc_attn, gradient
    )
    grad_input, gain_zero = pull_enc_attn(inputs_total(back_query + back_key))
    encoder_in_grad = gradient + grad_input
    summed = (
        lax.psum_scatter(
            jnp.stack([in_enc, in_self, in_cross]), "dp", scatter_dimension=2, tiled=True
        ),
        lax.psum_scatter(
            jnp.stack([out_enc, out_self, out_cross]), "dp", scatter_dimension=2, tiled=True
        ),
        lax.psum_scatter(jnp.stack([up_enc, up_dec]), "dp", scatter_dimension=1, tiled=True),
        lax.psum_scatter(jnp.stack([down_enc, down_dec]), "dp", scatter_dimension=2, tiled=True),
        lax.psum_scatter(
            jnp.stack([gain_zero, gain_one, gain_two, gain_three, gain_four]),
            "dp",
            scatter_dimension=1,
            tiled=True,
        ),
    )
    grad_in, grad_out, grad_up, grad_down, grad_gain = summed
    dp_index = lax.axis_index("dp")
    mp_index = lax.axis_index("mp")
    local_square = (
        jnp.sum(grad_in * grad_in)
        + jnp.sum(grad_out * grad_out)
        + jnp.sum(grad_up * grad_up)
        + jnp.sum(grad_down * grad_down)
        + jnp.where(mp_index == 0, jnp.sum(grad_gain * grad_gain), jnp.float32(0.0))
    )
    row_in, col_in = spread(grad_in, dp_index, mp_index, D, D)
    row_out, col_out = spread(grad_out, mp_index, dp_index, D, D)
    row_up, col_up = spread(grad_up, dp_index, mp_index, D, FF)
    row_down, col_down = spread(grad_down, mp_index, dp_index, FF, D)
    row_in, col_in, row_out, col_out, row_up, col_up, row_down, col_down = (
        row_in,
        col_in,
        row_out,
        col_out,
        row_up,
        col_up,
        row_down,
        col_down,
    )
    total, row_in, col_in, row_out, col_out, row_up, col_up, row_down, col_down = lax.psum(
        (local_square, row_in, col_in, row_out, col_out, row_up, col_up, row_down, col_down),
        ("dp", "mp"),
    )
    grad_norm = jnp.sqrt(total)
    factor = jnp.minimum(1.0, 1.0 / grad_norm)
    squared = factor * factor
    row_in, col_in, row_out, col_out = (
        row_in * squared,
        col_in * squared,
        row_out * squared,
        col_out * squared,
    )
    row_up, col_up, row_down, col_down = (
        row_up * squared,
        col_up * squared,
        row_down * squared,
        col_down * squared,
    )
    grad_in, grad_out, grad_up, grad_down = (
        grad_in * factor,
        grad_out * factor,
        grad_up * factor,
        grad_down * factor,
    )
    grad_gain = grad_gain * factor
    pin = update_matrix(
        grad_in,
        project_in,
        project_in_rows,
        project_in_cols,
        project_in_moment,
        project_in_average,
        row_in,
        col_in,
        dp_index,
        mp_index,
    )
    pout = update_matrix(
        grad_out,
        project_out,
        project_out_rows,
        project_out_cols,
        project_out_moment,
        project_out_average,
        row_out,
        col_out,
        mp_index,
        dp_index,
    )
    pexp = update_matrix(
        grad_up,
        expand,
        expand_rows,
        expand_cols,
        expand_moment,
        expand_average,
        row_up,
        col_up,
        dp_index,
        mp_index,
    )
    pcon = update_matrix(
        grad_down,
        contract,
        contract_rows,
        contract_cols,
        contract_moment,
        contract_average,
        row_down,
        col_down,
        mp_index,
        dp_index,
    )
    square_new = DECAY * norm_gains_square + (1.0 - DECAY) * (grad_gain * grad_gain + EPS_STAT)
    stepped = grad_gain * lax.rsqrt(square_new)
    moment_new = MOMENTUM * norm_gains_moment + stepped
    gains_new = norm_gains - RATE_GAIN * (MOMENTUM * moment_new + stepped)
    average_new = AVERAGE * norm_gains_average + (1.0 - AVERAGE) * gains_new
    return (
        decoder_out,
        encoder_in_grad,
        decoder_in_grad,
        grad_norm,
        pin[0],
        pin[1],
        pin[2],
        pin[3],
        pin[4],
        pin[5],
        pin[6],
        pout[0],
        pout[1],
        pout[2],
        pout[3],
        pout[4],
        pout[5],
        pout[6],
        pexp[0],
        pexp[1],
        pexp[2],
        pexp[3],
        pexp[4],
        pexp[5],
        pexp[6],
        pcon[0],
        pcon[1],
        pcon[2],
        pcon[3],
        pcon[4],
        pcon[5],
        pcon[6],
        grad_gain,
        square_new,
        moment_new,
        gains_new,
        average_new,
        gains_new.astype(jnp.bfloat16),
    )


def solution(mesh):
    placed = (
        P("dp", None),
        P("dp", None),
        P("dp", None),
        P("dp", None),
        P("dp"),
        P("dp"),
        P(None, None, "dp", "mp"),
        P(),
        P(),
        P(None, None, "dp", "mp"),
        P(None, None, "dp", "mp"),
        P(None, "mp", "dp"),
        P(),
        P(),
        P(None, "mp", "dp"),
        P(None, "mp", "dp"),
        P(None, "dp", "mp"),
        P(),
        P(),
        P(None, "dp", "mp"),
        P(None, "dp", "mp"),
        P(None, "mp", "dp"),
        P(),
        P(),
        P(None, "mp", "dp"),
        P(None, "mp", "dp"),
        P(None, "dp"),
        P(None, "dp"),
        P(None, "dp"),
        P(None, "dp"),
    )
    return jax.shard_map(
        on_device,
        mesh=mesh,
        in_specs=placed,
        out_specs=(
            P("dp", None),
            P("dp", None),
            P("dp", None),
            P(),
            P(None, None, "dp", "mp"),
            P(),
            P(),
            P(None, None, "dp", "mp"),
            P(None, None, "dp", "mp"),
            P(None, None, "dp", "mp"),
            P(None, None, "dp", "mp"),
            P(None, "mp", "dp"),
            P(),
            P(),
            P(None, "mp", "dp"),
            P(None, "mp", "dp"),
            P(None, "mp", "dp"),
            P(None, "mp", "dp"),
            P(None, "dp", "mp"),
            P(),
            P(),
            P(None, "dp", "mp"),
            P(None, "dp", "mp"),
            P(None, "dp", "mp"),
            P(None, "dp", "mp"),
            P(None, "mp", "dp"),
            P(),
            P(),
            P(None, "mp", "dp"),
            P(None, "mp", "dp"),
            P(None, "mp", "dp"),
            P(None, "mp", "dp"),
            P(None, "dp"),
            P(None, "dp"),
            P(None, "dp"),
            P(None, "dp"),
            P(None, "dp"),
            P(None, "dp"),
        ),
        check_vma=False,
    )
```

profile of v0, /device:TPU:0, one launch (start us, length us, event | category | flops | bytes accessed | tf_op | source)
XLA Modules:
  0.0 1309.5 jit_solution(17161166580539261949)
XLA Ops:
  10.0 28.0 %all-gather = bf16[8,96,5]{1,2,0:T(8,128)(2,1)S(1)} all-gather(bf16[1,96,5]{1,2,0:T(8,128)(2,1)S(1)} %convert_bitcast_fusion), channel_id=1, replica_groups=mesh['dp'=8,'mp'=4] {'dp'}, dimensions={0}, use_global_device_ids=true | all-gather | bytes 8640 | tf_op jit(solution)/shard_map/all_gather | solution.py:180
  39.2 44.4 %all_gather.17 = bf16[3,192,768]{1,0,2:T(4,128)(2,1)S(1)} all-gather(bf16[3,192,96]{1,0,2:T(4,128)(2,1)S(1)} %copy.399), channel_id=1, replica_groups=mesh['dp'=8,'mp'=4] {'dp'}, dimensions={2}, use_global_device_ids=true | all-gather | bytes 995328 | tf_op jit(solution)/shard_map/all_gather | solution.py:177
  89.5 11.3 all-gather.5.cloned.1.call-done
  136.8 42.5 %all-reduce.15.cloned.1.call-done = f32[912,768]{1,0:T(8,128)} async-done(((f32[912,768]{1,0:T(8,128)}), f32[912,768]{1,0:T(8,128)}) %all-reduce.15.cloned.1.call-update) | async-done | bytes 2801680 | tf_op jit(solution)/shard_map/psum | solution.py:188
  183.4 50.8 %all-gather.7.cloned.1.call-done = bf16[2,768,768]{2,1,0:T(8,128)(2,1)} async-done(((bf16[2,96,768]{2,1,0:T(8,128)(2,1)}), bf16[2,768,768]{2,1,0:T(8,128)(2,1)}) %all-gather.7.cloned.1.call-update) | async-done | bytes 2359312 | tf_op jit(solution)/shard_map/all_gather | solution.py:178
  234.3 5.0 fusion.48
  239.3 48.5 %all-gather.9.cloned.1.call-done = bf16[2,768,768]{1,2,0:T(8,128)(2,1)} async-done(((bf16[2,768,96]{1,2,0:T(8,128)(2,1)}), bf16[2,768,768]{1,2,0:T(8,128)(2,1)}) %all-gather.9.cloned.1.call-update) | async-done | bytes 2359312 | tf_op jit(solution)/shard_map/all_gather | solution.py:179
  287.8 5.4 fusion.50
  296.1 65.4 %all-reduce.27.cloned.1.call-done = (f32[128,768]{1,0:T(8,128)}, f32[912,768]{1,0:T(8,128)}) async-done(((f32[128,768]{1,0:T(8,128)}, f32[912,768]{1,0:T(8,128)}), (f32[128,768]{1,0:T(8,128)}, f32[912,768]{1,0:T(8,128)})) %all-reduce.27.cloned.1.call-update) | async-done | bytes 3194896 | tf_op jit(solution)/shard_map/psum | solution.py:188
  387.2 32.0 %all-reduce.17.cloned.1.call-done = f32[128,768]{1,0:T(8,128)} async-done(((f32[128,768]{1,0:T(8,128)}), f32[128,768]{1,0:T(8,128)}) %all-reduce.17.cloned.1.call-update) | async-done | bytes 393232 | tf_op jit(solution)/shard_map/psum | solution.py:188
  426.3 31.6 %all-reduce.19.cloned.1.call-done = f32[128,768]{1,0:T(8,128)} async-done(((f32[128,768]{1,0:T(8,128)}), f32[128,768]{1,0:T(8,128)}) %all-reduce.19.cloned.1.call-update) | async-done | bytes 393232 | tf_op jit(solution)/shard_map/psum | solution.py:191
  490.0 39.6 %all-reduce.29.cloned.1.call-done = (bf16[912,768]{1,0:T(8,128)(2,1)}, bf16[128,768]{1,0:T(8,128)(2,1)}) async-done(((bf16[912,768]{1,0:T(8,128)(2,1)}, bf16[128,768]{1,0:T(8,128)(2,1)}), (bf16[912,768]{1,0:T(8,128)(2,1)}, bf16[128,768]{1,0:T(8,128)(2,1)})) %all-reduce.29.cloned.1.call-update) | async-done | bytes 1597456 | tf_op jit(solution)/shard_map/psum | solution.py:311
  529.6 5.2 fusion.10
  563.7 38.3 %all-reduce.21.cloned.1.call-done = f32[912,768]{1,0:T(8,128)} async-done(((f32[912,768]{1,0:T(8,128)}), f32[912,768]{1,0:T(8,128)}) %all-reduce.21.cloned.1.call-update) | async-done | bytes 2801680 | tf_op jit(solution)/shard_map/psum | solution.py:191
  636.1 69.4 %all-reduce.25.cloned.1.call-done = (f32[128,768]{1,0:T(8,128)}, f32[912,768]{1,0:T(8,128)}, f32[128,768]{1,0:T(8,128)}) async-done(((f32[128,768]{1,0:T(8,128)}, f32[912,768]{1,0:T(8,128)}, f32[128,768]{1,0:T(8,128)}), (f32[128,768]{1,0:T(8,128)}, f32[912,768]{1,0:T(8,128)}, f32[128,768]{1,0:T(8,128)})) %all-reduce.25.cloned.1.call-update) | async-done | bytes 3588112 | tf_op jit(solution)/shard_map/psum | solution.py:188
  709.6 4.9 pad_maximum_fusion.2
  714.5 8.2 copy.443
  754.9 9.9 copy.460
  764.7 11.3 reshape.475
  793.5 149.8 %all-reduce.23.cloned.1.call-done = f32[2,768,768]{1,0,2:T(2,128)} async-done(((f32[2,768,768]{1,0,2:T(2,128)}), f32[2,768,768]{1,0,2:T(2,128)}) %all-reduce.23.cloned.1.call-update) | async-done | bytes 4718608
  946.8 65.8 %reduce-scatter.15.cloned.1.call-done = f32[96,576]{1,0:T(8,128)} async-done(((f32[768,576]{1,0:T(8,128)}), f32[96,576]{1,0:T(8,128)}) %reduce-scatter.15.cloned.1.call-update) | async-done | bytes 221200
  1015.0 95.7 %reduce-scatter.11.cloned.1.call-done = f32[2,96,768]{2,1,0:T(8,128)} async-done(((f32[2,768,768]{2,1,0:T(8,128)}), f32[2,96,768]{2,1,0:T(8,128)}) %reduce-scatter.11.cloned.1.call-update) | async-done | bytes 589840 | tf_op jit(solution)/shard_map/reduce_scatter | solution.py:335
  1112.7 107.9 %reduce-scatter.13.cloned.1.call-done = f32[96,1728]{1,0:T(8,128)} async-done(((f32[768,1728]{1,0:T(8,128)}), f32[96,1728]{1,0:T(8,128)}) %reduce-scatter.13.cloned.1.call-update) | async-done | bytes 663568
  1229.2 44.7 %all-reduce.30 = (f32[]{:T(128)}, f32[3,3,768]{2,1,0:T(4,128)S(1)}, f32[3,3,768]{2,1,0:T(4,128)S(1)}, f32[3,768]{1,0:T(4,128)}, f32[3,768]{1,0:T(4,128)}, /*inde...) all-reduce(f32[]{:T(128)S(6)} %add.359, ...), channel_id=1, replica_groups=mesh['dp'=8,'mp'=4] {'dp','mp'}, use_global_device_ids=true, to_apply=%region_45.46 | all-reduce | flops 33793 | bytes 270344 | tf_op jit(solution)/shard_map/psum | solution.py:368
  (577 shorter events, 270.2 us)
Async XLA Ops:
  7.2 93.6 %all-gather.5.cloned.1.call-start = ((), (), s32[]{:S(2)}) async-start(), calls=%async_computation.4 | async-start | bytes 3981312 | tf_op jit(solution)/shard_map/all_gather | solution.py:176
  9.3 170.0 %all-reduce.15.cloned.1.call-start = ((), (), s32[]{:S(2)}) async-start(), calls=%async_computation.5 | async-start | bytes 5603328 | tf_op jit(solution)/shard_map/psum | solution.py:188
  88.1 146.2 %copy-start.105 = (f32[768]{0:T(1024)}, f32[768]{0:T(1024)S(1)}, u32[]{:S(2)}) copy-start(f32[768]{0:T(1024)S(1)} %get-tuple-element.290) | copy-start | bytes 9220
  88.1 283.1 %copy-start.82 = (f32[768]{0:T(1024)}, f32[768]{0:T(1024)S(1)}, u32[]{:S(2)}) copy-start(f32[768]{0:T(1024)S(1)} %get-tuple-element.289) | copy-start | bytes 9220
  88.1 371.6 %copy-start.85 = (f32[768]{0:T(1024)}, f32[768]{0:T(1024)S(1)}, u32[]{:S(2)}) copy-start(f32[768]{0:T(1024)S(1)} %get-tuple-element.288) | copy-start | bytes 9220
  116.1 118.2 %all-gather.7.cloned.1.call-start = ((), (), s32[]{:S(2)}) async-start(), calls=%async_computation.6 | async-start | bytes 2654208 | tf_op jit(solution)/shard_map/all_gather | solution.py:178
  118.0 169.8 %all-gather.9.cloned.1.call-start = ((), (), s32[]{:S(2)}) async-start(), calls=%async_computation.7 | async-start | bytes 2654208 | tf_op jit(solution)/shard_map/all_gather | solution.py:179
  119.9 241.6 %all-reduce.27.cloned.1.call-start = ((), (), s32[]{:S(2)}) async-start(), calls=%async_computation.17 | async-start | bytes 6389760 | tf_op jit(solution)/shard_map/psum | solution.py:188
  293.2 126.0 %all-reduce.17.cloned.1.call-start = ((), (), s32[]{:S(2)}) async-start(), calls=%async_computation.8 | async-start | bytes 786432 | tf_op jit(solution)/shard_map/psum | solution.py:188
  386.4 71.4 %all-reduce.19.cloned.1.call-start = ((), (), s32[]{:S(2)}) async-start(), calls=%async_computation.9 | async-start | bytes 786432 | tf_op jit(solution)/shard_map/psum | solution.py:191
  425.1 104.5 %all-reduce.29.cloned.1.call-start = ((), (), s32[]{:S(2)}) async-start(), calls=%async_computation.18 | async-start | bytes 3194880 | tf_op jit(solution)/shard_map/psum | solution.py:311
  485.9 116.0 %all-reduce.21.cloned.1.call-start = ((), (), s32[]{:S(2)}) async-start(), calls=%async_computation.10 | async-start | bytes 5603328 | tf_op jit(solution)/shard_map/psum | solution.py:191
  538.8 166.7 %all-reduce.25.cloned.1.call-start = ((), (), s32[]{:S(2)}) async-start(), calls=%async_computation.16 | async-start | bytes 7176192 | tf_op jit(solution)/shard_map/psum | solution.py:188
  629.2 162.2 %reduce-scatter.17.cloned.1.call-start = ((), (), s32[]{:S(2)}) async-start(), calls=%async_computation.14 | async-start | bytes 442368
  632.8 72.7 %copy-start.9 = (bf16[912,768]{1,0:T(8,128)(2,1)S(1)}, bf16[912,768]{1,0:T(8,128)(2,1)}, u32[]{:S(2)}) copy-start(bf16[912,768]{1,0:T(8,128)(2,1)} %param.30) | copy-start | bytes 4202500
  632.8 72.7 %copy-start.93 = (f32[768]{0:T(1024)S(1)}, f32[768]{0:T(1024)}, u32[]{:S(2)}) copy-start(f32[768]{0:T(1024)} %copy-done.92) | copy-start | bytes 9220
  632.8 72.7 %copy-start.95 = (f32[912]{0:T(1024)S(1)}, f32[912]{0:T(1024)}, u32[]{:S(2)}) copy-start(f32[912]{0:T(1024)} %copy-done.94) | copy-start | bytes 10948
  709.6 233.7 %all-reduce.23.cloned.1.call-start = ((), (), s32[]{:S(2)}) async-start(), calls=%async_computation.15 | async-start | bytes 9437184
  722.8 289.8 %reduce-scatter.15.cloned.1.call-start = ((), (), s32[]{:S(2)}) async-start(), calls=%async_computation.13 | async-start | bytes 2211840
  737.4 373.3 %reduce-scatter.11.cloned.1.call-start = ((), (), s32[]{:S(2)}) async-start(), calls=%async_computation.11 | async-start | bytes 5308416 | tf_op jit(solution)/shard_map/reduce_scatter | solution.py:335
  744.9 475.7 %reduce-scatter.13.cloned.1.call-start = ((), (), s32[]{:S(2)}) async-start(), calls=%async_computation.12 | async-start | bytes 6193152
  1015.0 212.4 %copy-start.11 = (f32[128,768]{1,0:T(8,128)S(1)}, f32[128,768]{1,0:T(8,128)}, u32[]{:S(2)}) copy-start(f32[128,768]{1,0:T(8,128)} %copy-done.10) | copy-start | bytes 1179652
  1112.7 161.9 %copy-start.103 = (f32[3,3,768]{2,1,0:T(4,128)S(1)}, f32[3,3,768]{2,1,0:T(4,128)}, u32[]{:S(2)}) copy-start(f32[3,3,768]{2,1,0:T(4,128)} %param.37) | copy-start | bytes 82948
  1112.7 162.0 %copy-start.104 = (f32[3,3,768]{2,1,0:T(4,128)S(1)}, f32[3,3,768]{2,1,0:T(4,128)}, u32[]{:S(2)}) copy-start(f32[3,3,768]{2,1,0:T(4,128)} %param.38) | copy-start | bytes 82948
  (141 other events, 1438.8 us)
Sparse Core Ops, SparseCore 0:
  10.8 89.9 all-gather.4
  116.2 63.0 all-reduce.14
  182.3 51.9 all-gather.6
  237.1 50.6 all-gather.8
  293.3 68.1 all-reduce.26
  386.5 32.6 all-reduce.16
  425.2 32.6 all-reduce.18
  486.1 43.5 all-reduce.28
  538.9 63.0 all-reduce.20
  629.3 76.1 all-reduce.24
  709.7 61.3 reduce-scatter.16
  774.6 168.6 all-reduce.22
  946.8 65.7 reduce-scatter.14
  1016.5 94.1 reduce-scatter.10
  1114.6 105.9 reduce-scatter.12
where the time goes:
time: 1320 us; the launch traced here: 1310 us
  waiting for transfers between devices  849 us (64%)
  local copies, waits for them, and re-layouts  126 us (10%)
  blocking collectives  117 us (9%)
  matrix products  107 us (8%)
  other arithmetic  85.4 us (6%)
  between operations  23.7 us (2%)
    unnamed x19, waiting for transfers between devices  324 us
    psum x4, waiting for transfers between devices, heads_total(): return lax.psum(partial_value, 'mp')  209 us
    reduce_scatter x1, waiting for transfers between devices, on_device(): lax.psum_scatter(jnp.stack([up_enc, up_dec]), 'dp', scatter_dimension=1,...  95.7 us
    unnamed x322, local copies, waits for them, and re-layouts  71.5 us
    psum x2, waiting for transfers between devices, inputs_total(): return lax.psum(partial_value, 'mp')  69.9 us
    all_gather x1, waiting for transfers between devices, on_device(): lax.all_gather(expand.astype(jnp.bfloat16), 'dp', axis=1, tiled=True)  50.8 us
    all_gather x1, waiting for transfers between devices, on_device(): lax.all_gather(contract.astype(jnp.bfloat16), 'dp', axis=2, tiled=True)  48.5 us
    psum x1, blocking collectives, on_device(): lax.psum((local_square, row_in, col_in, row_out, col_out, row_up, col_up,...  44.7 us
  transfers between devices with their start and end apart: 15, of which 14 were waited for; matrix products, arithmetic and copies ran while one was open for 12% of the time, Pallas kernels for 0%

commit v1 on v0

v1 whole, which is shorter than its diff:
```python
import functools

import jax
import jax.numpy as jnp
from jax import lax
from jax.sharding import PartitionSpec as P

D = 768
HEAD_DIM = 64
FF = 3072
PATCHES = 196
SUFFIX = 32
ENC_LEN = 228


EPS_NORM = 1e-06
EPS_STAT = 1e-30
DECAY = 0.99
MOMENTUM = 0.9
AVERAGE = 0.6
RATE_MATRIX = 0.004
RATE_GAIN = 0.05
MASKED = -1000000000.0


def rmsnorm(inputs, gain):
    return inputs * lax.rsqrt(jnp.mean(inputs * inputs, -1, keepdims=True) + EPS_NORM) * gain


def gelu_tanh(values):
    return jax.nn.gelu(values, approximate=True)


def attend(queries, keys_all, values_all, allowed):
    scores = jnp.einsum(
        "pqhd,pkhd->phqk", queries, keys_all, preferred_element_type=jnp.float32
    ) * HEAD_DIM ** (-0.5)
    scores = jnp.where(allowed, scores, MASKED)
    highest = jnp.max(scores, -1, keepdims=True)
    expons = jnp.exp(scores - highest)
    totals = jnp.sum(expons, -1, keepdims=True)
    probs = (expons / totals).astype(jnp.bfloat16)
    mixed = jnp.einsum(
        "phqk,pkhd->pqhd", probs, values_all, preferred_element_type=jnp.float32
    ).astype(jnp.bfloat16)
    return (mixed, highest + jnp.log(totals))


def attend_back(queries, keys_all, values_all, allowed, logsum, grad_mixed):
    scale = HEAD_DIM ** (-0.5)
    scores = (
        jnp.einsum("pqhd,pkhd->phqk", queries, keys_all, preferred_element_type=jnp.float32) * scale
    )
    scores = jnp.where(allowed, scores, MASKED)
    probs = jnp.exp(scores - logsum)
    grad_probs = jnp.einsum(
        "pqhd,pkhd->phqk", grad_mixed, values_all, preferred_element_type=jnp.float32
    )
    grad_scores = (probs * (grad_probs - jnp.sum(grad_probs * probs, -1, keepdims=True))).astype(
        jnp.bfloat16
    )
    grad_query = (
        jnp.einsum("phqk,pkhd->pqhd", grad_scores, keys_all, preferred_element_type=jnp.float32)
        * scale
    ).astype(jnp.bfloat16)
    grad_key = (
        jnp.einsum("phqk,pqhd->pkhd", grad_scores, queries, preferred_element_type=jnp.float32)
        * scale
    ).astype(jnp.bfloat16)
    grad_value = jnp.einsum(
        "phqk,pqhd->pkhd",
        probs.astype(jnp.bfloat16),
        grad_mixed,
        preferred_element_type=jnp.float32,
    ).astype(jnp.bfloat16)
    return (grad_query, grad_key, grad_value)


def update_matrix(
    gradient, weight, rows_old, cols_old, moment, average, row_sum, col_sum, row_index, col_index
):
    full_rows = rows_old.shape[-1]
    full_cols = cols_old.shape[-1]
    rows_new = DECAY * rows_old + (1.0 - DECAY) * (row_sum / full_cols + EPS_STAT)
    cols_new = DECAY * cols_old + (1.0 - DECAY) * (col_sum / full_rows + EPS_STAT)
    row_local = lax.dynamic_slice_in_dim(
        rows_new, row_index * gradient.shape[-2], gradient.shape[-2], rows_new.ndim - 1
    )
    col_local = lax.dynamic_slice_in_dim(
        cols_new, col_index * gradient.shape[-1], gradient.shape[-1], cols_new.ndim - 1
    )
    second = (
        row_local[..., :, None] * col_local[..., None, :] / jnp.mean(rows_new, -1)[..., None, None]
    )
    stepped = gradient * lax.rsqrt(second)
    moment_new = MOMENTUM * moment + stepped
    weight_new = weight - RATE_MATRIX * (MOMENTUM * moment_new + stepped)
    average_new = AVERAGE * average + (1.0 - AVERAGE) * weight_new
    return (
        gradient,
        rows_new,
        cols_new,
        moment_new,
        weight_new,
        average_new,
        weight_new.astype(jnp.bfloat16),
    )


def on_device(
    sizes,
    encoder_in,
    decoder_in,
    decoder_cotangent,
    counts,
    prefix_len,
    suffix_len,
    project_in,
    project_in_rows,
    project_in_cols,
    project_in_moment,
    project_in_average,
    project_out,
    project_out_rows,
    project_out_cols,
    project_out_moment,
    project_out_average,
    expand,
    expand_rows,
    expand_cols,
    expand_moment,
    expand_average,
    contract,
    contract_rows,
    contract_cols,
    contract_moment,
    contract_average,
    norm_gains,
    norm_gains_square,
    norm_gains_moment,
    norm_gains_average,
):

    dp_n, mp_n = sizes
    dp_index = lax.axis_index("dp")
    mp_index = lax.axis_index("mp")
    side = mp_index % 2
    pairs = prefix_len.shape[0]
    half = pairs // 2
    width = project_in.shape[-1]
    heads = width // HEAD_DIM
    hidden = expand.shape[-1]
    block = project_in.shape[-2]
    low = jnp.bfloat16
    f32 = jnp.float32

    def swap(value, axis, bit):
        count = dp_n if axis == "dp" else mp_n
        return lax.ppermute(value, axis, [(i, i ^ bit) for i in range(count)])

    def bits(count):
        return [1 << i for i in range(count.bit_length() - 1)]

    def gather(own):
        if dp_n > 8:
            return lax.all_gather(own, "dp", axis=1, tiled=True)
        rel = {0: own}
        for bit in reversed(bits(dp_n)):
            rel.update({place ^ bit: swap(piece, "dp", bit) for place, piece in list(rel.items())})
        full = jnp.zeros((own.shape[0], dp_n) + own.shape[1:], own.dtype)
        for place, piece in rel.items():
            full = lax.dynamic_update_slice(
                full, piece[:, None], (0, jnp.bitwise_xor(dp_index, place), 0, 0)
            )
        return full.reshape(own.shape[0], dp_n * own.shape[1], own.shape[2])

    def scatter(full):
        if dp_n > 8:
            return lax.psum_scatter(full, "dp", scatter_dimension=1, tiled=True)
        count = full.shape[0]
        keep = full
        for bit in bits(dp_n):
            mine = (dp_index // bit) % 2
            split = keep.reshape(count, -1, 2, block, full.shape[2])
            away = lax.dynamic_index_in_dim(split, 1 - mine, 2, False).astype(low)
            keep = lax.dynamic_index_in_dim(split, mine, 2, False) + swap(away, "dp", bit).astype(f32)
        return keep.reshape(count, block, full.shape[2])

    def total_dp(value):
        for bit in bits(dp_n):
            value = value + swap(value, "dp", bit)
        return value

    def reduce_own(partial):
        away = partial[half:].astype(low)
        mine = partial[:half] + swap(away, "mp", 1).astype(f32)
        for bit in bits(mp_n)[1:]:
            sent = mine.astype(low)
            mine = sent.astype(f32) + swap(sent, "mp", bit).astype(f32)
        return mine

    def both(own):
        return jnp.concatenate([own, swap(own, "mp", 1)], 0)

    def relative(value):
        split = value.reshape((half, 2) + value.shape[1:])
        return jnp.concatenate(
            [
                lax.dynamic_index_in_dim(split, side, 1, False),
                lax.dynamic_index_in_dim(split, 1 - side, 1, False),
            ],
            0,
        )

    def absolute(own):
        other = swap(own, "mp", 1)
        even = jnp.where(side == 0, own, other)
        odd = jnp.where(side == 0, other, own)
        return jnp.stack([even, odd], 1).reshape((pairs,) + own.shape[1:])

    gain_low = norm_gains.astype(low)
    gain_full = lax.dynamic_update_slice(
        jnp.zeros((5, D), low), gain_low, (0, dp_index * block)
    )
    gain_rows = total_dp(gain_full).astype(f32)

    def attention_block(layer):
        return jnp.concatenate(
            [project_in[layer, 0], project_in[layer, 1], project_in[layer, 2], project_out[layer].T], 1
        ).astype(low)[None]

    def feed_block(layer):
        return jnp.stack([expand[layer], contract[layer].T]).astype(low)

    own_blocks = [
        attention_block(0), feed_block(0), attention_block(1), attention_block(2), feed_block(1)
    ]
    enc_att, enc_feed, self_att, cross_att, dec_feed = [gather(item) for item in own_blocks]
    enc_att, self_att, cross_att = enc_att[0], self_att[0], cross_att[0]

    position = jnp.arange(pairs)
    own_place = 2 * jnp.arange(half) + side
    place_rel = jnp.concatenate([own_place, 2 * jnp.arange(half) + 1 - side])
    prefix_rel = relative(prefix_len)
    suffix_rel = relative(suffix_len)
    images = place_rel < counts[0, 0]
    active = place_rel < counts[0, 0] + counts[0, 1]
    place = jnp.arange(ENC_LEN)
    key_ok = jnp.where(
        place[None, :] < PATCHES, images[:, None], place[None, :] - PATCHES < prefix_rel[:, None]
    )[:, None, None, :]
    steps = jnp.arange(SUFFIX)
    causal = (
        (steps[None, None, :] <= steps[None, :, None])
        & (steps[None, None, :] < suffix_rel[:, None, None])
    )[:, None]
    live = active[:, None] & (steps[None, :] < suffix_rel[:, None])

    def mm(left, right):
        return jnp.einsum("ptd,dm->ptm", left, right, preferred_element_type=f32)

    def mm_t(left, right):
        return jnp.einsum("ptm,dm->ptd", left, right, preferred_element_type=f32)

    def outer(left, right):
        return jnp.einsum("ptd,ptm->dm", left, right, preferred_element_type=f32)

    def split_heads(flat):
        return flat.reshape(flat.shape[:2] + (heads, HEAD_DIM))

    def attn_forward(query_in, key_in, weight, allowed):
        queries = mm(query_in, weight[:, :width]).astype(low)
        keys_all = mm(key_in, weight[:, width : 2 * width]).astype(low)
        values_all = mm(key_in, weight[:, 2 * width : 3 * width]).astype(low)
        mixed, logsum = attend(
            split_heads(queries), split_heads(keys_all), split_heads(values_all), allowed
        )
        flat = mixed.reshape(queries.shape)
        partial = mm_t(flat, weight[:, 3 * width :])
        return partial, (queries, keys_all, values_all, flat, logsum)

    def attn_backward(query_in, key_in, weight, allowed, stored, grad_low):
        queries, keys_all, values_all, flat, logsum = stored
        grad_out = outer(grad_low, flat)
        grad_mixed = mm(grad_low, weight[:, 3 * width :]).astype(low)
        grad_query, grad_key, grad_value = attend_back(
            split_heads(queries),
            split_heads(keys_all),
            split_heads(values_all),
            allowed,
            logsum,
            split_heads(grad_mixed),
        )
        grad_query = grad_query.reshape(queries.shape)
        grad_key = grad_key.reshape(keys_all.shape)
        grad_value = grad_value.reshape(keys_all.shape)
        grads = jnp.concatenate(
            [outer(query_in, grad_query), outer(key_in, grad_key), outer(key_in, grad_value), grad_out], 1
        )
        back_query = mm_t(grad_query, weight[:, :width])
        back_key = mm_t(grad_key, weight[:, width : 2 * width]) + mm_t(
            grad_value, weight[:, 2 * width : 3 * width]
        )
        return grads[None], back_query, back_key

    def feed_forward(normed_low, weight):
        upper = mm(normed_low, weight[0])
        active_low = gelu_tanh(upper).astype(low)
        return mm_t(active_low, weight[1]), (upper, active_low)

    def feed_backward(normed_low, weight, stored, grad_low):
        upper, active_low = stored
        grad_down = outer(grad_low, active_low)
        grad_active = mm(grad_low, weight[1])
        pull = jax.vjp(gelu_tanh, upper)[1]
        grad_upper = pull(grad_active)[0].astype(low)
        grad_up = outer(normed_low, grad_upper)
        back = mm_t(grad_upper, weight[0])
        return jnp.stack([grad_up, grad_down]), back

    enc_rel = relative(encoder_in.reshape(pairs, ENC_LEN, D))
    dec_rel = relative(decoder_in.reshape(pairs, SUFFIX, D))
    cot_rel = relative(decoder_cotangent.reshape(pairs, SUFFIX, D))
    enc_x = enc_rel.astype(f32)
    dec_x = dec_rel.astype(f32)

    norm_enc = rmsnorm(enc_x, gain_rows[0]).astype(low)
    partial, kept_enc = attn_forward(norm_enc, norm_enc, enc_att, key_ok)
    norm_self = rmsnorm(dec_x, gain_rows[2]).astype(low)
    enc_mid = enc_x[:half] + reduce_own(partial)
    partial, kept_self = attn_forward(norm_self, norm_self, self_att, causal)
    dec_one = dec_x[:half] + reduce_own(partial)
    norm_mid = both(rmsnorm(enc_mid, gain_rows[1]).astype(low))
    partial, kept_feed = feed_forward(norm_mid, enc_feed)
    memory = both((enc_mid + reduce_own(partial)).astype(low))
    norm_cross = both(rmsnorm(dec_one, gain_rows[3]).astype(low))
    partial, kept_cross = attn_forward(norm_cross, memory, cross_att, key_ok)
    dec_two = dec_one + reduce_own(partial)
    norm_last = both(rmsnorm(dec_two, gain_rows[4]).astype(low))
    partial, kept_last = feed_forward(norm_last, dec_feed)
    out_own = dec_two + reduce_own(partial)
    decoder_out = absolute(out_own).reshape(pairs * SUFFIX, D)

    cot = jnp.where(live[:, :, None], cot_rel, f32(0.0))
    grads_dec, back = feed_backward(norm_last, dec_feed, kept_last, cot.astype(low))
    sum_dec = scatter(grads_dec)
    pull = jax.vjp(rmsnorm, dec_two, gain_rows[4])[1]
    grad_in, gain_four = pull(reduce_own(back))
    grad = cot[:half] + grad_in
    grads_cross, back_query, back_memory = attn_backward(
        norm_cross, memory, cross_att, key_ok, kept_cross, both(grad.astype(low))
    )
    sum_cross = scatter(grads_cross)
    grad_enc = reduce_own(back_memory)
    pull = jax.vjp(rmsnorm, dec_one, gain_rows[3])[1]
    grad_in, gain_three = pull(reduce_own(back_query))
    grad = grad + grad_in
    grads_self, back_query, back_key = attn_backward(
        norm_self, norm_self, self_att, causal, kept_self, both(grad.astype(low))
    )
    sum_self = scatter(grads_self)
    pull = jax.vjp(rmsnorm, dec_x[:half], gain_rows[2])[1]
    grad_in, gain_two = pull(reduce_own(back_query + back_key))
    decoder_in_grad = absolute(grad + grad_in).reshape(pairs * SUFFIX, D)

    grads_enc, back = feed_backward(norm_mid, enc_feed, kept_feed, both(grad_enc.astype(low)))
    sum_enc = scatter(grads_enc)
    pull = jax.vjp(rmsnorm, enc_mid, gain_rows[1])[1]
    grad_in, gain_one = pull(reduce_own(back))
    grad_enc = grad_enc + grad_in
    grads_att, back_query, back_key = attn_backward(
        norm_enc, norm_enc, enc_att, key_ok, kept_enc, both(grad_enc.astype(low))
    )
    sum_att = scatter(grads_att)
    pull = jax.vjp(rmsnorm, enc_x[:half], gain_rows[0])[1]
    grad_in, gain_zero = pull(reduce_own(back_query + back_key))
    encoder_in_grad = absolute(grad_enc + grad_in).reshape(pairs * ENC_LEN, D)

    gain_grad = jnp.stack([gain_zero, gain_one, gain_two, gain_three, gain_four])
    gain_grad = total_dp(gain_grad + swap(gain_grad, "mp", 1))
    grad_gain = lax.dynamic_slice(gain_grad, (0, dp_index * block), (5, block))

    att = jnp.concatenate([sum_att, sum_self, sum_cross], 0)
    grad_in = att[:, :, : 3 * width].reshape(3, block, 3, width).transpose(0, 2, 1, 3)
    grad_out = att[:, :, 3 * width :].transpose(0, 2, 1)
    grad_up = jnp.stack([sum_enc[0], sum_dec[0]])
    grad_down = jnp.stack([sum_enc[1], sum_dec[1]]).transpose(0, 2, 1)

    squares = [item * item for item in (grad_in, grad_out, grad_up, grad_down)]
    rows_part = [jnp.sum(item, -1) for item in squares]
    cols_part = [jnp.sum(item, -2) for item in squares]
    along_dp = [rows_part[0], cols_part[1], rows_part[2], cols_part[3]]
    along_mp = [cols_part[0], rows_part[1], cols_part[2], rows_part[3]]

    def spread_all(parts, axis, other):
        index, count = (dp_index, dp_n) if axis == "dp" else (mp_index, mp_n)
        flat = jnp.concatenate([item.reshape(-1) for item in parts])
        for bit in bits(mp_n if axis == "dp" else dp_n):
            flat = flat + swap(flat, other, bit)
        full = lax.dynamic_update_slice(
            jnp.zeros((count, flat.shape[0]), f32), flat[None], (index, 0)
        )
        for bit in bits(count):
            full = full + swap(full, axis, bit)
        result, start = [], 0
        for item in parts:
            size = item.size
            piece = full[:, start : start + size].reshape((count,) + item.shape)
            start += size
            piece = jnp.moveaxis(piece, 0, -2)
            result.append(piece.reshape(item.shape[:-1] + (count * item.shape[-1],)))
        return result

    row_in, col_out, row_up, col_down = spread_all(along_dp, "dp", "mp")
    col_in, row_out, col_up, row_down = spread_all(along_mp, "mp", "dp")
    total = (
        jnp.sum(row_in) + jnp.sum(row_out) + jnp.sum(row_up) + jnp.sum(row_down)
        + jnp.sum(gain_grad * gain_grad)
    )
    grad_norm = jnp.sqrt(total)
    factor = jnp.minimum(1.0, 1.0 / grad_norm)
    squared = factor * factor
    row_in, col_in, row_out, col_out = (
        row_in * squared,
        col_in * squared,
        row_out * squared,
        col_out * squared,
    )
    row_up, col_up, row_down, col_down = (
        row_up * squared,
        col_up * squared,
        row_down * squared,
        col_down * squared,
    )
    grad_in, grad_out, grad_up, grad_down = (
        grad_in * factor,
        grad_out * factor,
        grad_up * factor,
        grad_down * factor,
    )
    grad_gain = grad_gain * factor
    pin = update_matrix(
        grad_in,
        project_in,
        project_in_rows,
        project_in_cols,
        project_in_moment,
        project_in_average,
        row_in,
        col_in,
        dp_index,
        mp_index,
    )
    pout = update_matrix(
        grad_out,
        project_out,
        project_out_rows,
        project_out_cols,
        project_out_moment,
        project_out_average,
        row_out,
        col_out,
        mp_index,
        dp_index,
    )
    pexp = update_matrix(
        grad_up,
        expand,
        expand_rows,
        expand_cols,
        expand_moment,
        expand_average,
        row_up,
        col_up,
        dp_index,
        mp_index,
    )
    pcon = update_matrix(
        grad_down,
        contract,
        contract_rows,
        contract_cols,
        contract_moment,
        contract_average,
        row_down,
        col_down,
        mp_index,
        dp_index,
    )
    square_new = DECAY * norm_gains_square + (1.0 - DECAY) * (grad_gain * grad_gain + EPS_STAT)
    stepped = grad_gain * lax.rsqrt(square_new)
    moment_new = MOMENTUM * norm_gains_moment + stepped
    gains_new = norm_gains - RATE_GAIN * (MOMENTUM * moment_new + stepped)
    average_new = AVERAGE * norm_gains_average + (1.0 - AVERAGE) * gains_new
    return (
        decoder_out,
        encoder_in_grad,
        decoder_in_grad,
        grad_norm,
        pin[0],
        pin[1],
        pin[2],
        pin[3],
        pin[4],
        pin[5],
        pin[6],
        pout[0],
        pout[1],
        pout[2],
        pout[3],
        pout[4],
        pout[5],
        pout[6],
        pexp[0],
        pexp[1],
        pexp[2],
        pexp[3],
        pexp[4],
        pexp[5],
        pexp[6],
        pcon[0],
        pcon[1],
        pcon[2],
        pcon[3],
        pcon[4],
        pcon[5],
        pcon[6],
        grad_gain,
        square_new,
        moment_new,
        gains_new,
        average_new,
        gains_new.astype(jnp.bfloat16),
    )


def solution(mesh):
    placed = (
        P("dp", None),
        P("dp", None),
        P("dp", None),
        P("dp", None),
        P("dp"),
        P("dp"),
        P(None, None, "dp", "mp"),
        P(),
        P(),
        P(None, None, "dp", "mp"),
        P(None, None, "dp", "mp"),
        P(None, "mp", "dp"),
        P(),
        P(),
        P(None, "mp", "dp"),
        P(None, "mp", "dp"),
        P(None, "dp", "mp"),
        P(),
        P(),
        P(None, "dp", "mp"),
        P(None, "dp", "mp"),
        P(None, "mp", "dp"),
        P(),
        P(),
        P(None, "mp", "dp"),
        P(None, "mp", "dp"),
        P(None, "dp"),
        P(None, "dp"),
        P(None, "dp"),
        P(None, "dp"),
    )
    return jax.shard_map(
        functools.partial(on_device, (mesh.shape["dp"], mesh.shape["mp"])),
        mesh=mesh,
        in_specs=placed,
        out_specs=(
            P("dp", None),
            P("dp", None),
            P("dp", None),
            P(),
            P(None, None, "dp", "mp"),
            P(),
            P(),
            P(None, None, "dp", "mp"),
            P(None, None, "dp", "mp"),
            P(None, None, "dp", "mp"),
            P(None, None, "dp", "mp"),
            P(None, "mp", "dp"),
            P(),
            P(),
            P(None, "mp", "dp"),
            P(None, "mp", "dp"),
            P(None, "mp", "dp"),
            P(None, "mp", "dp"),
            P(None, "dp", "mp"),
            P(),
            P(),
            P(None, "dp", "mp"),
            P(None, "dp", "mp"),
            P(None, "dp", "mp"),
            P(None, "dp", "mp"),
            P(None, "mp", "dp"),
            P(),
            P(),
            P(None, "mp", "dp"),
            P(None, "mp", "dp"),
            P(None, "mp", "dp"),
            P(None, "mp", "dp"),
            P(None, "dp"),
            P(None, "dp"),
            P(None, "dp"),
            P(None, "dp"),
            P(None, "dp"),
            P(None, "dp"),
        ),
        check_vma=False,
    )
```

time: 1320 us -> 639 us (0.48)
  waiting for transfers between devices: 849 us -> 219 us
  blocking collectives: 117 us -> 0 us
  starting transfers between devices: 1.88 us -> 70 us
  local copies, waits for them, and re-layouts: 126 us -> 162 us
  matrix products: 107 us -> 72.8 us
  between operations: 23.7 us -> 10.1 us
    unnamed x19 -> x0, waiting for transfers between devices: 324 us -> none
    psum x7 -> x0, waiting for transfers between devices: 319 us -> none  [the longest x4 209 us: heads_total(): return lax.psum(partial_value, 'mp')]
    ppermute x0 -> x100, waiting for transfers between devices: none -> 219 us  [swap(): return lax.ppermute(value, axis, [(i, i ^ bit) for i in range(count)])]
    all_gather x3 -> x0, waiting for transfers between devices: 111 us -> none  [the longest x1 50.8 us: on_device(): lax.all_gather(expand.astype(jnp.bfloat16), 'dp', axis=1, tiled=True)]
    reduce_scatter x1 -> x0, waiting for transfers between devices: 95.7 us -> none  [on_device(): lax.psum_scatter(jnp.stack([up_enc, up_dec]), 'dp', scatter_dimension=1,...]
    all_gather x2 -> x0, blocking collectives: 72.4 us -> none  [the longest x1 44.4 us: on_device(): lax.all_gather(project_out.astype(jnp.bfloat16), 'dp', axis=2, tiled=True)]
    ppermute x0 -> x100, starting transfers between devices: none -> 70 us  [swap(): return lax.ppermute(value, axis, [(i, i ^ bit) for i in range(count)])]
    psum x1 -> x0, blocking collectives: 44.7 us -> none  [on_device(): lax.psum((local_square, row_in, col_in, row_out, col_out, row_up, col_up,...]
  transfers between devices with their start and end apart: 15 -> 100, of which waited for: 14 -> 42; matrix products, arithmetic and copies ran while one was open for 12% -> 45% of each run, Pallas kernels for 0% -> 0%
where the time goes in v1:
time: 639 us; the launch traced here: 632 us
  waiting for transfers between devices  219 us (34%)
  local copies, waits for them, and re-layouts  162 us (25%)
  other arithmetic  97.8 us (15%)
  matrix products  72.8 us (11%)
  starting transfers between devices  70 us (11%)
  between operations  10.1 us (2%)
    ppermute x100, waiting for transfers between devices, swap(): return lax.ppermute(value, axis, [(i, i ^ bit) for i in range(count)])  219 us
    ppermute x100, starting transfers between devices, swap(): return lax.ppermute(value, axis, [(i, i ^ bit) for i in range(count)])  70 us
    unnamed x502, local copies, waits for them, and re-layouts  41.7 us
    dot_general x16, matrix products, mm_t(): return jnp.einsum('ptm,dm->ptd', left, right, preferred_element_type=f32)  25.1 us
    dynamic_update_slice x33, local copies, waits for them, and re-layouts, gather(): lax.dynamic_update_slice(full, piece[:, None], (0, jnp.bitwise_xor(dp_ind...  24.7 us
    dot_general x16, matrix products, mm(): return jnp.einsum('ptd,dm->ptm', left, right, preferred_element_type=f32)  22.2 us
    dot_general x16, matrix products, outer(): return jnp.einsum('ptd,ptm->dm', left, right, preferred_element_type=f32)  13.7 us
  transfers between devices with their start and end apart: 100, of which 42 were waited for; matrix products, arithmetic and copies ran while one was open for 45% of the time, Pallas kernels for 0%

profile of v1, /device:TPU:0, one launch (start us, length us, event | category | flops | bytes accessed | tf_op | source)
XLA Modules:
  0.0 631.7 jit_solution(3016046597003207833)
XLA Ops:
  5.4 4.0 collective-permute-start.3
  65.5 7.4 %collective-permute-done.32 = bf16[1,96,768]{2,1,0:T(8,128)(2,1)S(1)} collective-permute-done((bf16[1,96,768]{2,1,0:T(8,128)(2,1)}, bf16[1,96,768]{2,1,0:T(8,128)(2,1)S(1)}, u32[]{:S(2)}, u32[]{:S(2)}) %collective-permute-start.32) | collective-permute-done | bytes 147488 | tf_op jit(solution)/shard_map/ppermute | solution.py:159
  74.2 13.3 %collective-permute-done.43 = bf16[2,96,768]{2,1,0:T(8,128)(2,1)} collective-permute-done((bf16[2,96,768]{2,1,0:T(8,128)(2,1)}, bf16[2,96,768]{2,1,0:T(8,128)(2,1)}, u32[]{:S(2)}, u32[]{:S(2)}) %collective-permute-start.43) | collective-permute-done | bytes 294944 | tf_op jit(solution)/shard_map/ppermute | solution.py:159
  88.6 6.8 %collective-permute-done.22 = bf16[2,96,768]{2,1,0:T(8,128)(2,1)S(1)} collective-permute-done((bf16[2,96,768]{2,1,0:T(8,128)(2,1)}, bf16[2,96,768]{2,1,0:T(8,128)(2,1)S(1)}, u32[]{:S(2)}, u32[]{:S(2)}) %collective-permute-start.22) | collective-permute-done | bytes 294944 | tf_op jit(solution)/shard_map/ppermute | solution.py:159
  100.9 4.6 collective-permute-done.5
  105.5 5.3 collective-permute-done.14
  114.6 6.5 %collective-permute-done.7 = bf16[1,96,768]{2,1,0:T(8,128)(2,1)S(1)} collective-permute-done((bf16[1,96,768]{2,1,0:T(8,128)(2,1)}, bf16[1,96,768]{2,1,0:T(8,128)(2,1)S(1)}, u32[]{:S(2)}, u32[]{:S(2)}) %collective-permute-start.7) | collective-permute-done | bytes 147488 | tf_op jit(solution)/shard_map/ppermute | solution.py:159
  121.9 6.2 collective-permute-done.16
  128.9 6.0 collective-permute-done.17
  157.3 3.5 fusion.77
  183.9 10.6 %collective-permute-done.20 = bf16[2,228,768]{2,0,1:T(2,128)(2,1)S(1)} collective-permute-done((bf16[2,228,768]{2,0,1:T(2,128)(2,1)S(1)}, bf16[2,228,768]{2,0,1:T(2,128)(2,1)S(1)}, u32[]{:S(2)}, u32[]{:S(2)}) %collective-permute-start.20) | collective-permute-done | bytes 700448 | tf_op jit(solution)/shard_map/ppermute | solution.py:159
  215.6 17.0 %collective-permute-done.11 = bf16[2,32,768]{2,1,0:T(8,128)(2,1)S(1)} collective-permute-done((bf16[2,32,768]{2,1,0:T(8,128)(2,1)S(1)}, bf16[2,32,768]{2,1,0:T(8,128)(2,1)S(1)}, u32[]{:S(2)}, u32[]{:S(2)}) %collective-permute-start.11) | collective-permute-done | bytes 98336 | tf_op jit(solution)/shard_map/ppermute | solution.py:159
  264.7 3.5 collective-permute-done.54
  353.5 10.8 %collective-permute-done.57 = bf16[2,228,768]{2,0,1:T(2,128)(2,1)S(1)} collective-permute-done((bf16[2,228,768]{2,0,1:T(2,128)(2,1)S(1)}, bf16[2,228,768]{2,0,1:T(2,128)(2,1)S(1)}, u32[]{:S(2)}, u32[]{:S(2)}) %collective-permute-start.57) | collective-permute-done | bytes 700448 | tf_op jit(solution)/shard_map/ppermute | solution.py:159
  366.5 11.3 %collective-permute-done.75 = bf16[1,2,96,768]{3,2,1,0:T(8,128)(2,1)S(1)} collective-permute-done((bf16[1,2,96,768]{3,2,1,0:T(8,128)(2,1)S(1)}, bf16[1,2,96,768]{3,2,1,0:T(8,128)(2,1)S(1)}, u32[]{:S(2)}, u32[]{:S(2)}) %collective-permute-start.75) | collective-permute-done | bytes 294944 | tf_op jit(solution)/shard_map/ppermute | solution.py:159
  378.0 3.5 fusion.6
  388.9 8.2 %collective-permute-done.76 = bf16[1,1,96,768]{3,2,1,0:T(8,128)(2,1)S(1)} collective-permute-done((bf16[1,1,96,768]{3,2,1,0:T(8,128)(2,1)S(1)}, bf16[1,1,96,768]{3,2,1,0:T(8,128)(2,1)S(1)}, u32[]{:S(2)}, u32[]{:S(2)}) %collective-permute-start.76) | collective-permute-done | bytes 147488 | tf_op jit(solution)/shard_map/ppermute | solution.py:159
  400.5 14.8 %collective-permute-done.80 = bf16[2,4,96,768]{3,2,1,0:T(8,128)(2,1)S(1)} collective-permute-done((bf16[2,4,96,768]{3,2,1,0:T(8,128)(2,1)S(1)}, bf16[2,4,96,768]{3,2,1,0:T(8,128)(2,1)S(1)}, u32[]{:S(2)}, u32[]{:S(2)}) %collective-permute-start.80) | collective-permute-done | bytes 1179680 | tf_op jit(solution)/shard_map/ppermute | solution.py:159
  419.5 11.2 %collective-permute-done.81 = bf16[2,2,96,768]{3,2,1,0:T(8,128)(2,1)S(1)} collective-permute-done((bf16[2,2,96,768]{3,2,1,0:T(8,128)(2,1)S(1)}, bf16[2,2,96,768]{3,2,1,0:T(8,128)(2,1)S(1)}, u32[]{:S(2)}, u32[]{:S(2)}) %collective-permute-start.81) | collective-permute-done | bytes 589856 | tf_op jit(solution)/shard_map/ppermute | solution.py:159
  431.9 14.0 %collective-permute-done.82 = bf16[2,1,96,768]{3,2,1,0:T(8,128)(2,1)S(1)} collective-permute-done((bf16[2,1,96,768]{3,2,1,0:T(8,128)(2,1)S(1)}, bf16[2,1,96,768]{3,2,1,0:T(8,128)(2,1)S(1)}, u32[]{:S(2)}, u32[]{:S(2)}) %collective-permute-start.82) | collective-permute-done | bytes 294944 | tf_op jit(solution)/shard_map/ppermute | solution.py:159
  467.2 9.7 %collective-permute-done.71 = bf16[1,4,96,768]{3,2,1,0:T(8,128)(2,1)} collective-permute-done((bf16[1,4,96,768]{3,2,1,0:T(8,128)(2,1)}, bf16[1,4,96,768]{3,2,1,0:T(8,128)(2,1)}, u32[]{:S(2)}, u32[]{:S(2)}) %collective-permute-start.71) | collective-permute-done | bytes 589856 | tf_op jit(solution)/shard_map/ppermute | solution.py:159
  478.9 7.4 %collective-permute-done.72 = bf16[1,2,96,768]{3,2,1,0:T(8,128)(2,1)S(1)} collective-permute-done((bf16[1,2,96,768]{3,2,1,0:T(8,128)(2,1)S(1)}, bf16[1,2,96,768]{3,2,1,0:T(8,128)(2,1)S(1)}, u32[]{:S(2)}, u32[]{:S(2)}) %collective-permute-start.72) | collective-permute-done | bytes 294944 | tf_op jit(solution)/shard_map/ppermute | solution.py:159
  489.6 4.8 collective-permute-done.73
  553.7 10.9 %collective-permute-done.95 = f32[4,5376]{1,0:T(4,128)S(1)} collective-permute-done((f32[4,5376]{1,0:T(4,128)}, f32[4,5376]{1,0:T(4,128)S(1)}, u32[]{:S(2)}, u32[]{:S(2)}) %collective-permute-start.95) | collective-permute-done | bytes 86048 | tf_op jit(solution)/shard_map/ppermute | solution.py:159
  (1081 shorter events, 420.1 us)
Async XLA Ops:
  5.4 52.6 %collective-permute-start.3 = (bf16[1,96,768]{2,1,0:T(8,128)(2,1)}, bf16[1,96,768]{2,1,0:T(8,128)(2,1)}, u32[]{:S(2)}, u32[]{:S(2)}) collective-permute-start(bf16[1,96,768]{2,1,0:T(8,128)(2,1)} %pad_maximum_fusion.26), channel_id=1, source_target_pairs={{0,16},{4,20},{8,24},{12,28},{16,0},{20,4},{24,8},{28,12},{1,17},{... | collective-permute-start | bytes 442376 | tf_op jit(solution)/shard_map/ppermute | solution.py:159
  9.5 52.8 %collective-permute-start.4 = (bf16[1,96,768]{2,1,0:T(8,128)(2,1)}, bf16[1,96,768]{2,1,0:T(8,128)(2,1)}, u32[]{:S(2)}, u32[]{:S(2)}) collective-permute-start(bf16[1,96,768]{2,1,0:T(8,128)(2,1)} %pad_maximum_fusion.26), channel_id=1, source_target_pairs={{0,8},{4,12},{8,0},{12,4},{16,24},{20,28},{24,16},{28,20},{1,9},{5... | collective-permute-start | bytes 442376 | tf_op jit(solution)/shard_map/ppermute | solution.py:159
  11.1 100.4 %collective-permute-start.6 = (bf16[1,96,768]{2,1,0:T(8,128)(2,1)}, bf16[1,96,768]{2,1,0:T(8,128)(2,1)}, u32[]{:S(2)}, u32[]{:S(2)}) collective-permute-start(bf16[1,96,768]{2,1,0:T(8,128)(2,1)} %pad_maximum_fusion.26), channel_id=1, source_target_pairs={{0,4},{4,0},{8,12},{12,8},{16,20},{20,16},{24,28},{28,24},{1,5},{5... | collective-permute-start | bytes 442376 | tf_op jit(solution)/shard_map/ppermute | solution.py:159
  13.3 47.7 %collective-permute-start.12 = (bf16[1,96,768]{2,1,0:T(8,128)(2,1)}, bf16[1,96,768]{2,1,0:T(8,128)(2,1)}, u32[]{:S(2)}, u32[]{:S(2)}) collective-permute-start(bf16[1,96,768]{2,1,0:T(8,128)(2,1)} %pad_maximum_fusion.27), channel_id=1, source_target_pairs={{0,16},{4,20},{8,24},{12,28},{16,0},{20,4},{24,8},{28,12},{1,17},{... | collective-permute-start | bytes 442376 | tf_op jit(solution)/shard_map/ppermute | solution.py:159
  58.0 55.8 %collective-permute-start.15 = (bf16[1,96,768]{2,1,0:T(8,128)(2,1)}, bf16[1,96,768]{2,1,0:T(8,128)(2,1)S(1)}, u32[]{:S(2)}, u32[]{:S(2)}) collective-permute-start(bf16[1,96,768]{2,1,0:T(8,128)(2,1)} %pad_maximum_fusion.27), channel_id=1, source_target_pairs={{0,4},{4,0},{8,12},{12,8},{16,20},{20,16},{24,28},{28,24},{1,5},{5... | collective-permute-start | bytes 442376 | tf_op jit(solution)/shard_map/ppermute | solution.py:159
  64.8 73.8 %collective-permute-start.35 = (bf16[1,96,768]{2,1,0:T(8,128)(2,1)}, bf16[1,96,768]{2,1,0:T(8,128)(2,1)S(1)}, u32[]{:S(2)}, u32[]{:S(2)}) collective-permute-start(bf16[1,96,768]{2,1,0:T(8,128)(2,1)} %pad_maximum_fusion.28), channel_id=1, source_target_pairs={{0,4},{4,0},{8,12},{12,8},{16,20},{20,16},{24,28},{28,24},{1,5},{5... | collective-permute-start | bytes 442376 | tf_op jit(solution)/shard_map/ppermute | solution.py:159
  95.4 70.6 %collective-permute-start.46 = (bf16[2,96,768]{2,1,0:T(8,128)(2,1)}, bf16[2,96,768]{2,1,0:T(8,128)(2,1)}, u32[]{:S(2)}, u32[]{:S(2)}) collective-permute-start(bf16[2,96,768]{2,1,0:T(8,128)(2,1)} %pad_maximum_fusion.21), channel_id=1, source_target_pairs={{0,4},{4,0},{8,12},{12,8},{16,20},{20,16},{24,28},{28,24},{1,5},{5... | collective-permute-start | bytes 884744 | tf_op jit(solution)/shard_map/ppermute | solution.py:159
  110.8 68.6 %collective-permute-start.25 = (bf16[2,96,768]{2,1,0:T(8,128)(2,1)}, bf16[2,96,768]{2,1,0:T(8,128)(2,1)}, u32[]{:S(2)}, u32[]{:S(2)}) collective-permute-start(bf16[2,96,768]{2,1,0:T(8,128)(2,1)} %pad_maximum_fusion.20), channel_id=1, source_target_pairs={{0,4},{4,0},{8,12},{12,8},{16,20},{20,16},{24,28},{28,24},{1,5},{5... | collective-permute-start | bytes 884744 | tf_op jit(solution)/shard_map/ppermute | solution.py:159
  142.0 66.9 %collective-permute-start.38 = (bf16[1,96,768]{2,1,0:T(8,128)(2,1)}, bf16[1,96,768]{2,1,0:T(8,128)(2,1)}, u32[]{:S(2)}, u32[]{:S(2)}) collective-permute-start(bf16[1,96,768]{2,1,0:T(8,128)(2,1)} %collective-permute-done.34), channel_id=1, source_target_pairs={{0,4},{4,0},{8,12},{12,8},{16,20},{20,16},{24,28},{28,24},{1,5},{5... | collective-permute-start | bytes 442376 | tf_op jit(solution)/shard_map/ppermute | solution.py:159
  145.3 22.4 %collective-permute-start.47 = (bf16[2,96,768]{2,1,0:T(8,128)(2,1)}, bf16[2,96,768]{2,1,0:T(8,128)(2,1)}, u32[]{:S(2)}, u32[]{:S(2)}) collective-permute-start(bf16[2,96,768]{2,1,0:T(8,128)(2,1)} %collective-permute-done.43), channel_id=1, source_target_pairs={{0,4},{4,0},{8,12},{12,8},{16,20},{20,16},{24,28},{28,24},{1,5},{5... | collective-permute-start | bytes 884744 | tf_op jit(solution)/shard_map/ppermute | solution.py:159
  171.8 25.2 %collective-permute-start.27 = (bf16[2,96,768]{2,1,0:T(8,128)(2,1)S(1)}, bf16[2,96,768]{2,1,0:T(8,128)(2,1)S(1)}, u32[]{:S(2)}, u32[]{:S(2)}) collective-permute-start(bf16[2,96,768]{2,1,0:T(8,128)(2,1)S(1)} %copy-done.152), channel_id=1, source_target_pairs={{0,4},{4,0},{8,12},{12,8},{16,20},{20,16},{24,28},{28,24},{1,5},{5... | collective-permute-start | bytes 884744 | tf_op jit(solution)/shard_map/ppermute | solution.py:159
  271.7 76.2 %collective-permute-start.83 = (bf16[2,4,96,768]{3,2,1,0:T(8,128)(2,1)}, bf16[2,4,96,768]{3,2,1,0:T(8,128)(2,1)}, u32[]{:S(2)}, u32[]{:S(2)}) collective-permute-start(bf16[2,4,96,768]{3,2,1,0:T(8,128)(2,1)} %fusion.44), channel_id=1, source_target_pairs={{0,4},{4,0},{8,12},{12,8},{16,20},{20,16},{24,28},{28,24},{1,5},{5... | collective-permute-start | bytes 3538952 | tf_op jit(solution)/shard_map/ppermute | solution.py:159
  273.2 36.7 %collective-permute-start.52 = (f32[2,32,768]{2,1,0:T(8,128)}, f32[2,32,768]{2,1,0:T(8,128)}, u32[]{:S(2)}, u32[]{:S(2)}) collective-permute-start(f32[2,32,768]{2,1,0:T(8,128)} %get-tuple-element.260), channel_id=1, source_target_pairs={{0,1},{1,0},{2,3},{3,2},{4,5},{5,4},{6,7},{7,6},{8,9},{9,8},{10,11... | collective-permute-start | bytes 589832 | tf_op jit(solution)/shard_map/ppermute | solution.py:159
  296.7 47.8 %collective-permute-start.56 = (bf16[2,228,768]{2,0,1:T(2,128)(2,1)}, bf16[2,228,768]{2,0,1:T(2,128)(2,1)}, u32[]{:S(2)}, u32[]{:S(2)}) collective-permute-start(bf16[2,228,768]{2,0,1:T(2,128)(2,1)} %copy.374), channel_id=1, source_target_pairs={{0,1},{1,0},{2,3},{3,2},{4,5},{5,4},{6,7},{7,6},{8,9},{9,8},{10,11... | collective-permute-start | bytes 2101256 | tf_op jit(solution)/shard_map/ppermute | solution.py:159
  307.0 34.7 %collective-permute-start.77 = (bf16[1,4,96,768]{3,2,1,0:T(8,128)(2,1)}, bf16[1,4,96,768]{3,2,1,0:T(8,128)(2,1)}, u32[]{:S(2)}, u32[]{:S(2)}) collective-permute-start(bf16[1,4,96,768]{3,2,1,0:T(8,128)(2,1)} %fusion.60), channel_id=1, source_target_pairs={{0,4},{4,0},{8,12},{12,8},{16,20},{20,16},{24,28},{28,24},{1,5},{5... | collective-permute-start | bytes 1769480 | tf_op jit(solution)/shard_map/ppermute | solution.py:159
  341.7 178.1 %collective-permute-start.70 = (f32[2,32,768]{2,1,0:T(8,128)}, f32[2,32,768]{2,1,0:T(8,128)}, u32[]{:S(2)}, u32[]{:S(2)}) collective-permute-start(f32[2,32,768]{2,1,0:T(8,128)} %fusion.86), channel_id=1, source_target_pairs={{0,1},{1,0},{2,3},{3,2},{4,5},{5,4},{6,7},{7,6},{8,9},{9,8},{10,11... | collective-permute-start | bytes 589832 | tf_op jit(solution)/shard_map/ppermute | solution.py:159
  343.2 22.8 %collective-permute-start.78 = (bf16[1,2,96,768]{3,2,1,0:T(8,128)(2,1)S(1)}, bf16[1,2,96,768]{3,2,1,0:T(8,128)(2,1)S(1)}, u32[]{:S(2)}, u32[]{:S(2)}) collective-permute-start(bf16[1,2,96,768]{3,2,1,0:T(8,128)(2,1)S(1)} %fusion.83), channel_id=1, source_target_pairs={{0,8},{4,12},{8,0},{12,4},{16,24},{20,28},{24,16},{28,20},{1,9},{5... | collective-permute-start | bytes 884744 | tf_op jit(solution)/shard_map/ppermute | solution.py:159
  349.7 50.5 %collective-permute-start.84 = (bf16[2,2,96,768]{3,2,1,0:T(8,128)(2,1)S(1)}, bf16[2,2,96,768]{3,2,1,0:T(8,128)(2,1)S(1)}, u32[]{:S(2)}, u32[]{:S(2)}) collective-permute-start(bf16[2,2,96,768]{3,2,1,0:T(8,128)(2,1)S(1)} %fusion.62), channel_id=1, source_target_pairs={{0,8},{4,12},{8,0},{12,4},{16,24},{20,28},{24,16},{28,20},{1,9},{5... | collective-permute-start | bytes 1769480 | tf_op jit(solution)/shard_map/ppermute | solution.py:159
  366.1 22.0 %collective-permute-start.79 = (bf16[1,1,96,768]{3,2,1,0:T(8,128)(2,1)S(1)}, bf16[1,1,96,768]{3,2,1,0:T(8,128)(2,1)S(1)}, u32[]{:S(2)}, u32[]{:S(2)}) collective-permute-start(bf16[1,1,96,768]{3,2,1,0:T(8,128)(2,1)S(1)} %dynamic-slice_convert_fusion.7), channel_id=1, source_target_pairs={{0,16},{4,20},{8,24},{12,28},{16,0},{20,4},{24,8},{28,12},{1,17},{... | collective-permute-start | bytes 442376 | tf_op jit(solution)/shard_map/ppermute | solution.py:159
  386.9 28.4 %collective-permute-start.80 = (bf16[2,4,96,768]{3,2,1,0:T(8,128)(2,1)S(1)}, bf16[2,4,96,768]{3,2,1,0:T(8,128)(2,1)S(1)}, u32[]{:S(2)}, u32[]{:S(2)}) collective-permute-start(bf16[2,4,96,768]{3,2,1,0:T(8,128)(2,1)S(1)} %fusion.43), channel_id=1, source_target_pairs={{0,4},{4,0},{8,12},{12,8},{16,20},{20,16},{24,28},{28,24},{1,5},{5... | collective-permute-start | bytes 3538952 | tf_op jit(solution)/shard_map/ppermute | solution.py:159
  400.4 30.6 %collective-permute-start.85 = (bf16[2,1,96,768]{3,2,1,0:T(8,128)(2,1)S(1)}, bf16[2,1,96,768]{3,2,1,0:T(8,128)(2,1)S(1)}, u32[]{:S(2)}, u32[]{:S(2)}) collective-permute-start(bf16[2,1,96,768]{3,2,1,0:T(8,128)(2,1)S(1)} %dynamic-slice_convert_fusion.4), channel_id=1, source_target_pairs={{0,16},{4,20},{8,24},{12,28},{16,0},{20,4},{24,8},{28,12},{1,17},{... | collective-permute-start | bytes 884744 | tf_op jit(solution)/shard_map/ppermute | solution.py:159
  419.5 27.4 %collective-permute-start.61 = (bf16[2,228,768]{2,0,1:T(2,128)(2,1)S(1)}, bf16[2,228,768]{2,0,1:T(2,128)(2,1)S(1)}, u32[]{:S(2)}, u32[]{:S(2)}) collective-permute-start(bf16[2,228,768]{2,0,1:T(2,128)(2,1)S(1)} %copy.384), channel_id=1, source_target_pairs={{0,1},{1,0},{2,3},{3,2},{4,5},{5,4},{6,7},{7,6},{8,9},{9,8},{10,11... | collective-permute-start | bytes 2101256 | tf_op jit(solution)/shard_map/ppermute | solution.py:159
  489.6 51.4 %collective-permute-start.62 = (bf16[2,228,768]{2,0,1:T(2,128)(2,1)}, bf16[2,228,768]{2,0,1:T(2,128)(2,1)}, u32[]{:S(2)}, u32[]{:S(2)}) collective-permute-start(bf16[2,228,768]{2,0,1:T(2,128)(2,1)} %copy.389), channel_id=1, source_target_pairs={{0,1},{1,0},{2,3},{3,2},{4,5},{5,4},{6,7},{7,6},{8,9},{9,8},{10,11... | collective-permute-start | bytes 2101256 | tf_op jit(solution)/shard_map/ppermute | solution.py:159
  589.3 36.5 %collective-permute-start.64 = (f32[2,228,768]{2,0,1:T(2,128)}, f32[2,228,768]{2,0,1:T(2,128)}, u32[]{:S(2)}, u32[]{:S(2)}) collective-permute-start(f32[2,228,768]{2,0,1:T(2,128)} %copy.393), channel_id=1, source_target_pairs={{0,1},{1,0},{2,3},{3,2},{4,5},{5,4},{6,7},{7,6},{8,9},{9,8},{10,11... | collective-permute-start | bytes 4202504 | tf_op jit(solution)/shard_map/ppermute | solution.py:159
  (318 other events, 2507.4 us)

commit v2 on v1

v2 whole, which is shorter than its diff:
```python
import functools

import jax
import jax.numpy as jnp
from jax import lax
from jax.experimental import pallas as pl
from jax.experimental.pallas import tpu as pltpu
from jax.sharding import PartitionSpec as P

D = 768
HEAD_DIM = 64
FF = 3072
PATCHES = 196
SUFFIX = 32
ENC_LEN = 228


EPS_NORM = 1e-06
EPS_STAT = 1e-30
DECAY = 0.99
MOMENTUM = 0.9
AVERAGE = 0.6
RATE_MATRIX = 0.004
RATE_GAIN = 0.05
MASKED = -1000000000.0


LOW = jnp.bfloat16
F32 = jnp.float32
VMEM_LIMIT = 56 * 1024 * 1024


def dot(left, right, contract):
    return lax.dot_general(left, right, (contract, ((), ())), preferred_element_type=F32)


def mm(left, right):
    return dot(left, right, ((1,), (0,)))


def mm_t(left, right):
    return dot(left, right, ((1,), (1,)))


def t_mm(left, right):
    return dot(left, right, ((0,), (0,)))


def rms_scale(value):
    return lax.rsqrt(jnp.mean(value * value, -1, keepdims=True) + EPS_NORM)


def softmax(scores):
    expons = jnp.exp(scores - jnp.max(scores, -1, keepdims=True))
    return expons / jnp.sum(expons, -1, keepdims=True)


def gelu_parts(upper):
    inner = 0.7978845608028654 * (upper + 0.044715 * upper * upper * upper)
    bent = jnp.tanh(inner)
    value = 0.5 * upper * (1.0 + bent)
    slope = 0.5 * (1.0 + bent) + 0.5 * upper * (1.0 - bent * bent) * 0.7978845608028654 * (
        1.0 + 3.0 * 0.044715 * upper * upper
    )
    return value, slope


class Plan:
    def __init__(self, dp_n, block, width, hidden, pairs):
        self.dp_n, self.block, self.width, self.hidden, self.pairs = dp_n, block, width, hidden, pairs
        self.half = pairs // 2
        self.heads = width // HEAD_DIM
        self.direct = dp_n == 8

    def weight_specs(self, pieces):
        return [pl.BlockSpec(item.shape, lambda *_, n=item.ndim: (0,) * n) for item in pieces]

    def weight_scratch(self, pieces, count):
        return [pltpu.VMEM((count, D, D), LOW)]

    def assemble(self, meta, refs, scratch):
        if not self.direct:
            scratch[...] = refs[0][...]
            return
        for ref, places in zip(refs, ((0, 4, 2, 6), (1, 5, 3, 7))):
            for index, place in enumerate(places):
                row = pl.multiple_of(jnp.bitwise_xor(meta[0], place) * self.block, 32)
                scratch[:, pl.ds(row, self.block), :] = ref[index]

    def grad_shapes(self, count):
        if not self.direct:
            return [jax.ShapeDtypeStruct((count, D, D), F32)]
        shape = (count, self.dp_n // 2, self.block, D)
        return [jax.ShapeDtypeStruct(shape, LOW), jax.ShapeDtypeStruct(shape, F32)]

    def emit(self, meta, acc, refs):
        if not self.direct:
            refs[0][...] = acc[...]
            return
        mine = jnp.bitwise_and(meta[0], 1)
        for index in range(self.dp_n // 2):
            away = pl.multiple_of((2 * index + 1 - mine) * self.block, 32)
            here = pl.multiple_of((2 * index + mine) * self.block, 32)
            for count in range(acc.shape[0]):
                refs[0][count, index] = acc[count, pl.ds(away, self.block), :].astype(LOW)
                refs[1][count, index] = acc[count, pl.ds(here, self.block), :]


def whole(shape):
    return pl.BlockSpec(shape, lambda *_: (0,) * len(shape))


def own_spec(count, base, shape):
    return pl.BlockSpec(
        (1,) + shape, lambda p, _: (base + jnp.maximum(p - count, 0),) + (0,) * len(shape)
    )


def oth_spec(count, base, shape):
    return pl.BlockSpec(
        (1,) + shape, lambda p, _: (base + jnp.minimum(p, count - 1),) + (0,) * len(shape)
    )


def step_spec(shape):
    return pl.BlockSpec((1,) + shape, lambda p, _: (p,) + (0,) * len(shape))


def call(name, body, grid, meta, inputs, in_specs, outs, out_specs, scratch):
    return pl.pallas_call(
        body,
        name=name,
        out_shape=outs,
        grid_spec=pltpu.PrefetchScalarGridSpec(
            num_scalar_prefetch=1,
            grid=grid,
            in_specs=in_specs,
            out_specs=out_specs,
            scratch_shapes=scratch,
        ),
        compiler_params=pltpu.CompilerParams(
            dimension_semantics=("arbitrary",) * len(grid), vmem_limit_bytes=VMEM_LIMIT
        ),
    )(meta, *inputs)


def key_mask(meta, pairs, slot):
    place = lax.broadcasted_iota(jnp.int32, (1, ENC_LEN), 1)
    image, prefix = meta[1 + slot], meta[1 + pairs + slot]
    return (place < image * PATCHES) | ((place >= PATCHES) & (place < PATCHES + prefix))


def attend_heads(plan, queries, keys, values, allowed):
    mixed = []
    for head in range(plan.heads):
        cut = slice(head * HEAD_DIM, (head + 1) * HEAD_DIM)
        scores = jnp.where(allowed, mm_t(queries[:, cut], keys[:, cut]) * 0.125, MASKED)
        mixed.append(mm(softmax(scores).astype(LOW), values[:, cut]).astype(LOW))
    return jnp.concatenate(mixed, 1)


def attend_heads_back(plan, queries, keys, values, allowed, grad_mixed):
    grads = ([], [], [])
    for head in range(plan.heads):
        cut = slice(head * HEAD_DIM, (head + 1) * HEAD_DIM)
        query, key, value, grad = queries[:, cut], keys[:, cut], values[:, cut], grad_mixed[:, cut]
        probs = softmax(jnp.where(allowed, mm_t(query, key) * 0.125, MASKED))
        grad_probs = mm_t(grad, value)
        inner = jnp.sum(grad_probs * probs, -1, keepdims=True)
        grad_scores = (probs * (grad_probs - inner)).astype(LOW)
        grads[0].append((mm(grad_scores, key) * 0.125).astype(LOW))
        grads[1].append((t_mm(grad_scores, query) * 0.125).astype(LOW))
        grads[2].append(t_mm(probs.astype(LOW), grad).astype(LOW))
    return tuple(jnp.concatenate(item, 1) for item in grads)


def slot_of(plan, count, base, step):
    return jnp.where(step < count, plan.half + base + step, base + step - count)


def put(step, count, own, oth, value):
    @pl.when(step < count)
    def _():
        oth[0] = value

    @pl.when(step >= count)
    def _():
        own[0] = value


def encoder_attention(plan, meta, own, oth, gain, pieces, base, count):
    w3 = 3 * plan.width
    n = len(pieces)

    def body(meta, own_ref, oth_ref, gain_ref, *rest):
        refs, (own_out, oth_out, kept, weight) = rest[:n], rest[n:]
        step = pl.program_id(0)

        @pl.when(step == 0)
        def _():
            plan.assemble(meta, refs, weight)

        value = jnp.where(step < count, oth_ref[0], own_ref[0]).astype(F32)
        normed = (value * rms_scale(value) * gain_ref[...]).astype(LOW)
        joined = mm(normed, weight[0, :, :w3]).astype(LOW)
        allowed = key_mask(meta, plan.pairs, slot_of(plan, count, base, step))
        width = plan.width
        mixed = attend_heads(
            plan, joined[:, :width], joined[:, width : 2 * width], joined[:, 2 * width :], allowed
        )
        kept[0, :, :w3] = joined
        kept[0, :, w3:] = mixed
        put(step, count, own_out, oth_out, mm_t(mixed, weight[0, :, w3:]).astype(LOW))

    rows = (ENC_LEN, D)
    return call(
        "encoder_attention",
        body,
        (2 * count,),
        meta,
        (own, oth, gain, *pieces),
        [own_spec(count, base, rows), oth_spec(count, base, rows), whole((1, D)), *plan.weight_specs(pieces)],
        [jax.ShapeDtypeStruct((count,) + rows, LOW)] * 2
        + [jax.ShapeDtypeStruct((2 * count, ENC_LEN, w3 + plan.width), LOW)],
        [own_spec(count, 0, rows), oth_spec(count, 0, rows), step_spec((ENC_LEN, w3 + plan.width))],
        plan.weight_scratch(pieces, 1),
    )


def encoder_attention_back(plan, meta, own, oth, gain, pieces, kept, grad_own, grad_oth):
    count = plan.half
    width, w3 = plan.width, 3 * plan.width
    n = len(pieces)

    def body(meta, own_ref, oth_ref, gain_ref, kept_ref, grad_own_ref, grad_oth_ref, *rest):
        refs, (own_out, oth_out), grad_refs = rest[:n], rest[n : n + 2], rest[n + 2 : -2]
        weight, acc = rest[-2:]
        step = pl.program_id(0)

        @pl.when(step == 0)
        def _():
            plan.assemble(meta, refs, weight)
            acc[...] = jnp.zeros_like(acc)

        value = jnp.where(step < count, oth_ref[0], own_ref[0]).astype(F32)
        normed = (value * rms_scale(value) * gain_ref[...]).astype(LOW)
        grad = jnp.where(step < count, grad_oth_ref[0], grad_own_ref[0])
        allowed = key_mask(meta, plan.pairs, slot_of(plan, count, 0, step))
        grad_mixed = mm(grad, weight[0, :, w3:]).astype(LOW)
        acc[0, :, w3:] += t_mm(grad, kept_ref[0, :, w3:])
        joined = kept_ref[0, :, :w3]
        grads = attend_heads_back(
            plan, joined[:, :width], joined[:, width : 2 * width], joined[:, 2 * width :], allowed, grad_mixed
        )
        together = jnp.concatenate(grads, 1)
        acc[0, :, :w3] += t_mm(normed, together)
        put(step, count, own_out, oth_out, mm_t(together, weight[0, :, :w3]).astype(LOW))

        @pl.when(step == 2 * count - 1)
        def _():
            plan.emit(meta, acc, grad_refs)

    rows = (ENC_LEN, D)
    shapes = plan.grad_shapes(1)
    pair_specs = [own_spec(count, 0, rows), oth_spec(count, 0, rows)]
    return call(
        "encoder_attention_back",
        body,
        (2 * count,),
        meta,
        (own, oth, gain, kept, grad_own, grad_oth, *pieces),
        [*pair_specs, whole((1, D)), step_spec(kept.shape[1:]), *pair_specs, *plan.weight_specs(pieces)],
        [jax.ShapeDtypeStruct((count,) + rows, LOW)] * 2 + shapes,
        [*pair_specs, *[whole(item.shape) for item in shapes]],
        plan.weight_scratch(pieces, 1) + [pltpu.VMEM((1, D, D), F32)],
    )


def encoder_feed(plan, meta, own, oth, pieces, base, count):
    n = len(pieces)

    def body(meta, own_ref, oth_ref, *rest):
        refs, (own_out, oth_out, weight) = rest[:n], rest[n:]
        step = pl.program_id(0)

        @pl.when(step == 0)
        def _():
            plan.assemble(meta, refs, weight)

        normed = jnp.where(step < count, oth_ref[0], own_ref[0])
        active = gelu_parts(mm(normed, weight[0]))[0].astype(LOW)
        put(step, count, own_out, oth_out, mm_t(active, weight[1]).astype(LOW))

    rows = (ENC_LEN, D)
    return call(
        "encoder_feed",
        body,
        (2 * count,),
        meta,
        (own, oth, *pieces),
        [own_spec(count, base, rows), oth_spec(count, base, rows), *plan.weight_specs(pieces)],
        [jax.ShapeDtypeStruct((count,) + rows, LOW)] * 2,
        [own_spec(count, 0, rows), oth_spec(count, 0, rows)],
        plan.weight_scratch(pieces, 2),
    )


def encoder_feed_back(plan, meta, own, oth, grad_own, grad_oth, pieces):
    n = len(pieces)
    count = plan.half

    def body(meta, own_ref, oth_ref, grad_own_ref, grad_oth_ref, *rest):
        refs, (own_out, oth_out), grad_refs = rest[:n], rest[n : n + 2], rest[n + 2 : -2]
        weight, acc = rest[-2:]
        step = pl.program_id(0)

        @pl.when(step == 0)
        def _():
            plan.assemble(meta, refs, weight)
            acc[...] = jnp.zeros_like(acc)

        normed = jnp.where(step < count, oth_ref[0], own_ref[0])
        grad = jnp.where(step < count, grad_oth_ref[0], grad_own_ref[0])
        active, slope = gelu_parts(mm(normed, weight[0]))
        grad_upper = (slope * mm(grad, weight[1])).astype(LOW)
        put(step, count, own_out, oth_out, mm_t(grad_upper, weight[0]).astype(LOW))
        acc[0] += t_mm(normed, grad_upper)
        acc[1] += t_mm(grad, active.astype(LOW))

        @pl.when(step == 2 * count - 1)
        def _():
            plan.emit(meta, acc, grad_refs)

    rows = (ENC_LEN, D)
    shapes = plan.grad_shapes(2)
    pair_specs = [own_spec(count, 0, rows), oth_spec(count, 0, rows)]
    return call(
        "encoder_feed_back",
        body,
        (2 * count,),
        meta,
        (own, oth, grad_own, grad_oth, *pieces),
        [*pair_specs, *pair_specs, *plan.weight_specs(pieces)],
        [jax.ShapeDtypeStruct((count,) + rows, LOW)] * 2 + shapes,
        [*pair_specs, *[whole(item.shape) for item in shapes]],
        plan.weight_scratch(pieces, 2) + [pltpu.VMEM((2, D, D), F32)],
    )


def self_mask(plan, meta):
    rows = plan.pairs * SUFFIX
    query = lax.broadcasted_iota(jnp.int32, (rows, rows), 0)
    key = lax.broadcasted_iota(jnp.int32, (rows, rows), 1)
    pair = key // SUFFIX
    limit = jnp.zeros_like(key)
    for slot in range(plan.pairs):
        limit = jnp.where(pair == slot, meta[1 + 2 * plan.pairs + slot], limit)
    return (query // SUFFIX == pair) & (key <= query) & (key - pair * SUFFIX < limit)


def decoder_self(plan, meta, rows_in, gain, pieces):
    n = len(pieces)
    width, w3 = plan.width, 3 * plan.width
    rows = plan.pairs * SUFFIX
    mid = rows // 2

    def body(meta, in_ref, gain_ref, *rest):
        refs, (own_out, oth_out, kept, weight) = rest[:n], rest[n:]
        plan.assemble(meta, refs, weight)
        value = in_ref[...].astype(F32)
        normed = (value * rms_scale(value) * gain_ref[...]).astype(LOW)
        joined = mm(normed, weight[0, :, :w3]).astype(LOW)
        mixed = attend_heads(
            plan, joined[:, :width], joined[:, width : 2 * width], joined[:, 2 * width :], self_mask(plan, meta)
        )
        kept[:, :w3] = joined
        kept[:, w3:] = mixed
        partial = mm_t(mixed, weight[0, :, w3:]).astype(LOW)
        own_out[...] = partial[:mid]
        oth_out[...] = partial[mid:]

    return call(
        "decoder_self",
        body,
        (1,),
        meta,
        (rows_in, gain, *pieces),
        [whole((rows, D)), whole((1, D)), *plan.weight_specs(pieces)],
        [jax.ShapeDtypeStruct((mid, D), LOW)] * 2 + [jax.ShapeDtypeStruct((rows, 4 * width), LOW)],
        [whole((mid, D))] * 2 + [whole((rows, 4 * width))],
        plan.weight_scratch(pieces, 1),
    )


def decoder_self_back(plan, meta, rows_in, gain, pieces, kept, grad_own, grad_oth):
    n = len(pieces)
    width, w3 = plan.width, 3 * plan.width
    rows = plan.pairs * SUFFIX
    mid = rows // 2

    def body(meta, in_ref, gain_ref, kept_ref, grad_own_ref, grad_oth_ref, *rest):
        refs, (own_out, oth_out), grad_refs = rest[:n], rest[n : n + 2], rest[n + 2 : -2]
        weight, acc = rest[-2:]
        plan.assemble(meta, refs, weight)
        value = in_ref[...].astype(F32)
        normed = (value * rms_scale(value) * gain_ref[...]).astype(LOW)
        grad = jnp.concatenate([grad_own_ref[...], grad_oth_ref[...]], 0)
        grad_mixed = mm(grad, weight[0, :, w3:]).astype(LOW)
        acc[0, :, w3:] = t_mm(grad, kept_ref[:, w3:])
        joined = kept_ref[:, :w3]
        grads = attend_heads_back(
            plan,
            joined[:, :width],
            joined[:, width : 2 * width],
            joined[:, 2 * width :],
            self_mask(plan, meta),
            grad_mixed,
        )
        together = jnp.concatenate(grads, 1)
        acc[0, :, :w3] = t_mm(normed, together)
        partial = mm_t(together, weight[0, :, :w3]).astype(LOW)
        own_out[...] = partial[:mid]
        oth_out[...] = partial[mid:]
        plan.emit(meta, acc, grad_refs)

    shapes = plan.grad_shapes(1)
    return call(
        "decoder_self_back",
        body,
        (1,),
        meta,
        (rows_in, gain, kept, grad_own, grad_oth, *pieces),
        [whole((rows, D)), whole((1, D)), whole(kept.shape), whole((mid, D)), whole((mid, D)), *plan.weight_specs(pieces)],
        [jax.ShapeDtypeStruct((mid, D), LOW)] * 2 + shapes,
        [whole((mid, D))] * 2 + [whole(item.shape) for item in shapes],
        plan.weight_scratch(pieces, 1) + [pltpu.VMEM((1, D, D), F32)],
    )


def decoder_cross(plan, meta, own, oth, memory_own, memory_oth, pieces):
    n = len(pieces)
    count = plan.half
    width, w3 = plan.width, 3 * plan.width

    def body(meta, own_ref, oth_ref, memory_own_ref, memory_oth_ref, *rest):
        refs, (own_out, oth_out, kept_query, kept_key, weight) = rest[:n], rest[n:]
        step = pl.program_id(0)

        @pl.when(step == 0)
        def _():
            plan.assemble(meta, refs, weight)

        normed = jnp.where(step < count, oth_ref[0], own_ref[0])
        memory = jnp.where(step < count, memory_oth_ref[0], memory_own_ref[0])
        queries = mm(normed, weight[0, :, :width]).astype(LOW)
        both = mm(memory, weight[0, :, width:w3]).astype(LOW)
        allowed = key_mask(meta, plan.pairs, slot_of(plan, count, 0, step))
        mixed = attend_heads(plan, queries, both[:, :width], both[:, width:], allowed)
        kept_query[0, :, :width] = queries
        kept_query[0, :, width:] = mixed
        kept_key[0] = both
        put(step, count, own_out, oth_out, mm_t(mixed, weight[0, :, w3:]).astype(LOW))

    rows, long = (SUFFIX, D), (ENC_LEN, D)
    return call(
        "decoder_cross",
        body,
        (2 * count,),
        meta,
        (own, oth, memory_own, memory_oth, *pieces),
        [
            own_spec(count, 0, rows),
            oth_spec(count, 0, rows),
            own_spec(count, 0, long),
            oth_spec(count, 0, long),
            *plan.weight_specs(pieces),
        ],
        [jax.ShapeDtypeStruct((count,) + rows, LOW)] * 2
        + [
            jax.ShapeDtypeStruct((2 * count, SUFFIX, 2 * width), LOW),
            jax.ShapeDtypeStruct((2 * count, ENC_LEN, 2 * width), LOW),
        ],
        [
            own_spec(count, 0, rows),
            oth_spec(count, 0, rows),
            step_spec((SUFFIX, 2 * width)),
            step_spec((ENC_LEN, 2 * width)),
        ],
        plan.weight_scratch(pieces, 1),
    )


def decoder_cross_back(
    plan, meta, own, oth, memory_own, memory_oth, pieces, kept_query, kept_key, grad_own, grad_oth
):
    n = len(pieces)
    count = plan.half
    width, w3 = plan.width, 3 * plan.width

    def body(
        meta, own_ref, oth_ref, memory_own_ref, memory_oth_ref, query_ref, key_ref, grad_own_ref, grad_oth_ref, *rest
    ):
        refs, outs, grad_refs = rest[:n], rest[n : n + 4], rest[n + 4 : -2]
        weight, acc = rest[-2:]
        step = pl.program_id(0)

        @pl.when(step == 0)
        def _():
            plan.assemble(meta, refs, weight)
            acc[...] = jnp.zeros_like(acc)

        normed = jnp.where(step < count, oth_ref[0], own_ref[0])
        memory = jnp.where(step < count, memory_oth_ref[0], memory_own_ref[0])
        grad = jnp.where(step < count, grad_oth_ref[0], grad_own_ref[0])
        allowed = key_mask(meta, plan.pairs, slot_of(plan, count, 0, step))
        grad_mixed = mm(grad, weight[0, :, w3:]).astype(LOW)
        acc[0, :, w3:] += t_mm(grad, query_ref[0, :, width:])
        both = key_ref[0]
        grad_query, grad_key, grad_value = attend_heads_back(
            plan, query_ref[0, :, :width], both[:, :width], both[:, width:], allowed, grad_mixed
        )
        together = jnp.concatenate([grad_key, grad_value], 1)
        acc[0, :, :width] += t_mm(normed, grad_query)
        acc[0, :, width:w3] += t_mm(memory, together)
        put(step, count, outs[0], outs[1], mm_t(grad_query, weight[0, :, :width]).astype(LOW))
        put(step, count, outs[2], outs[3], mm_t(together, weight[0, :, width:w3]).astype(LOW))

        @pl.when(step == 2 * count - 1)
        def _():
            plan.emit(meta, acc, grad_refs)

    rows, long = (SUFFIX, D), (ENC_LEN, D)
    shapes = plan.grad_shapes(1)
    row_specs = [own_spec(count, 0, rows), oth_spec(count, 0, rows)]
    long_specs = [own_spec(count, 0, long), oth_spec(count, 0, long)]
    return call(
        "decoder_cross_back",
        body,
        (2 * count,),
        meta,
        (own, oth, memory_own, memory_oth, kept_query, kept_key, grad_own, grad_oth, *pieces),
        [
            *row_specs,
            *long_specs,
            step_spec(kept_query.shape[1:]),
            step_spec(kept_key.shape[1:]),
            *row_specs,
            *plan.weight_specs(pieces),
        ],
        [jax.ShapeDtypeStruct((count,) + rows, LOW)] * 2
        + [jax.ShapeDtypeStruct((count,) + long, LOW)] * 2
        + shapes,
        [*row_specs, *long_specs, *[whole(item.shape) for item in shapes]],
        plan.weight_scratch(pieces, 1) + [pltpu.VMEM((1, D, D), F32)],
    )


def decoder_feed(plan, meta, own, oth, grad_in, pieces):
    n = len(pieces)
    rows = plan.pairs * SUFFIX
    mid = rows // 2

    def body(meta, own_ref, oth_ref, grad_ref, *rest):
        refs, (own_out, oth_out), grad_refs = rest[:n], rest[n : n + 2], rest[n + 2 : -2]
        weight, acc = rest[-2:]
        plan.assemble(meta, refs, weight)
        normed = jnp.concatenate([own_ref[...], oth_ref[...]], 0)
        grad = grad_ref[...]
        active, slope = gelu_parts(mm(normed, weight[0]))
        active = active.astype(LOW)
        partial = mm_t(active, weight[1]).astype(LOW)
        grad_upper = (slope * mm(grad, weight[1])).astype(LOW)
        back = mm_t(grad_upper, weight[0]).astype(LOW)
        own_out[0] = partial[:mid]
        own_out[1] = back[:mid]
        oth_out[0] = partial[mid:]
        oth_out[1] = back[mid:]
        acc[0] = t_mm(normed, grad_upper)
        acc[1] = t_mm(grad, active)
        plan.emit(meta, acc, grad_refs)

    shapes = plan.grad_shapes(2)
    return call(
        "decoder_feed",
        body,
        (1,),
        meta,
        (own, oth, grad_in, *pieces),
        [whole((mid, D))] * 2 + [whole((rows, D)), *plan.weight_specs(pieces)],
        [jax.ShapeDtypeStruct((2, mid, D), LOW)] * 2 + shapes,
        [whole((2, mid, D))] * 2 + [whole(item.shape) for item in shapes],
        plan.weight_scratch(pieces, 2) + [pltpu.VMEM((2, D, D), F32)],
    )


def add_norm(meta, name, base, first, second, gain):
    def body(meta, base_ref, first_ref, second_ref, gain_ref, sum_ref, norm_ref):
        value = base_ref[...].astype(F32) + (first_ref[...].astype(F32) + second_ref[...].astype(F32))
        sum_ref[...] = value
        norm_ref[...] = (value * rms_scale(value) * gain_ref[...]).astype(LOW)

    shape = base.shape
    part = (1,) + shape[1:] if len(shape) == 3 else shape
    spec = (
        pl.BlockSpec(part, lambda p, _: (p, 0, 0)) if len(shape) == 3 else whole(shape)
    )
    return call(
        name,
        body,
        (shape[0] if len(shape) == 3 else 1,),
        meta,
        (base, first, second, gain),
        [spec, spec, spec, whole((1, D))],
        [jax.ShapeDtypeStruct(shape, F32), jax.ShapeDtypeStruct(shape, LOW)],
        [spec, spec],
        [],
    )


def norm_back(meta, name, inputs, gain, grad, first, second, want_low):
    def body(meta, in_ref, gain_ref, grad_ref, first_ref, second_ref, *outs):
        value = in_ref[...].astype(F32)
        scale = rms_scale(value)
        unit = value * scale
        back = first_ref[...].astype(F32) + second_ref[...].astype(F32)
        product = back * unit
        axes = tuple(range(value.ndim - 1))
        part = jnp.sum(product, axes)[None]
        weighted = product * gain_ref[...]
        total = grad_ref[...].astype(F32) + scale * (
            back * gain_ref[...] - unit * jnp.mean(weighted, -1, keepdims=True)
        )
        outs[0][...] = total
        if want_low:
            outs[1][...] = total.astype(LOW)
        step = pl.program_id(0)

        @pl.when(step == 0)
        def _():
            outs[-1][...] = part

        @pl.when(step > 0)
        def _():
            outs[-1][...] += part

    shape = inputs.shape
    part = (1,) + shape[1:] if len(shape) == 3 else shape
    spec = pl.BlockSpec(part, lambda p, _: (p, 0, 0)) if len(shape) == 3 else whole(shape)
    return call(
        name,
        body,
        (shape[0] if len(shape) == 3 else 1,),
        meta,
        (inputs, gain, grad, first, second),
        [spec, whole((1, D)), spec, spec, spec],
        [jax.ShapeDtypeStruct(shape, F32)]
        + [jax.ShapeDtypeStruct(shape, LOW)] * want_low
        + [jax.ShapeDtypeStruct((1, D), F32)],
        [spec] * (1 + want_low) + [whole((1, D))],
        [],
    )


def update_matrix(
    gradient, weight, rows_old, cols_old, moment, average, row_sum, col_sum, row_index, col_index
):
    full_rows = rows_old.shape[-1]
    full_cols = cols_old.shape[-1]
    rows_new = DECAY * rows_old + (1.0 - DECAY) * (row_sum / full_cols + EPS_STAT)
    cols_new = DECAY * cols_old + (1.0 - DECAY) * (col_sum / full_rows + EPS_STAT)
    row_local = lax.dynamic_slice_in_dim(
        rows_new, row_index * gradient.shape[-2], gradient.shape[-2], rows_new.ndim - 1
    )
    col_local = lax.dynamic_slice_in_dim(
        cols_new, col_index * gradient.shape[-1], gradient.shape[-1], cols_new.ndim - 1
    )
    second = (
        row_local[..., :, None] * col_local[..., None, :] / jnp.mean(rows_new, -1)[..., None, None]
    )
    stepped = gradient * lax.rsqrt(second)
    moment_new = MOMENTUM * moment + stepped
    weight_new = weight - RATE_MATRIX * (MOMENTUM * moment_new + stepped)
    average_new = AVERAGE * average + (1.0 - AVERAGE) * weight_new
    return (
        gradient,
        rows_new,
        cols_new,
        moment_new,
        weight_new,
        average_new,
        weight_new.astype(jnp.bfloat16),
    )


def on_device(
    sizes,
    encoder_in,
    decoder_in,
    decoder_cotangent,
    counts,
    prefix_len,
    suffix_len,
    project_in,
    project_in_rows,
    project_in_cols,
    project_in_moment,
    project_in_average,
    project_out,
    project_out_rows,
    project_out_cols,
    project_out_moment,
    project_out_average,
    expand,
    expand_rows,
    expand_cols,
    expand_moment,
    expand_average,
    contract,
    contract_rows,
    contract_cols,
    contract_moment,
    contract_average,
    norm_gains,
    norm_gains_square,
    norm_gains_moment,
    norm_gains_average,
):
    dp_n, mp_n = sizes
    dp_index = lax.axis_index("dp")
    mp_index = lax.axis_index("mp")
    side = mp_index % 2
    pairs = prefix_len.shape[0]
    half = pairs // 2
    width = project_in.shape[-1]
    block = project_in.shape[-2]
    plan = Plan(dp_n, block, width, expand.shape[-1], pairs)
    low, f32 = LOW, F32

    def swap(value, axis, bit):
        count = dp_n if axis == "dp" else mp_n
        return lax.ppermute(value, axis, [(i, i ^ bit) for i in range(count)])

    def bits(count):
        return [1 << i for i in range(count.bit_length() - 1)]

    def after(value, other):
        return lax.optimization_barrier((value, other))[0]

    def gather(own, gate):
        if gate is not None:
            own = after(own, gate)
        if not plan.direct:
            return [lax.all_gather(own, "dp", axis=1, tiled=True)], None
        two = jnp.stack([own, swap(own, "dp", 4)])
        more = swap(two, "dp", 2)
        four = jnp.concatenate([two, more], 0)
        return [four, swap(four, "dp", 1)], more

    def scatter(parts):
        if not plan.direct:
            return lax.psum_scatter(parts[0], "dp", scatter_dimension=1, tiled=True)
        away, keep = parts
        count = keep.shape[0]
        keep = keep + swap(away, "dp", 1).astype(f32)
        for bit in (2, 4):
            mine = (dp_index // bit) % 2
            split = keep.reshape(count, -1, 2, block, D)
            away = lax.dynamic_index_in_dim(split, 1 - mine, 2, False).astype(low)
            keep = lax.dynamic_index_in_dim(split, mine, 2, False) + swap(away, "dp", bit).astype(f32)
        return keep.reshape(count, block, D)

    def total_dp(value):
        for bit in bits(dp_n):
            value = value + swap(value, "dp", bit)
        return value

    def reduce_own(own, oth):
        sent = (own.astype(f32) + swap(oth, "mp", 1).astype(f32)).astype(low)
        for bit in bits(mp_n)[1:-1]:
            sent = (sent.astype(f32) + swap(sent, "mp", bit).astype(f32)).astype(low)
        return sent, swap(sent, "mp", bits(mp_n)[-1])

    def relative(value):
        split = value.reshape((half, 2) + value.shape[1:])
        return (
            lax.dynamic_index_in_dim(split, side, 1, False),
            lax.dynamic_index_in_dim(split, 1 - side, 1, False),
        )

    def absolute(own):
        other = swap(own, "mp", 1)
        even = jnp.where(side == 0, own, other)
        odd = jnp.where(side == 0, other, own)
        return jnp.stack([even, odd], 1).reshape((pairs,) + own.shape[1:])

    def core(value):
        return swap(value, "mp", 1)

    def attention_block(layer):
        return jnp.concatenate(
            [project_in[layer, 0], project_in[layer, 1], project_in[layer, 2], project_out[layer].T], 1
        ).astype(low)[None]

    def feed_block(layer):
        return jnp.stack([expand[layer], contract[layer].T]).astype(low)

    gain_full = lax.dynamic_update_slice(
        jnp.zeros((5, D), low), norm_gains.astype(low), (0, dp_index * block)
    )
    gain_rows = total_dp(gain_full).astype(f32)
    gains = [gain_rows[i : i + 1] for i in range(5)]

    enc_att, gate = gather(attention_block(0), None)
    enc_feed, gate = gather(feed_block(0), gate)
    self_att, gate = gather(attention_block(1), gate)
    cross_att, gate = gather(attention_block(2), gate)
    dec_feed, gate = gather(feed_block(1), gate)

    place_rel = jnp.concatenate([2 * jnp.arange(half) + side, 2 * jnp.arange(half) + 1 - side])
    prefix_rel = jnp.concatenate(relative(prefix_len))
    suffix_rel = jnp.concatenate(relative(suffix_len))
    images = place_rel < counts[0, 0]
    active = place_rel < counts[0, 0] + counts[0, 1]
    meta = jnp.concatenate(
        [dp_index[None].astype(jnp.int32), images.astype(jnp.int32), prefix_rel, suffix_rel]
    )
    steps = jnp.arange(SUFFIX)
    live = active[:, None] & (steps[None, :] < suffix_rel[:, None])

    mid = half * SUFFIX
    enc_own, enc_oth = relative(encoder_in.reshape(pairs, ENC_LEN, D))
    dec_rel = jnp.concatenate(relative(decoder_in.reshape(pairs, SUFFIX, D))).reshape(2 * mid, D)
    cot = jnp.concatenate(relative(decoder_cotangent.reshape(pairs, SUFFIX, D)))
    cot = jnp.where(live[:, :, None], cot, f32(0.0)).reshape(2 * mid, D)

    part = encoder_attention(plan, meta, enc_own, enc_oth, gains[0], enc_att, 0, half)
    kept_enc = part[2]
    sums = reduce_own(part[0], part[1])
    enc_mid, norm_mid = add_norm(meta, "add_norm_mid", enc_own, *sums, gains[1])
    norm_mid_oth = core(norm_mid)

    part = decoder_self(plan, meta, dec_rel, gains[2], self_att)
    kept_self = part[2]
    sums = reduce_own(part[0], part[1])
    dec_one, norm_cross = add_norm(meta, "add_norm_cross", dec_rel[:mid], *sums, gains[3])
    norm_cross_oth = core(norm_cross)

    part = encoder_feed(plan, meta, norm_mid, norm_mid_oth, enc_feed, 0, half)
    sums = reduce_own(part[0], part[1])
    memory = (enc_mid + (sums[0].astype(f32) + sums[1].astype(f32))).astype(low)
    memory_oth = core(memory)

    def triple(value):
        return value.reshape(half, SUFFIX, D)

    cross_in = (triple(norm_cross), triple(norm_cross_oth), memory, memory_oth, cross_att)
    part = decoder_cross(plan, meta, *cross_in)
    kept_cross = part[2:]
    sums = reduce_own(part[0], part[1])
    dec_two, norm_last = add_norm(
        meta, "add_norm_last", dec_one, sums[0].reshape(mid, D), sums[1].reshape(mid, D), gains[4]
    )
    part = decoder_feed(plan, meta, norm_last, core(norm_last), cot.astype(low), dec_feed)
    sum_dec = scatter(part[2:])
    sums = reduce_own(part[0], part[1])
    out_own = dec_two + (sums[0][0].astype(f32) + sums[1][0].astype(f32))
    decoder_out = absolute(triple(out_own)).reshape(2 * mid, D)
    grad, grad_low, gain_four = norm_back(
        meta, "norm_back_last", dec_two, gains[4], cot[:mid], sums[0][1], sums[1][1], True
    )
    part = decoder_cross_back(
        plan, meta, *cross_in, *kept_cross, triple(grad_low), triple(core(grad_low))
    )
    sum_cross = scatter(part[4:])
    sums_enc = reduce_own(part[2], part[3])
    sums = reduce_own(part[0], part[1])
    grad_enc = sums_enc[0].astype(f32) + sums_enc[1].astype(f32)
    enc_low = grad_enc.astype(low)
    grad, grad_low, gain_three = norm_back(
        meta, "norm_back_cross", dec_one, gains[3], grad, sums[0].reshape(mid, D), sums[1].reshape(mid, D), True
    )
    part = encoder_feed_back(plan, meta, norm_mid, norm_mid_oth, enc_low, core(enc_low), enc_feed)
    sum_enc = scatter(part[2:])
    sums = reduce_own(part[0], part[1])
    grad_enc, enc_low, gain_one = norm_back(
        meta, "norm_back_mid", enc_mid, gains[1], grad_enc, *sums, True
    )

    part = decoder_self_back(
        plan, meta, dec_rel, gains[2], self_att, kept_self, grad_low, core(grad_low)
    )
    sum_self = scatter(part[2:])
    sums = reduce_own(part[0], part[1])
    grad, gain_two = norm_back(meta, "norm_back_self", dec_rel[:mid], gains[2], grad, *sums, False)
    decoder_in_grad = absolute(triple(grad)).reshape(2 * mid, D)

    part = encoder_attention_back(
        plan, meta, enc_own, enc_oth, gains[0], enc_att, kept_enc, enc_low, core(enc_low)
    )
    sum_att = scatter(part[2:])
    sums = reduce_own(part[0], part[1])
    grad_enc, gain_zero = norm_back(meta, "norm_back_enc", enc_own, gains[0], grad_enc, *sums, False)
    encoder_in_grad = absolute(grad_enc).reshape(pairs * ENC_LEN, D)

    gain_grad = jnp.concatenate([gain_zero, gain_one, gain_two, gain_three, gain_four])
    gain_grad = total_dp(gain_grad + swap(gain_grad, "mp", 1))
    grad_gain = lax.dynamic_slice(gain_grad, (0, dp_index * block), (5, block))

    att = jnp.concatenate([sum_att, sum_self, sum_cross], 0)
    grad_in = att[:, :, : 3 * width].reshape(3, block, 3, width).transpose(0, 2, 1, 3)
    grad_out = att[:, :, 3 * width :].transpose(0, 2, 1)
    grad_up = jnp.stack([sum_enc[0], sum_dec[0]])
    grad_down = jnp.stack([sum_enc[1], sum_dec[1]]).transpose(0, 2, 1)

    squares = [item * item for item in (grad_in, grad_out, grad_up, grad_down)]
    rows_part = [jnp.sum(item, -1) for item in squares]
    cols_part = [jnp.sum(item, -2) for item in squares]
    along_dp = [rows_part[0], cols_part[1], rows_part[2], cols_part[3]]
    along_mp = [cols_part[0], rows_part[1], cols_part[2], rows_part[3]]

    def spread_all(parts, axis, other):
        index, count = (dp_index, dp_n) if axis == "dp" else (mp_index, mp_n)
        flat = jnp.concatenate([item.reshape(-1) for item in parts])
        for bit in bits(mp_n if axis == "dp" else dp_n):
            flat = flat + swap(flat, other, bit)
        full = lax.dynamic_update_slice(
            jnp.zeros((count, flat.shape[0]), f32), flat[None], (index, 0)
        )
        for bit in bits(count):
            full = full + swap(full, axis, bit)
        result, start = [], 0
        for item in parts:
            size = item.size
            piece = full[:, start : start + size].reshape((count,) + item.shape)
            start += size
            piece = jnp.moveaxis(piece, 0, -2)
            result.append(piece.reshape(item.shape[:-1] + (count * item.shape[-1],)))
        return result

    row_in, col_out, row_up, col_down = spread_all(along_dp, "dp", "mp")
    col_in, row_out, col_up, row_down = spread_all(along_mp, "mp", "dp")
    total = (
        jnp.sum(row_in) + jnp.sum(row_out) + jnp.sum(row_up) + jnp.sum(row_down)
        + jnp.sum(gain_grad * gain_grad)
    )
    grad_norm = jnp.sqrt(total)
    factor = jnp.minimum(1.0, 1.0 / grad_norm)
    squared = factor * factor
    row_in, col_in, row_out, col_out = (
        row_in * squared,
        col_in * squared,
        row_out * squared,
        col_out * squared,
    )
    row_up, col_up, row_down, col_down = (
        row_up * squared,
        col_up * squared,
        row_down * squared,
        col_down * squared,
    )
    grad_in, grad_out, grad_up, grad_down = (
        grad_in * factor,
        grad_out * factor,
        grad_up * factor,
        grad_down * factor,
    )
    grad_gain = grad_gain * factor
    pin = update_matrix(
        grad_in,
        project_in,
        project_in_rows,
        project_in_cols,
        project_in_moment,
        project_in_average,
        row_in,
        col_in,
        dp_index,
        mp_index,
    )
    pout = update_matrix(
        grad_out,
        project_out,
        project_out_rows,
        project_out_cols,
        project_out_moment,
        project_out_average,
        row_out,
        col_out,
        mp_index,
        dp_index,
    )
    pexp = update_matrix(
        grad_up,
        expand,
        expand_rows,
        expand_cols,
        expand_moment,
        expand_average,
        row_up,
        col_up,
        dp_index,
        mp_index,
    )
    pcon = update_matrix(
        grad_down,
        contract,
        contract_rows,
        contract_cols,
        contract_moment,
        contract_average,
        row_down,
        col_down,
        mp_index,
        dp_index,
    )
    square_new = DECAY * norm_gains_square + (1.0 - DECAY) * (grad_gain * grad_gain + EPS_STAT)
    stepped = grad_gain * lax.rsqrt(square_new)
    moment_new = MOMENTUM * norm_gains_moment + stepped
    gains_new = norm_gains - RATE_GAIN * (MOMENTUM * moment_new + stepped)
    average_new = AVERAGE * norm_gains_average + (1.0 - AVERAGE) * gains_new
    return (
        decoder_out,
        encoder_in_grad,
        decoder_in_grad,
        grad_norm,
        pin[0],
        pin[1],
        pin[2],
        pin[3],
        pin[4],
        pin[5],
        pin[6],
        pout[0],
        pout[1],
        pout[2],
        pout[3],
        pout[4],
        pout[5],
        pout[6],
        pexp[0],
        pexp[1],
        pexp[2],
        pexp[3],
        pexp[4],
        pexp[5],
        pexp[6],
        pcon[0],
        pcon[1],
        pcon[2],
        pcon[3],
        pcon[4],
        pcon[5],
        pcon[6],
        grad_gain,
        square_new,
        moment_new,
        gains_new,
        average_new,
        gains_new.astype(jnp.bfloat16),
    )


def solution(mesh):
    placed = (
        P("dp", None),
        P("dp", None),
        P("dp", None),
        P("dp", None),
        P("dp"),
        P("dp"),
        P(None, None, "dp", "mp"),
        P(),
        P(),
        P(None, None, "dp", "mp"),
        P(None, None, "dp", "mp"),
        P(None, "mp", "dp"),
        P(),
        P(),
        P(None, "mp", "dp"),
        P(None, "mp", "dp"),
        P(None, "dp", "mp"),
        P(),
        P(),
        P(None, "dp", "mp"),
        P(None, "dp", "mp"),
        P(None, "mp", "dp"),
        P(),
        P(),
        P(None, "mp", "dp"),
        P(None, "mp", "dp"),
        P(None, "dp"),
        P(None, "dp"),
        P(None, "dp"),
        P(None, "dp"),
    )
    return jax.shard_map(
        functools.partial(on_device, (mesh.shape["dp"], mesh.shape["mp"])),
        mesh=mesh,
        in_specs=placed,
        out_specs=(
            P("dp", None),
            P("dp", None),
            P("dp", None),
            P(),
            P(None, None, "dp", "mp"),
            P(),
            P(),
            P(None, None, "dp", "mp"),
            P(None, None, "dp", "mp"),
            P(None, None, "dp", "mp"),
            P(None, None, "dp", "mp"),
            P(None, "mp", "dp"),
            P(),
            P(),
            P(None, "mp", "dp"),
            P(None, "mp", "dp"),
            P(None, "mp", "dp"),
            P(None, "mp", "dp"),
            P(None, "dp", "mp"),
            P(),
            P(),
            P(None, "dp", "mp"),
            P(None, "dp", "mp"),
            P(None, "dp", "mp"),
            P(None, "dp", "mp"),
            P(None, "mp", "dp"),
            P(),
            P(),
            P(None, "mp", "dp"),
            P(None, "mp", "dp"),
            P(None, "mp", "dp"),
            P(None, "mp", "dp"),
            P(None, "dp"),
            P(None, "dp"),
            P(None, "dp"),
            P(None, "dp"),
            P(None, "dp"),
            P(None, "dp"),
        ),
        check_vma=False,
    )
```

time: 639 us -> 524 us (0.82)
  Pallas kernels: 0 us -> 117 us
  local copies, waits for them, and re-layouts: 162 us -> 78.1 us
  matrix products: 72.8 us -> 0 us
  other arithmetic: 97.8 us -> 50.7 us
  waiting for transfers between devices: 219 us -> 179 us
  starting transfers between devices: 70 us -> 82.5 us
    pallas_call x0 -> x17, Pallas kernels: none -> 117 us  [call(): pl.pallas_call(body, name=name, out_shape=outs, grid_spec=pltpu.PrefetchS...]
    dot_general x66 -> x0, matrix products: 72.8 us -> none  [the longest x16 25.1 us: mm_t(): return jnp.einsum('ptm,dm->ptd', left, right, preferred_element_type=f32)]
    ppermute x100 -> x78, waiting for transfers between devices: 219 us -> 179 us  [swap(): return lax.ppermute(value, axis, [(i, i ^ bit) for i in range(count)])]
    dynamic_update_slice x34 -> x1, local copies, waits for them, and re-layouts: 26 us -> 0.09 us  [on_device(): lax.dynamic_update_slice(jnp.zeros((5, D), low), norm_gains.astype(low),...]
    unnamed x502 -> x226, local copies, waits for them, and re-layouts: 41.7 us -> 17.8 us
    pallas_call x0 -> x8, local copies, waits for them, and re-layouts: none -> 16.7 us  [call(): pl.pallas_call(body, name=name, out_shape=outs, grid_spec=pltpu.PrefetchS...]
    ppermute x100 -> x78, starting transfers between devices: 70 us -> 82.5 us  [swap(): return lax.ppermute(value, axis, [(i, i ^ bit) for i in range(count)])]
    slice x19 -> x1, local copies, waits for them, and re-layouts: 12.5 us -> 0.6 us  [on_device(): gains = [gain_rows[i:i + 1] for i in range(5)]]
  transfers between devices with their start and end apart: 100 -> 78, of which waited for: 42 -> 37; matrix products, arithmetic and copies ran while one was open for 45% -> 21% of each run, Pallas kernels for 0% -> 16%
where the time goes in v2:
time: 524 us; the launch traced here: 516 us
  waiting for transfers between devices  179 us (34%)
  Pallas kernels  117 us (22%)
  starting transfers between devices  82.5 us (16%)
  local copies, waits for them, and re-layouts  78.1 us (15%)
  other arithmetic  50.7 us (10%)
  between operations  8.66 us (2%)
    ppermute x78, waiting for transfers between devices, swap(): return lax.ppermute(value, axis, [(i, i ^ bit) for i in range(count)])  179 us
    pallas_call x17, Pallas kernels, call(): pl.pallas_call(body, name=name, out_shape=outs, grid_spec=pltpu.PrefetchS...  117 us
    ppermute x78, starting transfers between devices, swap(): return lax.ppermute(value, axis, [(i, i ^ bit) for i in range(count)])  82.5 us
    unnamed x226, local copies, waits for them, and re-layouts  17.8 us
    pallas_call x8, local copies, waits for them, and re-layouts, call(): pl.pallas_call(body, name=name, out_shape=outs, grid_spec=pltpu.PrefetchS...  16.7 us
  transfers between devices with their start and end apart: 78, of which 37 were waited for; matrix products, arithmetic and copies ran while one was open for 21% of the time, Pallas kernels for 16%

profile of v2, /device:TPU:0, one launch (start us, length us, event | category | flops | bytes accessed | tf_op | source)
XLA Modules:
  0.0 515.9 jit_solution(10431430996159201820)
XLA Ops:
  20.9 5.2 collective-permute-done.4
  34.5 6.1 %collective-permute-done.13.rest_1_ = bf16[4,1,96,768]{3,2,1,0:T(8,128)(2,1)S(1)} collective-permute-done((bf16[4,1,96,768]{3,2,1,0:T(8,128)(2,1)S(1)}, bf16[4,1,96,768]{3,2,1,0:T(8,128)(2,1)S(1)}, u32[]{:S(2)}, u32[]{:S(2)}) %collective-permute-start.13) | collective-permute-done | bytes 589856 | tf_op jit(solution)/shard_map/ppermute | solution.py:741
  41.4 9.4 %encoder_attention.1 = (bf16[2,228,768]{2,1,0:T(8,128)(2,1)}, bf16[2,228,768]{2,1,0:T(8,128)(2,1)}, bf16[4,228,768]{2,1,0:T(8,128)(2,1)}) custom-call(s32[13]{0:T(128)} %concatenate.124.meta, bf16[2,228,768]{2,1,0:T(8,128)(2,1)} %get-tuple-element.196.own_ref.base_ref.in_ref, bf16[2,228,768]{2,1,0:T(8,128)(2,1)} %get-tuple-element.195.oth_ref, ...), custom_call_target="tpu_custom_call" | custom-call | tf_op jit(solution)/shard_map/encoder_attention/pallas_call | solution.py:130
  57.0 14.0 %collective-permute-done.5 = bf16[2,96,768]{2,1,0:T(8,128)(2,1)S(1)} collective-permute-done((bf16[2,96,768]{2,1,0:T(8,128)(2,1)S(1)}, bf16[2,96,768]{2,1,0:T(8,128)(2,1)S(1)}, u32[]{:S(2)}, u32[]{:S(2)}) %collective-permute-start.5) | collective-permute-done | bytes 294944 | tf_op jit(solution)/shard_map/ppermute | solution.py:741
  74.1 12.2 %collective-permute-done.6 = bf16[2,2,96,768]{3,2,1,0:T(8,128)(2,1)S(1)} collective-permute-done((bf16[2,2,96,768]{3,2,1,0:T(8,128)(2,1)S(1)}, bf16[2,2,96,768]{3,2,1,0:T(8,128)(2,1)S(1)}, u32[]{:S(2)}, u32[]{:S(2)}) %collective-permute-start.6) | collective-permute-done | bytes 589856 | tf_op jit(solution)/shard_map/ppermute | solution.py:741
  99.5 7.6 %collective-permute-done.7 = bf16[1,96,768]{2,1,0:T(8,128)(2,1)S(1)} collective-permute-done((bf16[1,96,768]{2,1,0:T(8,128)(2,1)S(1)}, bf16[1,96,768]{2,1,0:T(8,128)(2,1)S(1)}, u32[]{:S(2)}, u32[]{:S(2)}) %collective-permute-start.7) | collective-permute-done | bytes 147488 | tf_op jit(solution)/shard_map/ppermute | solution.py:741
  108.2 5.2 %collective-permute-done.17.rest_1_ = bf16[4,2,96,768]{3,2,1,0:T(8,128)(2,1)S(1)} collective-permute-done((bf16[4,2,96,768]{3,2,1,0:T(8,128)(2,1)S(1)}, bf16[4,2,96,768]{3,2,1,0:T(8,128)(2,1)S(1)}, u32[]{:S(2)}, u32[]{:S(2)}) %collective-permute-start.17) | collective-permute-done | bytes 1179680 | tf_op jit(solution)/shard_map/ppermute | solution.py:741
  114.5 7.9 %encoder_feed.1 = (bf16[2,228,768]{2,1,0:T(8,128)(2,1)}, bf16[2,228,768]{2,1,0:T(8,128)(2,1)}) custom-call(s32[13]{0:T(128)} %concatenate.124.meta, bf16[2,228,768]{2,1,0:T(8,128)(2,1)} %get-tuple-element.104.own_ref, bf16[2,228,768]{2,1,0:T(8,128)(2,1)} %copy.132.oth_ref, bf16[4,2,96,768]{3,2,1,0:T(8,128)(2,1)} %copy-done.1, bf16[4,2,96,768]{3,2,1,0:T(8,128)(2,1)} %copy-done.12), custom_call_target="tpu_custom_call" | custom-call | tf_op jit(solution)/shard_map/encoder_feed/pallas_call | solution.py:130
  127.2 7.7 %collective-permute-done.21 = bf16[1,96,768]{2,1,0:T(8,128)(2,1)S(1)} collective-permute-done((bf16[1,96,768]{2,1,0:T(8,128)(2,1)S(1)}, bf16[1,96,768]{2,1,0:T(8,128)(2,1)S(1)}, u32[]{:S(2)}, u32[]{:S(2)}) %collective-permute-start.21) | collective-permute-done | bytes 147488 | tf_op jit(solution)/shard_map/ppermute | solution.py:741
  135.7 8.0 %collective-permute-done.22 = bf16[2,1,96,768]{3,2,1,0:T(8,128)(2,1)S(1)} collective-permute-done((bf16[2,1,96,768]{3,2,1,0:T(8,128)(2,1)S(1)}, bf16[2,1,96,768]{3,2,1,0:T(8,128)(2,1)S(1)}, u32[]{:S(2)}, u32[]{:S(2)}) %collective-permute-start.22) | collective-permute-done | bytes 294944 | tf_op jit(solution)/shard_map/ppermute | solution.py:741
  149.0 10.1 %collective-permute-done.27 = bf16[2,96,768]{2,1,0:T(8,128)(2,1)S(1)} collective-permute-done((bf16[2,96,768]{2,1,0:T(8,128)(2,1)S(1)}, bf16[2,96,768]{2,1,0:T(8,128)(2,1)S(1)}, u32[]{:S(2)}, u32[]{:S(2)}) %collective-permute-start.27) | collective-permute-done | bytes 294944 | tf_op jit(solution)/shard_map/ppermute | solution.py:741
  186.0 8.2 %decoder_cross.1 = (bf16[2,32,768]{2,1,0:T(8,128)(2,1)}, bf16[2,32,768]{2,1,0:T(8,128)(2,1)}, bf16[4,32,384]{2,1,0:T(8,128)(2,1)}, bf16[4,228,384]{2,1,0:T(8,128)(2,1)}) custom-call(s32[13]{0:T(128)} %concatenate.124.meta, bf16[2,32,768]{2,1,0:T(8,128)(2,1)} %bitcast.235, bf16[2,32,768]{2,1,0:T(8,128)(2,1)} %bitcast.237, bf16[2,228,768]{2,1,0:T(8,128)(2,1)} %copy-done, ...), custom_call_target="tpu_custom_call" | custom-call | tf_op jit(solution)/shard_map/decoder_cross/pallas_call | solution.py:130
  207.3 7.1 %decoder_feed.1 = (bf16[2,64,768]{2,1,0:T(8,128)(2,1)}, bf16[2,64,768]{2,1,0:T(8,128)(2,1)}, bf16[2,4,96,768]{3,2,1,0:T(8,128)(2,1)}, f32[2,4,96,768]{3,2,1,0:T(8,128)}) custom-call(s32[13]{0:T(128)} %concatenate.124.meta, bf16[64,768]{1,0:T(8,128)(2,1)} %get-tuple-element.111.own_ref, bf16[64,768]{1,0:T(8,128)(2,1)} %copy-done.72, ...), custom_call_target="tpu_custom_call" | custom-call | tf_op jit(solution)/shard_map/decoder_feed/pallas_call | solution.py:130
  219.3 4.8 collective-permute-done.31
  229.6 17.2 %decoder_cross_back.1 = (bf16[2,32,768]{2,1,0:T(8,128)(2,1)}, bf16[2,32,768]{2,1,0:T(8,128)(2,1)}, bf16[2,228,768]{2,1,0:T(8,128)(2,1)}, bf16[2,228,768]{2,1,0:T...) custom-call(s32[13]{0:T(128)} %concatenate.124.meta, bf16[2,32,768]{2,1,0:T(8,128)(2,1)} %bitcast.236, ...), custom_call_target="tpu_custom_call" | custom-call | tf_op jit(solution)/shard_map/decoder_cross_back/pallas_call | solution.py:130
  259.8 6.4 %decoder_self_back.1 = (bf16[64,768]{1,0:T(8,128)(2,1)}, bf16[64,768]{1,0:T(8,128)(2,1)}, bf16[1,4,96,768]{3,2,1,0:T(8,128)(2,1)}, f32[1,4,96,768]{3,2,1,0:T(8,128)}) custom-call(s32[13]{0:T(128)} %concatenate.124.meta, bf16[128,768]{1,0:T(8,128)(2,1)} %bitcast.211, f32[1,768]{1,0:T(1,128)} %get-tuple-element.238.gain_ref, ...), custom_call_target="tpu_custom_call" | custom-call | tf_op jit(solution)/shard_map/decoder_self_back/pallas_call | solution.py:130
  277.9 21.3 %collective-permute-done.55 = bf16[1,4,96,768]{3,2,1,0:T(8,128)(2,1)S(1)} collective-permute-done((bf16[1,4,96,768]{3,2,1,0:T(8,128)(2,1)S(1)}, bf16[1,4,96,768]{3,2,1,0:T(8,128)(2,1)S(1)}, u32[]{:S(2)}, u32[]{:S(2)}) %collective-permute-start.55) | collective-permute-done | bytes 589856 | tf_op jit(solution)/shard_map/ppermute | solution.py:741
  319.3 14.7 %encoder_feed_back.1 = (bf16[2,228,768]{2,1,0:T(8,128)(2,1)}, bf16[2,228,768]{2,1,0:T(8,128)(2,1)}, bf16[2,4,96,768]{3,2,1,0:T(8,128)(2,1)}, f32[2,4,96,768]{3,2,1,0:T(8,128)}) custom-call(s32[13]{0:T(128)} %concatenate.124.meta, bf16[2,228,768]{2,1,0:T(8,128)(2,1)} %get-tuple-element.104.own_ref, bf16[2,228,768]{2,1,0:T(8,128)(2,1)} %copy.132.oth_ref, ...), custom_call_target="tpu_custom_call" | custom-call | tf_op jit(solution)/shard_map/encoder_feed_back/pallas_call | solution.py:130
  359.6 7.8 %collective-permute-done.38 = bf16[2,228,768]{2,0,1:T(2,128)(2,1)S(1)} collective-permute-done((bf16[2,228,768]{2,0,1:T(2,128)(2,1)S(1)}, bf16[2,228,768]{2,0,1:T(2,128)(2,1)S(1)}, u32[]{:S(2)}, u32[]{:S(2)}) %collective-permute-start.38) | collective-permute-done | bytes 700448 | tf_op jit(solution)/shard_map/ppermute | solution.py:741
  368.3 4.4 norm_back_mid.1
  380.8 16.8 %encoder_attention_back.1 = (bf16[2,228,768]{2,1,0:T(8,128)(2,1)}, bf16[2,228,768]{2,1,0:T(8,128)(2,1)}, bf16[1,4,96,768]{3,2,1,0:T(8,128)(2,1)}, f32[1,4,96,768]{3,2,1,0:T(8,128)}) custom-call(s32[13]{0:T(128)} %concatenate.124.meta, bf16[2,228,768]{2,1,0:T(8,128)(2,1)} %get-tuple-element.196.own_ref.base_ref.in_ref, ...), custom_call_target="tpu_custom_call" | custom-call | tf_op jit(solution)/shard_map/encoder_attention_back/pallas_call | solution.py:130
  401.1 11.2 %collective-permute-done.49 = bf16[1,4,96,768]{3,2,1,0:T(8,128)(2,1)S(1)} collective-permute-done((bf16[1,4,96,768]{3,2,1,0:T(8,128)(2,1)}, bf16[1,4,96,768]{3,2,1,0:T(8,128)(2,1)S(1)}, u32[]{:S(2)}, u32[]{:S(2)}) %collective-permute-start.49) | collective-permute-done | bytes 589856 | tf_op jit(solution)/shard_map/ppermute | solution.py:741
  420.5 5.0 collective-permute-done.50
  431.5 5.3 %collective-permute-done.51 = bf16[1,1,96,768]{2,3,1,0:T(8,128)(2,1)S(1)} collective-permute-done((bf16[1,1,96,768]{2,3,1,0:T(8,128)(2,1)S(1)}, bf16[1,1,96,768]{2,3,1,0:T(8,128)(2,1)S(1)}, u32[]{:S(2)}, u32[]{:S(2)}) %collective-permute-start.51) | collective-permute-done | bytes 147488 | tf_op jit(solution)/shard_map/ppermute | solution.py:741
  (603 shorter events, 284.0 us)
Async XLA Ops:
  1.6 17.7 %collective-permute-start = (bf16[5,768]{1,0:T(8,128)(2,1)S(1)}, bf16[5,768]{1,0:T(8,128)(2,1)S(1)}, u32[]{:S(2)}, u32[]{:S(2)}) collective-permute-start(bf16[5,768]{1,0:T(8,128)(2,1)S(1)} %dynamic_update_slice.15), channel_id=1, source_target_pairs={{0,4},{4,0},{8,12},{12,8},{16,20},{20,16},{24,28},{28,24},{1,5},{5... | collective-permute-start | bytes 23048 | tf_op jit(solution)/shard_map/ppermute | solution.py:741
  52.5 19.3 %collective-permute-start.14 = (bf16[2,228,768]{2,0,1:T(2,128)(2,1)S(1)}, bf16[2,228,768]{2,0,1:T(2,128)(2,1)S(1)}, u32[]{:S(2)}, u32[]{:S(2)}) collective-permute-start(bf16[2,228,768]{2,0,1:T(2,128)(2,1)S(1)} %copy.127), channel_id=1, source_target_pairs={{0,1},{1,0},{2,3},{3,2},{4,5},{5,4},{6,7},{7,6},{8,9},{9,8},{10,11... | collective-permute-start | bytes 2101256 | tf_op jit(solution)/shard_map/ppermute | solution.py:741
  52.6 18.4 %collective-permute-start.5 = (bf16[2,96,768]{2,1,0:T(8,128)(2,1)S(1)}, bf16[2,96,768]{2,1,0:T(8,128)(2,1)S(1)}, u32[]{:S(2)}, u32[]{:S(2)}) collective-permute-start(bf16[2,96,768]{2,1,0:T(8,128)(2,1)S(1)} %pad_maximum_fusion.15), channel_id=1, source_target_pairs={{0,16},{4,20},{8,24},{12,28},{16,0},{20,4},{24,8},{28,12},{1,17},{... | collective-permute-start | bytes 884744 | tf_op jit(solution)/shard_map/ppermute | solution.py:741
  72.5 17.4 %collective-permute-start.15 = (bf16[2,228,768]{2,0,1:T(2,128)(2,1)S(1)}, bf16[2,228,768]{2,0,1:T(2,128)(2,1)S(1)}, u32[]{:S(2)}, u32[]{:S(2)}) collective-permute-start(bf16[2,228,768]{2,0,1:T(2,128)(2,1)S(1)} %copy.129), channel_id=1, source_target_pairs={{0,2},{1,3},{2,0},{3,1},{4,6},{5,7},{6,4},{7,5},{8,10},{9,11},{10,... | collective-permute-start | bytes 2101256 | tf_op jit(solution)/shard_map/ppermute | solution.py:741
  86.4 27.0 %collective-permute-start.17 = (bf16[4,2,96,768]{3,2,1,0:T(8,128)(2,1)S(1)}, bf16[4,2,96,768]{3,2,1,0:T(8,128)(2,1)S(1)}, u32[]{:S(2)}, u32[]{:S(2)}) collective-permute-start(bf16[4,2,96,768]{3,2,1,0:T(8,128)(2,1)S(1)} %pad_maximum_fusion.1.rest_0_), channel_id=1, source_target_pairs={{0,4},{4,0},{8,12},{12,8},{16,20},{20,16},{24,28},{28,24},{1,5},{5... | collective-permute-start | bytes 3538952 | tf_op jit(solution)/shard_map/ppermute | solution.py:741
  107.2 17.2 %collective-permute-start.8 = (bf16[2,1,96,768]{3,2,1,0:T(8,128)(2,1)S(1)}, bf16[2,1,96,768]{3,2,1,0:T(8,128)(2,1)S(1)}, u32[]{:S(2)}, u32[]{:S(2)}) collective-permute-start(bf16[2,1,96,768]{3,2,1,0:T(8,128)(2,1)S(1)} %pad_maximum_fusion.17), channel_id=1, source_target_pairs={{0,8},{4,12},{8,0},{12,4},{16,24},{20,28},{24,16},{28,20},{1,9},{5... | collective-permute-start | bytes 884744 | tf_op jit(solution)/shard_map/ppermute | solution.py:741
  124.1 22.1 %collective-permute-start.18 = (bf16[2,228,768]{2,0,1:T(2,128)(2,1)S(1)}, bf16[2,228,768]{2,0,1:T(2,128)(2,1)S(1)}, u32[]{:S(2)}, u32[]{:S(2)}) collective-permute-start(bf16[2,228,768]{2,0,1:T(2,128)(2,1)S(1)} %copy.133), channel_id=1, source_target_pairs={{0,1},{1,0},{2,3},{3,2},{4,5},{5,4},{6,7},{7,6},{8,9},{9,8},{10,11... | collective-permute-start | bytes 2101256 | tf_op jit(solution)/shard_map/ppermute | solution.py:741
  146.9 20.6 %collective-permute-start.19 = (bf16[2,228,768]{2,0,1:T(2,128)(2,1)S(1)}, bf16[2,228,768]{2,0,1:T(2,128)(2,1)S(1)}, u32[]{:S(2)}, u32[]{:S(2)}) collective-permute-start(bf16[2,228,768]{2,0,1:T(2,128)(2,1)S(1)} %copy.135), channel_id=1, source_target_pairs={{0,2},{1,3},{2,0},{3,1},{4,6},{5,7},{6,4},{7,5},{8,10},{9,11},{10,... | collective-permute-start | bytes 2101256 | tf_op jit(solution)/shard_map/ppermute | solution.py:741
  160.8 24.6 %collective-permute-start.23 = (bf16[4,1,96,768]{3,2,1,0:T(8,128)(2,1)S(1)}, bf16[4,1,96,768]{3,2,1,0:T(8,128)(2,1)}, u32[]{:S(2)}, u32[]{:S(2)}) collective-permute-start(bf16[4,1,96,768]{3,2,1,0:T(8,128)(2,1)S(1)} %pad_maximum_fusion.7.rest_0_), channel_id=1, source_target_pairs={{0,4},{4,0},{8,12},{12,8},{16,20},{20,16},{24,28},{28,24},{1,5},{5... | collective-permute-start | bytes 1769480 | tf_op jit(solution)/shard_map/ppermute | solution.py:741
  174.9 31.0 %collective-permute-start.29 = (bf16[4,2,96,768]{3,2,1,0:T(8,128)(2,1)S(1)}, bf16[4,2,96,768]{3,2,1,0:T(8,128)(2,1)}, u32[]{:S(2)}, u32[]{:S(2)}) collective-permute-start(bf16[4,2,96,768]{3,2,1,0:T(8,128)(2,1)S(1)} %pad_maximum_fusion.2.rest_0_), channel_id=1, source_target_pairs={{0,4},{4,0},{8,12},{12,8},{16,20},{20,16},{24,28},{28,24},{1,5},{5... | collective-permute-start | bytes 3538952 | tf_op jit(solution)/shard_map/ppermute | solution.py:741
  248.7 22.1 %collective-permute-start.34 = (bf16[2,228,768]{2,0,1:T(2,128)(2,1)S(1)}, bf16[2,228,768]{2,0,1:T(2,128)(2,1)S(1)}, u32[]{:S(2)}, u32[]{:S(2)}) collective-permute-start(bf16[2,228,768]{2,0,1:T(2,128)(2,1)S(1)} %copy.141), channel_id=1, source_target_pairs={{0,1},{1,0},{2,3},{3,2},{4,5},{5,4},{6,7},{7,6},{8,9},{9,8},{10,11... | collective-permute-start | bytes 2101256 | tf_op jit(solution)/shard_map/ppermute | solution.py:741
  257.6 49.0 %collective-permute-start.61 = (bf16[2,4,96,768]{3,2,1,0:T(8,128)(2,1)}, bf16[2,4,96,768]{3,2,1,0:T(8,128)(2,1)}, u32[]{:S(2)}, u32[]{:S(2)}) collective-permute-start(bf16[2,4,96,768]{3,2,1,0:T(8,128)(2,1)} %get-tuple-element.146), channel_id=1, source_target_pairs={{0,4},{4,0},{8,12},{12,8},{16,20},{20,16},{24,28},{28,24},{1,5},{5... | collective-permute-start | bytes 3538952 | tf_op jit(solution)/shard_map/ppermute | solution.py:741
  266.8 32.3 %collective-permute-start.55 = (bf16[1,4,96,768]{3,2,1,0:T(8,128)(2,1)S(1)}, bf16[1,4,96,768]{3,2,1,0:T(8,128)(2,1)S(1)}, u32[]{:S(2)}, u32[]{:S(2)}) collective-permute-start(bf16[1,4,96,768]{3,2,1,0:T(8,128)(2,1)S(1)} %copy-done.107), channel_id=1, source_target_pairs={{0,4},{4,0},{8,12},{12,8},{16,20},{20,16},{24,28},{28,24},{1,5},{5... | collective-permute-start | bytes 1769480 | tf_op jit(solution)/shard_map/ppermute | solution.py:741
  272.3 31.0 %collective-permute-start.35 = (bf16[2,228,768]{2,0,1:T(2,128)(2,1)}, bf16[2,228,768]{2,0,1:T(2,128)(2,1)}, u32[]{:S(2)}, u32[]{:S(2)}) collective-permute-start(bf16[2,228,768]{2,0,1:T(2,128)(2,1)} %copy.143), channel_id=1, source_target_pairs={{0,2},{1,3},{2,0},{3,1},{4,6},{5,7},{6,4},{7,5},{8,10},{9,11},{10,... | collective-permute-start | bytes 2101256 | tf_op jit(solution)/shard_map/ppermute | solution.py:741
  273.7 62.9 %collective-permute-start.52 = (bf16[1,4,96,768]{3,2,1,0:T(8,128)(2,1)}, bf16[1,4,96,768]{3,2,1,0:T(8,128)(2,1)}, u32[]{:S(2)}, u32[]{:S(2)}) collective-permute-start(bf16[1,4,96,768]{3,2,1,0:T(8,128)(2,1)} %get-tuple-element.140), channel_id=1, source_target_pairs={{0,4},{4,0},{8,12},{12,8},{16,20},{20,16},{24,28},{28,24},{1,5},{5... | collective-permute-start | bytes 1769480 | tf_op jit(solution)/shard_map/ppermute | solution.py:741
  277.9 165.4 %collective-permute-start.48 = (f32[2,32,768]{2,1,0:T(8,128)}, f32[2,32,768]{2,1,0:T(8,128)}, u32[]{:S(2)}, u32[]{:S(2)}) collective-permute-start(f32[2,32,768]{2,1,0:T(8,128)} %bitcast.249), channel_id=1, source_target_pairs={{0,1},{1,0},{2,3},{3,2},{4,5},{5,4},{6,7},{7,6},{8,9},{9,8},{10,11... | collective-permute-start | bytes 589832 | tf_op jit(solution)/shard_map/ppermute | solution.py:741
  309.1 46.3 %collective-permute-start.62 = (bf16[2,2,96,768]{3,2,1,0:T(8,128)(2,1)}, bf16[2,2,96,768]{3,2,1,0:T(8,128)(2,1)}, u32[]{:S(2)}, u32[]{:S(2)}) collective-permute-start(bf16[2,2,96,768]{3,2,1,0:T(8,128)(2,1)} %fusion.1), channel_id=1, source_target_pairs={{0,8},{4,12},{8,0},{12,4},{16,24},{20,28},{24,16},{28,20},{1,9},{5... | collective-permute-start | bytes 1769480 | tf_op jit(solution)/shard_map/ppermute | solution.py:741
  314.8 30.3 %collective-permute-start.57 = (bf16[1,1,96,768]{2,3,1,0:T(8,128)(2,1)}, bf16[1,1,96,768]{2,3,1,0:T(8,128)(2,1)}, u32[]{:S(2)}, u32[]{:S(2)}) collective-permute-start(bf16[1,1,96,768]{2,3,1,0:T(8,128)(2,1)} %dynamic-slice_convert_fusion.2), channel_id=1, source_target_pairs={{0,16},{4,20},{8,24},{12,28},{16,0},{20,4},{24,8},{28,12},{1,17},{... | collective-permute-start | bytes 442376 | tf_op jit(solution)/shard_map/ppermute | solution.py:741
  345.2 29.3 %collective-permute-start.58 = (bf16[2,4,96,768]{3,2,1,0:T(8,128)(2,1)}, bf16[2,4,96,768]{3,2,1,0:T(8,128)(2,1)S(1)}, u32[]{:S(2)}, u32[]{:S(2)}) collective-permute-start(bf16[2,4,96,768]{3,2,1,0:T(8,128)(2,1)} %get-tuple-element.144), channel_id=1, source_target_pairs={{0,4},{4,0},{8,12},{12,8},{16,20},{20,16},{24,28},{28,24},{1,5},{5... | collective-permute-start | bytes 3538952 | tf_op jit(solution)/shard_map/ppermute | solution.py:741
  349.8 17.6 %collective-permute-start.38 = (bf16[2,228,768]{2,0,1:T(2,128)(2,1)S(1)}, bf16[2,228,768]{2,0,1:T(2,128)(2,1)S(1)}, u32[]{:S(2)}, u32[]{:S(2)}) collective-permute-start(bf16[2,228,768]{2,0,1:T(2,128)(2,1)S(1)} %copy.150), channel_id=1, source_target_pairs={{0,2},{1,3},{2,0},{3,1},{4,6},{5,7},{6,4},{7,5},{8,10},{9,11},{10,... | collective-permute-start | bytes 2101256 | tf_op jit(solution)/shard_map/ppermute | solution.py:741
  355.3 22.2 %collective-permute-start.54 = (bf16[1,1,96,768]{2,3,1,0:T(8,128)(2,1)S(1)}, bf16[1,1,96,768]{2,3,1,0:T(8,128)(2,1)}, u32[]{:S(2)}, u32[]{:S(2)}) collective-permute-start(bf16[1,1,96,768]{2,3,1,0:T(8,128)(2,1)S(1)} %dynamic-slice_convert_fusion.3), channel_id=1, source_target_pairs={{0,16},{4,20},{8,24},{12,28},{16,0},{20,4},{24,8},{28,12},{1,17},{... | collective-permute-start | bytes 442376 | tf_op jit(solution)/shard_map/ppermute | solution.py:741
  356.6 23.2 %collective-permute-start.63 = (bf16[2,1,96,768]{3,2,1,0:T(8,128)(2,1)S(1)}, bf16[2,1,96,768]{3,2,1,0:T(8,128)(2,1)S(1)}, u32[]{:S(2)}, u32[]{:S(2)}) collective-permute-start(bf16[2,1,96,768]{3,2,1,0:T(8,128)(2,1)S(1)} %dynamic-slice_convert_fusion), channel_id=1, source_target_pairs={{0,16},{4,20},{8,24},{12,28},{16,0},{20,4},{24,8},{28,12},{1,17},{... | collective-permute-start | bytes 884744 | tf_op jit(solution)/shard_map/ppermute | solution.py:741
  377.1 23.1 %collective-permute-start.59 = (bf16[2,2,96,768]{3,2,1,0:T(8,128)(2,1)S(1)}, bf16[2,2,96,768]{3,2,1,0:T(8,128)(2,1)S(1)}, u32[]{:S(2)}, u32[]{:S(2)}) collective-permute-start(bf16[2,2,96,768]{3,2,1,0:T(8,128)(2,1)S(1)} %fusion), channel_id=1, source_target_pairs={{0,8},{4,12},{8,0},{12,4},{16,24},{20,28},{24,16},{28,20},{1,9},{5... | collective-permute-start | bytes 1769480 | tf_op jit(solution)/shard_map/ppermute | solution.py:741
  450.2 17.6 %collective-permute-start.41 = (bf16[2,228,768]{2,0,1:T(2,128)(2,1)}, bf16[2,228,768]{2,0,1:T(2,128)(2,1)}, u32[]{:S(2)}, u32[]{:S(2)}) collective-permute-start(bf16[2,228,768]{2,0,1:T(2,128)(2,1)} %copy.156), channel_id=1, source_target_pairs={{0,2},{1,3},{2,0},{3,1},{4,6},{5,7},{6,4},{7,5},{8,10},{9,11},{10,... | collective-permute-start | bytes 2101256 | tf_op jit(solution)/shard_map/ppermute | solution.py:741
  (164 other events, 986.5 us)

commit v3 on v2

--- a/solution.py
+++ b/solution.py
@@ -28,6 +28,8 @@
 LOW = jnp.bfloat16
 F32 = jnp.float32
 VMEM_LIMIT = 56 * 1024 * 1024
+LONG = (ENC_LEN + 7) // 8 * 8
+EXACT = lax.Precision.HIGHEST
 
 
 def dot(left, right, contract):
@@ -65,6 +67,11 @@
     return value, slope
 
 
+class Weight:
+    def __init__(self, arrays, first=0, count=1):
+        self.arrays, self.first, self.count = tuple(arrays), first, count
+
+
 class Plan:
     def __init__(self, dp_n, block, width, hidden, pairs):
         self.dp_n, self.block, self.width, self.hidden, self.pairs = dp_n, block, width, hidden, pairs
@@ -73,37 +80,42 @@
         self.direct = dp_n == 8
 
     def weight_specs(self, pieces):
-        return [pl.BlockSpec(item.shape, lambda *_, n=item.ndim: (0,) * n) for item in pieces]
+        specs = []
+        for item in pieces.arrays:
+            lead = item.shape[:-3]
+            shape = lead + (pieces.count,) + item.shape[-2:]
+            at = (0,) * len(lead) + (pieces.first // pieces.count, 0, 0)
+            specs.append(pl.BlockSpec(shape, lambda *_, at=at: at))
+        return specs
 
     def weight_scratch(self, pieces, count):
         return [pltpu.VMEM((count, D, D), LOW)]
 
-    def assemble(self, meta, refs, scratch):
+    def assemble(self, meta, pieces, refs, scratch):
         if not self.direct:
             scratch[...] = refs[0][...]
             return
-        for ref, places in zip(refs, ((0, 4, 2, 6), (1, 5, 3, 7))):
+        for ref, places in zip(refs, ((0, 4), (2, 6), (1, 5), (3, 7))):
             for index, place in enumerate(places):
                 row = pl.multiple_of(jnp.bitwise_xor(meta[0], place) * self.block, 32)
-                scratch[:, pl.ds(row, self.block), :] = ref[index]
+                scratch[:, pl.ds(row, self.block), :] = ref[index, :, : self.block]
 
     def grad_shapes(self, count):
         if not self.direct:
             return [jax.ShapeDtypeStruct((count, D, D), F32)]
-        shape = (count, self.dp_n // 2, self.block, D)
+        shape = (self.dp_n // 2, count, self.block, D)
         return [jax.ShapeDtypeStruct(shape, LOW), jax.ShapeDtypeStruct(shape, F32)]
 
     def emit(self, meta, acc, refs):
         if not self.direct:
             refs[0][...] = acc[...]
             return
-        mine = jnp.bitwise_and(meta[0], 1)
         for index in range(self.dp_n // 2):
-            away = pl.multiple_of((2 * index + 1 - mine) * self.block, 32)
-            here = pl.multiple_of((2 * index + mine) * self.block, 32)
+            here = pl.multiple_of(jnp.bitwise_xor(meta[0], 2 * index) * self.block, 32)
+            away = pl.multiple_of(jnp.bitwise_xor(meta[0], 2 * index + 1) * self.block, 32)
             for count in range(acc.shape[0]):
-                refs[0][count, index] = acc[count, pl.ds(away, self.block), :].astype(LOW)
-                refs[1][count, index] = acc[count, pl.ds(here, self.block), :]
+                refs[0][index, count] = acc[count, pl.ds(away, self.block), :].astype(LOW)
+                refs[1][index, count] = acc[count, pl.ds(here, self.block), :]
 
 
 def whole(shape):
@@ -138,6 +150,7 @@
             out_specs=out_specs,
             scratch_shapes=scratch,
         ),
+        cost_estimate=pl.CostEstimate(flops=1, transcendentals=0, bytes_accessed=1),
         compiler_params=pltpu.CompilerParams(
             dimension_semantics=("arbitrary",) * len(grid), vmem_limit_bytes=VMEM_LIMIT
         ),
@@ -178,19 +191,23 @@
     return jnp.where(step < count, plan.half + base + step, base + step - count)
 
 
+def pick(step, count, own, oth, rows):
+    return jnp.where(step < count, oth[0, :rows], own[0, :rows])
+
+
 def put(step, count, own, oth, value):
     @pl.when(step < count)
     def _():
-        oth[0] = value
+        oth[0, : value.shape[0]] = value
 
     @pl.when(step >= count)
     def _():
-        own[0] = value
+        own[0, : value.shape[0]] = value
 
 
 def encoder_attention(plan, meta, own, oth, gain, pieces, base, count):
     w3 = 3 * plan.width
-    n = len(pieces)
+    n = len(pieces.arrays)
 
     def body(meta, own_ref, oth_ref, gain_ref, *rest):
         refs, (own_out, oth_out, kept, weight) = rest[:n], rest[n:]
@@ -198,9 +215,9 @@
 
         @pl.when(step == 0)
         def _():
-            plan.assemble(meta, refs, weight)
-
-        value = jnp.where(step < count, oth_ref[0], own_ref[0]).astype(F32)
+            plan.assemble(meta, pieces, refs, weight)
+
+        value = pick(step, count, own_ref, oth_ref, ENC_LEN).astype(F32)
         normed = (value * rms_scale(value) * gain_ref[...]).astype(LOW)
         joined = mm(normed, weight[0, :, :w3]).astype(LOW)
         allowed = key_mask(meta, plan.pairs, slot_of(plan, count, base, step))
@@ -212,13 +229,13 @@
         kept[0, :, w3:] = mixed
         put(step, count, own_out, oth_out, mm_t(mixed, weight[0, :, w3:]).astype(LOW))
 
-    rows = (ENC_LEN, D)
+    rows = (LONG, D)
     return call(
         "encoder_attention",
         body,
         (2 * count,),
         meta,
-        (own, oth, gain, *pieces),
+        (own, oth, gain, *pieces.arrays),
         [own_spec(count, base, rows), oth_spec(count, base, rows), whole((1, D)), *plan.weight_specs(pieces)],
         [jax.ShapeDtypeStruct((count,) + rows, LOW)] * 2
         + [jax.ShapeDtypeStruct((2 * count, ENC_LEN, w3 + plan.width), LOW)],
@@ -230,7 +247,7 @@
 def encoder_attention_back(plan, meta, own, oth, gain, pieces, kept, grad_own, grad_oth):
     count = plan.half
     width, w3 = plan.width, 3 * plan.width
-    n = len(pieces)
+    n = len(pieces.arrays)
 
     def body(meta, own_ref, oth_ref, gain_ref, kept_ref, grad_own_ref, grad_oth_ref, *rest):
         refs, (own_out, oth_out), grad_refs = rest[:n], rest[n : n + 2], rest[n + 2 : -2]
@@ -239,12 +256,12 @@
 
         @pl.when(step == 0)
         def _():
-            plan.assemble(meta, refs, weight)
+            plan.assemble(meta, pieces, refs, weight)
             acc[...] = jnp.zeros_like(acc)
 
-        value = jnp.where(step < count, oth_ref[0], own_ref[0]).astype(F32)
+        value = pick(step, count, own_ref, oth_ref, ENC_LEN).astype(F32)
         normed = (value * rms_scale(value) * gain_ref[...]).astype(LOW)
-        grad = jnp.where(step < count, grad_oth_ref[0], grad_own_ref[0])
+        grad = pick(step, count, grad_own_ref, grad_oth_ref, ENC_LEN)
         allowed = key_mask(meta, plan.pairs, slot_of(plan, count, 0, step))
         grad_mixed = mm(grad, weight[0, :, w3:]).astype(LOW)
         acc[0, :, w3:] += t_mm(grad, kept_ref[0, :, w3:])
@@ -260,7 +277,7 @@
         def _():
             plan.emit(meta, acc, grad_refs)
 
-    rows = (ENC_LEN, D)
+    rows = (LONG, D)
     shapes = plan.grad_shapes(1)
     pair_specs = [own_spec(count, 0, rows), oth_spec(count, 0, rows)]
     return call(
@@ -268,7 +285,7 @@
         body,
         (2 * count,),
         meta,
-        (own, oth, gain, kept, grad_own, grad_oth, *pieces),
+        (own, oth, gain, kept, grad_own, grad_oth, *pieces.arrays),
         [*pair_specs, whole((1, D)), step_spec(kept.shape[1:]), *pair_specs, *plan.weight_specs(pieces)],
         [jax.ShapeDtypeStruct((count,) + rows, LOW)] * 2 + shapes,
         [*pair_specs, *[whole(item.shape) for item in shapes]],
@@ -277,7 +294,7 @@
 
 
 def encoder_feed(plan, meta, own, oth, pieces, base, count):
-    n = len(pieces)
+    n = len(pieces.arrays)
 
     def body(meta, own_ref, oth_ref, *rest):
         refs, (own_out, oth_out, weight) = rest[:n], rest[n:]
@@ -285,19 +302,19 @@
 
         @pl.when(step == 0)
         def _():
-            plan.assemble(meta, refs, weight)
-
-        normed = jnp.where(step < count, oth_ref[0], own_ref[0])
+            plan.assemble(meta, pieces, refs, weight)
+
+        normed = pick(step, count, own_ref, oth_ref, ENC_LEN)
         active = gelu_parts(mm(normed, weight[0]))[0].astype(LOW)
         put(step, count, own_out, oth_out, mm_t(active, weight[1]).astype(LOW))
 
-    rows = (ENC_LEN, D)
+    rows = (LONG, D)
     return call(
         "encoder_feed",
         body,
         (2 * count,),
         meta,
-        (own, oth, *pieces),
+        (own, oth, *pieces.arrays),
         [own_spec(count, base, rows), oth_spec(count, base, rows), *plan.weight_specs(pieces)],
         [jax.ShapeDtypeStruct((count,) + rows, LOW)] * 2,
         [own_spec(count, 0, rows), oth_spec(count, 0, rows)],
@@ -306,7 +323,7 @@
 
 
 def encoder_feed_back(plan, meta, own, oth, grad_own, grad_oth, pieces):
-    n = len(pieces)
+    n = len(pieces.arrays)
     count = plan.half
 
     def body(meta, own_ref, oth_ref, grad_own_ref, grad_oth_ref, *rest):
@@ -316,11 +333,11 @@
 
         @pl.when(step == 0)
         def _():
-            plan.assemble(meta, refs, weight)
+            plan.assemble(meta, pieces, refs, weight)
             acc[...] = jnp.zeros_like(acc)
 
-        normed = jnp.where(step < count, oth_ref[0], own_ref[0])
-        grad = jnp.where(step < count, grad_oth_ref[0], grad_own_ref[0])
+        normed = pick(step, count, own_ref, oth_ref, ENC_LEN)
+        grad = pick(step, count, grad_own_ref, grad_oth_ref, ENC_LEN)
         active, slope = gelu_parts(mm(normed, weight[0]))
         grad_upper = (slope * mm(grad, weight[1])).astype(LOW)
         put(step, count, own_out, oth_out, mm_t(grad_upper, weight[0]).astype(LOW))
@@ -331,7 +348,7 @@
         def _():
             plan.emit(meta, acc, grad_refs)
 
-    rows = (ENC_LEN, D)
+    rows = (LONG, D)
     shapes = plan.grad_shapes(2)
     pair_specs = [own_spec(count, 0, rows), oth_spec(count, 0, rows)]
     return call(
@@ -339,7 +356,7 @@
         body,
         (2 * count,),
         meta,
-        (own, oth, grad_own, grad_oth, *pieces),
+        (own, oth, grad_own, grad_oth, *pieces.arrays),
         [*pair_specs, *pair_specs, *plan.weight_specs(pieces)],
         [jax.ShapeDtypeStruct((count,) + rows, LOW)] * 2 + shapes,
         [*pair_specs, *[whole(item.shape) for item in shapes]],
@@ -359,14 +376,14 @@
 
 
 def decoder_self(plan, meta, rows_in, gain, pieces):
-    n = len(pieces)
+    n = len(pieces.arrays)
     width, w3 = plan.width, 3 * plan.width
     rows = plan.pairs * SUFFIX
     mid = rows // 2
 
     def body(meta, in_ref, gain_ref, *rest):
         refs, (own_out, oth_out, kept, weight) = rest[:n], rest[n:]
-        plan.assemble(meta, refs, weight)
+        plan.assemble(meta, pieces, refs, weight)
         value = in_ref[...].astype(F32)
         normed = (value * rms_scale(value) * gain_ref[...]).astype(LOW)
         joined = mm(normed, weight[0, :, :w3]).astype(LOW)
@@ -384,7 +401,7 @@
         body,
         (1,),
         meta,
-        (rows_in, gain, *pieces),
+        (rows_in, gain, *pieces.arrays),
         [whole((rows, D)), whole((1, D)), *plan.weight_specs(pieces)],
         [jax.ShapeDtypeStruct((mid, D), LOW)] * 2 + [jax.ShapeDtypeStruct((rows, 4 * width), LOW)],
         [whole((mid, D))] * 2 + [whole((rows, 4 * width))],
@@ -393,7 +410,7 @@
 
 
 def decoder_self_back(plan, meta, rows_in, gain, pieces, kept, grad_own, grad_oth):
-    n = len(pieces)
+    n = len(pieces.arrays)
     width, w3 = plan.width, 3 * plan.width
     rows = plan.pairs * SUFFIX
     mid = rows // 2
@@ -401,7 +418,7 @@
     def body(meta, in_ref, gain_ref, kept_ref, grad_own_ref, grad_oth_ref, *rest):
         refs, (own_out, oth_out), grad_refs = rest[:n], rest[n : n + 2], rest[n + 2 : -2]
         weight, acc = rest[-2:]
-        plan.assemble(meta, refs, weight)
+        plan.assemble(meta, pieces, refs, weight)
         value = in_ref[...].astype(F32)
         normed = (value * rms_scale(value) * gain_ref[...]).astype(LOW)
         grad = jnp.concatenate([grad_own_ref[...], grad_oth_ref[...]], 0)
@@ -429,7 +446,7 @@
         body,
         (1,),
         meta,
-        (rows_in, gain, kept, grad_own, grad_oth, *pieces),
+        (rows_in, gain, kept, grad_own, grad_oth, *pieces.arrays),
         [whole((rows, D)), whole((1, D)), whole(kept.shape), whole((mid, D)), whole((mid, D)), *plan.weight_specs(pieces)],
         [jax.ShapeDtypeStruct((mid, D), LOW)] * 2 + shapes,
         [whole((mid, D))] * 2 + [whole(item.shape) for item in shapes],
@@ -438,7 +455,7 @@
 
 
 def decoder_cross(plan, meta, own, oth, memory_own, memory_oth, pieces):
-    n = len(pieces)
+    n = len(pieces.arrays)
     count = plan.half
     width, w3 = plan.width, 3 * plan.width
 
@@ -448,10 +465,10 @@
 
         @pl.when(step == 0)
         def _():
-            plan.assemble(meta, refs, weight)
-
-        normed = jnp.where(step < count, oth_ref[0], own_ref[0])
-        memory = jnp.where(step < count, memory_oth_ref[0], memory_own_ref[0])
+            plan.assemble(meta, pieces, refs, weight)
+
+        normed = pick(step, count, own_ref, oth_ref, SUFFIX)
+        memory = pick(step, count, memory_own_ref, memory_oth_ref, ENC_LEN)
         queries = mm(normed, weight[0, :, :width]).astype(LOW)
         both = mm(memory, weight[0, :, width:w3]).astype(LOW)
         allowed = key_mask(meta, plan.pairs, slot_of(plan, count, 0, step))
@@ -461,13 +478,13 @@
         kept_key[0] = both
         put(step, count, own_out, oth_out, mm_t(mixed, weight[0, :, w3:]).astype(LOW))
 
-    rows, long = (SUFFIX, D), (ENC_LEN, D)
+    rows, long = (SUFFIX, D), (LONG, D)
     return call(
         "decoder_cross",
         body,
         (2 * count,),
         meta,
-        (own, oth, memory_own, memory_oth, *pieces),
+        (own, oth, memory_own, memory_oth, *pieces.arrays),
         [
             own_spec(count, 0, rows),
             oth_spec(count, 0, rows),
@@ -493,7 +510,7 @@
 def decoder_cross_back(
     plan, meta, own, oth, memory_own, memory_oth, pieces, kept_query, kept_key, grad_own, grad_oth
 ):
-    n = len(pieces)
+    n = len(pieces.arrays)
     count = plan.half
     width, w3 = plan.width, 3 * plan.width
 
@@ -506,12 +523,12 @@
 
         @pl.when(step == 0)
         def _():
-            plan.assemble(meta, refs, weight)
+            plan.assemble(meta, pieces, refs, weight)
             acc[...] = jnp.zeros_like(acc)
 
-        normed = jnp.where(step < count, oth_ref[0], own_ref[0])
-        memory = jnp.where(step < count, memory_oth_ref[0], memory_own_ref[0])
-        grad = jnp.where(step < count, grad_oth_ref[0], grad_own_ref[0])
+        normed = pick(step, count, own_ref, oth_ref, SUFFIX)
+        memory = pick(step, count, memory_own_ref, memory_oth_ref, ENC_LEN)
+        grad = pick(step, count, grad_own_ref, grad_oth_ref, SUFFIX)
         allowed = key_mask(meta, plan.pairs, slot_of(plan, count, 0, step))
         grad_mixed = mm(grad, weight[0, :, w3:]).astype(LOW)
         acc[0, :, w3:] += t_mm(grad, query_ref[0, :, width:])
@@ -529,7 +546,7 @@
         def _():
             plan.emit(meta, acc, grad_refs)
 
-    rows, long = (SUFFIX, D), (ENC_LEN, D)
+    rows, long = (SUFFIX, D), (LONG, D)
     shapes = plan.grad_shapes(1)
     row_specs = [own_spec(count, 0, rows), oth_spec(count, 0, rows)]
     long_specs = [own_spec(count, 0, long), oth_spec(count, 0, long)]
@@ -538,7 +555,7 @@
         body,
         (2 * count,),
         meta,
-        (own, oth, memory_own, memory_oth, kept_query, kept_key, grad_own, grad_oth, *pieces),
+        (own, oth, memory_own, memory_oth, kept_query, kept_key, grad_own, grad_oth, *pieces.arrays),
         [
             *row_specs,
             *long_specs,
@@ -556,14 +573,14 @@
 
 
 def decoder_feed(plan, meta, own, oth, grad_in, pieces):
-    n = len(pieces)
+    n = len(pieces.arrays)
     rows = plan.pairs * SUFFIX
     mid = rows // 2
 
     def body(meta, own_ref, oth_ref, grad_ref, *rest):
         refs, (own_out, oth_out), grad_refs = rest[:n], rest[n : n + 2], rest[n + 2 : -2]
         weight, acc = rest[-2:]
-        plan.assemble(meta, refs, weight)
+        plan.assemble(meta, pieces, refs, weight)
         normed = jnp.concatenate([own_ref[...], oth_ref[...]], 0)
         grad = grad_ref[...]
         active, slope = gelu_parts(mm(normed, weight[0]))
@@ -585,7 +602,7 @@
         body,
         (1,),
         meta,
-        (own, oth, grad_in, *pieces),
+        (own, oth, grad_in, *pieces.arrays),
         [whole((mid, D))] * 2 + [whole((rows, D)), *plan.weight_specs(pieces)],
         [jax.ShapeDtypeStruct((2, mid, D), LOW)] * 2 + shapes,
         [whole((2, mid, D))] * 2 + [whole(item.shape) for item in shapes],
@@ -624,8 +641,8 @@
         unit = value * scale
         back = first_ref[...].astype(F32) + second_ref[...].astype(F32)
         product = back * unit
-        axes = tuple(range(value.ndim - 1))
-        part = jnp.sum(product, axes)[None]
+        real = product[0, :ENC_LEN] if value.ndim == 3 else product
+        part = jnp.sum(real, 0, keepdims=True)
         weighted = product * gain_ref[...]
         total = grad_ref[...].astype(F32) + scale * (
             back * gain_ref[...] - unit * jnp.mean(weighted, -1, keepdims=True)
@@ -661,35 +678,317 @@
     )
 
 
-def update_matrix(
-    gradient, weight, rows_old, cols_old, moment, average, row_sum, col_sum, row_index, col_index
-):
-    full_rows = rows_old.shape[-1]
-    full_cols = cols_old.shape[-1]
-    rows_new = DECAY * rows_old + (1.0 - DECAY) * (row_sum / full_cols + EPS_STAT)
-    cols_new = DECAY * cols_old + (1.0 - DECAY) * (col_sum / full_rows + EPS_STAT)
-    row_local = lax.dynamic_slice_in_dim(
-        rows_new, row_index * gradient.shape[-2], gradient.shape[-2], rows_new.ndim - 1
-    )
-    col_local = lax.dynamic_slice_in_dim(
-        cols_new, col_index * gradient.shape[-1], gradient.shape[-1], cols_new.ndim - 1
-    )
-    second = (
-        row_local[..., :, None] * col_local[..., None, :] / jnp.mean(rows_new, -1)[..., None, None]
-    )
-    stepped = gradient * lax.rsqrt(second)
+def fold(plan, meta, keeps, mores, split):
+    n = len(keeps)
+    counts = [item.shape[1] for item in keeps]
+    total = sum(counts)
+    tail = keeps[0].shape[2:]
+    blocks = keeps[0].shape[0]
+
+    def body(meta, *rest):
+        keep_refs, more_refs, outs = rest[:n], rest[n : 2 * n], rest[2 * n :]
+        for index in range(blocks):
+            start = 0
+            out, at = split(index)
+            for keep_ref, more_ref, count in zip(keep_refs, more_refs, counts):
+                value = keep_ref[index] + more_ref[index].astype(F32)
+                outs[out][at, start : start + count] = value.astype(outs[out].dtype)
+                start += count
+
+    places = [split(index) for index in range(blocks)]
+    outs = [
+        jax.ShapeDtypeStruct((sum(place[0] == out for place in places), total) + tail, LOW if out else F32)
+        for out in range(1 + max(place[0] for place in places))
+    ]
+    return call(
+        "fold",
+        body,
+        (1,),
+        meta,
+        (*keeps, *mores),
+        [whole(item.shape) for item in (*keeps, *mores)],
+        outs,
+        [whole(item.shape) for item in outs],
+        [],
+    )
+
+
+def halves(index):
+    return index % 2, index // 2
+
+
+def apart(index):
+    return index, 0
+
+
+def one_hot(rows, offset):
+    row = lax.broadcasted_iota(jnp.int32, (rows, D), 0)
+    lane = lax.broadcasted_iota(jnp.int32, (rows, D), 1)
+    return (lane == row + offset).astype(F32)
+
+
+def collect(plan, meta, pieces, attention):
+    count = pieces[0].shape[-3]
+    n = len(pieces)
+    shape = pieces[0].shape[-3:]
+    groups = D // plan.width
+
+    def body(meta, *rest):
+        refs, (out, tile_out) = rest[:n], rest[n:]
+        dp_at, mp_at = meta[0], meta[1 + 3 * plan.pairs]
+        group = lax.broadcasted_iota(jnp.int32, (8, D), 1) // plan.width
+        row = lax.broadcasted_iota(jnp.int32, (8, D), 0)
+        place = one_hot(plan.block, dp_at * plan.block)
+        for index in range(count):
+            value = refs[0][0, index]
+            for ref in refs[1:]:
+                value = value + ref[0, index].astype(F32)
+            out[index] = value
+            square = value * value
+            lanes = jnp.broadcast_to(jnp.sum(square, 0, keepdims=True), (8, D))
+            if attention:
+                mask = (group == row).astype(F32)
+            else:
+                mask = (row == 0).astype(F32)
+            sums = lax.dot_general(
+                mask, square, (((1,), (1,)), ((), ())), precision=EXACT, preferred_element_type=F32
+            )
+            tile = lax.dot_general(
+                sums, place, (((1,), (0,)), ((), ())), precision=EXACT, preferred_element_type=F32
+            )
+            if attention:
+                spread = jnp.zeros_like(tile)
+                for part in range(groups):
+                    shift = lax.rem(mp_at * plan.width + (D - part * plan.width), D)
+                    moved = pltpu.roll(jnp.where(group == part, lanes, 0.0), shift, 1)
+                    spread = jnp.where(row == 4 + part, moved, spread)
+            else:
+                spread = jnp.where(row == 4 + mp_at, lanes, 0.0)
+            tile_out[index] = jnp.where(row < 4, tile, spread)
+
+    return call(
+        "collect",
+        body,
+        (1,),
+        meta,
+        tuple(pieces),
+        [whole(item.shape) for item in pieces],
+        [jax.ShapeDtypeStruct(shape, F32), jax.ShapeDtypeStruct((count, 8, D), F32)],
+        [whole(shape), whole((count, 8, D))],
+        [],
+    )
+
+
+def finish(plan, meta, early, late, statistics, gain_state):
+    counts = [item.shape for item in statistics]
+
+    def body(meta, early_ref, late_ref, *rest):
+        olds, gains = rest[:8], rest[8:12]
+        norm_out, news, rates, gain_outs = rest[12], rest[13:21], rest[21], rest[22:]
+        tiles = [late_ref[2], early_ref[1], early_ref[0]]
+        feeds = [(late_ref[0], late_ref[1]), (early_ref[2], early_ref[3])]
+        gain_sum = 0.5 * late_ref[3]
+        total = jnp.sum(gain_sum * gain_sum)
+        for tile in tiles:
+            total = total + jnp.sum(tile[:4])
+        for up, down in feeds:
+            total = total + jnp.sum(up[:1]) + jnp.sum(down[:1])
+        totals = jnp.full((8, D), total, F32)
+        norm = jnp.sqrt(totals)
+        factor = jnp.minimum(1.0, 1.0 / norm)
+        squared = (factor * factor)[:1]
+        norm_out[...] = norm[:, :128]
+        rates[...] = factor[:, :128]
+
+        def renew(old, sums, number):
+            return DECAY * old + (1.0 - DECAY) * (sums * squared / number + EPS_STAT)
+
+        for layer, tile in enumerate(tiles):
+            for part in range(3):
+                news[0][layer, part : part + 1] = renew(olds[0][layer, part : part + 1], tile[part : part + 1], D)
+                news[1][layer, part : part + 1] = renew(
+                    olds[1][layer, part : part + 1], tile[4 + part : 5 + part], D
+                )
+            news[2][layer : layer + 1] = renew(olds[2][layer : layer + 1], tile[7:8], D)
+            news[3][layer : layer + 1] = renew(olds[3][layer : layer + 1], tile[3:4], D)
+        for layer, (up, down) in enumerate(feeds):
+            news[4][layer : layer + 1] = renew(olds[4][layer : layer + 1], up[:1], FF)
+            news[7][layer : layer + 1] = renew(olds[7][layer : layer + 1], down[:1], FF)
+            for part in range(FF // D):
+                cut = slice(part * D, (part + 1) * D)
+                news[5][layer : layer + 1, cut] = renew(
+                    olds[5][layer : layer + 1, cut], up[4 + part : 5 + part], D
+                )
+                news[6][layer : layer + 1, cut] = renew(
+                    olds[6][layer : layer + 1, cut], down[4 + part : 5 + part], D
+                )
+        shift = lax.rem(D - meta[0] * plan.block, D)
+        grad = (pltpu.roll(gain_sum, shift, 1) * factor)[:5, : plan.block]
+        master, square, moment, average = [item[...] for item in gains]
+        square_new = DECAY * square + (1.0 - DECAY) * (grad * grad + EPS_STAT)
+        stepped = grad * lax.rsqrt(square_new)
+        moment_new = MOMENTUM * moment + stepped
+        master_new = master - RATE_GAIN * (MOMENTUM * moment_new + stepped)
+        values = (
+            grad,
+            square_new,
+            moment_new,
+            master_new,
+            AVERAGE * average + (1.0 - AVERAGE) * master_new,
+            master_new,
+        )
+        for out, value in zip(gain_outs, values):
+            out[...] = value.astype(out.dtype)
+
+    small = gain_state[0].shape
+    outs = (
+        [jax.ShapeDtypeStruct((8, 128), F32)]
+        + [jax.ShapeDtypeStruct(shape, F32) for shape in counts]
+        + [jax.ShapeDtypeStruct((8, 128), F32)]
+        + [jax.ShapeDtypeStruct(small, F32)] * 5
+        + [jax.ShapeDtypeStruct(small, LOW)]
+    )
+    inputs = (early, late, *statistics, *gain_state)
+    return call(
+        "finish",
+        body,
+        (1,),
+        meta,
+        inputs,
+        [whole(item.shape) for item in inputs],
+        outs,
+        [whole(item.shape) for item in outs],
+        [],
+    )
+
+
+def step_values(grad, scale, master, moment, average):
+    stepped = grad * scale
     moment_new = MOMENTUM * moment + stepped
-    weight_new = weight - RATE_MATRIX * (MOMENTUM * moment_new + stepped)
-    average_new = AVERAGE * average + (1.0 - AVERAGE) * weight_new
-    return (
-        gradient,
-        rows_new,
-        cols_new,
-        moment_new,
-        weight_new,
-        average_new,
-        weight_new.astype(jnp.bfloat16),
-    )
+    master_new = master - RATE_MATRIX * (MOMENTUM * moment_new + stepped)
+    return grad, moment_new, master_new, AVERAGE * average + (1.0 - AVERAGE) * master_new
+
+
+def exact(left, right, contract):
+    return lax.dot_general(left, right, (contract, ((), ())), precision=EXACT, preferred_element_type=F32)
+
+
+def update_attention(plan, meta, rates, grads, rows_in, cols_in, rows_out, cols_out, state_in, state_out):
+    width, block = plan.width, plan.block
+
+    def body(meta, rates_ref, grad_a, grad_b, rin, cin, rout, cout, *rest):
+        ins, outs = rest[:6], rest[6:]
+        layer = pl.program_id(0)
+        dp_at, mp_at = meta[0], meta[1 + 3 * plan.pairs]
+        grad = jnp.where(layer == 0, grad_a[0], jnp.where(layer == 1, grad_b[1], grad_b[0]))
+        grad = grad * rates_ref[:1, :1]
+        local = one_hot(block, dp_at * block)
+        means = jnp.mean(rin[0], -1, keepdims=True)
+        row_scale = lax.rsqrt(exact(local, rin[0] / means, ((1,), (1,))))
+        shift = lax.rem(D - mp_at * width, D)
+        col_scale = lax.rsqrt(pltpu.roll(jnp.concatenate([cin[0]] * 3, 0)[:8], shift, 1)[:3, :width])
+        for part in range(3):
+            values = step_values(
+                grad[:, part * width : (part + 1) * width],
+                row_scale[:, part : part + 1] * col_scale[part : part + 1],
+                ins[0][0, part],
+                ins[1][0, part],
+                ins[2][0, part],
+            )
+            for out, value in zip(outs[:4], values):
+                out[0, part] = value
+            outs[4][0, part] = values[2].astype(LOW)
+        turned = jnp.transpose(grad[:, 3 * width :])
+        row, col = rout[pl.ds(layer, 1), :], cout[pl.ds(layer, 1), :]
+        mean = jnp.mean(row, -1, keepdims=True)
+        row_scale = lax.rsqrt(
+            exact(one_hot(width, mp_at * width), jnp.broadcast_to(row / mean, (8, D)), ((1,), (1,)))
+        )[:, :1]
+        shift = lax.rem(D - dp_at * block, D)
+        col_scale = lax.rsqrt(pltpu.roll(jnp.broadcast_to(col, (8, D)), shift, 1)[:1, :block])
+        values = step_values(turned, row_scale * col_scale, ins[3][0], ins[4][0], ins[5][0])
+        for out, value in zip(outs[5:9], values):
+            out[0] = value
+        outs[9][0] = values[2].astype(LOW)
+
+    def spec(shape):
+        return pl.BlockSpec((1,) + shape, lambda p, _: (p,) + (0,) * len(shape))
+
+    shape_in, shape_out = (3, block, width), (width, block)
+    outs = (
+        [jax.ShapeDtypeStruct((3,) + shape_in, F32)] * 4
+        + [jax.ShapeDtypeStruct((3,) + shape_in, LOW)]
+        + [jax.ShapeDtypeStruct((3,) + shape_out, F32)] * 4
+        + [jax.ShapeDtypeStruct((3,) + shape_out, LOW)]
+    )
+    return call(
+        "update_attention",
+        body,
+        (3,),
+        meta,
+        (rates, *grads, rows_in, cols_in, rows_out, cols_out, *state_in, *state_out),
+        [whole((8, 128)), whole((1, block, D)), whole((2, block, D))]
+        + [spec((3, D)), spec((3, D)), whole((3, D)), whole((3, D))]
+        + [spec(shape_in)] * 3
+        + [spec(shape_out)] * 3,
+        outs,
+        [spec(shape_in)] * 5 + [spec(shape_out)] * 5,
+        [],
+    )
+
+
+def update_feed(plan, meta, rates, grads, rows_up, cols_up, rows_down, cols_down, state_up, state_down):
+    hidden, block = plan.hidden, plan.block
+
+    def body(meta, rates_ref, grad_a, grad_b, rup, cup, rdown, cdown, *rest):
+        ins, outs = rest[:6], rest[6:]
+        layer = pl.program_id(0)
+        local = one_hot(block, meta[0] * block)
+        lanes = pl.ds(pl.multiple_of(meta[1 + 3 * plan.pairs] * hidden, 128), hidden)
+        one = pl.ds(layer, 1)
+        mean_up = jnp.mean(rup[one, :], -1, keepdims=True)
+        mean_down = jnp.mean(rdown[one, :], -1, keepdims=True)
+        along = (rup[one, :] / mean_up, cdown[one, :])
+        across = (cup[one, lanes], rdown[one, lanes] / mean_down)
+        for part in range(2):
+            grad = jnp.where(layer == 0, grad_a[part], grad_b[part]) * rates_ref[:1, :1]
+            row_scale = lax.rsqrt(exact(local, jnp.broadcast_to(along[part], (8, D)), ((1,), (1,))))[:, :1]
+            values = step_values(
+                grad,
+                row_scale * lax.rsqrt(across[part]),
+                ins[3 * part][0],
+                ins[3 * part + 1][0],
+                ins[3 * part + 2][0],
+            )
+            for out, value in zip(outs[5 * part : 5 * part + 4], values):
+                out[0] = value
+            outs[5 * part + 4][0] = values[2].astype(LOW)
+
+    state = pl.BlockSpec((1, block, hidden), lambda p, _: (p, 0, 0))
+    outs = ([jax.ShapeDtypeStruct((2, block, hidden), F32)] * 4 + [jax.ShapeDtypeStruct((2, block, hidden), LOW)]) * 2
+    values = call(
+        "update_feed",
+        body,
+        (2,),
+        meta,
+        (
+            rates,
+            *grads,
+            rows_up,
+            cols_up,
+            rows_down,
+            cols_down,
+            *state_up,
+            *[item.transpose(0, 2, 1) for item in state_down],
+        ),
+        [whole((8, 128)), *[whole((2, block, D))] * 2]
+        + [whole((2, D)), whole((2, FF)), whole((2, FF)), whole((2, D))]
+        + [state] * 6,
+        outs,
+        [state] * 10,
+        [],
+    )
+    return [*values[:5], *[item.transpose(0, 2, 1) for item in values[5:]]]
 
 
 def on_device(
@@ -743,36 +1042,25 @@
     def bits(count):
         return [1 << i for i in range(count.bit_length() - 1)]
 
-    def after(value, other):
-        return lax.optimization_barrier((value, other))[0]
-
-    def gather(own, gate):
-        if gate is not None:
-            own = after(own, gate)
-        if not plan.direct:
-            return [lax.all_gather(own, "dp", axis=1, tiled=True)], None
-        two = jnp.stack([own, swap(own, "dp", 4)])
-        more = swap(two, "dp", 2)
-        four = jnp.concatenate([two, more], 0)
-        return [four, swap(four, "dp", 1)], more
-
-    def scatter(parts):
-        if not plan.direct:
-            return lax.psum_scatter(parts[0], "dp", scatter_dimension=1, tiled=True)
-        away, keep = parts
-        count = keep.shape[0]
-        keep = keep + swap(away, "dp", 1).astype(f32)
-        for bit in (2, 4):
-            mine = (dp_index // bit) % 2
-            split = keep.reshape(count, -1, 2, block, D)
-            away = lax.dynamic_index_in_dim(split, 1 - mine, 2, False).astype(low)
-            keep = lax.dynamic_index_in_dim(split, mine, 2, False) + swap(away, "dp", bit).astype(f32)
-        return keep.reshape(count, block, D)
+    hold = lax.optimization_barrier
+
+    def widen(own, four):
+        two = jnp.stack([own, four])
+        return two, swap(two, "dp", 2), swap(two, "dp", 1)
+
+    def scatter(parts, attention):
+        summed = lax.psum_scatter(parts[0], "dp", scatter_dimension=1, tiled=True)
+        return collect(plan, meta, [summed[None]], attention)
 
     def total_dp(value):
         for bit in bits(dp_n):
             value = value + swap(value, "dp", bit)
         return value
+
+    def total_all(value):
+        for bit in bits(mp_n):
+            value = value + swap(value, "mp", bit)
+        return total_dp(value)
 
     def reduce_own(own, oth):
         sent = (own.astype(f32) + swap(oth, "mp", 1).astype(f32)).astype(low)
@@ -804,17 +1092,26 @@
     def feed_block(layer):
         return jnp.stack([expand[layer], contract[layer].T]).astype(low)
 
+    direct = plan.direct
+    own_a = attention_block(0)
+    own_b = feed_block(0)
+    own_c = jnp.concatenate([attention_block(1), attention_block(2)], 0)
+    own_d = feed_block(1)
     gain_full = lax.dynamic_update_slice(
-        jnp.zeros((5, D), low), norm_gains.astype(low), (0, dp_index * block)
-    )
-    gain_rows = total_dp(gain_full).astype(f32)
+        jnp.zeros((8, D), low), norm_gains.astype(low), (0, dp_index * block)
+    )
+    if direct:
+        own_a = jnp.concatenate([own_a, gain_full[None]], 1)
+        four, own_b = hold((swap(own_a, "dp", 4), own_b))
+        two, far, side_one = widen(own_a, four)
+        four_b = swap(own_b, "dp", 4)
+        far, side_one = hold((far, side_one))
+        arrays = (two, far, side_one, swap(far, "dp", 1))
+        gain_rows = sum(jnp.sum(item[:, 0, block:].astype(f32), 0) for item in arrays)
+    else:
+        arrays = [lax.all_gather(own_a, "dp", axis=1, tiled=True)]
+        gain_rows = total_dp(gain_full).astype(f32)
     gains = [gain_rows[i : i + 1] for i in range(5)]
-
-    enc_att, gate = gather(attention_block(0), None)
-    enc_feed, gate = gather(feed_block(0), gate)
-    self_att, gate = gather(attention_block(1), gate)
-    cross_att, gate = gather(attention_block(2), gate)
-    dec_feed, gate = gather(feed_block(1), gate)
 
     place_rel = jnp.concatenate([2 * jnp.arange(half) + side, 2 * jnp.arange(half) + 1 - side])
     prefix_rel = jnp.concatenate(relative(prefix_len))
@@ -822,241 +1119,247 @@
     images = place_rel < counts[0, 0]
     active = place_rel < counts[0, 0] + counts[0, 1]
     meta = jnp.concatenate(
-        [dp_index[None].astype(jnp.int32), images.astype(jnp.int32), prefix_rel, suffix_rel]
+        [
+            dp_index[None].astype(jnp.int32),
+            images.astype(jnp.int32),
+            prefix_rel,
+            suffix_rel,
+            mp_index[None].astype(jnp.int32),
+        ]
     )
     steps = jnp.arange(SUFFIX)
     live = active[:, None] & (steps[None, :] < suffix_rel[:, None])
 
     mid = half * SUFFIX
-    enc_own, enc_oth = relative(encoder_in.reshape(pairs, ENC_LEN, D))
+    enc_own, enc_oth = relative(
+        jnp.pad(encoder_in.reshape(pairs, ENC_LEN, D), ((0, 0), (0, LONG - ENC_LEN), (0, 0)))
+    )
     dec_rel = jnp.concatenate(relative(decoder_in.reshape(pairs, SUFFIX, D))).reshape(2 * mid, D)
     cot = jnp.concatenate(relative(decoder_cotangent.reshape(pairs, SUFFIX, D)))
     cot = jnp.where(live[:, :, None], cot, f32(0.0)).reshape(2 * mid, D)
-
-    part = encoder_attention(plan, meta, enc_own, enc_oth, gains[0], enc_att, 0, half)
-    kept_enc = part[2]
-    sums = reduce_own(part[0], part[1])
+    cot_low = cot.astype(low)
+
+    def triple(value):
+        return value.reshape(half, SUFFIX, D)
+
+    if direct:
+        *arrays, four_b, own_c = hold((*arrays, four_b, own_c))
+        two, far, side_one = widen(own_b, four_b)
+        four_c = swap(own_c, "dp", 4)
+    enc_att = Weight(arrays)
+    own, oth, kept_enc = encoder_attention(plan, meta, enc_own, enc_oth, gains[0], enc_att, 0, half)
+    if direct:
+        own, oth, dec_rel, cot, cot_low = hold((own, oth, dec_rel, cot, cot_low))
+    sums = reduce_own(own, oth)
+    if direct:
+        far, side_one, _ = hold((far, side_one, sums[0]))
+        arrays = (two, far, side_one, swap(far, "dp", 1))
+    else:
+        arrays = [lax.all_gather(own_b, "dp", axis=1, tiled=True)]
+    enc_feed = Weight(arrays, 0, 2)
     enc_mid, norm_mid = add_norm(meta, "add_norm_mid", enc_own, *sums, gains[1])
     norm_mid_oth = core(norm_mid)
 
-    part = decoder_self(plan, meta, dec_rel, gains[2], self_att)
-    kept_self = part[2]
-    sums = reduce_own(part[0], part[1])
-    dec_one, norm_cross = add_norm(meta, "add_norm_cross", dec_rel[:mid], *sums, gains[3])
-    norm_cross_oth = core(norm_cross)
-
-    part = encoder_feed(plan, meta, norm_mid, norm_mid_oth, enc_feed, 0, half)
-    sums = reduce_own(part[0], part[1])
+    if direct:
+        norm_mid_oth, four_c, own_d = hold((norm_mid_oth, four_c, own_d))
+        two, far, side_one = widen(own_c, four_c)
+        four_d = swap(own_d, "dp", 4)
+    own, oth = encoder_feed(plan, meta, norm_mid, norm_mid_oth, enc_feed, 0, half)
+    sums = reduce_own(own, oth)
+    if direct:
+        far, side_one, _ = hold((far, side_one, sums[0]))
+        arrays = (two, far, side_one, swap(far, "dp", 1))
+    else:
+        arrays = [lax.all_gather(own_c, "dp", axis=1, tiled=True)]
+    if direct:
+        *arrays, four_d = hold((*arrays, four_d))
+        two, far, side_one = widen(own_d, four_d)
+    self_att, cross_att = Weight(arrays, 0), Weight(arrays, 1)
+
+    own, oth, kept_self = decoder_self(plan, meta, dec_rel, gains[2], self_att)
+    sums_self = reduce_own(own, oth)
     memory = (enc_mid + (sums[0].astype(f32) + sums[1].astype(f32))).astype(low)
     memory_oth = core(memory)
-
-    def triple(value):
-        return value.reshape(half, SUFFIX, D)
-
+    dec_one, norm_cross = add_norm(meta, "add_norm_cross", dec_rel[:mid], *sums_self, gains[3])
+    norm_cross_oth = core(norm_cross)
+
+    if direct:
+        norm_cross_oth, far, side_one = hold((norm_cross_oth, far, side_one))
+        arrays = (two, far, side_one, swap(far, "dp", 1))
     cross_in = (triple(norm_cross), triple(norm_cross_oth), memory, memory_oth, cross_att)
-    part = decoder_cross(plan, meta, *cross_in)
-    kept_cross = part[2:]
-    sums = reduce_own(part[0], part[1])
+    own, oth, *kept_cross = decoder_cross(plan, meta, *cross_in)
+    sums = reduce_own(own, oth)
+    if not direct:
+        arrays = [lax.all_gather(own_d, "dp", axis=1, tiled=True)]
+    dec_feed = Weight(arrays, 0, 2)
     dec_two, norm_last = add_norm(
         meta, "add_norm_last", dec_one, sums[0].reshape(mid, D), sums[1].reshape(mid, D), gains[4]
     )
-    part = decoder_feed(plan, meta, norm_last, core(norm_last), cot.astype(low), dec_feed)
-    sum_dec = scatter(part[2:])
-    sums = reduce_own(part[0], part[1])
+
+    own, oth, *grads_dec = decoder_feed(plan, meta, norm_last, core(norm_last), cot_low, dec_feed)
+    if direct:
+        more_dec = swap(grads_dec[0], "dp", 1)
+    sums = reduce_own(own, oth)
     out_own = dec_two + (sums[0][0].astype(f32) + sums[1][0].astype(f32))
-    decoder_out = absolute(triple(out_own)).reshape(2 * mid, D)
     grad, grad_low, gain_four = norm_back(
         meta, "norm_back_last", dec_two, gains[4], cot[:mid], sums[0][1], sums[1][1], True
     )
-    part = decoder_cross_back(
+
+    own, oth, own_long, oth_long, *grads_cross = decoder_cross_back(
         plan, meta, *cross_in, *kept_cross, triple(grad_low), triple(core(grad_low))
     )
-    sum_cross = scatter(part[4:])
-    sums_enc = reduce_own(part[2], part[3])
-    sums = reduce_own(part[0], part[1])
+    if direct:
+        own, oth, own_long, oth_long, more_dec = hold((own, oth, own_long, oth_long, more_dec))
+        more_cross = swap(grads_cross[0], "dp", 1)
+    sums = reduce_own(own, oth)
+    if direct:
+        own_long, oth_long, _ = hold((own_long, oth_long, sums[0]))
+    sums_enc = reduce_own(own_long, oth_long)
+    grad, grad_low, gain_three = norm_back(
+        meta, "norm_back_cross", dec_one, gains[3], grad, sums[0].reshape(mid, D), sums[1].reshape(mid, D), True
+    )
+    grad_low_oth = core(grad_low)
+    if direct:
+        keep, more_dec, _, grad_low_oth = hold((grads_dec[1], more_dec, sums_enc[0], grad_low_oth))
+        keep_dec, away_dec = fold(plan, meta, [keep], [more_dec], halves)
+
+    own_self, oth_self, *grads_self = decoder_self_back(
+        plan, meta, dec_rel, gains[2], self_att, kept_self, grad_low, grad_low_oth
+    )
+    decoder_out = absolute(triple(out_own)).reshape(2 * mid, D)
+    if direct:
+        *sums_enc, own_self, oth_self, away_dec = hold((*sums_enc, own_self, oth_self, away_dec))
+    sums_self = reduce_own(own_self, oth_self)
     grad_enc = sums_enc[0].astype(f32) + sums_enc[1].astype(f32)
     enc_low = grad_enc.astype(low)
-    grad, grad_low, gain_three = norm_back(
-        meta, "norm_back_cross", dec_one, gains[3], grad, sums[0].reshape(mid, D), sums[1].reshape(mid, D), True
-    )
-    part = encoder_feed_back(plan, meta, norm_mid, norm_mid_oth, enc_low, core(enc_low), enc_feed)
-    sum_enc = scatter(part[2:])
-    sums = reduce_own(part[0], part[1])
+    enc_low_oth = core(enc_low)
+
+    if direct:
+        enc_low_oth, decoder_out, away_dec, more_cross, away_self = hold(
+            (enc_low_oth, decoder_out, away_dec, more_cross, grads_self[0])
+        )
+        more_self = swap(away_self, "dp", 1)
+        more_dec = swap(away_dec, "dp", 2)
+    own, oth, *grads_enc = encoder_feed_back(plan, meta, norm_mid, norm_mid_oth, enc_low, enc_low_oth, enc_feed)
+    if direct:
+        own, oth, more_self, more_dec, *sums_self = hold((own, oth, more_self, more_dec, *sums_self))
+        more_enc = swap(grads_enc[0], "dp", 1)
+    sums = reduce_own(own, oth)
+    if direct:
+        keep_cross, keep_self, more_cross, more_self, keep_dec, more_dec, *sums_self, _ = hold(
+            (grads_cross[1], grads_self[1], more_cross, more_self, keep_dec, more_dec, *sums_self, sums[0])
+        )
+        keep_dec, away_dec = fold(plan, meta, [keep_dec], [more_dec], halves)
+        more_dec = swap(away_dec, "dp", 4)
+        keep_mid, away_mid = fold(plan, meta, [keep_cross, keep_self], [more_cross, more_self], halves)
+        more_mid = swap(away_mid, "dp", 2)
+    grad, gain_two = norm_back(meta, "norm_back_self", dec_rel[:mid], gains[2], grad, *sums_self, False)
+    decoder_in_grad = absolute(triple(grad)).reshape(2 * mid, D)
+    if direct:
+        *sums, away_mid, away_dec, decoder_in_grad = hold((*sums, away_mid, away_dec, decoder_in_grad))
     grad_enc, enc_low, gain_one = norm_back(
         meta, "norm_back_mid", enc_mid, gains[1], grad_enc, *sums, True
     )
-
-    part = decoder_self_back(
-        plan, meta, dec_rel, gains[2], self_att, kept_self, grad_low, core(grad_low)
-    )
-    sum_self = scatter(part[2:])
-    sums = reduce_own(part[0], part[1])
-    grad, gain_two = norm_back(meta, "norm_back_self", dec_rel[:mid], gains[2], grad, *sums, False)
-    decoder_in_grad = absolute(triple(grad)).reshape(2 * mid, D)
-
-    part = encoder_attention_back(
-        plan, meta, enc_own, enc_oth, gains[0], enc_att, kept_enc, enc_low, core(enc_low)
-    )
-    sum_att = scatter(part[2:])
-    sums = reduce_own(part[0], part[1])
+    enc_low_oth = core(enc_low)
+
+    if direct:
+        keep_enc, away_enc = fold(plan, meta, [grads_enc[1]], [more_enc], halves)
+        enc_low_oth, decoder_in_grad, away_enc, more_dec = hold((enc_low_oth, decoder_in_grad, away_enc, more_dec))
+        more_enc = swap(away_enc, "dp", 2)
+    own, oth, *grads_att = encoder_attention_back(
+        plan, meta, enc_own, enc_oth, gains[0], enc_att, kept_enc, enc_low, enc_low_oth
+    )
+    if direct:
+        more_att = swap(grads_att[0], "dp", 1)
+        own, oth, more_mid = hold((own, oth, more_mid))
+    sums = reduce_own(own, oth)
+    if direct:
+        keep_mid, more_mid, keep_enc, keep_dec, _ = hold((keep_mid, more_mid, keep_enc, keep_dec, sums[0]))
+        keep_mid, away_mid = fold(plan, meta, [keep_mid], [more_mid], halves)
+        more_mid = swap(away_mid, "dp", 4)
+        keep_enc, away_enc = fold(plan, meta, [keep_enc], [more_enc], halves)
+        more_enc = swap(away_enc, "dp", 4)
+        sum_dec = collect(plan, meta, [keep_dec, more_dec], False)
+        mine, *others = fold(plan, meta, [grads_att[1]], [more_att], apart)
+        mine, *others, more_mid, _ = hold((mine, *others, more_mid, sum_dec[1]))
+        pieces_att = [mine] + [swap(item, "dp", 2 * (i + 1)) for i, item in enumerate(others)]
+        sum_mid = collect(plan, meta, [keep_mid, more_mid], True)
+    else:
+        sum_dec = scatter(grads_dec, False)
+        sum_mid = [
+            jnp.concatenate(item) for item in zip(scatter(grads_cross, True), scatter(grads_self, True))
+        ]
+    early = total_all(jnp.concatenate([sum_mid[1], sum_dec[1]]))
     grad_enc, gain_zero = norm_back(meta, "norm_back_enc", enc_own, gains[0], grad_enc, *sums, False)
-    encoder_in_grad = absolute(grad_enc).reshape(pairs * ENC_LEN, D)
-
-    gain_grad = jnp.concatenate([gain_zero, gain_one, gain_two, gain_three, gain_four])
-    gain_grad = total_dp(gain_grad + swap(gain_grad, "mp", 1))
-    grad_gain = lax.dynamic_slice(gain_grad, (0, dp_index * block), (5, block))
-
-    att = jnp.concatenate([sum_att, sum_self, sum_cross], 0)
-    grad_in = att[:, :, : 3 * width].reshape(3, block, 3, width).transpose(0, 2, 1, 3)
-    grad_out = att[:, :, 3 * width :].transpose(0, 2, 1)
-    grad_up = jnp.stack([sum_enc[0], sum_dec[0]])
-    grad_down = jnp.stack([sum_enc[1], sum_dec[1]]).transpose(0, 2, 1)
-
-    squares = [item * item for item in (grad_in, grad_out, grad_up, grad_down)]
-    rows_part = [jnp.sum(item, -1) for item in squares]
-    cols_part = [jnp.sum(item, -2) for item in squares]
-    along_dp = [rows_part[0], cols_part[1], rows_part[2], cols_part[3]]
-    along_mp = [cols_part[0], rows_part[1], cols_part[2], rows_part[3]]
-
-    def spread_all(parts, axis, other):
-        index, count = (dp_index, dp_n) if axis == "dp" else (mp_index, mp_n)
-        flat = jnp.concatenate([item.reshape(-1) for item in parts])
-        for bit in bits(mp_n if axis == "dp" else dp_n):
-            flat = flat + swap(flat, other, bit)
-        full = lax.dynamic_update_slice(
-            jnp.zeros((count, flat.shape[0]), f32), flat[None], (index, 0)
-        )
-        for bit in bits(count):
-            full = full + swap(full, axis, bit)
-        result, start = [], 0
-        for item in parts:
-            size = item.size
-            piece = full[:, start : start + size].reshape((count,) + item.shape)
-            start += size
-            piece = jnp.moveaxis(piece, 0, -2)
-            result.append(piece.reshape(item.shape[:-1] + (count * item.shape[-1],)))
-        return result
-
-    row_in, col_out, row_up, col_down = spread_all(along_dp, "dp", "mp")
-    col_in, row_out, col_up, row_down = spread_all(along_mp, "mp", "dp")
-    total = (
-        jnp.sum(row_in) + jnp.sum(row_out) + jnp.sum(row_up) + jnp.sum(row_down)
-        + jnp.sum(gain_grad * gain_grad)
-    )
-    grad_norm = jnp.sqrt(total)
-    factor = jnp.minimum(1.0, 1.0 / grad_norm)
-    squared = factor * factor
-    row_in, col_in, row_out, col_out = (
-        row_in * squared,
-        col_in * squared,
-        row_out * squared,
-        col_out * squared,
-    )
-    row_up, col_up, row_down, col_down = (
-        row_up * squared,
-        col_up * squared,
-        row_down * squared,
-        col_down * squared,
-    )
-    grad_in, grad_out, grad_up, grad_down = (
-        grad_in * factor,
-        grad_out * factor,
-        grad_up * factor,
-        grad_down * factor,
-    )
-    grad_gain = grad_gain * factor
-    pin = update_matrix(
-        grad_in,
-        project_in,
-        project_in_rows,
-        project_in_cols,
-        project_in_moment,
-        project_in_average,
-        row_in,
-        col_in,
-        dp_index,
-        mp_index,
-    )
-    pout = update_matrix(
-        grad_out,
-        project_out,
-        project_out_rows,
-        project_out_cols,
-        project_out_moment,
-        project_out_average,
-        row_out,
-        col_out,
-        mp_index,
-        dp_index,
-    )
-    pexp = update_matrix(
-        grad_up,
-        expand,
-        expand_rows,
-        expand_cols,
-        expand_moment,
-        expand_average,
-        row_up,
-        col_up,
-        dp_index,
-        mp_index,
-    )
-    pcon = update_matrix(
-        grad_down,
-        contract,
-        contract_rows,
-        contract_cols,
-        contract_moment,
-        contract_average,
-        row_down,
-        col_down,
-        mp_index,
-        dp_index,
-    )
-    square_new = DECAY * norm_gains_square + (1.0 - DECAY) * (grad_gain * grad_gain + EPS_STAT)
-    stepped = grad_gain * lax.rsqrt(square_new)
-    moment_new = MOMENTUM * norm_gains_moment + stepped
-    gains_new = norm_gains - RATE_GAIN * (MOMENTUM * moment_new + stepped)
-    average_new = AVERAGE * norm_gains_average + (1.0 - AVERAGE) * gains_new
+    if direct:
+        sum_enc = collect(plan, meta, [keep_enc, more_enc], False)
+        sum_att = collect(plan, meta, pieces_att, True)
+    else:
+        sum_enc = scatter(grads_enc, False)
+        sum_att = scatter(grads_att, True)
+    encoder_in_grad = absolute(grad_enc)[:, :ENC_LEN].reshape(pairs * ENC_LEN, D)
+    gain_tile = jnp.concatenate(
+        [gain_zero, gain_one, gain_two, gain_three, gain_four, jnp.zeros((3, D), f32)]
+    )[None]
+    late = total_all(jnp.concatenate([sum_enc[1], sum_att[1], gain_tile]))
+    done = finish(
+        plan,
+        meta,
+        early,
+        late,
+        (
+            project_in_rows,
+            project_in_cols,
+            project_out_rows,
+            project_out_cols,
+            expand_rows,
+            expand_cols,
+            contract_rows,
+            contract_cols,
+        ),
+        (norm_gains, norm_gains_square, norm_gains_moment, norm_gains_average),
+    )
+    grad_norm, news, rates, pgain = done[0][0, 0], done[1:9], done[9], done[10:]
+    att = update_attention(
+        plan,
+        meta,
+        rates,
+        (sum_att[0], sum_mid[0]),
+        *news[:4],
+        (project_in, project_in_moment, project_in_average),
+        (project_out, project_out_moment, project_out_average),
+    )
+    feed = update_feed(
+        plan,
+        meta,
+        rates,
+        (sum_enc[0], sum_dec[0]),
+        *news[4:],
+        (expand, expand_moment, expand_average),
+        (contract, contract_moment, contract_average),
+    )
     return (
         decoder_out,
         encoder_in_grad,
         decoder_in_grad,
         grad_norm,
-        pin[0],
-        pin[1],
-        pin[2],
-        pin[3],
-        pin[4],
-        pin[5],
-        pin[6],
-        pout[0],
-        pout[1],
-        pout[2],
-        pout[3],
-        pout[4],
-        pout[5],
-        pout[6],
-        pexp[0],
-        pexp[1],
-        pexp[2],
-        pexp[3],
-        pexp[4],
-        pexp[5],
-        pexp[6],
-        pcon[0],
-        pcon[1],
-        pcon[2],
-        pcon[3],
-        pcon[4],
-        pcon[5],
-        pcon[6],
-        grad_gain,
-        square_new,
-        moment_new,
-        gains_new,
-        average_new,
-        gains_new.astype(jnp.bfloat16),
+        att[0],
+        news[0],
+        news[1],
+        *att[1:5],
+        att[5],
+        news[2],
+        news[3],
+        *att[6:10],
+        feed[0],
+        news[4],
+        news[5],
+        *feed[1:5],
+        feed[5],
+        news[6],
+        news[7],
+        *feed[6:10],
+        *pgain,
     )
 
 

time: 524 us -> 486 us (0.927)
  Pallas kernels: 117 us -> 171 us
  local copies, waits for them, and re-layouts: 78.1 us -> 32.6 us
  other arithmetic: 50.7 us -> 22.5 us
  starting transfers between devices: 82.5 us -> 59.6 us
  waiting for transfers between devices: 179 us -> 187 us
    pallas_call x17 -> x31, Pallas kernels: 117 us -> 171 us  [call(): pl.pallas_call(body, name=name, out_shape=outs, grid_spec=pltpu.PrefetchS...]
    ppermute x78 -> x71, starting transfers between devices: 82.5 us -> 59.6 us  [swap(): return lax.ppermute(value, axis, [(i, i ^ bit) for i in range(count)])]
    pallas_call x8 -> x0, local copies, waits for them, and re-layouts: 16.7 us -> none  [call(): pl.pallas_call(body, name=name, out_shape=outs, grid_spec=pltpu.PrefetchS...]
    add x30 -> x6, other arithmetic: 15 us -> 2.21 us  [the longest x1 1.33 us: on_device(): grad_enc = sums_enc[0].astype(f32) + sums_enc[1].astype(f32)]
    convert_element_type x14 -> x0, local copies, waits for them, and re-layouts: 9.84 us -> none  [the longest x5 4.41 us: reduce_own(): sent = (own.astype(f32) + swap(oth, 'mp', 1).astype(f32)).astype(low)]
    convert_element_type x9 -> x1, other arithmetic: 10 us -> 0.78 us  [on_device(): cot_low = cot.astype(low)]
    ppermute x7 -> x0, local copies, waits for them, and re-layouts: 8.7 us -> none  [swap(): return lax.ppermute(value, axis, [(i, i ^ bit) for i in range(count)])]
    dynamic_slice x17 -> x0, local copies, waits for them, and re-layouts: 8.58 us -> none  [the longest x6 6.54 us: scatter(): lax.dynamic_index_in_dim(split, mine, 2, False)]
  transfers between devices with their start and end apart: 78 -> 71, of which waited for: 37 -> 43; matrix products, arithmetic and copies ran while one was open for 21% -> 6% of each run, Pallas kernels for 16% -> 31%
where the time goes in v3:
time: 486 us; the launch traced here: 477 us
  waiting for transfers between devices  187 us (38%)
  Pallas kernels  171 us (35%)
  starting transfers between devices  59.6 us (12%)
  local copies, waits for them, and re-layouts  32.6 us (7%)
  other arithmetic  22.5 us (5%)
    ppermute x71, waiting for transfers between devices, swap(): return lax.ppermute(value, axis, [(i, i ^ bit) for i in range(count)])  187 us
    pallas_call x31, Pallas kernels, call(): pl.pallas_call(body, name=name, out_shape=outs, grid_spec=pltpu.PrefetchS...  171 us
    ppermute x71, starting transfers between devices, swap(): return lax.ppermute(value, axis, [(i, i ^ bit) for i in range(count)])  59.6 us
    unnamed x176, local copies, waits for them, and re-layouts  18 us
  transfers between devices with their start and end apart: 71, of which 43 were waited for; matrix products, arithmetic and copies ran while one was open for 6% of the time, Pallas kernels for 31%

profile of v3, /device:TPU:0, one launch (start us, length us, event | category | flops | bytes accessed | tf_op | source)
XLA Modules:
  0.0 476.8 jit_solution(17650664869024277422)
XLA Ops:
  34.9 9.1 %collective-permute-done.4 = bf16[2,96,768]{2,1,0:T(8,128)(2,1)S(1)} collective-permute-done((bf16[2,96,768]{2,1,0:T(8,128)(2,1)S(1)}, bf16[2,96,768]{2,1,0:T(8,128)(2,1)S(1)}, u32[]{:S(2)}, u32[]{:S(2)}) %collective-permute-start.4) | collective-permute-done | bytes 294944 | tf_op jit(solution)/shard_map/ppermute | solution.py:1040
  44.0 9.4 %encoder_attention.1 = (bf16[2,232,768]{2,1,0:T(8,128)(2,1)}, bf16[2,232,768]{2,1,0:T(8,128)(2,1)}, bf16[4,228,768]{2,1,0:T(8,128)(2,1)}) custom-call(s32[14]{0:T(128)} %concatenate.95.meta, bf16[2,232,768]{2,1,0:T(8,128)(2,1)} %get-tuple-element.441.own_ref.base_ref.in_ref, bf16[2,232,768]{2,1,0:T(8,128)(2,1)} %get-tuple-element.440.oth_ref, ...), custom_call_target="tpu_custom_call" | custom-call | flops 1 | bytes 1 | tf_op jit(solution)/shard_map/encoder_attention/pallas_call | solution.py:142
  59.2 15.9 %collective-permute-done.6.second_ref = bf16[2,232,768]{2,1,0:T(8,128)(2,1)S(1)} collective-permute-done((bf16[2,232,768]{2,1,0:T(8,128)(2,1)S(1)}, bf16[2,232,768]{2,1,0:T(8,128)(2,1)S(1)}, u32[]{:S(2)}, u32[]{:S(2)}) %collective-permute-start.6) | collective-permute-done | bytes 712736 | tf_op jit(solution)/shard_map/ppermute | solution.py:1040
  80.0 16.3 %collective-permute-done.8 = bf16[2,96,768]{2,1,0:T(8,128)(2,1)S(1)} collective-permute-done((bf16[2,96,768]{2,1,0:T(8,128)(2,1)S(1)}, bf16[2,96,768]{2,1,0:T(8,128)(2,1)S(1)}, u32[]{:S(2)}, u32[]{:S(2)}) %collective-permute-start.8) | collective-permute-done | bytes 294944 | tf_op jit(solution)/shard_map/ppermute | solution.py:1040
  98.0 7.4 %encoder_feed.1 = (bf16[2,232,768]{2,1,0:T(8,128)(2,1)}, bf16[2,232,768]{2,1,0:T(8,128)(2,1)}) custom-call(s32[14]{0:T(128)} %concatenate.95.meta, bf16[2,232,768]{2,1,0:T(8,128)(2,1)} %get-tuple-element.248.own_ref, bf16[2,232,768]{2,1,0:T(8,128)(2,1)} %copy-done.13, bf16[2,2,96,768]{3,2,1,0:T(8,128)(2,1)} %copy-done.6, bf16[2,2,96,768]{3,2,1,0:T(8,128)(2,1)} %copy-done.18, ...), custom_call_target="tpu_custom_call" | custom-call | flops 1 | bytes 1 | tf_op jit(solution)/shard_map/encoder_feed/pallas_call | solution.py:142
  109.6 11.7 %collective-permute-done.9.rest_1_ = bf16[2,2,96,768]{3,2,1,0:T(8,128)(2,1)S(1)} collective-permute-done((bf16[2,2,96,768]{3,2,1,0:T(8,128)(2,1)S(1)}, bf16[2,2,96,768]{3,2,1,0:T(8,128)(2,1)S(1)}, u32[]{:S(2)}, u32[]{:S(2)}) %collective-permute-start.9) | collective-permute-done | bytes 589856 | tf_op jit(solution)/shard_map/ppermute | solution.py:1040
  124.4 14.2 %collective-permute-done.16 = bf16[2,96,768]{2,1,0:T(8,128)(2,1)S(1)} collective-permute-done((bf16[2,96,768]{2,1,0:T(8,128)(2,1)S(1)}, bf16[2,96,768]{2,1,0:T(8,128)(2,1)S(1)}, u32[]{:S(2)}, u32[]{:S(2)}) %collective-permute-start.16) | collective-permute-done | bytes 294944 | tf_op jit(solution)/shard_map/ppermute | solution.py:1040
  158.8 8.4 %decoder_cross.1 = (bf16[2,32,768]{2,1,0:T(8,128)(2,1)}, bf16[2,32,768]{2,1,0:T(8,128)(2,1)}, bf16[4,32,384]{2,1,0:T(8,128)(2,1)}, bf16[4,228,384]{2,1,0:T(8,128)(2,1)}) custom-call(s32[14]{0:T(128)} %concatenate.95.meta, bf16[2,32,768]{2,1,0:T(8,128)(2,1)} %bitcast.144, bf16[2,32,768]{2,1,0:T(8,128)(2,1)} %bitcast.146, bf16[2,232,768]{2,1,0:T(8,128)(2,1)} %copy-done.4, ...), custom_call_target="tpu_custom_call" | custom-call | flops 1 | bytes 1 | tf_op jit(solution)/shard_map/decoder_cross/pallas_call | solution.py:142
  180.7 6.3 %decoder_feed.1 = (bf16[2,64,768]{2,1,0:T(8,128)(2,1)}, bf16[2,64,768]{2,1,0:T(8,128)(2,1)}, bf16[4,2,96,768]{3,2,1,0:T(8,128)(2,1)}, f32[4,2,96,768]{3,2,1,0:T(8,128)}) custom-call(s32[14]{0:T(128)} %concatenate.95.meta, bf16[64,768]{1,0:T(8,128)(2,1)} %get-tuple-element.276.own_ref, bf16[64,768]{1,0:T(8,128)(2,1)} %copy-done.62, ...), custom_call_target="tpu_custom_call" | custom-call | flops 1 | bytes 1 | tf_op jit(solution)/shard_map/decoder_feed/pallas_call | solution.py:142
  192.5 4.8 %collective-permute-done.29 = bf16[2,64,768]{2,1,0:T(8,128)(2,1)S(1)} collective-permute-done((bf16[2,64,768]{2,1,0:T(8,128)(2,1)S(1)}, bf16[2,64,768]{2,1,0:T(8,128)(2,1)S(1)}, u32[]{:S(2)}, u32[]{:S(2)}) %collective-permute-start.29) | collective-permute-done | bytes 196640 | tf_op jit(solution)/shard_map/ppermute | solution.py:1040
  202.7 16.9 %decoder_cross_back.1 = (bf16[2,32,768]{2,1,0:T(8,128)(2,1)}, bf16[2,32,768]{2,1,0:T(8,128)(2,1)}, bf16[2,232,768]{2,1,0:T(8,128)(2,1)}, bf16[2,232,768]{2,1,0:T...) custom-call(s32[14]{0:T(128)} %concatenate.95.meta, bf16[2,32,768]{2,1,0:T(8,128)(2,1)} %bitcast.145, ...), custom_call_target="tpu_custom_call" | custom-call | flops 1 | bytes 1 | tf_op jit(solution)/shard_map/decoder_cross_back/pallas_call | solution.py:142
  228.1 18.1 %collective-permute-done.35 = bf16[2,32,768]{2,1,0:T(8,128)(2,1)S(1)} collective-permute-done((bf16[2,32,768]{2,1,0:T(8,128)(2,1)S(1)}, bf16[2,32,768]{2,1,0:T(8,128)(2,1)S(1)}, u32[]{:S(2)}, u32[]{:S(2)}) %collective-permute-start.35) | collective-permute-done | bytes 98336 | tf_op jit(solution)/shard_map/ppermute | solution.py:1040
  251.7 5.9 %decoder_self_back.1 = (bf16[64,768]{1,0:T(8,128)(2,1)}, bf16[64,768]{1,0:T(8,128)(2,1)}, bf16[4,1,96,768]{3,2,1,0:T(8,128)(2,1)}, f32[4,1,96,768]{3,2,1,0:T(8,128)}) custom-call(s32[14]{0:T(128)} %concatenate.95.meta, bf16[128,768]{1,0:T(8,128)(2,1)} %bitcast.127, f32[1,768]{1,0:T(1,128)} %get-tuple-element.469.gain_ref, ...), custom_call_target="tpu_custom_call" | custom-call | flops 1 | bytes 1 | tf_op jit(solution)/shard_map/decoder_self_back/pallas_call | solution.py:142
  272.6 14.7 %encoder_feed_back.1 = (bf16[2,232,768]{2,1,0:T(8,128)(2,1)}, bf16[2,232,768]{2,1,0:T(8,128)(2,1)}, bf16[4,2,96,768]{3,2,1,0:T(8,128)(2,1)}, f32[4,2,96,768]{3,2,1,0:T(8,128)}) custom-call(s32[14]{0:T(128)} %concatenate.95.meta, bf16[2,232,768]{2,1,0:T(8,128)(2,1)} %get-tuple-element.248.own_ref, bf16[2,232,768]{2,1,0:T(8,128)(2,1)} %copy-done.13, ...), custom_call_target="tpu_custom_call" | custom-call | flops 1 | bytes 1 | tf_op jit(solution)/shard_map/encoder_feed_back/pallas_call | solution.py:142
  303.1 6.2 %collective-permute-done.45.second_ref = bf16[2,232,768]{2,1,0:T(8,128)(2,1)S(1)} collective-permute-done((bf16[2,232,768]{2,1,0:T(8,128)(2,1)S(1)}, bf16[2,232,768]{2,1,0:T(8,128)(2,1)S(1)}, u32[]{:S(2)}, u32[]{:S(2)}) %collective-permute-start.45) | collective-permute-done | bytes 712736 | tf_op jit(solution)/shard_map/ppermute | solution.py:1040
  310.1 4.4 norm_back_mid.1
  316.3 6.4 %collective-permute-done.48.rest_1_ = bf16[4,2,96,768]{3,2,1,0:T(8,128)(2,1)S(1)} collective-permute-done((bf16[4,2,96,768]{3,2,1,0:T(8,128)(2,1)S(1)}, bf16[4,2,96,768]{3,2,1,0:T(8,128)(2,1)S(1)}, u32[]{:S(2)}, u32[]{:S(2)}) %collective-permute-start.48) | collective-permute-done | bytes 1179680 | tf_op jit(solution)/shard_map/ppermute | solution.py:1040
  327.8 6.6 %collective-permute-done.49.rest_1_ = bf16[1,2,96,768]{3,2,1,0:T(8,128)(2,1)S(1)} collective-permute-done((bf16[1,2,96,768]{3,2,1,0:T(8,128)(2,1)S(1)}, bf16[1,2,96,768]{3,2,1,0:T(8,128)(2,1)S(1)}, u32[]{:S(2)}, u32[]{:S(2)}) %collective-permute-start.49) | collective-permute-done | bytes 294944 | tf_op jit(solution)/shard_map/ppermute | solution.py:1040
  335.3 16.6 %encoder_attention_back.1 = (bf16[2,232,768]{2,1,0:T(8,128)(2,1)}, bf16[2,232,768]{2,1,0:T(8,128)(2,1)}, bf16[4,1,96,768]{3,2,1,0:T(8,128)(2,1)}, f32[4,1,96,768]{3,2,1,0:T(8,128)}) custom-call(s32[14]{0:T(128)} %concatenate.95.meta, bf16[2,232,768]{2,1,0:T(8,128)(2,1)} %get-tuple-element.441.own_ref.base_ref.in_ref, ...), custom_call_target="tpu_custom_call" | custom-call | flops 1 | bytes 1 | tf_op jit(solution)/shard_map/encoder_attention_back/pallas_call | solution.py:142
  359.1 14.7 %collective-permute-done.52.second_ref = bf16[2,232,768]{2,1,0:T(8,128)(2,1)S(1)} collective-permute-done((bf16[2,232,768]{2,1,0:T(8,128)(2,1)S(1)}, bf16[2,232,768]{2,1,0:T(8,128)(2,1)S(1)}, u32[]{:S(2)}, u32[]{:S(2)}) %collective-permute-start.52) | collective-permute-done | bytes 712736 | tf_op jit(solution)/shard_map/ppermute | solution.py:1040
  397.1 8.9 %collective-permute-done.55.rest_1_ = bf16[1,2,96,768]{3,2,1,0:T(8,128)(2,1)S(1)} collective-permute-done((bf16[1,2,96,768]{3,2,1,0:T(8,128)(2,1)}, bf16[1,2,96,768]{3,2,1,0:T(8,128)(2,1)S(1)}, u32[]{:S(2)}, u32[]{:S(2)}) %collective-permute-start.55) | collective-permute-done | bytes 294944 | tf_op jit(solution)/shard_map/ppermute | solution.py:1040
  449.4 5.1 %collective-permute-done.60 = f32[4,8,768]{2,1,0:T(8,128)S(1)} collective-permute-done((f32[4,8,768]{2,1,0:T(8,128)S(1)}, f32[4,8,768]{2,1,0:T(8,128)S(1)}, u32[]{:S(2)}, u32[]{:S(2)}) %collective-permute-start.60) | collective-permute-done | bytes 98336 | tf_op jit(solution)/shard_map/ppermute | solution.py:1040
  458.8 7.6 %update_attention.1 = (f32[3,3,96,192]{3,2,1,0:T(8,128)}, f32[3,3,96,192]{3,2,1,0:T(8,128)}, f32[3,3,96,192]{3,2,1,0:T(8,128)}, f32[3,3,96,192]{3,2,1,0:T(8,128)...) custom-call(s32[14]{0:T(128)} %concatenate.95.meta, ...), custom_call_target="tpu_custom_call" | custom-call | flops 1 | bytes 1 | tf_op jit(solution)/shard_map/update_attention/pallas_call | solution.py:142
  466.3 6.3 %update_feed.1 = (f32[2,96,768]{2,1,0:T(8,128)}, f32[2,96,768]{2,1,0:T(8,128)}, f32[2,96,768]{2,1,0:T(8,128)}, f32[2,96,768]{2,1,0:T(8,128)}, bf16[2,96,768]{2,1...) custom-call(s32[14]{0:T(128)} %concatenate.95.meta, ...), custom_call_target="tpu_custom_call" | custom-call | flops 1 | bytes 1 | tf_op jit(solution)/shard_map/update_feed/pallas_call | solution.py:142
  (409 shorter events, 231.1 us)
Async XLA Ops:
  57.1 18.1 %collective-permute-start.6 = (bf16[2,232,768]{2,1,0:T(8,128)(2,1)S(1)}, bf16[2,232,768]{2,1,0:T(8,128)(2,1)S(1)}, u32[]{:S(2)}, u32[]{:S(2)}) collective-permute-start(bf16[2,232,768]{2,1,0:T(8,128)(2,1)S(1)} %add_convert_fusion.5.first_ref), channel_id=1, source_target_pairs={{0,2},{1,3},{2,0},{3,1},{4,6},{5,7},{6,4},{7,5},{8,10},{9,11},{10,... | collective-permute-start | bytes 2138120 | tf_op jit(solution)/shard_map/ppermute | solution.py:1040
  58.8 20.7 %collective-permute-start.11 = (bf16[2,2,96,768]{3,2,1,0:T(8,128)(2,1)S(1)}, bf16[2,2,96,768]{3,2,1,0:T(8,128)(2,1)S(1)}, u32[]{:S(2)}, u32[]{:S(2)}) collective-permute-start(bf16[2,2,96,768]{3,2,1,0:T(8,128)(2,1)S(1)} %pad_maximum_fusion.2.rest_0_), channel_id=1, source_target_pairs={{0,8},{4,12},{8,0},{12,4},{16,24},{20,28},{24,16},{28,20},{1,9},{5... | collective-permute-start | bytes 1769480 | tf_op jit(solution)/shard_map/ppermute | solution.py:1040
  58.9 20.6 %collective-permute-start.12 = (bf16[2,2,96,768]{3,2,1,0:T(8,128)(2,1)S(1)}, bf16[2,2,96,768]{3,2,1,0:T(8,128)(2,1)S(1)}, u32[]{:S(2)}, u32[]{:S(2)}) collective-permute-start(bf16[2,2,96,768]{3,2,1,0:T(8,128)(2,1)S(1)} %pad_maximum_fusion.2.rest_0_), channel_id=1, source_target_pairs={{0,4},{4,0},{8,12},{12,8},{16,20},{20,16},{24,28},{28,24},{1,5},{5... | collective-permute-start | bytes 1769480 | tf_op jit(solution)/shard_map/ppermute | solution.py:1040
  108.0 30.6 %collective-permute-start.22 = (bf16[2,232,768]{2,1,0:T(8,128)(2,1)S(1)}, bf16[2,232,768]{2,1,0:T(8,128)(2,1)S(1)}, u32[]{:S(2)}, u32[]{:S(2)}) collective-permute-start(bf16[2,232,768]{2,1,0:T(8,128)(2,1)S(1)} %add_convert_fusion.4), channel_id=1, source_target_pairs={{0,2},{1,3},{2,0},{3,1},{4,6},{5,7},{6,4},{7,5},{8,10},{9,11},{10,... | collective-permute-start | bytes 2138120 | tf_op jit(solution)/shard_map/ppermute | solution.py:1040
  139.4 18.5 %collective-permute-start.23 = (bf16[2,232,768]{2,1,0:T(8,128)(2,1)S(1)}, bf16[2,232,768]{2,1,0:T(8,128)(2,1)S(1)}, u32[]{:S(2)}, u32[]{:S(2)}) collective-permute-start(bf16[2,232,768]{2,1,0:T(8,128)(2,1)S(1)} %add_convert_fusion.3.memory_own_ref), channel_id=1, source_target_pairs={{0,1},{1,0},{2,3},{3,2},{4,5},{5,4},{6,7},{7,6},{8,9},{9,8},{10,11... | collective-permute-start | bytes 2138120 | tf_op jit(solution)/shard_map/ppermute | solution.py:1040
  156.4 22.8 %collective-permute-start.27 = (bf16[2,2,96,768]{3,2,1,0:T(8,128)(2,1)S(1)}, bf16[2,2,96,768]{3,2,1,0:T(8,128)(2,1)S(1)}, u32[]{:S(2)}, u32[]{:S(2)}) collective-permute-start(bf16[2,2,96,768]{3,2,1,0:T(8,128)(2,1)S(1)} %collective-permute-done.20.rest_1_), channel_id=1, source_target_pairs={{0,4},{4,0},{8,12},{12,8},{16,20},{20,16},{24,28},{28,24},{1,5},{5... | collective-permute-start | bytes 1769480 | tf_op jit(solution)/shard_map/ppermute | solution.py:1040
  187.0 32.7 %collective-permute-start.31 = (bf16[4,2,96,768]{3,2,1,0:T(8,128)(2,1)}, bf16[4,2,96,768]{3,2,1,0:T(8,128)(2,1)S(1)}, u32[]{:S(2)}, u32[]{:S(2)}) collective-permute-start(bf16[4,2,96,768]{3,2,1,0:T(8,128)(2,1)} %get-tuple-element.287), channel_id=1, source_target_pairs={{0,4},{4,0},{8,12},{12,8},{16,20},{20,16},{24,28},{28,24},{1,5},{5... | collective-permute-start | bytes 3538952 | tf_op jit(solution)/shard_map/ppermute | solution.py:1040
  226.0 35.6 %collective-permute-start.34 = (bf16[2,232,768]{2,1,0:T(8,128)(2,1)S(1)}, bf16[2,232,768]{2,1,0:T(8,128)(2,1)S(1)}, u32[]{:S(2)}, u32[]{:S(2)}) collective-permute-start(bf16[2,232,768]{2,1,0:T(8,128)(2,1)S(1)} %add_convert_fusion.2), channel_id=1, source_target_pairs={{0,2},{1,3},{2,0},{3,1},{4,6},{5,7},{6,4},{7,5},{8,10},{9,11},{10,... | collective-permute-start | bytes 2138120 | tf_op jit(solution)/shard_map/ppermute | solution.py:1040
  227.6 18.6 %collective-permute-start.35 = (bf16[2,32,768]{2,1,0:T(8,128)(2,1)S(1)}, bf16[2,32,768]{2,1,0:T(8,128)(2,1)S(1)}, u32[]{:S(2)}, u32[]{:S(2)}) collective-permute-start(bf16[2,32,768]{2,1,0:T(8,128)(2,1)S(1)} %add_convert_fusion.8), channel_id=1, source_target_pairs={{0,2},{1,3},{2,0},{3,1},{4,6},{5,7},{6,4},{7,5},{8,10},{9,11},{10,... | collective-permute-start | bytes 294920 | tf_op jit(solution)/shard_map/ppermute | solution.py:1040
  266.3 21.1 %collective-permute-start.40 = (bf16[4,1,96,768]{3,2,1,0:T(8,128)(2,1)S(1)}, bf16[4,1,96,768]{3,2,1,0:T(8,128)(2,1)S(1)}, u32[]{:S(2)}, u32[]{:S(2)}) collective-permute-start(bf16[4,1,96,768]{3,2,1,0:T(8,128)(2,1)S(1)} %copy-done.78), channel_id=1, source_target_pairs={{0,4},{4,0},{8,12},{12,8},{16,20},{20,16},{24,28},{28,24},{1,5},{5... | collective-permute-start | bytes 1769480 | tf_op jit(solution)/shard_map/ppermute | solution.py:1040
  267.8 19.6 %collective-permute-start.41 = (bf16[2,2,96,768]{3,2,1,0:T(8,128)(2,1)S(1)}, bf16[2,2,96,768]{3,2,1,0:T(8,128)(2,1)S(1)}, u32[]{:S(2)}, u32[]{:S(2)}) collective-permute-start(bf16[2,2,96,768]{3,2,1,0:T(8,128)(2,1)S(1)} %copy-done.79), channel_id=1, source_target_pairs={{0,8},{4,12},{8,0},{12,4},{16,24},{20,28},{24,16},{28,20},{1,9},{5... | collective-permute-start | bytes 1769480 | tf_op jit(solution)/shard_map/ppermute | solution.py:1040
  291.2 18.1 %collective-permute-start.45 = (bf16[2,232,768]{2,1,0:T(8,128)(2,1)S(1)}, bf16[2,232,768]{2,1,0:T(8,128)(2,1)S(1)}, u32[]{:S(2)}, u32[]{:S(2)}) collective-permute-start(bf16[2,232,768]{2,1,0:T(8,128)(2,1)S(1)} %add_convert_fusion.1.first_ref), channel_id=1, source_target_pairs={{0,2},{1,3},{2,0},{3,1},{4,6},{5,7},{6,4},{7,5},{8,10},{9,11},{10,... | collective-permute-start | bytes 2138120 | tf_op jit(solution)/shard_map/ppermute | solution.py:1040
  294.4 28.4 %collective-permute-start.48 = (bf16[4,2,96,768]{3,2,1,0:T(8,128)(2,1)S(1)}, bf16[4,2,96,768]{3,2,1,0:T(8,128)(2,1)S(1)}, u32[]{:S(2)}, u32[]{:S(2)}) collective-permute-start(bf16[4,2,96,768]{3,2,1,0:T(8,128)(2,1)S(1)} %copy-done.76), channel_id=1, source_target_pairs={{0,4},{4,0},{8,12},{12,8},{16,20},{20,16},{24,28},{28,24},{1,5},{5... | collective-permute-start | bytes 3538952 | tf_op jit(solution)/shard_map/ppermute | solution.py:1040
  314.6 19.9 %collective-permute-start.47 = (bf16[2,232,768]{2,1,0:T(8,128)(2,1)}, bf16[2,232,768]{2,1,0:T(8,128)(2,1)S(1)}, u32[]{:S(2)}, u32[]{:S(2)}) collective-permute-start(bf16[2,232,768]{2,1,0:T(8,128)(2,1)} %get-tuple-element.344.grad_own_ref), channel_id=1, source_target_pairs={{0,1},{1,0},{2,3},{3,2},{4,5},{5,4},{6,7},{7,6},{8,9},{9,8},{10,11... | collective-permute-start | bytes 2138120 | tf_op jit(solution)/shard_map/ppermute | solution.py:1040
  314.6 37.4 %collective-permute-start.50 = (bf16[2,2,96,768]{3,2,1,0:T(8,128)(2,1)S(1)}, bf16[2,2,96,768]{3,2,1,0:T(8,128)(2,1)S(1)}, u32[]{:S(2)}, u32[]{:S(2)}) collective-permute-start(bf16[2,2,96,768]{3,2,1,0:T(8,128)(2,1)S(1)} %copy-done.82), channel_id=1, source_target_pairs={{0,8},{4,12},{8,0},{12,4},{16,24},{20,28},{24,16},{28,20},{1,9},{5... | collective-permute-start | bytes 1769480 | tf_op jit(solution)/shard_map/ppermute | solution.py:1040
  314.8 19.6 %collective-permute-start.49 = (bf16[1,2,96,768]{3,2,1,0:T(8,128)(2,1)S(1)}, bf16[1,2,96,768]{3,2,1,0:T(8,128)(2,1)S(1)}, u32[]{:S(2)}, u32[]{:S(2)}) collective-permute-start(bf16[1,2,96,768]{3,2,1,0:T(8,128)(2,1)S(1)} %copy-done.83), channel_id=1, source_target_pairs={{0,16},{4,20},{8,24},{12,28},{16,0},{20,4},{24,8},{28,12},{1,17},{... | collective-permute-start | bytes 884744 | tf_op jit(solution)/shard_map/ppermute | solution.py:1040
  355.7 18.1 %collective-permute-start.52 = (bf16[2,232,768]{2,1,0:T(8,128)(2,1)S(1)}, bf16[2,232,768]{2,1,0:T(8,128)(2,1)S(1)}, u32[]{:S(2)}, u32[]{:S(2)}) collective-permute-start(bf16[2,232,768]{2,1,0:T(8,128)(2,1)S(1)} %add_convert_fusion.first_ref), channel_id=1, source_target_pairs={{0,2},{1,3},{2,0},{3,1},{4,6},{5,7},{6,4},{7,5},{8,10},{9,11},{10,... | collective-permute-start | bytes 2138120 | tf_op jit(solution)/shard_map/ppermute | solution.py:1040
  356.3 29.1 %collective-permute-start.61 = (bf16[2,2,96,768]{3,2,1,0:T(8,128)(2,1)S(1)}, bf16[2,2,96,768]{3,2,1,0:T(8,128)(2,1)S(1)}, u32[]{:S(2)}, u32[]{:S(2)}) collective-permute-start(bf16[2,2,96,768]{3,2,1,0:T(8,128)(2,1)S(1)} %copy-done.80), channel_id=1, source_target_pairs={{0,8},{4,12},{8,0},{12,4},{16,24},{20,28},{24,16},{28,20},{1,9},{5... | collective-permute-start | bytes 1769480 | tf_op jit(solution)/shard_map/ppermute | solution.py:1040
  358.5 30.8 %collective-permute-start.54 = (bf16[4,1,96,768]{3,2,1,0:T(8,128)(2,1)S(1)}, bf16[4,1,96,768]{3,2,1,0:T(8,128)(2,1)S(1)}, u32[]{:S(2)}, u32[]{:S(2)}) collective-permute-start(bf16[4,1,96,768]{3,2,1,0:T(8,128)(2,1)S(1)} %copy-done.81), channel_id=1, source_target_pairs={{0,4},{4,0},{8,12},{12,8},{16,20},{20,16},{24,28},{28,24},{1,5},{5... | collective-permute-start | bytes 1769480 | tf_op jit(solution)/shard_map/ppermute | solution.py:1040
  378.8 94.9 %collective-permute-start.53 = (f32[2,232,768]{2,1,0:T(8,128)}, f32[2,232,768]{2,1,0:T(8,128)S(1)}, u32[]{:S(2)}, u32[]{:S(2)}) collective-permute-start(f32[2,232,768]{2,1,0:T(8,128)} %get-tuple-element.354), channel_id=1, source_target_pairs={{0,1},{1,0},{2,3},{3,2},{4,5},{5,4},{6,7},{7,6},{8,9},{9,8},{10,11... | collective-permute-start | bytes 4276232 | tf_op jit(solution)/shard_map/ppermute | solution.py:1040
  382.0 24.1 %collective-permute-start.55 = (bf16[1,2,96,768]{3,2,1,0:T(8,128)(2,1)}, bf16[1,2,96,768]{3,2,1,0:T(8,128)(2,1)S(1)}, u32[]{:S(2)}, u32[]{:S(2)}) collective-permute-start(bf16[1,2,96,768]{3,2,1,0:T(8,128)(2,1)} %get-tuple-element.369), channel_id=1, source_target_pairs={{0,16},{4,20},{8,24},{12,28},{16,0},{20,4},{24,8},{28,12},{1,17},{... | collective-permute-start | bytes 884744 | tf_op jit(solution)/shard_map/ppermute | solution.py:1040
  389.2 29.5 %collective-permute-start.62 = (bf16[1,2,96,768]{3,2,1,0:T(8,128)(2,1)}, bf16[1,2,96,768]{3,2,1,0:T(8,128)(2,1)S(1)}, u32[]{:S(2)}, u32[]{:S(2)}) collective-permute-start(bf16[1,2,96,768]{3,2,1,0:T(8,128)(2,1)} %get-tuple-element.378), channel_id=1, source_target_pairs={{0,16},{4,20},{8,24},{12,28},{16,0},{20,4},{24,8},{28,12},{1,17},{... | collective-permute-start | bytes 884744 | tf_op jit(solution)/shard_map/ppermute | solution.py:1040
  406.1 17.5 %collective-permute-start.63 = (bf16[1,1,96,768]{3,2,1,0:T(8,128)(2,1)}, bf16[1,1,96,768]{3,2,1,0:T(8,128)(2,1)S(1)}, u32[]{:S(2)}, u32[]{:S(2)}) collective-permute-start(bf16[1,1,96,768]{3,2,1,0:T(8,128)(2,1)} %get-tuple-element.381), channel_id=1, source_target_pairs={{0,8},{4,12},{8,0},{12,4},{16,24},{20,28},{24,16},{28,20},{1,9},{5... | collective-permute-start | bytes 442376 | tf_op jit(solution)/shard_map/ppermute | solution.py:1040
  406.1 17.5 %collective-permute-start.64 = (bf16[1,1,96,768]{3,2,1,0:T(8,128)(2,1)}, bf16[1,1,96,768]{3,2,1,0:T(8,128)(2,1)S(1)}, u32[]{:S(2)}, u32[]{:S(2)}) collective-permute-start(bf16[1,1,96,768]{3,2,1,0:T(8,128)(2,1)} %get-tuple-element.382), channel_id=1, source_target_pairs={{0,16},{4,20},{8,24},{12,28},{16,0},{20,4},{24,8},{28,12},{1,17},{... | collective-permute-start | bytes 442376 | tf_op jit(solution)/shard_map/ppermute | solution.py:1040
  (134 other events, 1281.3 us)

commit v4 on v3

--- a/solution.py
+++ b/solution.py
@@ -67,11 +67,6 @@
     return value, slope
 
 
-class Weight:
-    def __init__(self, arrays, first=0, count=1):
-        self.arrays, self.first, self.count = tuple(arrays), first, count
-
-
 class Plan:
     def __init__(self, dp_n, block, width, hidden, pairs):
         self.dp_n, self.block, self.width, self.hidden, self.pairs = dp_n, block, width, hidden, pairs
@@ -80,25 +75,24 @@
         self.direct = dp_n == 8
 
     def weight_specs(self, pieces):
-        specs = []
-        for item in pieces.arrays:
-            lead = item.shape[:-3]
-            shape = lead + (pieces.count,) + item.shape[-2:]
-            at = (0,) * len(lead) + (pieces.first // pieces.count, 0, 0)
-            specs.append(pl.BlockSpec(shape, lambda *_, at=at: at))
-        return specs
-
-    def weight_scratch(self, pieces, count):
-        return [pltpu.VMEM((count, D, D), LOW)]
+        return [whole(item.shape) for item in flat(pieces)]
+
+    def weight_scratch(self, pieces):
+        return [pltpu.VMEM((len(pieces), D, D), LOW)]
 
     def assemble(self, meta, pieces, refs, scratch):
-        if not self.direct:
-            scratch[...] = refs[0][...]
-            return
-        for ref, places in zip(refs, ((0, 4), (2, 6), (1, 5), (3, 7))):
-            for index, place in enumerate(places):
-                row = pl.multiple_of(jnp.bitwise_xor(meta[0], place) * self.block, 32)
-                scratch[:, pl.ds(row, self.block), :] = ref[index, :, : self.block]
+        refs = iter(refs)
+        for count in range(len(pieces)):
+            if not self.direct:
+                scratch[count] = next(refs)[...]
+                continue
+            _, height, start = pieces[count]
+            for places in ((0, 4), (2, 6), (1, 5), (3, 7)):
+                ref = next(refs)
+                for index, place in enumerate(places):
+                    row = pl.multiple_of(jnp.bitwise_xor(meta[0], place) * self.block, 32)
+                    first = start + index * height
+                    scratch[count, pl.ds(row, self.block), :] = ref[first : first + self.block]
 
     def grad_shapes(self, count):
         if not self.direct:
@@ -116,6 +110,10 @@
             for count in range(acc.shape[0]):
                 refs[0][index, count] = acc[count, pl.ds(away, self.block), :].astype(LOW)
                 refs[1][index, count] = acc[count, pl.ds(here, self.block), :]
+
+
+def flat(pieces):
+    return [item for arrays, _, _ in pieces for item in arrays]
 
 
 def whole(shape):
@@ -207,7 +205,7 @@
 
 def encoder_attention(plan, meta, own, oth, gain, pieces, base, count):
     w3 = 3 * plan.width
-    n = len(pieces.arrays)
+    n = len(flat(pieces))
 
     def body(meta, own_ref, oth_ref, gain_ref, *rest):
         refs, (own_out, oth_out, kept, weight) = rest[:n], rest[n:]
@@ -235,19 +233,19 @@
         body,
         (2 * count,),
         meta,
-        (own, oth, gain, *pieces.arrays),
+        (own, oth, gain, *flat(pieces)),
         [own_spec(count, base, rows), oth_spec(count, base, rows), whole((1, D)), *plan.weight_specs(pieces)],
         [jax.ShapeDtypeStruct((count,) + rows, LOW)] * 2
         + [jax.ShapeDtypeStruct((2 * count, ENC_LEN, w3 + plan.width), LOW)],
         [own_spec(count, 0, rows), oth_spec(count, 0, rows), step_spec((ENC_LEN, w3 + plan.width))],
-        plan.weight_scratch(pieces, 1),
+        plan.weight_scratch(pieces),
     )
 
 
 def encoder_attention_back(plan, meta, own, oth, gain, pieces, kept, grad_own, grad_oth):
     count = plan.half
     width, w3 = plan.width, 3 * plan.width
-    n = len(pieces.arrays)
+    n = len(flat(pieces))
 
     def body(meta, own_ref, oth_ref, gain_ref, kept_ref, grad_own_ref, grad_oth_ref, *rest):
         refs, (own_out, oth_out), grad_refs = rest[:n], rest[n : n + 2], rest[n + 2 : -2]
@@ -285,16 +283,16 @@
         body,
         (2 * count,),
         meta,
-        (own, oth, gain, kept, grad_own, grad_oth, *pieces.arrays),
+        (own, oth, gain, kept, grad_own, grad_oth, *flat(pieces)),
         [*pair_specs, whole((1, D)), step_spec(kept.shape[1:]), *pair_specs, *plan.weight_specs(pieces)],
         [jax.ShapeDtypeStruct((count,) + rows, LOW)] * 2 + shapes,
         [*pair_specs, *[whole(item.shape) for item in shapes]],
-        plan.weight_scratch(pieces, 1) + [pltpu.VMEM((1, D, D), F32)],
+        plan.weight_scratch(pieces) + [pltpu.VMEM((1, D, D), F32)],
     )
 
 
 def encoder_feed(plan, meta, own, oth, pieces, base, count):
-    n = len(pieces.arrays)
+    n = len(flat(pieces))
 
     def body(meta, own_ref, oth_ref, *rest):
         refs, (own_out, oth_out, weight) = rest[:n], rest[n:]
@@ -314,16 +312,16 @@
         body,
         (2 * count,),
         meta,
-        (own, oth, *pieces.arrays),
+        (own, oth, *flat(pieces)),
         [own_spec(count, base, rows), oth_spec(count, base, rows), *plan.weight_specs(pieces)],
         [jax.ShapeDtypeStruct((count,) + rows, LOW)] * 2,
         [own_spec(count, 0, rows), oth_spec(count, 0, rows)],
-        plan.weight_scratch(pieces, 2),
+        plan.weight_scratch(pieces),
     )
 
 
 def encoder_feed_back(plan, meta, own, oth, grad_own, grad_oth, pieces):
-    n = len(pieces.arrays)
+    n = len(flat(pieces))
     count = plan.half
 
     def body(meta, own_ref, oth_ref, grad_own_ref, grad_oth_ref, *rest):
@@ -346,21 +344,23 @@
 
         @pl.when(step == 2 * count - 1)
         def _():
-            plan.emit(meta, acc, grad_refs)
+            for index in range(2):
+                size = len(grad_refs) // 2
+                plan.emit(meta, acc.at[pl.ds(index, 1)], grad_refs[index * size : (index + 1) * size])
 
     rows = (LONG, D)
-    shapes = plan.grad_shapes(2)
+    shapes = plan.grad_shapes(1) * 2
     pair_specs = [own_spec(count, 0, rows), oth_spec(count, 0, rows)]
     return call(
         "encoder_feed_back",
         body,
         (2 * count,),
         meta,
-        (own, oth, grad_own, grad_oth, *pieces.arrays),
+        (own, oth, grad_own, grad_oth, *flat(pieces)),
         [*pair_specs, *pair_specs, *plan.weight_specs(pieces)],
         [jax.ShapeDtypeStruct((count,) + rows, LOW)] * 2 + shapes,
         [*pair_specs, *[whole(item.shape) for item in shapes]],
-        plan.weight_scratch(pieces, 2) + [pltpu.VMEM((2, D, D), F32)],
+        plan.weight_scratch(pieces) + [pltpu.VMEM((2, D, D), F32)],
     )
 
 
@@ -376,7 +376,7 @@
 
 
 def decoder_self(plan, meta, rows_in, gain, pieces):
-    n = len(pieces.arrays)
+    n = len(flat(pieces))
     width, w3 = plan.width, 3 * plan.width
     rows = plan.pairs * SUFFIX
     mid = rows // 2
@@ -401,16 +401,16 @@
         body,
         (1,),
         meta,
-        (rows_in, gain, *pieces.arrays),
+        (rows_in, gain, *flat(pieces)),
         [whole((rows, D)), whole((1, D)), *plan.weight_specs(pieces)],
         [jax.ShapeDtypeStruct((mid, D), LOW)] * 2 + [jax.ShapeDtypeStruct((rows, 4 * width), LOW)],
         [whole((mid, D))] * 2 + [whole((rows, 4 * width))],
-        plan.weight_scratch(pieces, 1),
+        plan.weight_scratch(pieces),
     )
 
 
 def decoder_self_back(plan, meta, rows_in, gain, pieces, kept, grad_own, grad_oth):
-    n = len(pieces.arrays)
+    n = len(flat(pieces))
     width, w3 = plan.width, 3 * plan.width
     rows = plan.pairs * SUFFIX
     mid = rows // 2
@@ -446,16 +446,16 @@
         body,
         (1,),
         meta,
-        (rows_in, gain, kept, grad_own, grad_oth, *pieces.arrays),
+        (rows_in, gain, kept, grad_own, grad_oth, *flat(pieces)),
         [whole((rows, D)), whole((1, D)), whole(kept.shape), whole((mid, D)), whole((mid, D)), *plan.weight_specs(pieces)],
         [jax.ShapeDtypeStruct((mid, D), LOW)] * 2 + shapes,
         [whole((mid, D))] * 2 + [whole(item.shape) for item in shapes],
-        plan.weight_scratch(pieces, 1) + [pltpu.VMEM((1, D, D), F32)],
+        plan.weight_scratch(pieces) + [pltpu.VMEM((1, D, D), F32)],
     )
 
 
 def decoder_cross(plan, meta, own, oth, memory_own, memory_oth, pieces):
-    n = len(pieces.arrays)
+    n = len(flat(pieces))
     count = plan.half
     width, w3 = plan.width, 3 * plan.width
 
@@ -484,7 +484,7 @@
         body,
         (2 * count,),
         meta,
-        (own, oth, memory_own, memory_oth, *pieces.arrays),
+        (own, oth, memory_own, memory_oth, *flat(pieces)),
         [
             own_spec(count, 0, rows),
             oth_spec(count, 0, rows),
@@ -503,14 +503,14 @@
             step_spec((SUFFIX, 2 * width)),
             step_spec((ENC_LEN, 2 * width)),
         ],
-        plan.weight_scratch(pieces, 1),
+        plan.weight_scratch(pieces),
     )
 
 
 def decoder_cross_back(
     plan, meta, own, oth, memory_own, memory_oth, pieces, kept_query, kept_key, grad_own, grad_oth
 ):
-    n = len(pieces.arrays)
+    n = len(flat(pieces))
     count = plan.half
     width, w3 = plan.width, 3 * plan.width
 
@@ -555,7 +555,7 @@
         body,
         (2 * count,),
         meta,
-        (own, oth, memory_own, memory_oth, kept_query, kept_key, grad_own, grad_oth, *pieces.arrays),
+        (own, oth, memory_own, memory_oth, kept_query, kept_key, grad_own, grad_oth, *flat(pieces)),
         [
             *row_specs,
             *long_specs,
@@ -568,12 +568,12 @@
         + [jax.ShapeDtypeStruct((count,) + long, LOW)] * 2
         + shapes,
         [*row_specs, *long_specs, *[whole(item.shape) for item in shapes]],
-        plan.weight_scratch(pieces, 1) + [pltpu.VMEM((1, D, D), F32)],
+        plan.weight_scratch(pieces) + [pltpu.VMEM((1, D, D), F32)],
     )
 
 
 def decoder_feed(plan, meta, own, oth, grad_in, pieces):
-    n = len(pieces.arrays)
+    n = len(flat(pieces))
     rows = plan.pairs * SUFFIX
     mid = rows // 2
 
@@ -602,11 +602,11 @@
         body,
         (1,),
         meta,
-        (own, oth, grad_in, *pieces.arrays),
+        (own, oth, grad_in, *flat(pieces)),
         [whole((mid, D))] * 2 + [whole((rows, D)), *plan.weight_specs(pieces)],
         [jax.ShapeDtypeStruct((2, mid, D), LOW)] * 2 + shapes,
         [whole((2, mid, D))] * 2 + [whole(item.shape) for item in shapes],
-        plan.weight_scratch(pieces, 2) + [pltpu.VMEM((2, D, D), F32)],
+        plan.weight_scratch(pieces) + [pltpu.VMEM((2, D, D), F32)],
     )
 
 
@@ -739,32 +739,31 @@
         group = lax.broadcasted_iota(jnp.int32, (8, D), 1) // plan.width
         row = lax.broadcasted_iota(jnp.int32, (8, D), 0)
         place = one_hot(plan.block, dp_at * plan.block)
-        for index in range(count):
+        def one(index, _):
+            heads = (jnp.zeros((8, D), jnp.int32) + index) < attention
             value = refs[0][0, index]
             for ref in refs[1:]:
                 value = value + ref[0, index].astype(F32)
             out[index] = value
             square = value * value
             lanes = jnp.broadcast_to(jnp.sum(square, 0, keepdims=True), (8, D))
-            if attention:
-                mask = (group == row).astype(F32)
-            else:
-                mask = (row == 0).astype(F32)
+            mask = jnp.where(heads, (group == row).astype(F32), (row == 0).astype(F32))
             sums = lax.dot_general(
                 mask, square, (((1,), (1,)), ((), ())), precision=EXACT, preferred_element_type=F32
             )
             tile = lax.dot_general(
                 sums, place, (((1,), (0,)), ((), ())), precision=EXACT, preferred_element_type=F32
             )
-            if attention:
-                spread = jnp.zeros_like(tile)
-                for part in range(groups):
-                    shift = lax.rem(mp_at * plan.width + (D - part * plan.width), D)
-                    moved = pltpu.roll(jnp.where(group == part, lanes, 0.0), shift, 1)
-                    spread = jnp.where(row == 4 + part, moved, spread)
-            else:
-                spread = jnp.where(row == 4 + mp_at, lanes, 0.0)
+            spread = jnp.zeros_like(tile)
+            for part in range(groups):
+                shift = lax.rem(mp_at * plan.width + (D - part * plan.width), D)
+                moved = pltpu.roll(jnp.where(group == part, lanes, 0.0), shift, 1)
+                spread = jnp.where(row == 4 + part, moved, spread)
+            spread = jnp.where(heads, spread, jnp.where(row == 4 + mp_at, lanes, 0.0))
             tile_out[index] = jnp.where(row < 4, tile, spread)
+            return 0
+
+        lax.fori_loop(0, count, one, 0)
 
     return call(
         "collect",
@@ -779,15 +778,15 @@
     )
 
 
-def finish(plan, meta, early, late, statistics, gain_state):
+def finish(plan, meta, sums, statistics, gain_state):
     counts = [item.shape for item in statistics]
 
-    def body(meta, early_ref, late_ref, *rest):
+    def body(meta, sum_ref, *rest):
         olds, gains = rest[:8], rest[8:12]
         norm_out, news, rates, gain_outs = rest[12], rest[13:21], rest[21], rest[22:]
-        tiles = [late_ref[2], early_ref[1], early_ref[0]]
-        feeds = [(late_ref[0], late_ref[1]), (early_ref[2], early_ref[3])]
-        gain_sum = 0.5 * late_ref[3]
+        tiles = [sum_ref[6], sum_ref[1], sum_ref[0]]
+        feeds = [(sum_ref[2], sum_ref[3]), (sum_ref[4], sum_ref[5])]
+        gain_sum = 0.5 * sum_ref[7]
         total = jnp.sum(gain_sum * gain_sum)
         for tile in tiles:
             total = total + jnp.sum(tile[:4])
@@ -848,7 +847,7 @@
         + [jax.ShapeDtypeStruct(small, F32)] * 5
         + [jax.ShapeDtypeStruct(small, LOW)]
     )
-    inputs = (early, late, *statistics, *gain_state)
+    inputs = (sums, *statistics, *gain_state)
     return call(
         "finish",
         body,
@@ -869,8 +868,10 @@
     return grad, moment_new, master_new, AVERAGE * average + (1.0 - AVERAGE) * master_new
 
 
-def exact(left, right, contract):
-    return lax.dot_general(left, right, (contract, ((), ())), precision=EXACT, preferred_element_type=F32)
+def columns(rows, offset, size):
+    filled = jnp.concatenate([rows] * (8 // rows.shape[0] + 1), 0)[:8]
+    wide = (size + 127) // 128 * 128
+    return jnp.transpose(pltpu.roll(filled, lax.rem(D - offset, D), 1)[:, :wide])[:size]
 
 
 def update_attention(plan, meta, rates, grads, rows_in, cols_in, rows_out, cols_out, state_in, state_out):
@@ -882,9 +883,8 @@
         dp_at, mp_at = meta[0], meta[1 + 3 * plan.pairs]
         grad = jnp.where(layer == 0, grad_a[0], jnp.where(layer == 1, grad_b[1], grad_b[0]))
         grad = grad * rates_ref[:1, :1]
-        local = one_hot(block, dp_at * block)
         means = jnp.mean(rin[0], -1, keepdims=True)
-        row_scale = lax.rsqrt(exact(local, rin[0] / means, ((1,), (1,))))
+        row_scale = lax.rsqrt(columns(rin[0] / means, dp_at * block, block))
         shift = lax.rem(D - mp_at * width, D)
         col_scale = lax.rsqrt(pltpu.roll(jnp.concatenate([cin[0]] * 3, 0)[:8], shift, 1)[:3, :width])
         for part in range(3):
@@ -901,9 +901,7 @@
         turned = jnp.transpose(grad[:, 3 * width :])
         row, col = rout[pl.ds(layer, 1), :], cout[pl.ds(layer, 1), :]
         mean = jnp.mean(row, -1, keepdims=True)
-        row_scale = lax.rsqrt(
-            exact(one_hot(width, mp_at * width), jnp.broadcast_to(row / mean, (8, D)), ((1,), (1,)))
-        )[:, :1]
+        row_scale = lax.rsqrt(columns(row / mean, mp_at * width, width))[:, :1]
         shift = lax.rem(D - dp_at * block, D)
         col_scale = lax.rsqrt(pltpu.roll(jnp.broadcast_to(col, (8, D)), shift, 1)[:1, :block])
         values = step_values(turned, row_scale * col_scale, ins[3][0], ins[4][0], ins[5][0])
@@ -943,7 +941,6 @@
     def body(meta, rates_ref, grad_a, grad_b, rup, cup, rdown, cdown, *rest):
         ins, outs = rest[:6], rest[6:]
         layer = pl.program_id(0)
-        local = one_hot(block, meta[0] * block)
         lanes = pl.ds(pl.multiple_of(meta[1 + 3 * plan.pairs] * hidden, 128), hidden)
         one = pl.ds(layer, 1)
         mean_up = jnp.mean(rup[one, :], -1, keepdims=True)
@@ -952,7 +949,7 @@
         across = (cup[one, lanes], rdown[one, lanes] / mean_down)
         for part in range(2):
             grad = jnp.where(layer == 0, grad_a[part], grad_b[part]) * rates_ref[:1, :1]
-            row_scale = lax.rsqrt(exact(local, jnp.broadcast_to(along[part], (8, D)), ((1,), (1,))))[:, :1]
+            row_scale = lax.rsqrt(columns(along[part], meta[0] * block, block))[:, :1]
             values = step_values(
                 grad,
                 row_scale * lax.rsqrt(across[part]),
@@ -1044,28 +1041,78 @@
 
     hold = lax.optimization_barrier
 
-    def widen(own, four):
-        two = jnp.stack([own, four])
-        return two, swap(two, "dp", 2), swap(two, "dp", 1)
+    class Gather:
+        def __init__(self, blocks):
+            self.items, self.sent, self.own = [{} for _ in blocks], [], list(blocks)
+
+        def step(self, chain, *sends, later=()):
+            names = [(item, name) for item, name in self.sent if (name, item) not in later]
+            late = [(item, name) for item, name in self.sent if (name, item) in later]
+            chain, values, self.own = hold(
+                (list(chain), [self.items[item][name] for item, name in names], self.own)
+            )
+            for (item, name), value in zip(names, values):
+                self.items[item][name] = value
+            self.sent = late
+            for name, item in sends:
+                if name == "fours":
+                    four = swap(jnp.concatenate([self.own[at] for at in item]), "dp", 4)
+                    for place, at in enumerate(item):
+                        self.items[at]["four"] = four[place * block : (place + 1) * block]
+                        self.sent.append((at, "four"))
+                    continue
+                parts = self.items[item]
+                if name == "four":
+                    parts[name] = swap(self.own[item], "dp", 4)
+                    self.sent.append((item, name))
+                    continue
+                if "two" not in parts:
+                    parts["two"] = jnp.concatenate([self.own[item], parts["four"]])
+                if name == "far":
+                    parts[name] = swap(parts["two"], "dp", 2)
+                else:
+                    parts[name] = swap(parts["two" if name == "near" else "far"], "dp", 1)
+                self.sent.append((item, name))
+            return chain
+
+        def take(self, item, index=0):
+            parts = self.items[item]
+            height = self.own[item].shape[0]
+            return [parts[name] for name in ("two", "far", "near", "last")], height, index * block
+
+    class Plain:
+        def __init__(self, blocks):
+            self.own = list(blocks)
+
+        def step(self, chain, *sends, later=()):
+            return chain
+
+        def take(self, item, index=0):
+            own = self.own[item][index * block : (index + 1) * block]
+            return [lax.all_gather(own, "dp", axis=0, tiled=True)], D, 0
 
     def scatter(parts, attention):
         summed = lax.psum_scatter(parts[0], "dp", scatter_dimension=1, tiled=True)
         return collect(plan, meta, [summed[None]], attention)
 
+    def total(value, axes):
+        for axis, count in axes:
+            for bit in bits(count):
+                sent = value.astype(low)
+                value = sent.astype(value.dtype) + swap(sent, axis, bit).astype(value.dtype)
+        return value
+
     def total_dp(value):
-        for bit in bits(dp_n):
-            value = value + swap(value, "dp", bit)
-        return value
+        return total(value, [("dp", dp_n)])
 
     def total_all(value):
-        for bit in bits(mp_n):
-            value = value + swap(value, "mp", bit)
-        return total_dp(value)
-
-    def reduce_own(own, oth):
+        return total(value, [("mp", mp_n), ("dp", dp_n)])
+
+    def reduce_own(own, oth, first=()):
         sent = (own.astype(f32) + swap(oth, "mp", 1).astype(f32)).astype(low)
         for bit in bits(mp_n)[1:-1]:
             sent = (sent.astype(f32) + swap(sent, "mp", bit).astype(f32)).astype(low)
+        sent, first = hold((sent, first))
         return sent, swap(sent, "mp", bits(mp_n)[-1])
 
     def relative(value):
@@ -1087,29 +1134,35 @@
     def attention_block(layer):
         return jnp.concatenate(
             [project_in[layer, 0], project_in[layer, 1], project_in[layer, 2], project_out[layer].T], 1
-        ).astype(low)[None]
+        ).astype(low)
 
     def feed_block(layer):
-        return jnp.stack([expand[layer], contract[layer].T]).astype(low)
+        return [expand[layer].astype(low), contract[layer].T.astype(low)]
 
     direct = plan.direct
-    own_a = attention_block(0)
-    own_b = feed_block(0)
-    own_c = jnp.concatenate([attention_block(1), attention_block(2)], 0)
-    own_d = feed_block(1)
     gain_full = lax.dynamic_update_slice(
         jnp.zeros((8, D), low), norm_gains.astype(low), (0, dp_index * block)
     )
-    if direct:
-        own_a = jnp.concatenate([own_a, gain_full[None]], 1)
-        four, own_b = hold((swap(own_a, "dp", 4), own_b))
-        two, far, side_one = widen(own_a, four)
-        four_b = swap(own_b, "dp", 4)
-        far, side_one = hold((far, side_one))
-        arrays = (two, far, side_one, swap(far, "dp", 1))
-        gain_rows = sum(jnp.sum(item[:, 0, block:].astype(f32), 0) for item in arrays)
+    blocks = [
+        attention_block(0),
+        *feed_block(0),
+        attention_block(1),
+        attention_block(2),
+        jnp.concatenate(feed_block(1)),
+    ]
+    if direct:
+        blocks[0] = jnp.concatenate([blocks[0], gain_full], 0)
+    gather = (Gather if direct else Plain)(blocks)
+    gather.step((), ("four", 0))
+    gather.step((), ("far", 0), ("near", 0), ("four", 1))
+    gather.step((), ("last", 0), later=(("four", 1),))
+    enc_att = [gather.take(0)]
+    if direct:
+        height = block + 8
+        gain_rows = sum(
+            item[at : at + 8].astype(f32) for item in enc_att[0][0] for at in (block, height + block)
+        )
     else:
-        arrays = [lax.all_gather(own_a, "dp", axis=1, tiled=True)]
         gain_rows = total_dp(gain_full).astype(f32)
     gains = [gain_rows[i : i + 1] for i in range(5)]
 
@@ -1142,59 +1195,43 @@
     def triple(value):
         return value.reshape(half, SUFFIX, D)
 
-    if direct:
-        *arrays, four_b, own_c = hold((*arrays, four_b, own_c))
-        two, far, side_one = widen(own_b, four_b)
-        four_c = swap(own_c, "dp", 4)
-    enc_att = Weight(arrays)
+    (enc_oth,) = gather.step((enc_oth,), ("far", 1), ("near", 1), ("four", 2), later=(("last", 0),))
     own, oth, kept_enc = encoder_attention(plan, meta, enc_own, enc_oth, gains[0], enc_att, 0, half)
-    if direct:
-        own, oth, dec_rel, cot, cot_low = hold((own, oth, dec_rel, cot, cot_low))
-    sums = reduce_own(own, oth)
-    if direct:
-        far, side_one, _ = hold((far, side_one, sums[0]))
-        arrays = (two, far, side_one, swap(far, "dp", 1))
-    else:
-        arrays = [lax.all_gather(own_b, "dp", axis=1, tiled=True)]
-    enc_feed = Weight(arrays, 0, 2)
+    own, oth, dec_rel, cot, cot_low = gather.step(
+        (own, oth, dec_rel, cot, cot_low), ("last", 1), ("near", 2), ("far", 2), ("fours", (3, 4))
+    )
+    sums = gather.step(reduce_own(own, oth), ("last", 2))
+    enc_feed = [gather.take(1), gather.take(2)]
     enc_mid, norm_mid = add_norm(meta, "add_norm_mid", enc_own, *sums, gains[1])
     norm_mid_oth = core(norm_mid)
 
-    if direct:
-        norm_mid_oth, four_c, own_d = hold((norm_mid_oth, four_c, own_d))
-        two, far, side_one = widen(own_c, four_c)
-        four_d = swap(own_d, "dp", 4)
+    (norm_mid_oth,) = gather.step(
+        (norm_mid_oth,), ("far", 3), ("near", 3), ("four", 5), later=(("last", 2),)
+    )
     own, oth = encoder_feed(plan, meta, norm_mid, norm_mid_oth, enc_feed, 0, half)
+    own, oth = gather.step((own, oth), ("last", 3), ("far", 4), ("near", 4), later=(("four", 5),))
     sums = reduce_own(own, oth)
-    if direct:
-        far, side_one, _ = hold((far, side_one, sums[0]))
-        arrays = (two, far, side_one, swap(far, "dp", 1))
-    else:
-        arrays = [lax.all_gather(own_c, "dp", axis=1, tiled=True)]
-    if direct:
-        *arrays, four_d = hold((*arrays, four_d))
-        two, far, side_one = widen(own_d, four_d)
-    self_att, cross_att = Weight(arrays, 0), Weight(arrays, 1)
-
+    (dec_rel,) = gather.step((dec_rel,), ("last", 4), later=(("last", 3),))
+
+    self_att = [gather.take(3)]
     own, oth, kept_self = decoder_self(plan, meta, dec_rel, gains[2], self_att)
-    sums_self = reduce_own(own, oth)
+    sums = gather.step(sums)
+    sums_self = reduce_own(own, oth, sums)
+    gather.step((sums_self[0],), ("far", 5), ("near", 5))
+    cross_att = [gather.take(4)]
     memory = (enc_mid + (sums[0].astype(f32) + sums[1].astype(f32))).astype(low)
+    dec_one, norm_cross = add_norm(meta, "add_norm_cross", dec_rel[:mid], *sums_self, gains[3])
+    memory, norm_cross = gather.step((memory, norm_cross), ("last", 5))
     memory_oth = core(memory)
-    dec_one, norm_cross = add_norm(meta, "add_norm_cross", dec_rel[:mid], *sums_self, gains[3])
     norm_cross_oth = core(norm_cross)
 
-    if direct:
-        norm_cross_oth, far, side_one = hold((norm_cross_oth, far, side_one))
-        arrays = (two, far, side_one, swap(far, "dp", 1))
     cross_in = (triple(norm_cross), triple(norm_cross_oth), memory, memory_oth, cross_att)
     own, oth, *kept_cross = decoder_cross(plan, meta, *cross_in)
     sums = reduce_own(own, oth)
-    if not direct:
-        arrays = [lax.all_gather(own_d, "dp", axis=1, tiled=True)]
-    dec_feed = Weight(arrays, 0, 2)
     dec_two, norm_last = add_norm(
         meta, "add_norm_last", dec_one, sums[0].reshape(mid, D), sums[1].reshape(mid, D), gains[4]
     )
+    dec_feed = [gather.take(5), gather.take(5, 1)]
 
     own, oth, *grads_dec = decoder_feed(plan, meta, norm_last, core(norm_last), cot_low, dec_feed)
     if direct:
@@ -1212,101 +1249,102 @@
         own, oth, own_long, oth_long, more_dec = hold((own, oth, own_long, oth_long, more_dec))
         more_cross = swap(grads_cross[0], "dp", 1)
     sums = reduce_own(own, oth)
-    if direct:
-        own_long, oth_long, _ = hold((own_long, oth_long, sums[0]))
-    sums_enc = reduce_own(own_long, oth_long)
+    sums_enc = reduce_own(own_long, oth_long, sums)
+    if direct:
+        keep, more_dec, _ = hold((grads_dec[1], more_dec, sums[0]))
+        keep_dec, away_dec = fold(plan, meta, [keep], [more_dec], halves)
+        *sums, away_dec = hold((*sums, away_dec))
+        more_dec = swap(away_dec, "dp", 2)
     grad, grad_low, gain_three = norm_back(
         meta, "norm_back_cross", dec_one, gains[3], grad, sums[0].reshape(mid, D), sums[1].reshape(mid, D), True
     )
     grad_low_oth = core(grad_low)
-    if direct:
-        keep, more_dec, _, grad_low_oth = hold((grads_dec[1], more_dec, sums_enc[0], grad_low_oth))
-        keep_dec, away_dec = fold(plan, meta, [keep], [more_dec], halves)
 
     own_self, oth_self, *grads_self = decoder_self_back(
         plan, meta, dec_rel, gains[2], self_att, kept_self, grad_low, grad_low_oth
     )
     decoder_out = absolute(triple(out_own)).reshape(2 * mid, D)
     if direct:
-        *sums_enc, own_self, oth_self, away_dec = hold((*sums_enc, own_self, oth_self, away_dec))
+        own_self, oth_self, decoder_out = hold((own_self, oth_self, decoder_out))
     sums_self = reduce_own(own_self, oth_self)
+    if direct:
+        *sums_enc, _, decoder_out, more_cross, more_dec = hold(
+            (*sums_enc, sums_self[0], decoder_out, more_cross, more_dec)
+        )
     grad_enc = sums_enc[0].astype(f32) + sums_enc[1].astype(f32)
     enc_low = grad_enc.astype(low)
     enc_low_oth = core(enc_low)
 
     if direct:
-        enc_low_oth, decoder_out, away_dec, more_cross, away_self = hold(
-            (enc_low_oth, decoder_out, away_dec, more_cross, grads_self[0])
+        keep_dec, away_dec = fold(plan, meta, [keep_dec], [more_dec], halves)
+        enc_low_oth, away_self, away_dec = hold((enc_low_oth, grads_self[0], away_dec))
+        more_self = swap(away_self, "dp", 1)
+        more_dec = swap(away_dec, "dp", 4)
+    own, oth, *grads_enc = encoder_feed_back(plan, meta, norm_mid, norm_mid_oth, enc_low, enc_low_oth, enc_feed)
+    if direct:
+        own, oth, more_self, more_dec, *sums_self = hold((own, oth, more_self, more_dec, *sums_self))
+        more_up, more_down = [swap(item, "dp", 1) for item in grads_enc[::2]]
+    sums = reduce_own(own, oth)
+    if direct:
+        keep_cross, keep_self, more_cross, more_self, _ = hold(
+            (grads_cross[1], grads_self[1], more_cross, more_self, sums[0])
         )
-        more_self = swap(away_self, "dp", 1)
-        more_dec = swap(away_dec, "dp", 2)
-    own, oth, *grads_enc = encoder_feed_back(plan, meta, norm_mid, norm_mid_oth, enc_low, enc_low_oth, enc_feed)
-    if direct:
-        own, oth, more_self, more_dec, *sums_self = hold((own, oth, more_self, more_dec, *sums_self))
-        more_enc = swap(grads_enc[0], "dp", 1)
-    sums = reduce_own(own, oth)
-    if direct:
-        keep_cross, keep_self, more_cross, more_self, keep_dec, more_dec, *sums_self, _ = hold(
-            (grads_cross[1], grads_self[1], more_cross, more_self, keep_dec, more_dec, *sums_self, sums[0])
-        )
-        keep_dec, away_dec = fold(plan, meta, [keep_dec], [more_dec], halves)
-        more_dec = swap(away_dec, "dp", 4)
         keep_mid, away_mid = fold(plan, meta, [keep_cross, keep_self], [more_cross, more_self], halves)
         more_mid = swap(away_mid, "dp", 2)
+        sums_self, _ = hold((sums_self, away_mid))
     grad, gain_two = norm_back(meta, "norm_back_self", dec_rel[:mid], gains[2], grad, *sums_self, False)
     decoder_in_grad = absolute(triple(grad)).reshape(2 * mid, D)
     if direct:
-        *sums, away_mid, away_dec, decoder_in_grad = hold((*sums, away_mid, away_dec, decoder_in_grad))
+        sum_dec = collect(plan, meta, [keep_dec, more_dec], 0)
+        *sums, sum_dec, decoder_in_grad, more_up = hold((*sums, sum_dec, decoder_in_grad, more_up))
     grad_enc, enc_low, gain_one = norm_back(
         meta, "norm_back_mid", enc_mid, gains[1], grad_enc, *sums, True
     )
+    if direct:
+        enc_low, more_down, more_mid = hold((enc_low, more_down, more_mid))
     enc_low_oth = core(enc_low)
 
     if direct:
-        keep_enc, away_enc = fold(plan, meta, [grads_enc[1]], [more_enc], halves)
-        enc_low_oth, decoder_in_grad, away_enc, more_dec = hold((enc_low_oth, decoder_in_grad, away_enc, more_dec))
+        keep_mid, away_mid = fold(plan, meta, [keep_mid], [more_mid], halves)
+        keep_enc, away_enc = fold(plan, meta, grads_enc[1::2], [more_up, more_down], halves)
+        enc_low_oth, away_enc, away_mid = hold((enc_low_oth, away_enc, away_mid))
+        more_mid = swap(away_mid, "dp", 4)
         more_enc = swap(away_enc, "dp", 2)
     own, oth, *grads_att = encoder_attention_back(
         plan, meta, enc_own, enc_oth, gains[0], enc_att, kept_enc, enc_low, enc_low_oth
     )
     if direct:
         more_att = swap(grads_att[0], "dp", 1)
-        own, oth, more_mid = hold((own, oth, more_mid))
-    sums = reduce_own(own, oth)
-    if direct:
-        keep_mid, more_mid, keep_enc, keep_dec, _ = hold((keep_mid, more_mid, keep_enc, keep_dec, sums[0]))
-        keep_mid, away_mid = fold(plan, meta, [keep_mid], [more_mid], halves)
-        more_mid = swap(away_mid, "dp", 4)
+        own, oth, more_enc, more_mid = hold((own, oth, more_enc, more_mid))
         keep_enc, away_enc = fold(plan, meta, [keep_enc], [more_enc], halves)
         more_enc = swap(away_enc, "dp", 4)
-        sum_dec = collect(plan, meta, [keep_dec, more_dec], False)
-        mine, *others = fold(plan, meta, [grads_att[1]], [more_att], apart)
-        mine, *others, more_mid, _ = hold((mine, *others, more_mid, sum_dec[1]))
+    sums = reduce_own(own, oth)
+    if direct:
+        keep_att, more_att, _, _ = hold((grads_att[1], more_att, away_enc, sums[0]))
+        mine, *others = fold(plan, meta, [keep_att], [more_att], apart)
+        others, more_enc, sums = hold((others, more_enc, sums))
         pieces_att = [mine] + [swap(item, "dp", 2 * (i + 1)) for i, item in enumerate(others)]
-        sum_mid = collect(plan, meta, [keep_mid, more_mid], True)
+        sum_mid = collect(plan, meta, [keep_mid, more_mid], 2)
+        sum_enc = collect(plan, meta, [keep_enc, more_enc], 0)
+        tiles = [sum_mid[1], sum_enc[1], sum_dec[1]]
     else:
-        sum_dec = scatter(grads_dec, False)
-        sum_mid = [
-            jnp.concatenate(item) for item in zip(scatter(grads_cross, True), scatter(grads_self, True))
-        ]
-    early = total_all(jnp.concatenate([sum_mid[1], sum_dec[1]]))
+        sum_dec = scatter(grads_dec, 0)
+        sum_mid = [jnp.concatenate(item) for item in zip(scatter(grads_cross, 1), scatter(grads_self, 1))]
+        sum_enc = scatter([jnp.concatenate(grads_enc)], 0)
+        tiles = [sum_mid[1], sum_enc[1], sum_dec[1]]
     grad_enc, gain_zero = norm_back(meta, "norm_back_enc", enc_own, gains[0], grad_enc, *sums, False)
     if direct:
-        sum_enc = collect(plan, meta, [keep_enc, more_enc], False)
-        sum_att = collect(plan, meta, pieces_att, True)
-    else:
-        sum_enc = scatter(grads_enc, False)
-        sum_att = scatter(grads_att, True)
+        *pieces_att, _, _ = hold((*pieces_att, sum_enc[1], gain_zero))
+    sum_att = collect(plan, meta, pieces_att, 1) if direct else scatter(grads_att, 1)
     encoder_in_grad = absolute(grad_enc)[:, :ENC_LEN].reshape(pairs * ENC_LEN, D)
     gain_tile = jnp.concatenate(
         [gain_zero, gain_one, gain_two, gain_three, gain_four, jnp.zeros((3, D), f32)]
     )[None]
-    late = total_all(jnp.concatenate([sum_enc[1], sum_att[1], gain_tile]))
+    tiles = total_all(jnp.concatenate([*tiles, sum_att[1], gain_tile]))
     done = finish(
         plan,
         meta,
-        early,
-        late,
+        tiles,
         (
             project_in_rows,
             project_in_cols,

time: 486 us -> 424 us (0.87); the launches traced: 477 us -> 422 us
  waiting for transfers between devices: 187 us -> 122 us
  starting transfers between devices: 59.6 us -> 72.9 us
  local copies, waits for them, and re-layouts: 32.6 us -> 26.6 us
    ppermute x71 -> x74, waiting for transfers between devices: 187 us -> 122 us  [swap(): return lax.ppermute(value, axis, [(i, i ^ bit) for i in range(count)])]
    ppermute x71 -> x74, starting transfers between devices: 59.6 us -> 72.9 us  [swap(): return lax.ppermute(value, axis, [(i, i ^ bit) for i in range(count)])]
    unnamed x176 -> x201, local copies, waits for them, and re-layouts: 18 us -> 12 us
  transfers between devices with their start and end apart: 71 -> 74, of which waited for: 43 -> 45; matrix products, arithmetic and copies ran while one was open for 6% -> 6% of each run, Pallas kernels for 31% -> 36%
where the time goes in v4:
time: 424 us; the launch traced here: 422 us
  Pallas kernels  171 us (40%)
  waiting for transfers between devices  122 us (29%)
  starting transfers between devices  72.9 us (17%)
  other arithmetic  26.7 us (6%)
  local copies, waits for them, and re-layouts  26.6 us (6%)
    pallas_call x31, Pallas kernels, call(): pl.pallas_call(body, name=name, out_shape=outs, grid_spec=pltpu.PrefetchS...  171 us
    ppermute x74, waiting for transfers between devices, swap(): return lax.ppermute(value, axis, [(i, i ^ bit) for i in range(count)])  122 us
    ppermute x74, starting transfers between devices, swap(): return lax.ppermute(value, axis, [(i, i ^ bit) for i in range(count)])  72.9 us
    unnamed x201, local copies, waits for them, and re-layouts  12 us
    convert_element_type x10, other arithmetic, reduce_own(): sent = (own.astype(f32) + swap(oth, 'mp', 1).astype(f32)).astype(low)  11 us
  transfers between devices with their start and end apart: 74, of which 45 were waited for; matrix products, arithmetic and copies ran while one was open for 6% of the time, Pallas kernels for 36%

profile of v4, /device:TPU:0, one launch (start us, length us, event | category | flops | bytes accessed | tf_op | source)
XLA Modules:
  0.0 422.2 jit_solution(1350117881908507022)
XLA Ops:
  28.7 4.4 %collective-permute-done.2.rest_1_ = bf16[208,768]{1,0:T(8,128)(2,1)S(1)} collective-permute-done((bf16[208,768]{1,0:T(8,128)(2,1)S(1)}, bf16[208,768]{1,0:T(8,128)(2,1)S(1)}, u32[]{:S(2)}, u32[]{:S(2)}) %collective-permute-start.2) | collective-permute-done | bytes 319520 | tf_op jit(solution)/shard_map/ppermute | solution.py:1037
  36.9 4.1 collective-permute-start.7
  44.9 9.5 %encoder_attention.1 = (bf16[2,232,768]{2,1,0:T(8,128)(2,1)}, bf16[2,232,768]{2,1,0:T(8,128)(2,1)}, bf16[4,228,768]{2,1,0:T(8,128)(2,1)}) custom-call(s32[14]{0:T(128)} %concatenate.70.meta, bf16[2,232,768]{2,1,0:T(8,128)(2,1)} %get-tuple-element.551.own_ref.base_ref.in_ref, bf16[2,232,768]{2,1,0:T(8,128)(2,1)} %get-tuple-element.307.oth_ref, ...), custom_call_target="tpu_custom_call" | custom-call | flops 1 | bytes 1 | tf_op jit(solution)/shard_map/encoder_attention/pallas_call | solution.py:140
  67.2 8.8 %collective-permute-done.13 = bf16[192,768]{1,0:T(8,128)(2,1)S(1)} collective-permute-done((bf16[192,768]{1,0:T(8,128)(2,1)S(1)}, bf16[192,768]{1,0:T(8,128)(2,1)S(1)}, u32[]{:S(2)}, u32[]{:S(2)}) %collective-permute-start.13) | collective-permute-done | bytes 294944 | tf_op jit(solution)/shard_map/ppermute | solution.py:1037
  87.2 6.6 %collective-permute-done.15.rest_7_ = bf16[192,768]{1,0:T(8,128)(2,1)S(1)} collective-permute-done((bf16[192,768]{1,0:T(8,128)(2,1)S(1)}, bf16[192,768]{1,0:T(8,128)(2,1)S(1)}, u32[]{:S(2)}, u32[]{:S(2)}) %collective-permute-start.15) | collective-permute-done | bytes 294944 | tf_op jit(solution)/shard_map/ppermute | solution.py:1037
  94.5 7.5 %encoder_feed.1 = (bf16[2,232,768]{2,1,0:T(8,128)(2,1)}, bf16[2,232,768]{2,1,0:T(8,128)(2,1)}) custom-call(s32[14]{0:T(128)} %concatenate.70.meta, bf16[2,232,768]{2,1,0:T(8,128)(2,1)} %get-tuple-element.329.own_ref, bf16[2,232,768]{2,1,0:T(8,128)(2,1)} %copy-done.8, bf16[192,768]{1,0:T(8,128)(2,1)} %copy-done.18, bf16[192,768]{1,0:T(8,128)(2,1)} %copy-done.35, ...), custom_call_target="tpu_custom_call" | custom-call | flops 1 | bytes 1 | tf_op jit(solution)/shard_map/encoder_feed/pallas_call | solution.py:140
  108.9 9.7 %collective-permute-done.21 = bf16[192,768]{1,0:T(8,128)(2,1)S(1)} collective-permute-done((bf16[192,768]{1,0:T(8,128)(2,1)S(1)}, bf16[192,768]{1,0:T(8,128)(2,1)S(1)}, u32[]{:S(2)}, u32[]{:S(2)}) %collective-permute-start.21) | collective-permute-done | bytes 294944 | tf_op jit(solution)/shard_map/ppermute | solution.py:1037
  122.3 4.1 decoder_self.1
  129.0 6.8 %collective-permute-done.24.rest_3_ = bf16[192,768]{1,0:T(8,128)(2,1)S(1)} collective-permute-done((bf16[192,768]{1,0:T(8,128)(2,1)S(1)}, bf16[192,768]{1,0:T(8,128)(2,1)S(1)}, u32[]{:S(2)}, u32[]{:S(2)}) %collective-permute-start.24) | collective-permute-done | bytes 294944 | tf_op jit(solution)/shard_map/ppermute | solution.py:1037
  146.0 5.0 %collective-permute-done.28.rest_2_.rest_6_ = bf16[384,768]{1,0:T(8,128)(2,1)S(1)} collective-permute-done((bf16[384,768]{1,0:T(8,128)(2,1)S(1)}, bf16[384,768]{1,0:T(8,128)(2,1)S(1)}, u32[]{:S(2)}, u32[]{:S(2)}) %collective-permute-start.28) | collective-permute-done | bytes 589856 | tf_op jit(solution)/shard_map/ppermute | solution.py:1037
  155.6 8.1 %decoder_cross.1 = (bf16[2,32,768]{2,1,0:T(8,128)(2,1)}, bf16[2,32,768]{2,1,0:T(8,128)(2,1)}, bf16[4,32,384]{2,1,0:T(8,128)(2,1)}, bf16[4,228,384]{2,1,0:T(8,128)(2,1)}) custom-call(s32[14]{0:T(128)} %concatenate.70.meta, bf16[2,32,768]{2,1,0:T(8,128)(2,1)} %bitcast.118, bf16[2,32,768]{2,1,0:T(8,128)(2,1)} %bitcast.120, bf16[2,232,768]{2,1,0:T(8,128)(2,1)} %copy-done, ...), custom_call_target="tpu_custom_call" | custom-call | flops 1 | bytes 1 | tf_op jit(solution)/shard_map/decoder_cross/pallas_call | solution.py:140
  176.5 7.3 %decoder_feed.1 = (bf16[2,64,768]{2,1,0:T(8,128)(2,1)}, bf16[2,64,768]{2,1,0:T(8,128)(2,1)}, bf16[4,2,96,768]{3,2,1,0:T(8,128)(2,1)}, f32[4,2,96,768]{3,2,1,0:T(8,128)}) custom-call(s32[14]{0:T(128)} %concatenate.70.meta, bf16[64,768]{1,0:T(8,128)(2,1)} %get-tuple-element.375.own_ref, bf16[64,768]{1,0:T(8,128)(2,1)} %copy-done.77, ...), custom_call_target="tpu_custom_call" | custom-call | flops 1 | bytes 1 | tf_op jit(solution)/shard_map/decoder_feed/pallas_call | solution.py:140
  189.0 4.8 %collective-permute-done.36 = bf16[2,64,768]{2,1,0:T(8,128)(2,1)S(1)} collective-permute-done((bf16[2,64,768]{2,1,0:T(8,128)(2,1)S(1)}, bf16[2,64,768]{2,1,0:T(8,128)(2,1)S(1)}, u32[]{:S(2)}, u32[]{:S(2)}) %collective-permute-start.36) | collective-permute-done | bytes 196640 | tf_op jit(solution)/shard_map/ppermute | solution.py:1037
  199.3 17.2 %decoder_cross_back.1 = (bf16[2,32,768]{2,1,0:T(8,128)(2,1)}, bf16[2,32,768]{2,1,0:T(8,128)(2,1)}, bf16[2,232,768]{2,1,0:T(8,128)(2,1)}, bf16[2,232,768]{2,1,0:T...) custom-call(s32[14]{0:T(128)} %concatenate.70.meta, bf16[2,32,768]{2,1,0:T(8,128)(2,1)} %bitcast.119, ...), custom_call_target="tpu_custom_call" | custom-call | flops 1 | bytes 1 | tf_op jit(solution)/shard_map/decoder_cross_back/pallas_call | solution.py:140
  237.5 5.8 %decoder_self_back.1 = (bf16[64,768]{1,0:T(8,128)(2,1)}, bf16[64,768]{1,0:T(8,128)(2,1)}, bf16[4,1,96,768]{3,2,1,0:T(8,128)(2,1)}, f32[4,1,96,768]{3,2,1,0:T(8,128)}) custom-call(s32[14]{0:T(128)} %concatenate.70.meta, bf16[128,768]{1,0:T(8,128)(2,1)} %bitcast.111, f32[1,768]{1,0:T(1,128)} %get-tuple-element.580.gain_ref, ...), custom_call_target="tpu_custom_call" | custom-call | flops 1 | bytes 1 | tf_op jit(solution)/shard_map/decoder_self_back/pallas_call | solution.py:140
  254.1 14.8 %encoder_feed_back.1 = (bf16[2,232,768]{2,1,0:T(8,128)(2,1)}, bf16[2,232,768]{2,1,0:T(8,128)(2,1)}, bf16[4,1,96,768]{3,2,1,0:T(8,128)(2,1)}, f32[4,1,96,768]{3,2...) custom-call(s32[14]{0:T(128)} %concatenate.70.meta, ...), custom_call_target="tpu_custom_call" | custom-call | flops 1 | bytes 1 | tf_op jit(solution)/shard_map/encoder_feed_back/pallas_call | solution.py:140
  291.7 4.3 %norm_back_mid.1 = (f32[2,232,768]{2,1,0:T(8,128)}, bf16[2,232,768]{2,1,0:T(8,128)(2,1)}, f32[1,768]{1,0:T(1,128)}) custom-call(s32[14]{0:T(128)} %concatenate.70.meta, f32[2,232,768]{2,1,0:T(8,128)} %get-tuple-element.328.in_ref, f32[1,768]{1,0:T(1,128)} %get-tuple-element.581.gain_ref, f32[2,232,768]{2,1,0:T(8,128)} %get-tuple-element.549.grad_ref, ...), custom_call_target="tpu_custom_call" | custom-call | flops 1 | bytes 1 | tf_op jit(solution)/shard_map/norm_back_mid/pallas_call | solution.py:140
  295.9 5.1 %collective-permute-done.56.rest_3_ = bf16[4,1,96,768]{3,2,1,0:T(8,128)(2,1)S(1)} collective-permute-done((bf16[4,1,96,768]{3,2,1,0:T(8,128)(2,1)S(1)}, bf16[4,1,96,768]{3,2,1,0:T(8,128)(2,1)S(1)}, u32[]{:S(2)}, u32[]{:S(2)}) %collective-permute-start.56) | collective-permute-done | bytes 589856 | tf_op jit(solution)/shard_map/ppermute | solution.py:1037
  312.3 16.6 %encoder_attention_back.1 = (bf16[2,232,768]{2,1,0:T(8,128)(2,1)}, bf16[2,232,768]{2,1,0:T(8,128)(2,1)}, bf16[4,1,96,768]{3,2,1,0:T(8,128)(2,1)}, f32[4,1,96,768]{3,2,1,0:T(8,128)}) custom-call(s32[14]{0:T(128)} %concatenate.70.meta, bf16[2,232,768]{2,1,0:T(8,128)(2,1)} %get-tuple-element.551.own_ref.base_ref.in_ref, ...), custom_call_target="tpu_custom_call" | custom-call | flops 1 | bytes 1 | tf_op jit(solution)/shard_map/encoder_attention_back/pallas_call | solution.py:140
  342.2 4.1 collect.5
  366.6 4.2 %collect.6 = (f32[2,96,768]{2,1,0:T(8,128)}, f32[2,8,768]{2,1,0:T(8,128)}) custom-call(s32[14]{0:T(128)} %concatenate.70.meta, f32[1,2,96,768]{3,2,1,0:T(8,128)} %get-tuple-element.482.rest_0_, bf16[1,2,96,768]{3,2,1,0:T(8,128)(2,1)} %copy-done.66), custom_call_target="tpu_custom_call" | custom-call | flops 1 | bytes 1 | tf_op jit(solution)/shard_map/collect/pallas_call | solution.py:140
  371.8 4.4 %collective-permute-done.67.rest_2_ = bf16[1,1,96,768]{3,2,1,0:T(8,128)(2,1)S(1)} collective-permute-done((bf16[1,1,96,768]{3,2,1,0:T(8,128)(2,1)S(1)}, bf16[1,1,96,768]{3,2,1,0:T(8,128)(2,1)S(1)}, u32[]{:S(2)}, u32[]{:S(2)}) %collective-permute-start.67) | collective-permute-done | bytes 147488 | tf_op jit(solution)/shard_map/ppermute | solution.py:1037
  405.8 7.2 %update_attention.1 = (f32[3,3,96,192]{3,2,1,0:T(8,128)}, f32[3,3,96,192]{3,2,1,0:T(8,128)}, f32[3,3,96,192]{3,2,1,0:T(8,128)}, f32[3,3,96,192]{3,2,1,0:T(8,128)...) custom-call(s32[14]{0:T(128)} %concatenate.70.meta, ...), custom_call_target="tpu_custom_call" | custom-call | flops 1 | bytes 1 | tf_op jit(solution)/shard_map/update_attention/pallas_call | solution.py:140
  412.9 5.6 %update_feed.1 = (f32[2,96,768]{2,1,0:T(8,128)}, f32[2,96,768]{2,1,0:T(8,128)}, f32[2,96,768]{2,1,0:T(8,128)}, f32[2,96,768]{2,1,0:T(8,128)}, bf16[2,96,768]{2,1...) custom-call(s32[14]{0:T(128)} %concatenate.70.meta, ...), custom_call_target="tpu_custom_call" | custom-call | flops 1 | bytes 1 | tf_op jit(solution)/shard_map/update_feed/pallas_call | solution.py:140
  (442 shorter events, 243.2 us)
Async XLA Ops:
  34.4 20.0 %collective-permute-start.6 = (bf16[192,768]{1,0:T(8,128)(2,1)S(1)}, bf16[192,768]{1,0:T(8,128)(2,1)S(1)}, u32[]{:S(2)}, u32[]{:S(2)}) collective-permute-start(bf16[192,768]{1,0:T(8,128)(2,1)S(1)} %constant_dynamic-update-slice_fusion.2.rest_0_), channel_id=1, source_target_pairs={{0,4},{4,0},{8,12},{12,8},{16,20},{20,16},{24,28},{28,24},{1,5},{5... | collective-permute-start | bytes 884744 | tf_op jit(solution)/shard_map/ppermute | solution.py:1037
  35.9 18.5 %collective-permute-start.5 = (bf16[192,768]{1,0:T(8,128)(2,1)S(1)}, bf16[192,768]{1,0:T(8,128)(2,1)S(1)}, u32[]{:S(2)}, u32[]{:S(2)}) collective-permute-start(bf16[192,768]{1,0:T(8,128)(2,1)S(1)} %constant_dynamic-update-slice_fusion.2.rest_0_), channel_id=1, source_target_pairs={{0,8},{4,12},{8,0},{12,4},{16,24},{20,28},{24,16},{28,20},{1,9},{5... | collective-permute-start | bytes 884744 | tf_op jit(solution)/shard_map/ppermute | solution.py:1037
  36.9 17.5 %collective-permute-start.7 = (bf16[96,768]{1,0:T(8,128)(2,1)S(1)}, bf16[96,768]{1,0:T(8,128)(2,1)S(1)}, u32[]{:S(2)}, u32[]{:S(2)}) collective-permute-start(bf16[96,768]{1,0:T(8,128)(2,1)S(1)} %copy-done.48), channel_id=1, source_target_pairs={{0,16},{4,20},{8,24},{12,28},{16,0},{20,4},{24,8},{28,12},{1,17},{... | collective-permute-start | bytes 442376 | tf_op jit(solution)/shard_map/ppermute | solution.py:1037
  58.2 21.5 %collective-permute-start.9 = (bf16[2,232,768]{2,1,0:T(8,128)(2,1)S(1)}, bf16[2,232,768]{2,1,0:T(8,128)(2,1)S(1)}, u32[]{:S(2)}, u32[]{:S(2)}) collective-permute-start(bf16[2,232,768]{2,1,0:T(8,128)(2,1)S(1)} %add_convert_fusion.5.first_ref), channel_id=1, source_target_pairs={{0,2},{1,3},{2,0},{3,1},{4,6},{5,7},{6,4},{7,5},{8,10},{9,11},{10,... | collective-permute-start | bytes 2138120 | tf_op jit(solution)/shard_map/ppermute | solution.py:1037
  59.8 16.2 %collective-permute-start.13 = (bf16[192,768]{1,0:T(8,128)(2,1)S(1)}, bf16[192,768]{1,0:T(8,128)(2,1)S(1)}, u32[]{:S(2)}, u32[]{:S(2)}) collective-permute-start(bf16[192,768]{1,0:T(8,128)(2,1)S(1)} %pad_maximum_fusion.5), channel_id=1, source_target_pairs={{0,16},{4,20},{8,24},{12,28},{16,0},{20,4},{24,8},{28,12},{1,17},{... | collective-permute-start | bytes 884744 | tf_op jit(solution)/shard_map/ppermute | solution.py:1037
  86.4 15.6 %collective-permute-start.17 = (bf16[192,768]{1,0:T(8,128)(2,1)S(1)}, bf16[192,768]{1,0:T(8,128)(2,1)S(1)}, u32[]{:S(2)}, u32[]{:S(2)}) collective-permute-start(bf16[192,768]{1,0:T(8,128)(2,1)S(1)} %constant_dynamic-update-slice_fusion.6.rest_0_), channel_id=1, source_target_pairs={{0,4},{4,0},{8,12},{12,8},{16,20},{20,16},{24,28},{28,24},{1,5},{5... | collective-permute-start | bytes 884744 | tf_op jit(solution)/shard_map/ppermute | solution.py:1037
  102.1 16.5 %collective-permute-start.21 = (bf16[192,768]{1,0:T(8,128)(2,1)S(1)}, bf16[192,768]{1,0:T(8,128)(2,1)S(1)}, u32[]{:S(2)}, u32[]{:S(2)}) collective-permute-start(bf16[192,768]{1,0:T(8,128)(2,1)S(1)} %copy-done.26), channel_id=1, source_target_pairs={{0,16},{4,20},{8,24},{12,28},{16,0},{20,4},{24,8},{28,12},{1,17},{... | collective-permute-start | bytes 884744 | tf_op jit(solution)/shard_map/ppermute | solution.py:1037
  105.8 30.0 %collective-permute-start.19 = (bf16[2,232,768]{2,1,0:T(8,128)(2,1)S(1)}, bf16[2,232,768]{2,1,0:T(8,128)(2,1)}, u32[]{:S(2)}, u32[]{:S(2)}) collective-permute-start(bf16[2,232,768]{2,1,0:T(8,128)(2,1)S(1)} %add_convert_fusion.4), channel_id=1, source_target_pairs={{0,2},{1,3},{2,0},{3,1},{4,6},{5,7},{6,4},{7,5},{8,10},{9,11},{10,... | collective-permute-start | bytes 2138120 | tf_op jit(solution)/shard_map/ppermute | solution.py:1037
  152.8 21.5 %collective-permute-start.34 = (bf16[384,768]{1,0:T(8,128)(2,1)S(1)}, bf16[384,768]{1,0:T(8,128)(2,1)S(1)}, u32[]{:S(2)}, u32[]{:S(2)}) collective-permute-start(bf16[384,768]{1,0:T(8,128)(2,1)S(1)} %collective-permute-done.27.rest_1_.rest_5_), channel_id=1, source_target_pairs={{0,4},{4,0},{8,12},{12,8},{16,20},{20,16},{24,28},{28,24},{1,5},{5... | collective-permute-start | bytes 1769480 | tf_op jit(solution)/shard_map/ppermute | solution.py:1037
  183.8 32.7 %collective-permute-start.38 = (bf16[4,2,96,768]{3,2,1,0:T(8,128)(2,1)}, bf16[4,2,96,768]{3,2,1,0:T(8,128)(2,1)S(1)}, u32[]{:S(2)}, u32[]{:S(2)}) collective-permute-start(bf16[4,2,96,768]{3,2,1,0:T(8,128)(2,1)} %get-tuple-element.386), channel_id=1, source_target_pairs={{0,4},{4,0},{8,12},{12,8},{16,20},{20,16},{24,28},{28,24},{1,5},{5... | collective-permute-start | bytes 3538952 | tf_op jit(solution)/shard_map/ppermute | solution.py:1037
  225.1 21.4 %collective-permute-start.42 = (bf16[2,232,768]{2,1,0:T(8,128)(2,1)S(1)}, bf16[2,232,768]{2,1,0:T(8,128)(2,1)S(1)}, u32[]{:S(2)}, u32[]{:S(2)}) collective-permute-start(bf16[2,232,768]{2,1,0:T(8,128)(2,1)S(1)} %add_convert_fusion.2), channel_id=1, source_target_pairs={{0,2},{1,3},{2,0},{3,1},{4,6},{5,7},{6,4},{7,5},{8,10},{9,11},{10,... | collective-permute-start | bytes 2138120 | tf_op jit(solution)/shard_map/ppermute | solution.py:1037
  226.6 19.1 %collective-permute-start.46 = (bf16[4,1,96,768]{3,2,1,0:T(8,128)(2,1)S(1)}, bf16[4,1,96,768]{3,2,1,0:T(8,128)(2,1)S(1)}, u32[]{:S(2)}, u32[]{:S(2)}) collective-permute-start(bf16[4,1,96,768]{3,2,1,0:T(8,128)(2,1)S(1)} %copy-done.86), channel_id=1, source_target_pairs={{0,4},{4,0},{8,12},{12,8},{16,20},{20,16},{24,28},{28,24},{1,5},{5... | collective-permute-start | bytes 1769480 | tf_op jit(solution)/shard_map/ppermute | solution.py:1037
  251.1 17.9 %collective-permute-start.49 = (bf16[4,1,96,768]{3,2,1,0:T(8,128)(2,1)S(1)}, bf16[4,1,96,768]{3,2,1,0:T(8,128)(2,1)S(1)}, u32[]{:S(2)}, u32[]{:S(2)}) collective-permute-start(bf16[4,1,96,768]{3,2,1,0:T(8,128)(2,1)S(1)} %copy-done.89), channel_id=1, source_target_pairs={{0,4},{4,0},{8,12},{12,8},{16,20},{20,16},{24,28},{28,24},{1,5},{5... | collective-permute-start | bytes 1769480 | tf_op jit(solution)/shard_map/ppermute | solution.py:1037
  251.5 17.4 %collective-permute-start.50 = (bf16[1,2,96,768]{3,2,1,0:T(8,128)(2,1)}, bf16[1,2,96,768]{3,2,1,0:T(8,128)(2,1)S(1)}, u32[]{:S(2)}, u32[]{:S(2)}) collective-permute-start(bf16[1,2,96,768]{3,2,1,0:T(8,128)(2,1)} %get-tuple-element.420), channel_id=1, source_target_pairs={{0,16},{4,20},{8,24},{12,28},{16,0},{20,4},{24,8},{28,12},{1,17},{... | collective-permute-start | bytes 884744 | tf_op jit(solution)/shard_map/ppermute | solution.py:1037
  252.5 16.4 %collective-permute-start.51 = (bf16[64,768]{1,0:T(8,128)(2,1)S(1)}, bf16[64,768]{1,0:T(8,128)(2,1)S(1)}, u32[]{:S(2)}, u32[]{:S(2)}) collective-permute-start(bf16[64,768]{1,0:T(8,128)(2,1)S(1)} %add_convert_fusion.11.first_ref), channel_id=1, source_target_pairs={{0,2},{1,3},{2,0},{3,1},{4,6},{5,7},{6,4},{7,5},{8,10},{9,11},{10,... | collective-permute-start | bytes 294920 | tf_op jit(solution)/shard_map/ppermute | solution.py:1037
  272.7 18.1 %collective-permute-start.53 = (bf16[2,232,768]{2,1,0:T(8,128)(2,1)S(1)}, bf16[2,232,768]{2,1,0:T(8,128)(2,1)S(1)}, u32[]{:S(2)}, u32[]{:S(2)}) collective-permute-start(bf16[2,232,768]{2,1,0:T(8,128)(2,1)S(1)} %add_convert_fusion.1.first_ref), channel_id=1, source_target_pairs={{0,2},{1,3},{2,0},{3,1},{4,6},{5,7},{6,4},{7,5},{8,10},{9,11},{10,... | collective-permute-start | bytes 2138120 | tf_op jit(solution)/shard_map/ppermute | solution.py:1037
  273.3 16.2 %collective-permute-start.55 = (bf16[4,1,96,768]{3,2,1,0:T(8,128)(2,1)S(1)}, bf16[4,1,96,768]{3,2,1,0:T(8,128)(2,1)S(1)}, u32[]{:S(2)}, u32[]{:S(2)}) collective-permute-start(bf16[4,1,96,768]{3,2,1,0:T(8,128)(2,1)S(1)} %copy-done.88), channel_id=1, source_target_pairs={{0,4},{4,0},{8,12},{12,8},{16,20},{20,16},{24,28},{28,24},{1,5},{5... | collective-permute-start | bytes 1769480 | tf_op jit(solution)/shard_map/ppermute | solution.py:1037
  275.0 26.1 %collective-permute-start.56 = (bf16[4,1,96,768]{3,2,1,0:T(8,128)(2,1)S(1)}, bf16[4,1,96,768]{3,2,1,0:T(8,128)(2,1)S(1)}, u32[]{:S(2)}, u32[]{:S(2)}) collective-permute-start(bf16[4,1,96,768]{3,2,1,0:T(8,128)(2,1)S(1)} %copy-done.87), channel_id=1, source_target_pairs={{0,4},{4,0},{8,12},{12,8},{16,20},{20,16},{24,28},{28,24},{1,5},{5... | collective-permute-start | bytes 1769480 | tf_op jit(solution)/shard_map/ppermute | solution.py:1037
  279.3 21.7 %collective-permute-start.57 = (bf16[2,2,96,768]{3,2,1,0:T(8,128)(2,1)}, bf16[2,2,96,768]{3,2,1,0:T(8,128)(2,1)S(1)}, u32[]{:S(2)}, u32[]{:S(2)}) collective-permute-start(bf16[2,2,96,768]{3,2,1,0:T(8,128)(2,1)} %get-tuple-element.438), channel_id=1, source_target_pairs={{0,8},{4,12},{8,0},{12,4},{16,24},{20,28},{24,16},{28,20},{1,9},{5... | collective-permute-start | bytes 1769480 | tf_op jit(solution)/shard_map/ppermute | solution.py:1037
  309.0 21.5 %collective-permute-start.60 = (bf16[2,2,96,768]{3,2,1,0:T(8,128)(2,1)}, bf16[2,2,96,768]{3,2,1,0:T(8,128)(2,1)S(1)}, u32[]{:S(2)}, u32[]{:S(2)}) collective-permute-start(bf16[2,2,96,768]{3,2,1,0:T(8,128)(2,1)} %get-tuple-element.464), channel_id=1, source_target_pairs={{0,8},{4,12},{8,0},{12,4},{16,24},{20,28},{24,16},{28,20},{1,9},{5... | collective-permute-start | bytes 1769480 | tf_op jit(solution)/shard_map/ppermute | solution.py:1037
  310.0 19.0 %collective-permute-start.61 = (bf16[1,2,96,768]{3,2,1,0:T(8,128)(2,1)S(1)}, bf16[1,2,96,768]{3,2,1,0:T(8,128)(2,1)S(1)}, u32[]{:S(2)}, u32[]{:S(2)}) collective-permute-start(bf16[1,2,96,768]{3,2,1,0:T(8,128)(2,1)S(1)} %copy-done.91), channel_id=1, source_target_pairs={{0,16},{4,20},{8,24},{12,28},{16,0},{20,4},{24,8},{28,12},{1,17},{... | collective-permute-start | bytes 884744 | tf_op jit(solution)/shard_map/ppermute | solution.py:1037
  334.3 22.2 %collective-permute-start.64 = (bf16[2,232,768]{2,1,0:T(8,128)(2,1)S(1)}, bf16[2,232,768]{2,1,0:T(8,128)(2,1)S(1)}, u32[]{:S(2)}, u32[]{:S(2)}) collective-permute-start(bf16[2,232,768]{2,1,0:T(8,128)(2,1)S(1)} %add_convert_fusion.first_ref), channel_id=1, source_target_pairs={{0,2},{1,3},{2,0},{3,1},{4,6},{5,7},{6,4},{7,5},{8,10},{9,11},{10,... | collective-permute-start | bytes 2138120 | tf_op jit(solution)/shard_map/ppermute | solution.py:1037
  340.5 15.9 %collective-permute-start.63 = (bf16[1,2,96,768]{3,2,1,0:T(8,128)(2,1)}, bf16[1,2,96,768]{3,2,1,0:T(8,128)(2,1)S(1)}, u32[]{:S(2)}, u32[]{:S(2)}) collective-permute-start(bf16[1,2,96,768]{3,2,1,0:T(8,128)(2,1)} %get-tuple-element.467), channel_id=1, source_target_pairs={{0,16},{4,20},{8,24},{12,28},{16,0},{20,4},{24,8},{28,12},{1,17},{... | collective-permute-start | bytes 884744 | tf_op jit(solution)/shard_map/ppermute | solution.py:1037
  380.8 38.9 %collective-permute-start.65 = (f32[2,232,768]{2,1,0:T(8,128)S(1)}, f32[2,232,768]{2,1,0:T(8,128)S(1)}, u32[]{:S(2)}, u32[]{:S(2)}) collective-permute-start(f32[2,232,768]{2,1,0:T(8,128)S(1)} %copy-done.20), channel_id=1, source_target_pairs={{0,1},{1,0},{2,3},{3,2},{4,5},{5,4},{6,7},{7,6},{8,9},{9,8},{10,11... | collective-permute-start | bytes 4276232 | tf_op jit(solution)/shard_map/ppermute | solution.py:1037
  (147 other events, 1284.6 us)

commit v5 on v4

--- a/solution.py
+++ b/solution.py
@@ -513,42 +513,48 @@
     n = len(flat(pieces))
     count = plan.half
     width, w3 = plan.width, 3 * plan.width
+    rows = plan.pairs * SUFFIX
+    mid = rows // 2
 
     def body(
         meta, own_ref, oth_ref, memory_own_ref, memory_oth_ref, query_ref, key_ref, grad_own_ref, grad_oth_ref, *rest
     ):
-        refs, outs, grad_refs = rest[:n], rest[n : n + 4], rest[n + 4 : -2]
-        weight, acc = rest[-2:]
+        refs, outs, grad_refs = rest[:n], rest[n : n + 4], rest[n + 4 : -4]
+        weight, acc, grad_mixed, grad_query = rest[-4:]
         step = pl.program_id(0)
 
         @pl.when(step == 0)
         def _():
             plan.assemble(meta, pieces, refs, weight)
-            acc[...] = jnp.zeros_like(acc)
-
-        normed = pick(step, count, own_ref, oth_ref, SUFFIX)
+            grad = jnp.concatenate([grad_oth_ref[...], grad_own_ref[...]], 0).reshape(rows, D)
+            grad_mixed[...] = mm(grad, weight[0, :, w3:]).astype(LOW)
+            acc[0, :, w3:] = t_mm(grad, query_ref[:, :, width:].reshape(rows, width))
+            acc[0, :, width:w3] = jnp.zeros((D, w3 - width), F32)
+
         memory = pick(step, count, memory_own_ref, memory_oth_ref, ENC_LEN)
-        grad = pick(step, count, grad_own_ref, grad_oth_ref, SUFFIX)
         allowed = key_mask(meta, plan.pairs, slot_of(plan, count, 0, step))
-        grad_mixed = mm(grad, weight[0, :, w3:]).astype(LOW)
-        acc[0, :, w3:] += t_mm(grad, query_ref[0, :, width:])
         both = key_ref[0]
-        grad_query, grad_key, grad_value = attend_heads_back(
-            plan, query_ref[0, :, :width], both[:, :width], both[:, width:], allowed, grad_mixed
+        here = pl.ds(pl.multiple_of(step * SUFFIX, SUFFIX), SUFFIX)
+        query, grad_key, grad_value = attend_heads_back(
+            plan, query_ref[step, :, :width], both[:, :width], both[:, width:], allowed, grad_mixed[here, :]
         )
+        grad_query[here, :] = query
         together = jnp.concatenate([grad_key, grad_value], 1)
-        acc[0, :, :width] += t_mm(normed, grad_query)
         acc[0, :, width:w3] += t_mm(memory, together)
-        put(step, count, outs[0], outs[1], mm_t(grad_query, weight[0, :, :width]).astype(LOW))
         put(step, count, outs[2], outs[3], mm_t(together, weight[0, :, width:w3]).astype(LOW))
 
         @pl.when(step == 2 * count - 1)
         def _():
+            normed = jnp.concatenate([oth_ref[...], own_ref[...]], 0).reshape(rows, D)
+            queries = grad_query[...]
+            acc[0, :, :width] = t_mm(normed, queries)
+            back = mm_t(queries, weight[0, :, :width]).astype(LOW)
+            outs[1][...] = back[:mid].reshape(count, SUFFIX, D)
+            outs[0][...] = back[mid:].reshape(count, SUFFIX, D)
             plan.emit(meta, acc, grad_refs)
 
-    rows, long = (SUFFIX, D), (LONG, D)
+    part, long = (count, SUFFIX, D), (LONG, D)
     shapes = plan.grad_shapes(1)
-    row_specs = [own_spec(count, 0, rows), oth_spec(count, 0, rows)]
     long_specs = [own_spec(count, 0, long), oth_spec(count, 0, long)]
     return call(
         "decoder_cross_back",
@@ -557,18 +563,22 @@
         meta,
         (own, oth, memory_own, memory_oth, kept_query, kept_key, grad_own, grad_oth, *flat(pieces)),
         [
-            *row_specs,
+            whole(part),
+            whole(part),
             *long_specs,
-            step_spec(kept_query.shape[1:]),
+            whole(kept_query.shape),
             step_spec(kept_key.shape[1:]),
-            *row_specs,
+            whole(part),
+            whole(part),
             *plan.weight_specs(pieces),
         ],
-        [jax.ShapeDtypeStruct((count,) + rows, LOW)] * 2
+        [jax.ShapeDtypeStruct(part, LOW)] * 2
         + [jax.ShapeDtypeStruct((count,) + long, LOW)] * 2
         + shapes,
-        [*row_specs, *long_specs, *[whole(item.shape) for item in shapes]],
-        plan.weight_scratch(pieces) + [pltpu.VMEM((1, D, D), F32)],
+        [whole(part), whole(part), *long_specs, *[whole(item.shape) for item in shapes]],
+        plan.weight_scratch(pieces)
+        + [pltpu.VMEM((1, D, D), F32)]
+        + [pltpu.VMEM((rows, width), LOW), pltpu.VMEM((rows, width), LOW)],
     )
 
 
@@ -719,6 +729,34 @@
 
 def apart(index):
     return index, 0
+
+
+def pack_first(plan, meta, project_in, project_out, gains):
+    width, block = plan.width, plan.block
+
+    def body(meta, in_ref, out_ref, gain_ref, packed):
+        parts = [in_ref[0, index] for index in range(3)] + [jnp.transpose(out_ref[0])]
+        packed[:block] = jnp.concatenate(parts, 1).astype(LOW)
+        rows = jnp.concatenate([gain_ref[...], jnp.zeros((3, block), F32)], 0)
+        wide = jnp.concatenate([rows, jnp.zeros((8, D - block), F32)], 1)
+        packed[block:] = pltpu.roll(wide, meta[0] * block, 1).astype(LOW)
+
+    shape = (block + 8, D)
+    return call(
+        "pack_first",
+        body,
+        (1,),
+        meta,
+        (project_in, project_out, gains),
+        [
+            pl.BlockSpec((1,) + project_in.shape[1:], lambda *_: (0, 0, 0, 0)),
+            pl.BlockSpec((1,) + project_out.shape[1:], lambda *_: (0, 0, 0)),
+            whole(gains.shape),
+        ],
+        [jax.ShapeDtypeStruct(shape, LOW)],
+        [whole(shape)],
+        [],
+    )[0]
 
 
 def one_hot(rows, offset):
@@ -1048,9 +1086,9 @@
         def step(self, chain, *sends, later=()):
             names = [(item, name) for item, name in self.sent if (name, item) not in later]
             late = [(item, name) for item, name in self.sent if (name, item) in later]
-            chain, values, self.own = hold(
-                (list(chain), [self.items[item][name] for item, name in names], self.own)
-            )
+            values = [self.items[item][name] for item, name in names]
+            if names:
+                chain, values, self.own = hold((list(chain), values, self.own))
             for (item, name), value in zip(names, values):
                 self.items[item][name] = value
             self.sent = late
@@ -1140,18 +1178,18 @@
         return [expand[layer].astype(low), contract[layer].T.astype(low)]
 
     direct = plan.direct
-    gain_full = lax.dynamic_update_slice(
-        jnp.zeros((8, D), low), norm_gains.astype(low), (0, dp_index * block)
-    )
+    place = dp_index[None].astype(jnp.int32)
+    if direct:
+        first = pack_first(plan, place, project_in, project_out, norm_gains)
+    else:
+        first = attention_block(0)
     blocks = [
-        attention_block(0),
+        first,
         *feed_block(0),
         attention_block(1),
         attention_block(2),
         jnp.concatenate(feed_block(1)),
     ]
-    if direct:
-        blocks[0] = jnp.concatenate([blocks[0], gain_full], 0)
     gather = (Gather if direct else Plain)(blocks)
     gather.step((), ("four", 0))
     gather.step((), ("far", 0), ("near", 0), ("four", 1))
@@ -1163,6 +1201,9 @@
             item[at : at + 8].astype(f32) for item in enc_att[0][0] for at in (block, height + block)
         )
     else:
+        gain_full = lax.dynamic_update_slice(
+            jnp.zeros((8, D), low), norm_gains.astype(low), (0, dp_index * block)
+        )
         gain_rows = total_dp(gain_full).astype(f32)
     gains = [gain_rows[i : i + 1] for i in range(5)]
 

time: 424 us -> 410 us (0.967)
  waiting for transfers between devices: 122 us -> 112 us
    ppermute x74, waiting for transfers between devices: 122 us -> 112 us  [swap(): return lax.ppermute(value, axis, [(i, i ^ bit) for i in range(count)])]
    pallas_call x31 -> x32, Pallas kernels: 171 us -> 170 us  [call(): pl.pallas_call(body, name=name, out_shape=outs, grid_spec=pltpu.PrefetchS...]
    unnamed x201 -> x205, local copies, waits for them, and re-layouts: 12 us -> 12.1 us
  transfers between devices with their start and end apart: 74 -> 74, of which waited for: 45 -> 42; matrix products, arithmetic and copies ran while one was open for 6% -> 7% of each run, Pallas kernels for 36% -> 37%
where the time goes in v5:
time: 410 us; the launch traced here: 408 us
  Pallas kernels  170 us (41%)
  waiting for transfers between devices  112 us (27%)
  starting transfers between devices  72.7 us (18%)
  local copies, waits for them, and re-layouts  25.9 us (6%)
  other arithmetic  23.4 us (6%)
    pallas_call x32, Pallas kernels, call(): pl.pallas_call(body, name=name, out_shape=outs, grid_spec=pltpu.PrefetchS...  170 us
    ppermute x74, waiting for transfers between devices, swap(): return lax.ppermute(value, axis, [(i, i ^ bit) for i in range(count)])  112 us
    ppermute x74, starting transfers between devices, swap(): return lax.ppermute(value, axis, [(i, i ^ bit) for i in range(count)])  72.7 us
    unnamed x205, local copies, waits for them, and re-layouts  12.1 us
    convert_element_type x10, other arithmetic, reduce_own(): sent = (own.astype(f32) + swap(oth, 'mp', 1).astype(f32)).astype(low)  10.1 us
  transfers between devices with their start and end apart: 74, of which 42 were waited for; matrix products, arithmetic and copies ran while one was open for 7% of the time, Pallas kernels for 37%

profile of v5, /device:TPU:0, one launch (start us, length us, event | category | flops | bytes accessed | tf_op | source)
XLA Modules:
  0.0 407.8 jit_solution(8383405933973840384)
XLA Ops:
  25.4 4.4 %collective-permute-done.2.rest_1_ = bf16[208,768]{1,0:T(8,128)(2,1)S(1)} collective-permute-done((bf16[208,768]{1,0:T(8,128)(2,1)S(1)}, bf16[208,768]{1,0:T(8,128)(2,1)S(1)}, u32[]{:S(2)}, u32[]{:S(2)}) %collective-permute-start.2) | collective-permute-done | bytes 319520 | tf_op jit(solution)/shard_map/ppermute | solution.py:1075
  41.6 9.5 %encoder_attention.1 = (bf16[2,232,768]{2,1,0:T(8,128)(2,1)}, bf16[2,232,768]{2,1,0:T(8,128)(2,1)}, bf16[4,228,768]{2,1,0:T(8,128)(2,1)}) custom-call(s32[14]{0:T(128)} %concatenate.63.meta, bf16[2,232,768]{2,1,0:T(8,128)(2,1)} %get-tuple-element.529.own_ref.base_ref.in_ref, bf16[2,232,768]{2,1,0:T(8,128)(2,1)} %get-tuple-element.290.oth_ref, ...), custom_call_target="tpu_custom_call" | custom-call | flops 1 | bytes 1 | tf_op jit(solution)/shard_map/encoder_attention/pallas_call | solution.py:140
  62.5 10.1 %collective-permute-done.13 = bf16[192,768]{1,0:T(8,128)(2,1)S(1)} collective-permute-done((bf16[192,768]{1,0:T(8,128)(2,1)S(1)}, bf16[192,768]{1,0:T(8,128)(2,1)S(1)}, u32[]{:S(2)}, u32[]{:S(2)}) %collective-permute-start.13) | collective-permute-done | bytes 294944 | tf_op jit(solution)/shard_map/ppermute | solution.py:1075
  81.8 7.3 %collective-permute-done.15.rest_7_ = bf16[192,768]{1,0:T(8,128)(2,1)S(1)} collective-permute-done((bf16[192,768]{1,0:T(8,128)(2,1)S(1)}, bf16[192,768]{1,0:T(8,128)(2,1)S(1)}, u32[]{:S(2)}, u32[]{:S(2)}) %collective-permute-start.15) | collective-permute-done | bytes 294944 | tf_op jit(solution)/shard_map/ppermute | solution.py:1075
  90.7 7.4 %encoder_feed.1 = (bf16[2,232,768]{2,1,0:T(8,128)(2,1)}, bf16[2,232,768]{2,1,0:T(8,128)(2,1)}) custom-call(s32[14]{0:T(128)} %concatenate.63.meta, bf16[2,232,768]{2,1,0:T(8,128)(2,1)} %get-tuple-element.312.own_ref, bf16[2,232,768]{2,1,0:T(8,128)(2,1)} %copy-done.8, bf16[192,768]{1,0:T(8,128)(2,1)} %copy-done.20, bf16[192,768]{1,0:T(8,128)(2,1)} %copy-done.37, ...), custom_call_target="tpu_custom_call" | custom-call | flops 1 | bytes 1 | tf_op jit(solution)/shard_map/encoder_feed/pallas_call | solution.py:140
  105.1 9.7 %collective-permute-done.21 = bf16[192,768]{1,0:T(8,128)(2,1)S(1)} collective-permute-done((bf16[192,768]{1,0:T(8,128)(2,1)S(1)}, bf16[192,768]{1,0:T(8,128)(2,1)S(1)}, u32[]{:S(2)}, u32[]{:S(2)}) %collective-permute-start.21) | collective-permute-done | bytes 294944 | tf_op jit(solution)/shard_map/ppermute | solution.py:1075
  120.1 4.1 %decoder_self.1 = (bf16[64,768]{1,0:T(8,128)(2,1)}, bf16[64,768]{1,0:T(8,128)(2,1)}, bf16[128,768]{1,0:T(8,128)(2,1)}) custom-call(s32[14]{0:T(128)} %concatenate.63.meta, bf16[128,768]{1,0:T(8,128)(2,1)} %bitcast.100, f32[1,768]{1,0:T(1,128)} %get-tuple-element.554.gain_ref, bf16[192,768]{1,0:T(8,128)(2,1)} %copy-done.18, bf16[192,768]{1,0:T(8,128)(2,1)} %copy-done.31, ...), custom_call_target="tpu_custom_call" | custom-call | flops 1 | bytes 1 | tf_op jit(solution)/shard_map/decoder_self/pallas_call | solution.py:140
  135.7 4.4 %collective-permute-done.28.rest_2_.rest_6_ = bf16[384,768]{1,0:T(8,128)(2,1)S(1)} collective-permute-done((bf16[384,768]{1,0:T(8,128)(2,1)S(1)}, bf16[384,768]{1,0:T(8,128)(2,1)S(1)}, u32[]{:S(2)}, u32[]{:S(2)}) %collective-permute-start.28) | collective-permute-done | bytes 589856 | tf_op jit(solution)/shard_map/ppermute | solution.py:1075
  143.6 8.1 %decoder_cross.1 = (bf16[2,32,768]{2,1,0:T(8,128)(2,1)}, bf16[2,32,768]{2,1,0:T(8,128)(2,1)}, bf16[4,32,384]{2,1,0:T(8,128)(2,1)}, bf16[4,228,384]{2,1,0:T(8,128)(2,1)}) custom-call(s32[14]{0:T(128)} %concatenate.63.meta, bf16[2,32,768]{2,1,0:T(8,128)(2,1)} %bitcast.108, bf16[2,32,768]{2,1,0:T(8,128)(2,1)} %bitcast.110, bf16[2,232,768]{2,1,0:T(8,128)(2,1)} %copy-done.1, ...), custom_call_target="tpu_custom_call" | custom-call | flops 1 | bytes 1 | tf_op jit(solution)/shard_map/decoder_cross/pallas_call | solution.py:140
  164.5 7.3 %decoder_feed.1 = (bf16[2,64,768]{2,1,0:T(8,128)(2,1)}, bf16[2,64,768]{2,1,0:T(8,128)(2,1)}, bf16[4,2,96,768]{3,2,1,0:T(8,128)(2,1)}, f32[4,2,96,768]{3,2,1,0:T(8,128)}) custom-call(s32[14]{0:T(128)} %concatenate.63.meta, bf16[64,768]{1,0:T(8,128)(2,1)} %get-tuple-element.353.own_ref, bf16[64,768]{1,0:T(8,128)(2,1)} %copy-done.81, ...), custom_call_target="tpu_custom_call" | custom-call | flops 1 | bytes 1 | tf_op jit(solution)/shard_map/decoder_feed/pallas_call | solution.py:140
  178.1 4.8 %collective-permute-done.36 = bf16[2,64,768]{2,1,0:T(8,128)(2,1)S(1)} collective-permute-done((bf16[2,64,768]{2,1,0:T(8,128)(2,1)S(1)}, bf16[2,64,768]{2,1,0:T(8,128)(2,1)S(1)}, u32[]{:S(2)}, u32[]{:S(2)}) %collective-permute-start.36) | collective-permute-done | bytes 196640 | tf_op jit(solution)/shard_map/ppermute | solution.py:1075
  188.4 14.8 %decoder_cross_back.1 = (bf16[2,32,768]{2,1,0:T(8,128)(2,1)}, bf16[2,32,768]{2,1,0:T(8,128)(2,1)}, bf16[2,232,768]{2,1,0:T(8,128)(2,1)}, bf16[2,232,768]{2,1,0:T...) custom-call(s32[14]{0:T(128)} %concatenate.63.meta, bf16[2,32,768]{2,1,0:T(8,128)(2,1)} %bitcast.109, ...), custom_call_target="tpu_custom_call" | custom-call | flops 1 | bytes 1 | tf_op jit(solution)/shard_map/decoder_cross_back/pallas_call | solution.py:140
  223.4 5.8 %decoder_self_back.1 = (bf16[64,768]{1,0:T(8,128)(2,1)}, bf16[64,768]{1,0:T(8,128)(2,1)}, bf16[4,1,96,768]{3,2,1,0:T(8,128)(2,1)}, f32[4,1,96,768]{3,2,1,0:T(8,128)}) custom-call(s32[14]{0:T(128)} %concatenate.63.meta, bf16[128,768]{1,0:T(8,128)(2,1)} %bitcast.101, f32[1,768]{1,0:T(1,128)} %get-tuple-element.554.gain_ref, ...), custom_call_target="tpu_custom_call" | custom-call | flops 1 | bytes 1 | tf_op jit(solution)/shard_map/decoder_self_back/pallas_call | solution.py:140
  240.8 14.8 %encoder_feed_back.1 = (bf16[2,232,768]{2,1,0:T(8,128)(2,1)}, bf16[2,232,768]{2,1,0:T(8,128)(2,1)}, bf16[4,1,96,768]{3,2,1,0:T(8,128)(2,1)}, f32[4,1,96,768]{3,2...) custom-call(s32[14]{0:T(128)} %concatenate.63.meta, ...), custom_call_target="tpu_custom_call" | custom-call | flops 1 | bytes 1 | tf_op jit(solution)/shard_map/encoder_feed_back/pallas_call | solution.py:140
  269.5 4.1 %collect.4 = (f32[2,96,768]{2,1,0:T(8,128)}, f32[2,8,768]{2,1,0:T(8,128)}) custom-call(s32[14]{0:T(128)} %concatenate.63.meta, f32[1,2,96,768]{3,2,1,0:T(8,128)} %get-tuple-element.401.rest_0_, bf16[1,2,96,768]{3,2,1,0:T(8,128)(2,1)} %copy-done.65), custom_call_target="tpu_custom_call" | custom-call | flops 1 | bytes 1 | tf_op jit(solution)/shard_map/collect/pallas_call | solution.py:140
  278.3 4.3 %norm_back_mid.1 = (f32[2,232,768]{2,1,0:T(8,128)}, bf16[2,232,768]{2,1,0:T(8,128)(2,1)}, f32[1,768]{1,0:T(1,128)}) custom-call(s32[14]{0:T(128)} %concatenate.63.meta, f32[2,232,768]{2,1,0:T(8,128)} %get-tuple-element.311.in_ref, f32[1,768]{1,0:T(1,128)} %get-tuple-element.555.gain_ref, f32[2,232,768]{2,1,0:T(8,128)} %get-tuple-element.527.grad_ref, ...), custom_call_target="tpu_custom_call" | custom-call | flops 1 | bytes 1 | tf_op jit(solution)/shard_map/norm_back_mid/pallas_call | solution.py:140
  282.6 5.2 %collective-permute-done.56.rest_3_ = bf16[4,1,96,768]{3,2,1,0:T(8,128)(2,1)S(1)} collective-permute-done((bf16[4,1,96,768]{3,2,1,0:T(8,128)(2,1)S(1)}, bf16[4,1,96,768]{3,2,1,0:T(8,128)(2,1)S(1)}, u32[]{:S(2)}, u32[]{:S(2)}) %collective-permute-start.56) | collective-permute-done | bytes 589856 | tf_op jit(solution)/shard_map/ppermute | solution.py:1075
  299.0 16.6 %encoder_attention_back.1 = (bf16[2,232,768]{2,1,0:T(8,128)(2,1)}, bf16[2,232,768]{2,1,0:T(8,128)(2,1)}, bf16[4,1,96,768]{3,2,1,0:T(8,128)(2,1)}, f32[4,1,96,768]{3,2,1,0:T(8,128)}) custom-call(s32[14]{0:T(128)} %concatenate.63.meta, bf16[2,232,768]{2,1,0:T(8,128)(2,1)} %get-tuple-element.529.own_ref.base_ref.in_ref, ...), custom_call_target="tpu_custom_call" | custom-call | flops 1 | bytes 1 | tf_op jit(solution)/shard_map/encoder_attention_back/pallas_call | solution.py:140
  327.9 4.1 %collect.5 = (f32[2,96,768]{2,1,0:T(8,128)}, f32[2,8,768]{2,1,0:T(8,128)}) custom-call(s32[14]{0:T(128)} %concatenate.63.meta, f32[1,2,96,768]{3,2,1,0:T(8,128)} %get-tuple-element.457.rest_0_, bf16[1,2,96,768]{3,2,1,0:T(8,128)(2,1)} %copy-done.66), custom_call_target="tpu_custom_call" | custom-call | flops 1 | bytes 1 | tf_op jit(solution)/shard_map/collect/pallas_call | solution.py:140
  332.8 4.9 %collective-permute-done.59.rest_1_ = bf16[4,1,96,768]{3,2,1,0:T(8,128)(2,1)S(1)} collective-permute-done((bf16[4,1,96,768]{3,2,1,0:T(8,128)(2,1)S(1)}, bf16[4,1,96,768]{3,2,1,0:T(8,128)(2,1)S(1)}, u32[]{:S(2)}, u32[]{:S(2)}) %collective-permute-start.59) | collective-permute-done | bytes 589856 | tf_op jit(solution)/shard_map/ppermute | solution.py:1075
  352.3 4.2 %collect.6 = (f32[2,96,768]{2,1,0:T(8,128)}, f32[2,8,768]{2,1,0:T(8,128)}) custom-call(s32[14]{0:T(128)} %concatenate.63.meta, f32[1,2,96,768]{3,2,1,0:T(8,128)} %get-tuple-element.460.rest_0_, bf16[1,2,96,768]{3,2,1,0:T(8,128)(2,1)} %copy-done.67), custom_call_target="tpu_custom_call" | custom-call | flops 1 | bytes 1 | tf_op jit(solution)/shard_map/collect/pallas_call | solution.py:140
  357.4 4.5 %collective-permute-done.67.rest_2_ = bf16[1,1,96,768]{3,2,1,0:T(8,128)(2,1)S(1)} collective-permute-done((bf16[1,1,96,768]{3,2,1,0:T(8,128)(2,1)S(1)}, bf16[1,1,96,768]{3,2,1,0:T(8,128)(2,1)S(1)}, u32[]{:S(2)}, u32[]{:S(2)}) %collective-permute-start.67) | collective-permute-done | bytes 147488 | tf_op jit(solution)/shard_map/ppermute | solution.py:1075
  391.3 7.2 %update_attention.1 = (f32[3,3,96,192]{3,2,1,0:T(8,128)}, f32[3,3,96,192]{3,2,1,0:T(8,128)}, f32[3,3,96,192]{3,2,1,0:T(8,128)}, f32[3,3,96,192]{3,2,1,0:T(8,128)...) custom-call(s32[14]{0:T(128)} %concatenate.63.meta, ...), custom_call_target="tpu_custom_call" | custom-call | flops 1 | bytes 1 | tf_op jit(solution)/shard_map/update_attention/pallas_call | solution.py:140
  398.5 5.6 %update_feed.1 = (f32[2,96,768]{2,1,0:T(8,128)}, f32[2,96,768]{2,1,0:T(8,128)}, f32[2,96,768]{2,1,0:T(8,128)}, f32[2,96,768]{2,1,0:T(8,128)}, bf16[2,96,768]{2,1...) custom-call(s32[14]{0:T(128)} %concatenate.63.meta, ...), custom_call_target="tpu_custom_call" | custom-call | flops 1 | bytes 1 | tf_op jit(solution)/shard_map/update_feed/pallas_call | solution.py:140
  (443 shorter events, 231.3 us)
Async XLA Ops:
  31.1 20.0 %collective-permute-start.6 = (bf16[192,768]{1,0:T(8,128)(2,1)S(1)}, bf16[192,768]{1,0:T(8,128)(2,1)S(1)}, u32[]{:S(2)}, u32[]{:S(2)}) collective-permute-start(bf16[192,768]{1,0:T(8,128)(2,1)S(1)} %constant_dynamic-update-slice_fusion.2.rest_0_), channel_id=1, source_target_pairs={{0,4},{4,0},{8,12},{12,8},{16,20},{20,16},{24,28},{28,24},{1,5},{5... | collective-permute-start | bytes 884744 | tf_op jit(solution)/shard_map/ppermute | solution.py:1075
  32.6 18.5 %collective-permute-start.5 = (bf16[192,768]{1,0:T(8,128)(2,1)S(1)}, bf16[192,768]{1,0:T(8,128)(2,1)S(1)}, u32[]{:S(2)}, u32[]{:S(2)}) collective-permute-start(bf16[192,768]{1,0:T(8,128)(2,1)S(1)} %constant_dynamic-update-slice_fusion.2.rest_0_), channel_id=1, source_target_pairs={{0,8},{4,12},{8,0},{12,4},{16,24},{20,28},{24,16},{28,20},{1,9},{5... | collective-permute-start | bytes 884744 | tf_op jit(solution)/shard_map/ppermute | solution.py:1075
  32.6 18.5 %collective-permute-start.7 = (bf16[96,768]{1,0:T(8,128)(2,1)S(1)}, bf16[96,768]{1,0:T(8,128)(2,1)S(1)}, u32[]{:S(2)}, u32[]{:S(2)}) collective-permute-start(bf16[96,768]{1,0:T(8,128)(2,1)S(1)} %get-tuple-element.304), channel_id=1, source_target_pairs={{0,16},{4,20},{8,24},{12,28},{16,0},{20,4},{24,8},{28,12},{1,17},{... | collective-permute-start | bytes 442376 | tf_op jit(solution)/shard_map/ppermute | solution.py:1075
  54.8 20.2 %collective-permute-start.9 = (bf16[2,232,768]{2,1,0:T(8,128)(2,1)S(1)}, bf16[2,232,768]{2,1,0:T(8,128)(2,1)S(1)}, u32[]{:S(2)}, u32[]{:S(2)}) collective-permute-start(bf16[2,232,768]{2,1,0:T(8,128)(2,1)S(1)} %add_convert_fusion.5.first_ref), channel_id=1, source_target_pairs={{0,2},{1,3},{2,0},{3,1},{4,6},{5,7},{6,4},{7,5},{8,10},{9,11},{10,... | collective-permute-start | bytes 2138120 | tf_op jit(solution)/shard_map/ppermute | solution.py:1075
  56.5 16.2 %collective-permute-start.13 = (bf16[192,768]{1,0:T(8,128)(2,1)S(1)}, bf16[192,768]{1,0:T(8,128)(2,1)S(1)}, u32[]{:S(2)}, u32[]{:S(2)}) collective-permute-start(bf16[192,768]{1,0:T(8,128)(2,1)S(1)} %pad_maximum_fusion.5), channel_id=1, source_target_pairs={{0,16},{4,20},{8,24},{12,28},{16,0},{20,4},{24,8},{28,12},{1,17},{... | collective-permute-start | bytes 884744 | tf_op jit(solution)/shard_map/ppermute | solution.py:1075
  79.9 18.2 %collective-permute-start.17 = (bf16[192,768]{1,0:T(8,128)(2,1)S(1)}, bf16[192,768]{1,0:T(8,128)(2,1)S(1)}, u32[]{:S(2)}, u32[]{:S(2)}) collective-permute-start(bf16[192,768]{1,0:T(8,128)(2,1)S(1)} %constant_dynamic-update-slice_fusion.6.rest_0_), channel_id=1, source_target_pairs={{0,4},{4,0},{8,12},{12,8},{16,20},{20,16},{24,28},{28,24},{1,5},{5... | collective-permute-start | bytes 884744 | tf_op jit(solution)/shard_map/ppermute | solution.py:1075
  81.5 16.7 %collective-permute-start.16 = (bf16[192,768]{1,0:T(8,128)(2,1)S(1)}, bf16[192,768]{1,0:T(8,128)(2,1)S(1)}, u32[]{:S(2)}, u32[]{:S(2)}) collective-permute-start(bf16[192,768]{1,0:T(8,128)(2,1)S(1)} %constant_dynamic-update-slice_fusion.6.rest_0_), channel_id=1, source_target_pairs={{0,8},{4,12},{8,0},{12,4},{16,24},{20,28},{24,16},{28,20},{1,9},{5... | collective-permute-start | bytes 884744 | tf_op jit(solution)/shard_map/ppermute | solution.py:1075
  98.3 16.5 %collective-permute-start.21 = (bf16[192,768]{1,0:T(8,128)(2,1)S(1)}, bf16[192,768]{1,0:T(8,128)(2,1)S(1)}, u32[]{:S(2)}, u32[]{:S(2)}) collective-permute-start(bf16[192,768]{1,0:T(8,128)(2,1)S(1)} %copy-done.28), channel_id=1, source_target_pairs={{0,16},{4,20},{8,24},{12,28},{16,0},{20,4},{24,8},{28,12},{1,17},{... | collective-permute-start | bytes 884744 | tf_op jit(solution)/shard_map/ppermute | solution.py:1075
  101.9 23.6 %collective-permute-start.19 = (bf16[2,232,768]{2,1,0:T(8,128)(2,1)S(1)}, bf16[2,232,768]{2,1,0:T(8,128)(2,1)}, u32[]{:S(2)}, u32[]{:S(2)}) collective-permute-start(bf16[2,232,768]{2,1,0:T(8,128)(2,1)S(1)} %add_convert_fusion.4), channel_id=1, source_target_pairs={{0,2},{1,3},{2,0},{3,1},{4,6},{5,7},{6,4},{7,5},{8,10},{9,11},{10,... | collective-permute-start | bytes 2138120 | tf_op jit(solution)/shard_map/ppermute | solution.py:1075
  140.9 21.5 %collective-permute-start.34 = (bf16[384,768]{1,0:T(8,128)(2,1)S(1)}, bf16[384,768]{1,0:T(8,128)(2,1)S(1)}, u32[]{:S(2)}, u32[]{:S(2)}) collective-permute-start(bf16[384,768]{1,0:T(8,128)(2,1)S(1)} %collective-permute-done.27.rest_1_.rest_5_), channel_id=1, source_target_pairs={{0,4},{4,0},{8,12},{12,8},{16,20},{20,16},{24,28},{28,24},{1,5},{5... | collective-permute-start | bytes 1769480 | tf_op jit(solution)/shard_map/ppermute | solution.py:1075
  171.8 31.4 %collective-permute-start.38 = (bf16[4,2,96,768]{3,2,1,0:T(8,128)(2,1)}, bf16[4,2,96,768]{3,2,1,0:T(8,128)(2,1)S(1)}, u32[]{:S(2)}, u32[]{:S(2)}) collective-permute-start(bf16[4,2,96,768]{3,2,1,0:T(8,128)(2,1)} %get-tuple-element.364), channel_id=1, source_target_pairs={{0,4},{4,0},{8,12},{12,8},{16,20},{20,16},{24,28},{28,24},{1,5},{5... | collective-permute-start | bytes 3538952 | tf_op jit(solution)/shard_map/ppermute | solution.py:1075
  211.9 20.5 %collective-permute-start.42 = (bf16[2,232,768]{2,1,0:T(8,128)(2,1)S(1)}, bf16[2,232,768]{2,1,0:T(8,128)(2,1)S(1)}, u32[]{:S(2)}, u32[]{:S(2)}) collective-permute-start(bf16[2,232,768]{2,1,0:T(8,128)(2,1)S(1)} %add_convert_fusion.2), channel_id=1, source_target_pairs={{0,2},{1,3},{2,0},{3,1},{4,6},{5,7},{6,4},{7,5},{8,10},{9,11},{10,... | collective-permute-start | bytes 2138120 | tf_op jit(solution)/shard_map/ppermute | solution.py:1075
  213.4 18.3 %collective-permute-start.46 = (bf16[4,1,96,768]{3,2,1,0:T(8,128)(2,1)S(1)}, bf16[4,1,96,768]{3,2,1,0:T(8,128)(2,1)S(1)}, u32[]{:S(2)}, u32[]{:S(2)}) collective-permute-start(bf16[4,1,96,768]{3,2,1,0:T(8,128)(2,1)S(1)} %copy-done.88), channel_id=1, source_target_pairs={{0,4},{4,0},{8,12},{12,8},{16,20},{20,16},{24,28},{28,24},{1,5},{5... | collective-permute-start | bytes 1769480 | tf_op jit(solution)/shard_map/ppermute | solution.py:1075
  237.0 18.7 %collective-permute-start.49 = (bf16[4,1,96,768]{3,2,1,0:T(8,128)(2,1)S(1)}, bf16[4,1,96,768]{3,2,1,0:T(8,128)(2,1)S(1)}, u32[]{:S(2)}, u32[]{:S(2)}) collective-permute-start(bf16[4,1,96,768]{3,2,1,0:T(8,128)(2,1)S(1)} %copy-done.91), channel_id=1, source_target_pairs={{0,4},{4,0},{8,12},{12,8},{16,20},{20,16},{24,28},{28,24},{1,5},{5... | collective-permute-start | bytes 1769480 | tf_op jit(solution)/shard_map/ppermute | solution.py:1075
  238.3 17.4 %collective-permute-start.50 = (bf16[1,2,96,768]{3,2,1,0:T(8,128)(2,1)}, bf16[1,2,96,768]{3,2,1,0:T(8,128)(2,1)S(1)}, u32[]{:S(2)}, u32[]{:S(2)}) collective-permute-start(bf16[1,2,96,768]{3,2,1,0:T(8,128)(2,1)} %get-tuple-element.398), channel_id=1, source_target_pairs={{0,16},{4,20},{8,24},{12,28},{16,0},{20,4},{24,8},{28,12},{1,17},{... | collective-permute-start | bytes 884744 | tf_op jit(solution)/shard_map/ppermute | solution.py:1075
  239.3 16.3 %collective-permute-start.51 = (bf16[64,768]{1,0:T(8,128)(2,1)S(1)}, bf16[64,768]{1,0:T(8,128)(2,1)S(1)}, u32[]{:S(2)}, u32[]{:S(2)}) collective-permute-start(bf16[64,768]{1,0:T(8,128)(2,1)S(1)} %add_convert_fusion.11.first_ref), channel_id=1, source_target_pairs={{0,2},{1,3},{2,0},{3,1},{4,6},{5,7},{6,4},{7,5},{8,10},{9,11},{10,... | collective-permute-start | bytes 294920 | tf_op jit(solution)/shard_map/ppermute | solution.py:1075
  259.4 18.1 %collective-permute-start.53 = (bf16[2,232,768]{2,1,0:T(8,128)(2,1)S(1)}, bf16[2,232,768]{2,1,0:T(8,128)(2,1)S(1)}, u32[]{:S(2)}, u32[]{:S(2)}) collective-permute-start(bf16[2,232,768]{2,1,0:T(8,128)(2,1)S(1)} %add_convert_fusion.1.first_ref), channel_id=1, source_target_pairs={{0,2},{1,3},{2,0},{3,1},{4,6},{5,7},{6,4},{7,5},{8,10},{9,11},{10,... | collective-permute-start | bytes 2138120 | tf_op jit(solution)/shard_map/ppermute | solution.py:1075
  260.1 16.2 %collective-permute-start.55 = (bf16[4,1,96,768]{3,2,1,0:T(8,128)(2,1)S(1)}, bf16[4,1,96,768]{3,2,1,0:T(8,128)(2,1)S(1)}, u32[]{:S(2)}, u32[]{:S(2)}) collective-permute-start(bf16[4,1,96,768]{3,2,1,0:T(8,128)(2,1)S(1)} %copy-done.90), channel_id=1, source_target_pairs={{0,4},{4,0},{8,12},{12,8},{16,20},{20,16},{24,28},{28,24},{1,5},{5... | collective-permute-start | bytes 1769480 | tf_op jit(solution)/shard_map/ppermute | solution.py:1075
  260.6 27.2 %collective-permute-start.56 = (bf16[4,1,96,768]{3,2,1,0:T(8,128)(2,1)S(1)}, bf16[4,1,96,768]{3,2,1,0:T(8,128)(2,1)S(1)}, u32[]{:S(2)}, u32[]{:S(2)}) collective-permute-start(bf16[4,1,96,768]{3,2,1,0:T(8,128)(2,1)S(1)} %copy-done.89), channel_id=1, source_target_pairs={{0,4},{4,0},{8,12},{12,8},{16,20},{20,16},{24,28},{28,24},{1,5},{5... | collective-permute-start | bytes 1769480 | tf_op jit(solution)/shard_map/ppermute | solution.py:1075
  266.1 21.7 %collective-permute-start.57 = (bf16[2,2,96,768]{3,2,1,0:T(8,128)(2,1)}, bf16[2,2,96,768]{3,2,1,0:T(8,128)(2,1)S(1)}, u32[]{:S(2)}, u32[]{:S(2)}) collective-permute-start(bf16[2,2,96,768]{3,2,1,0:T(8,128)(2,1)} %get-tuple-element.416), channel_id=1, source_target_pairs={{0,8},{4,12},{8,0},{12,4},{16,24},{20,28},{24,16},{28,20},{1,9},{5... | collective-permute-start | bytes 1769480 | tf_op jit(solution)/shard_map/ppermute | solution.py:1075
  295.8 21.5 %collective-permute-start.60 = (bf16[2,2,96,768]{3,2,1,0:T(8,128)(2,1)}, bf16[2,2,96,768]{3,2,1,0:T(8,128)(2,1)S(1)}, u32[]{:S(2)}, u32[]{:S(2)}) collective-permute-start(bf16[2,2,96,768]{3,2,1,0:T(8,128)(2,1)} %get-tuple-element.442), channel_id=1, source_target_pairs={{0,8},{4,12},{8,0},{12,4},{16,24},{20,28},{24,16},{28,20},{1,9},{5... | collective-permute-start | bytes 1769480 | tf_op jit(solution)/shard_map/ppermute | solution.py:1075
  296.5 19.1 %collective-permute-start.61 = (bf16[1,2,96,768]{3,2,1,0:T(8,128)(2,1)S(1)}, bf16[1,2,96,768]{3,2,1,0:T(8,128)(2,1)S(1)}, u32[]{:S(2)}, u32[]{:S(2)}) collective-permute-start(bf16[1,2,96,768]{3,2,1,0:T(8,128)(2,1)S(1)} %copy-done.93), channel_id=1, source_target_pairs={{0,16},{4,20},{8,24},{12,28},{16,0},{20,4},{24,8},{28,12},{1,17},{... | collective-permute-start | bytes 884744 | tf_op jit(solution)/shard_map/ppermute | solution.py:1075
  321.0 21.0 %collective-permute-start.64 = (bf16[2,232,768]{2,1,0:T(8,128)(2,1)S(1)}, bf16[2,232,768]{2,1,0:T(8,128)(2,1)S(1)}, u32[]{:S(2)}, u32[]{:S(2)}) collective-permute-start(bf16[2,232,768]{2,1,0:T(8,128)(2,1)S(1)} %add_convert_fusion.first_ref), channel_id=1, source_target_pairs={{0,2},{1,3},{2,0},{3,1},{4,6},{5,7},{6,4},{7,5},{8,10},{9,11},{10,... | collective-permute-start | bytes 2138120 | tf_op jit(solution)/shard_map/ppermute | solution.py:1075
  366.6 38.6 %collective-permute-start.65 = (f32[2,232,768]{2,1,0:T(8,128)S(1)}, f32[2,232,768]{2,1,0:T(8,128)S(1)}, u32[]{:S(2)}, u32[]{:S(2)}) collective-permute-start(f32[2,232,768]{2,1,0:T(8,128)S(1)} %copy-done.22), channel_id=1, source_target_pairs={{0,1},{1,0},{2,3},{3,2},{4,5},{5,4},{6,7},{7,6},{8,9},{9,8},{10,11... | collective-permute-start | bytes 4276232 | tf_op jit(solution)/shard_map/ppermute | solution.py:1075
  (149 other events, 1239.9 us)

commit v6 on v5

--- a/solution.py
+++ b/solution.py
@@ -765,10 +765,12 @@
     return (lane == row + offset).astype(F32)
 
 
-def collect(plan, meta, pieces, attention):
-    count = pieces[0].shape[-3]
-    n = len(pieces)
-    shape = pieces[0].shape[-3:]
+def collect(plan, meta, sets, attention):
+    counts = [pieces[0].shape[-3] for pieces in sets]
+    count = sum(counts)
+    shape = (count,) + sets[0][0].shape[-2:]
+    arrays = [item for pieces in sets for item in pieces]
+    n = len(arrays)
     groups = D // plan.width
 
     def body(meta, *rest):
@@ -777,11 +779,12 @@
         group = lax.broadcasted_iota(jnp.int32, (8, D), 1) // plan.width
         row = lax.broadcasted_iota(jnp.int32, (8, D), 0)
         place = one_hot(plan.block, dp_at * plan.block)
-        def one(index, _):
+        def one(first, refs, at, _):
+            index = first + at
             heads = (jnp.zeros((8, D), jnp.int32) + index) < attention
-            value = refs[0][0, index]
+            value = refs[0][0, at]
             for ref in refs[1:]:
-                value = value + ref[0, index].astype(F32)
+                value = value + ref[0, at].astype(F32)
             out[index] = value
             square = value * value
             lanes = jnp.broadcast_to(jnp.sum(square, 0, keepdims=True), (8, D))
@@ -801,15 +804,18 @@
             tile_out[index] = jnp.where(row < 4, tile, spread)
             return 0
 
-        lax.fori_loop(0, count, one, 0)
+        first, start = 0, 0
+        for pieces, size in zip(sets, counts):
+            lax.fori_loop(0, size, functools.partial(one, first, refs[start : start + len(pieces)]), 0)
+            first, start = first + size, start + len(pieces)
 
     return call(
         "collect",
         body,
         (1,),
         meta,
-        tuple(pieces),
-        [whole(item.shape) for item in pieces],
+        tuple(arrays),
+        [whole(item.shape) for item in arrays],
         [jax.ShapeDtypeStruct(shape, F32), jax.ShapeDtypeStruct((count, 8, D), F32)],
         [whole(shape), whole((count, 8, D))],
         [],
@@ -899,6 +905,10 @@
     )
 
 
+def part_spec(block, place):
+    return pl.BlockSpec((2, block, D), lambda *_: (place, 0, 0))
+
+
 def step_values(grad, scale, master, moment, average):
     stepped = grad * scale
     moment_new = MOMENTUM * moment + stepped
@@ -963,7 +973,7 @@
         (3,),
         meta,
         (rates, *grads, rows_in, cols_in, rows_out, cols_out, *state_in, *state_out),
-        [whole((8, 128)), whole((1, block, D)), whole((2, block, D))]
+        [whole((8, 128)), whole((1, block, D)), part_spec(block, 0)]
         + [spec((3, D)), spec((3, D)), whole((3, D)), whole((3, D))]
         + [spec(shape_in)] * 3
         + [spec(shape_out)] * 3,
@@ -1016,7 +1026,7 @@
             *state_up,
             *[item.transpose(0, 2, 1) for item in state_down],
         ),
-        [whole((8, 128)), *[whole((2, block, D))] * 2]
+        [whole((8, 128)), part_spec(block, 1), part_spec(block, 2)]
         + [whole((2, D)), whole((2, FF)), whole((2, FF)), whole((2, D))]
         + [state] * 6,
         outs,
@@ -1129,10 +1139,6 @@
             own = self.own[item][index * block : (index + 1) * block]
             return [lax.all_gather(own, "dp", axis=0, tiled=True)], D, 0
 
-    def scatter(parts, attention):
-        summed = lax.psum_scatter(parts[0], "dp", scatter_dimension=1, tiled=True)
-        return collect(plan, meta, [summed[None]], attention)
-
     def total(value, axes):
         for axis, count in axes:
             for bit in bits(count):
@@ -1244,10 +1250,11 @@
     sums = gather.step(reduce_own(own, oth), ("last", 2))
     enc_feed = [gather.take(1), gather.take(2)]
     enc_mid, norm_mid = add_norm(meta, "add_norm_mid", enc_own, *sums, gains[1])
+    (norm_mid,) = gather.step((norm_mid,))
     norm_mid_oth = core(norm_mid)
 
     (norm_mid_oth,) = gather.step(
-        (norm_mid_oth,), ("far", 3), ("near", 3), ("four", 5), later=(("last", 2),)
+        (norm_mid_oth,), ("far", 3), ("near", 3), ("four", 5)
     )
     own, oth = encoder_feed(plan, meta, norm_mid, norm_mid_oth, enc_feed, 0, half)
     own, oth = gather.step((own, oth), ("last", 3), ("far", 4), ("near", 4), later=(("four", 5),))
@@ -1332,21 +1339,21 @@
         )
         keep_mid, away_mid = fold(plan, meta, [keep_cross, keep_self], [more_cross, more_self], halves)
         more_mid = swap(away_mid, "dp", 2)
-        sums_self, _ = hold((sums_self, away_mid))
+        sums_self, _, more_up = hold((sums_self, away_mid, more_up))
     grad, gain_two = norm_back(meta, "norm_back_self", dec_rel[:mid], gains[2], grad, *sums_self, False)
     decoder_in_grad = absolute(triple(grad)).reshape(2 * mid, D)
     if direct:
-        sum_dec = collect(plan, meta, [keep_dec, more_dec], 0)
-        *sums, sum_dec, decoder_in_grad, more_up = hold((*sums, sum_dec, decoder_in_grad, more_up))
+        *sums, decoder_in_grad, more_mid = hold((*sums, decoder_in_grad, more_mid))
     grad_enc, enc_low, gain_one = norm_back(
         meta, "norm_back_mid", enc_mid, gains[1], grad_enc, *sums, True
     )
     if direct:
-        enc_low, more_down, more_mid = hold((enc_low, more_down, more_mid))
+        keep_mid, _ = hold((keep_mid, enc_low))
+        keep_mid, away_mid = fold(plan, meta, [keep_mid], [more_mid], halves)
+        enc_low, more_down, away_mid = hold((enc_low, more_down, away_mid))
     enc_low_oth = core(enc_low)
 
     if direct:
-        keep_mid, away_mid = fold(plan, meta, [keep_mid], [more_mid], halves)
         keep_enc, away_enc = fold(plan, meta, grads_enc[1::2], [more_up, more_down], halves)
         enc_low_oth, away_enc, away_mid = hold((enc_low_oth, away_enc, away_mid))
         more_mid = swap(away_mid, "dp", 4)
@@ -1359,29 +1366,29 @@
         own, oth, more_enc, more_mid = hold((own, oth, more_enc, more_mid))
         keep_enc, away_enc = fold(plan, meta, [keep_enc], [more_enc], halves)
         more_enc = swap(away_enc, "dp", 4)
+        own, oth, _ = hold((own, oth, away_enc))
     sums = reduce_own(own, oth)
     if direct:
-        keep_att, more_att, _, _ = hold((grads_att[1], more_att, away_enc, sums[0]))
+        keep_att, more_att, _ = hold((grads_att[1], more_att, sums[0]))
         mine, *others = fold(plan, meta, [keep_att], [more_att], apart)
-        others, more_enc, sums = hold((others, more_enc, sums))
+        others, more_enc, keep_mid = hold((others, more_enc, keep_mid))
         pieces_att = [mine] + [swap(item, "dp", 2 * (i + 1)) for i, item in enumerate(others)]
-        sum_mid = collect(plan, meta, [keep_mid, more_mid], 2)
-        sum_enc = collect(plan, meta, [keep_enc, more_enc], 0)
-        tiles = [sum_mid[1], sum_enc[1], sum_dec[1]]
+        summed, tiles = collect(plan, meta, [[keep_mid, more_mid], [keep_enc, more_enc], [keep_dec, more_dec]], 2)
+        *pieces_att, _ = hold((*pieces_att, tiles))
+        *sums, _ = hold((*sums, pieces_att[1]))
+        sum_att, tile_att = collect(plan, meta, [pieces_att], 1)
     else:
-        sum_dec = scatter(grads_dec, 0)
-        sum_mid = [jnp.concatenate(item) for item in zip(scatter(grads_cross, 1), scatter(grads_self, 1))]
-        sum_enc = scatter([jnp.concatenate(grads_enc)], 0)
-        tiles = [sum_mid[1], sum_enc[1], sum_dec[1]]
+        parts = [grads_cross[0], grads_self[0], *grads_enc, grads_dec[0]]
+        whole_sum = lax.psum_scatter(jnp.concatenate(parts), "dp", scatter_dimension=1, tiled=True)
+        summed, tiles = collect(plan, meta, [[whole_sum[None]]], 2)
+        whole_sum = lax.psum_scatter(grads_att[0], "dp", scatter_dimension=1, tiled=True)
+        sum_att, tile_att = collect(plan, meta, [[whole_sum[None]]], 1)
     grad_enc, gain_zero = norm_back(meta, "norm_back_enc", enc_own, gains[0], grad_enc, *sums, False)
-    if direct:
-        *pieces_att, _, _ = hold((*pieces_att, sum_enc[1], gain_zero))
-    sum_att = collect(plan, meta, pieces_att, 1) if direct else scatter(grads_att, 1)
     encoder_in_grad = absolute(grad_enc)[:, :ENC_LEN].reshape(pairs * ENC_LEN, D)
     gain_tile = jnp.concatenate(
         [gain_zero, gain_one, gain_two, gain_three, gain_four, jnp.zeros((3, D), f32)]
     )[None]
-    tiles = total_all(jnp.concatenate([*tiles, sum_att[1], gain_tile]))
+    tiles = total_all(jnp.concatenate([tiles, tile_att, gain_tile]))
     done = finish(
         plan,
         meta,
@@ -1403,7 +1410,7 @@
         plan,
         meta,
         rates,
-        (sum_att[0], sum_mid[0]),
+        (sum_att, summed),
         *news[:4],
         (project_in, project_in_moment, project_in_average),
         (project_out, project_out_moment, project_out_average),
@@ -1412,7 +1419,7 @@
         plan,
         meta,
         rates,
-        (sum_enc[0], sum_dec[0]),
+        (summed, summed),
         *news[4:],
         (expand, expand_moment, expand_average),
         (contract, contract_moment, contract_average),

time: 410 us -> 402 us (0.980)
  starting transfers between devices: 72.7 us -> 68.5 us
    ppermute x74, starting transfers between devices: 72.7 us -> 68.5 us  [swap(): return lax.ppermute(value, axis, [(i, i ^ bit) for i in range(count)])]
    pallas_call x32 -> x30, Pallas kernels: 170 us -> 166 us  [call(): pl.pallas_call(body, name=name, out_shape=outs, grid_spec=pltpu.PrefetchS...]
    unnamed x205 -> x201, local copies, waits for them, and re-layouts: 12.1 us -> 11.6 us
  transfers between devices with their start and end apart: 74 -> 74, of which waited for: 42 -> 43; matrix products, arithmetic and copies ran while one was open for 7% -> 7% of each run, Pallas kernels for 37% -> 37%
where the time goes in v6:
time: 402 us; the launch traced here: 400 us
  Pallas kernels  166 us (41%)
  waiting for transfers between devices  115 us (29%)
  starting transfers between devices  68.5 us (17%)
  local copies, waits for them, and re-layouts  25.3 us (6%)
  other arithmetic  21.4 us (5%)
    pallas_call x30, Pallas kernels, call(): pl.pallas_call(body, name=name, out_shape=outs, grid_spec=pltpu.PrefetchS...  166 us
    ppermute x74, waiting for transfers between devices, swap(): return lax.ppermute(value, axis, [(i, i ^ bit) for i in range(count)])  115 us
    ppermute x74, starting transfers between devices, swap(): return lax.ppermute(value, axis, [(i, i ^ bit) for i in range(count)])  68.5 us
    unnamed x201, local copies, waits for them, and re-layouts  11.6 us
    convert_element_type x10, other arithmetic, reduce_own(): sent = (own.astype(f32) + swap(oth, 'mp', 1).astype(f32)).astype(low)  9.04 us
  transfers between devices with their start and end apart: 74, of which 43 were waited for; matrix products, arithmetic and copies ran while one was open for 7% of the time, Pallas kernels for 37%

profile of v6, /device:TPU:0, one launch (start us, length us, event | category | flops | bytes accessed | tf_op | source)
XLA Modules:
  0.0 400.1 jit_solution(16159068299400559000)
XLA Ops:
  25.4 4.4 %collective-permute-done.2.rest_1_ = bf16[208,768]{1,0:T(8,128)(2,1)S(1)} collective-permute-done((bf16[208,768]{1,0:T(8,128)(2,1)S(1)}, bf16[208,768]{1,0:T(8,128)(2,1)S(1)}, u32[]{:S(2)}, u32[]{:S(2)}) %collective-permute-start.2) | collective-permute-done | bytes 319520 | tf_op jit(solution)/shard_map/ppermute | solution.py:1085
  41.6 9.5 %encoder_attention.1 = (bf16[2,232,768]{2,1,0:T(8,128)(2,1)}, bf16[2,232,768]{2,1,0:T(8,128)(2,1)}, bf16[4,228,768]{2,1,0:T(8,128)(2,1)}) custom-call(s32[14]{0:T(128)} %concatenate.63.meta, bf16[2,232,768]{2,1,0:T(8,128)(2,1)} %get-tuple-element.535.own_ref.base_ref.in_ref, bf16[2,232,768]{2,1,0:T(8,128)(2,1)} %get-tuple-element.293.oth_ref, ...), custom_call_target="tpu_custom_call" | custom-call | flops 1 | bytes 1 | tf_op jit(solution)/shard_map/encoder_attention/pallas_call | solution.py:140
  62.5 10.1 %collective-permute-done.13 = bf16[192,768]{1,0:T(8,128)(2,1)S(1)} collective-permute-done((bf16[192,768]{1,0:T(8,128)(2,1)S(1)}, bf16[192,768]{1,0:T(8,128)(2,1)S(1)}, u32[]{:S(2)}, u32[]{:S(2)}) %collective-permute-start.13) | collective-permute-done | bytes 294944 | tf_op jit(solution)/shard_map/ppermute | solution.py:1085
  85.6 7.5 %encoder_feed.1 = (bf16[2,232,768]{2,1,0:T(8,128)(2,1)}, bf16[2,232,768]{2,1,0:T(8,128)(2,1)}) custom-call(s32[14]{0:T(128)} %concatenate.63.meta, bf16[2,232,768]{2,1,0:T(8,128)(2,1)} %get-tuple-element.320.own_ref, bf16[2,232,768]{2,1,0:T(8,128)(2,1)} %copy-done.8, bf16[192,768]{1,0:T(8,128)(2,1)} %copy-done.20, bf16[192,768]{1,0:T(8,128)(2,1)} %copy-done.37, ...), custom_call_target="tpu_custom_call" | custom-call | flops 1 | bytes 1 | tf_op jit(solution)/shard_map/encoder_feed/pallas_call | solution.py:140
  101.0 9.0 %collective-permute-done.21 = bf16[192,768]{1,0:T(8,128)(2,1)S(1)} collective-permute-done((bf16[192,768]{1,0:T(8,128)(2,1)S(1)}, bf16[192,768]{1,0:T(8,128)(2,1)S(1)}, u32[]{:S(2)}, u32[]{:S(2)}) %collective-permute-start.21) | collective-permute-done | bytes 294944 | tf_op jit(solution)/shard_map/ppermute | solution.py:1085
  114.3 4.1 %decoder_self.1 = (bf16[64,768]{1,0:T(8,128)(2,1)}, bf16[64,768]{1,0:T(8,128)(2,1)}, bf16[128,768]{1,0:T(8,128)(2,1)}) custom-call(s32[14]{0:T(128)} %concatenate.63.meta, bf16[128,768]{1,0:T(8,128)(2,1)} %bitcast.99, f32[1,768]{1,0:T(1,128)} %get-tuple-element.560.gain_ref, bf16[192,768]{1,0:T(8,128)(2,1)} %copy-done.18, bf16[192,768]{1,0:T(8,128)(2,1)} %copy-done.31, ...), custom_call_target="tpu_custom_call" | custom-call | flops 1 | bytes 1 | tf_op jit(solution)/shard_map/decoder_self/pallas_call | solution.py:140
  129.9 4.4 %collective-permute-done.28.rest_2_.rest_6_ = bf16[384,768]{1,0:T(8,128)(2,1)S(1)} collective-permute-done((bf16[384,768]{1,0:T(8,128)(2,1)S(1)}, bf16[384,768]{1,0:T(8,128)(2,1)S(1)}, u32[]{:S(2)}, u32[]{:S(2)}) %collective-permute-start.28) | collective-permute-done | bytes 589856 | tf_op jit(solution)/shard_map/ppermute | solution.py:1085
  139.0 8.1 %decoder_cross.1 = (bf16[2,32,768]{2,1,0:T(8,128)(2,1)}, bf16[2,32,768]{2,1,0:T(8,128)(2,1)}, bf16[4,32,384]{2,1,0:T(8,128)(2,1)}, bf16[4,228,384]{2,1,0:T(8,128)(2,1)}) custom-call(s32[14]{0:T(128)} %concatenate.63.meta, bf16[2,32,768]{2,1,0:T(8,128)(2,1)} %bitcast.107, bf16[2,32,768]{2,1,0:T(8,128)(2,1)} %bitcast.109, bf16[2,232,768]{2,1,0:T(8,128)(2,1)} %copy-done.1, ...), custom_call_target="tpu_custom_call" | custom-call | flops 1 | bytes 1 | tf_op jit(solution)/shard_map/decoder_cross/pallas_call | solution.py:140
  150.3 4.4 %collective-permute-done.32 = bf16[2,32,768]{2,1,0:T(8,128)(2,1)S(1)} collective-permute-done((bf16[2,32,768]{2,1,0:T(8,128)(2,1)S(1)}, bf16[2,32,768]{2,1,0:T(8,128)(2,1)S(1)}, u32[]{:S(2)}, u32[]{:S(2)}) %collective-permute-start.32) | collective-permute-done | bytes 98336 | tf_op jit(solution)/shard_map/ppermute | solution.py:1085
  160.0 7.3 %decoder_feed.1 = (bf16[2,64,768]{2,1,0:T(8,128)(2,1)}, bf16[2,64,768]{2,1,0:T(8,128)(2,1)}, bf16[4,2,96,768]{3,2,1,0:T(8,128)(2,1)}, f32[4,2,96,768]{3,2,1,0:T(8,128)}) custom-call(s32[14]{0:T(128)} %concatenate.63.meta, bf16[64,768]{1,0:T(8,128)(2,1)} %get-tuple-element.360.own_ref, bf16[64,768]{1,0:T(8,128)(2,1)} %copy-done.83, ...), custom_call_target="tpu_custom_call" | custom-call | flops 1 | bytes 1 | tf_op jit(solution)/shard_map/decoder_feed/pallas_call | solution.py:140
  172.6 4.7 %collective-permute-done.36 = bf16[2,64,768]{2,1,0:T(8,128)(2,1)S(1)} collective-permute-done((bf16[2,64,768]{2,1,0:T(8,128)(2,1)S(1)}, bf16[2,64,768]{2,1,0:T(8,128)(2,1)S(1)}, u32[]{:S(2)}, u32[]{:S(2)}) %collective-permute-start.36) | collective-permute-done | bytes 196640 | tf_op jit(solution)/shard_map/ppermute | solution.py:1085
  182.8 14.8 %decoder_cross_back.1 = (bf16[2,32,768]{2,1,0:T(8,128)(2,1)}, bf16[2,32,768]{2,1,0:T(8,128)(2,1)}, bf16[2,232,768]{2,1,0:T(8,128)(2,1)}, bf16[2,232,768]{2,1,0:T...) custom-call(s32[14]{0:T(128)} %concatenate.63.meta, bf16[2,32,768]{2,1,0:T(8,128)(2,1)} %bitcast.108, ...), custom_call_target="tpu_custom_call" | custom-call | flops 1 | bytes 1 | tf_op jit(solution)/shard_map/decoder_cross_back/pallas_call | solution.py:140
  217.7 5.8 %decoder_self_back.1 = (bf16[64,768]{1,0:T(8,128)(2,1)}, bf16[64,768]{1,0:T(8,128)(2,1)}, bf16[4,1,96,768]{3,2,1,0:T(8,128)(2,1)}, f32[4,1,96,768]{3,2,1,0:T(8,128)}) custom-call(s32[14]{0:T(128)} %concatenate.63.meta, bf16[128,768]{1,0:T(8,128)(2,1)} %bitcast.100, f32[1,768]{1,0:T(1,128)} %get-tuple-element.560.gain_ref, ...), custom_call_target="tpu_custom_call" | custom-call | flops 1 | bytes 1 | tf_op jit(solution)/shard_map/decoder_self_back/pallas_call | solution.py:140
  236.0 14.8 %encoder_feed_back.1 = (bf16[2,232,768]{2,1,0:T(8,128)(2,1)}, bf16[2,232,768]{2,1,0:T(8,128)(2,1)}, bf16[4,1,96,768]{3,2,1,0:T(8,128)(2,1)}, f32[4,1,96,768]{3,2...) custom-call(s32[14]{0:T(128)} %concatenate.63.meta, ...), custom_call_target="tpu_custom_call" | custom-call | flops 1 | bytes 1 | tf_op jit(solution)/shard_map/encoder_feed_back/pallas_call | solution.py:140
  255.1 4.1 %fold.9 = (f32[2,2,96,768]{3,2,1,0:T(8,128)}, bf16[2,2,96,768]{3,2,1,0:T(8,128)(2,1)}) custom-call(s32[14]{0:T(128)} %concatenate.63.meta, f32[4,1,96,768]{3,2,1,0:T(8,128)} %get-tuple-element.415.rest_0_, f32[4,1,96,768]{3,2,1,0:T(8,128)} %get-tuple-element.416.rest_1_, bf16[4,1,96,768]{3,2,1,0:T(8,128)(2,1)} %copy-done.57, bf16[4,1,96,768]{3,2,1,0:T(8,128)(2,1)} %copy-done.60), custom_call_target="tpu_custom_call" | custom-call | flops 1 | bytes 1 | tf_op jit(solution)/shard_map/fold/pallas_call | solution.py:140
  261.3 6.0 %collective-permute-done.54.rest_2_ = bf16[4,1,96,768]{3,2,1,0:T(8,128)(2,1)S(1)} collective-permute-done((bf16[4,1,96,768]{3,2,1,0:T(8,128)(2,1)}, bf16[4,1,96,768]{3,2,1,0:T(8,128)(2,1)S(1)}, u32[]{:S(2)}, u32[]{:S(2)}) %collective-permute-start.54) | collective-permute-done | bytes 589856 | tf_op jit(solution)/shard_map/ppermute | solution.py:1085
  275.5 4.3 %norm_back_mid.1 = (f32[2,232,768]{2,1,0:T(8,128)}, bf16[2,232,768]{2,1,0:T(8,128)(2,1)}, f32[1,768]{1,0:T(1,128)}) custom-call(s32[14]{0:T(128)} %concatenate.63.meta, f32[2,232,768]{2,1,0:T(8,128)} %get-tuple-element.314.in_ref, f32[1,768]{1,0:T(1,128)} %get-tuple-element.561.gain_ref, f32[2,232,768]{2,1,0:T(8,128)} %get-tuple-element.533.grad_ref, ...), custom_call_target="tpu_custom_call" | custom-call | flops 1 | bytes 1 | tf_op jit(solution)/shard_map/norm_back_mid/pallas_call | solution.py:140
  283.8 4.1 %fold.11 = (f32[2,2,96,768]{3,2,1,0:T(8,128)}, bf16[2,2,96,768]{3,2,1,0:T(8,128)(2,1)}) custom-call(s32[14]{0:T(128)} %concatenate.63.meta, f32[4,1,96,768]{3,2,1,0:T(8,128)} %get-tuple-element.435.rest_0_, f32[4,1,96,768]{3,2,1,0:T(8,128)} %get-tuple-element.436.rest_1_, bf16[4,1,96,768]{3,2,1,0:T(8,128)(2,1)} %copy-done.58, bf16[4,1,96,768]{3,2,1,0:T(8,128)(2,1)} %copy-done.59), custom_call_target="tpu_custom_call" | custom-call | flops 1 | bytes 1 | tf_op jit(solution)/shard_map/fold/pallas_call | solution.py:140
  290.5 16.6 %encoder_attention_back.1 = (bf16[2,232,768]{2,1,0:T(8,128)(2,1)}, bf16[2,232,768]{2,1,0:T(8,128)(2,1)}, bf16[4,1,96,768]{3,2,1,0:T(8,128)(2,1)}, f32[4,1,96,768]{3,2,1,0:T(8,128)}) custom-call(s32[14]{0:T(128)} %concatenate.63.meta, bf16[2,232,768]{2,1,0:T(8,128)(2,1)} %get-tuple-element.535.own_ref.base_ref.in_ref, ...), custom_call_target="tpu_custom_call" | custom-call | flops 1 | bytes 1 | tf_op jit(solution)/shard_map/encoder_attention_back/pallas_call | solution.py:140
  318.9 10.3 %collective-permute-done.63.rest_1_ = bf16[4,1,96,768]{3,2,1,0:T(8,128)(2,1)S(1)} collective-permute-done((bf16[4,1,96,768]{3,2,1,0:T(8,128)(2,1)}, bf16[4,1,96,768]{3,2,1,0:T(8,128)(2,1)S(1)}, u32[]{:S(2)}, u32[]{:S(2)}) %collective-permute-start.63) | collective-permute-done | bytes 589856 | tf_op jit(solution)/shard_map/ppermute | solution.py:1085
  337.6 7.9 %collect.2 = (f32[6,96,768]{2,1,0:T(8,128)}, f32[6,8,768]{2,1,0:T(8,128)}) custom-call(s32[14]{0:T(128)} %concatenate.63.meta, f32[1,2,96,768]{3,2,1,0:T(8,128)} %get-tuple-element.465.rest_0_, bf16[1,2,96,768]{3,2,1,0:T(8,128)(2,1)} %copy-done.68, f32[1,2,96,768]{3,2,1,0:T(8,128)} %get-tuple-element.467.rest_2_, bf16[1,2,96,768]{3,2,1,0:T(8,128)(2,1)} %copy-done.69, ...), custom_call_target="tpu_custom_call" | custom-call | flops 1 | bytes 1 | tf_op jit(solution)/shard_map/collect/pallas_call | solution.py:140
  360.7 4.2 %collective-permute-done.70 = bf16[8,8,768]{2,1,0:T(8,128)(2,1)S(1)} collective-permute-done((bf16[8,8,768]{2,1,0:T(8,128)(2,1)S(1)}, bf16[8,8,768]{2,1,0:T(8,128)(2,1)S(1)}, u32[]{:S(2)}, u32[]{:S(2)}) %collective-permute-start.70) | collective-permute-done | bytes 98336 | tf_op jit(solution)/shard_map/ppermute | solution.py:1085
  383.5 7.2 %update_attention.1 = (f32[3,3,96,192]{3,2,1,0:T(8,128)}, f32[3,3,96,192]{3,2,1,0:T(8,128)}, f32[3,3,96,192]{3,2,1,0:T(8,128)}, f32[3,3,96,192]{3,2,1,0:T(8,128)...) custom-call(s32[14]{0:T(128)} %concatenate.63.meta, ...), custom_call_target="tpu_custom_call" | custom-call | flops 1 | bytes 1 | tf_op jit(solution)/shard_map/update_attention/pallas_call | solution.py:140
  390.7 5.7 %update_feed.1 = (f32[2,96,768]{2,1,0:T(8,128)}, f32[2,96,768]{2,1,0:T(8,128)}, f32[2,96,768]{2,1,0:T(8,128)}, f32[2,96,768]{2,1,0:T(8,128)}, bf16[2,96,768]{2,1...) custom-call(s32[14]{0:T(128)} %concatenate.63.meta, ...), custom_call_target="tpu_custom_call" | custom-call | flops 1 | bytes 1 | tf_op jit(solution)/shard_map/update_feed/pallas_call | solution.py:140
  (435 shorter events, 217.7 us)
Async XLA Ops:
  31.0 20.0 %collective-permute-start.6 = (bf16[192,768]{1,0:T(8,128)(2,1)S(1)}, bf16[192,768]{1,0:T(8,128)(2,1)S(1)}, u32[]{:S(2)}, u32[]{:S(2)}) collective-permute-start(bf16[192,768]{1,0:T(8,128)(2,1)S(1)} %constant_dynamic-update-slice_fusion.2.rest_0_), channel_id=1, source_target_pairs={{0,4},{4,0},{8,12},{12,8},{16,20},{20,16},{24,28},{28,24},{1,5},{5... | collective-permute-start | bytes 884744 | tf_op jit(solution)/shard_map/ppermute | solution.py:1085
  32.6 18.5 %collective-permute-start.5 = (bf16[192,768]{1,0:T(8,128)(2,1)S(1)}, bf16[192,768]{1,0:T(8,128)(2,1)S(1)}, u32[]{:S(2)}, u32[]{:S(2)}) collective-permute-start(bf16[192,768]{1,0:T(8,128)(2,1)S(1)} %constant_dynamic-update-slice_fusion.2.rest_0_), channel_id=1, source_target_pairs={{0,8},{4,12},{8,0},{12,4},{16,24},{20,28},{24,16},{28,20},{1,9},{5... | collective-permute-start | bytes 884744 | tf_op jit(solution)/shard_map/ppermute | solution.py:1085
  32.6 18.5 %collective-permute-start.7 = (bf16[96,768]{1,0:T(8,128)(2,1)S(1)}, bf16[96,768]{1,0:T(8,128)(2,1)S(1)}, u32[]{:S(2)}, u32[]{:S(2)}) collective-permute-start(bf16[96,768]{1,0:T(8,128)(2,1)S(1)} %get-tuple-element.307), channel_id=1, source_target_pairs={{0,16},{4,20},{8,24},{12,28},{16,0},{20,4},{24,8},{28,12},{1,17},{... | collective-permute-start | bytes 442376 | tf_op jit(solution)/shard_map/ppermute | solution.py:1085
  54.9 20.2 %collective-permute-start.9 = (bf16[2,232,768]{2,1,0:T(8,128)(2,1)S(1)}, bf16[2,232,768]{2,1,0:T(8,128)(2,1)S(1)}, u32[]{:S(2)}, u32[]{:S(2)}) collective-permute-start(bf16[2,232,768]{2,1,0:T(8,128)(2,1)S(1)} %add_convert_fusion.5.first_ref), channel_id=1, source_target_pairs={{0,2},{1,3},{2,0},{3,1},{4,6},{5,7},{6,4},{7,5},{8,10},{9,11},{10,... | collective-permute-start | bytes 2138120 | tf_op jit(solution)/shard_map/ppermute | solution.py:1085
  56.5 16.2 %collective-permute-start.13 = (bf16[192,768]{1,0:T(8,128)(2,1)S(1)}, bf16[192,768]{1,0:T(8,128)(2,1)S(1)}, u32[]{:S(2)}, u32[]{:S(2)}) collective-permute-start(bf16[192,768]{1,0:T(8,128)(2,1)S(1)} %pad_maximum_fusion.5), channel_id=1, source_target_pairs={{0,16},{4,20},{8,24},{12,28},{16,0},{20,4},{24,8},{28,12},{1,17},{... | collective-permute-start | bytes 884744 | tf_op jit(solution)/shard_map/ppermute | solution.py:1085
  93.3 16.6 %collective-permute-start.21 = (bf16[192,768]{1,0:T(8,128)(2,1)S(1)}, bf16[192,768]{1,0:T(8,128)(2,1)S(1)}, u32[]{:S(2)}, u32[]{:S(2)}) collective-permute-start(bf16[192,768]{1,0:T(8,128)(2,1)S(1)} %copy-done.28), channel_id=1, source_target_pairs={{0,16},{4,20},{8,24},{12,28},{16,0},{20,4},{24,8},{28,12},{1,17},{... | collective-permute-start | bytes 884744 | tf_op jit(solution)/shard_map/ppermute | solution.py:1085
  96.9 24.2 %collective-permute-start.19 = (bf16[2,232,768]{2,1,0:T(8,128)(2,1)S(1)}, bf16[2,232,768]{2,1,0:T(8,128)(2,1)}, u32[]{:S(2)}, u32[]{:S(2)}) collective-permute-start(bf16[2,232,768]{2,1,0:T(8,128)(2,1)S(1)} %add_convert_fusion.4), channel_id=1, source_target_pairs={{0,2},{1,3},{2,0},{3,1},{4,6},{5,7},{6,4},{7,5},{8,10},{9,11},{10,... | collective-permute-start | bytes 2138120 | tf_op jit(solution)/shard_map/ppermute | solution.py:1085
  136.3 21.5 %collective-permute-start.34 = (bf16[384,768]{1,0:T(8,128)(2,1)S(1)}, bf16[384,768]{1,0:T(8,128)(2,1)S(1)}, u32[]{:S(2)}, u32[]{:S(2)}) collective-permute-start(bf16[384,768]{1,0:T(8,128)(2,1)S(1)} %collective-permute-done.27.rest_1_.rest_5_), channel_id=1, source_target_pairs={{0,4},{4,0},{8,12},{12,8},{16,20},{20,16},{24,28},{28,24},{1,5},{5... | collective-permute-start | bytes 1769480 | tf_op jit(solution)/shard_map/ppermute | solution.py:1085
  167.3 30.3 %collective-permute-start.38 = (bf16[4,2,96,768]{3,2,1,0:T(8,128)(2,1)}, bf16[4,2,96,768]{3,2,1,0:T(8,128)(2,1)S(1)}, u32[]{:S(2)}, u32[]{:S(2)}) collective-permute-start(bf16[4,2,96,768]{3,2,1,0:T(8,128)(2,1)} %get-tuple-element.371), channel_id=1, source_target_pairs={{0,4},{4,0},{8,12},{12,8},{16,20},{20,16},{24,28},{28,24},{1,5},{5... | collective-permute-start | bytes 3538952 | tf_op jit(solution)/shard_map/ppermute | solution.py:1085
  206.2 20.5 %collective-permute-start.42 = (bf16[2,232,768]{2,1,0:T(8,128)(2,1)S(1)}, bf16[2,232,768]{2,1,0:T(8,128)(2,1)S(1)}, u32[]{:S(2)}, u32[]{:S(2)}) collective-permute-start(bf16[2,232,768]{2,1,0:T(8,128)(2,1)S(1)} %add_convert_fusion.2), channel_id=1, source_target_pairs={{0,2},{1,3},{2,0},{3,1},{4,6},{5,7},{6,4},{7,5},{8,10},{9,11},{10,... | collective-permute-start | bytes 2138120 | tf_op jit(solution)/shard_map/ppermute | solution.py:1085
  207.9 18.1 %collective-permute-start.46 = (bf16[4,1,96,768]{3,2,1,0:T(8,128)(2,1)S(1)}, bf16[4,1,96,768]{3,2,1,0:T(8,128)(2,1)S(1)}, u32[]{:S(2)}, u32[]{:S(2)}) collective-permute-start(bf16[4,1,96,768]{3,2,1,0:T(8,128)(2,1)S(1)} %copy-done.90), channel_id=1, source_target_pairs={{0,4},{4,0},{8,12},{12,8},{16,20},{20,16},{24,28},{28,24},{1,5},{5... | collective-permute-start | bytes 1769480 | tf_op jit(solution)/shard_map/ppermute | solution.py:1085
  231.2 19.6 %collective-permute-start.49 = (bf16[4,1,96,768]{3,2,1,0:T(8,128)(2,1)S(1)}, bf16[4,1,96,768]{3,2,1,0:T(8,128)(2,1)S(1)}, u32[]{:S(2)}, u32[]{:S(2)}) collective-permute-start(bf16[4,1,96,768]{3,2,1,0:T(8,128)(2,1)S(1)} %copy-done.92), channel_id=1, source_target_pairs={{0,4},{4,0},{8,12},{12,8},{16,20},{20,16},{24,28},{28,24},{1,5},{5... | collective-permute-start | bytes 1769480 | tf_op jit(solution)/shard_map/ppermute | solution.py:1085
  232.8 18.0 %collective-permute-start.50 = (bf16[1,2,96,768]{3,2,1,0:T(8,128)(2,1)}, bf16[1,2,96,768]{3,2,1,0:T(8,128)(2,1)S(1)}, u32[]{:S(2)}, u32[]{:S(2)}) collective-permute-start(bf16[1,2,96,768]{3,2,1,0:T(8,128)(2,1)} %get-tuple-element.405), channel_id=1, source_target_pairs={{0,16},{4,20},{8,24},{12,28},{16,0},{20,4},{24,8},{28,12},{1,17},{... | collective-permute-start | bytes 884744 | tf_op jit(solution)/shard_map/ppermute | solution.py:1085
  234.4 16.3 %collective-permute-start.51 = (bf16[64,768]{1,0:T(8,128)(2,1)S(1)}, bf16[64,768]{1,0:T(8,128)(2,1)S(1)}, u32[]{:S(2)}, u32[]{:S(2)}) collective-permute-start(bf16[64,768]{1,0:T(8,128)(2,1)S(1)} %add_convert_fusion.11.first_ref), channel_id=1, source_target_pairs={{0,2},{1,3},{2,0},{3,1},{4,6},{5,7},{6,4},{7,5},{8,10},{9,11},{10,... | collective-permute-start | bytes 294920 | tf_op jit(solution)/shard_map/ppermute | solution.py:1085
  250.9 16.4 %collective-permute-start.54 = (bf16[4,1,96,768]{3,2,1,0:T(8,128)(2,1)}, bf16[4,1,96,768]{3,2,1,0:T(8,128)(2,1)S(1)}, u32[]{:S(2)}, u32[]{:S(2)}) collective-permute-start(bf16[4,1,96,768]{3,2,1,0:T(8,128)(2,1)} %get-tuple-element.420), channel_id=1, source_target_pairs={{0,4},{4,0},{8,12},{12,8},{16,20},{20,16},{24,28},{28,24},{1,5},{5... | collective-permute-start | bytes 1769480 | tf_op jit(solution)/shard_map/ppermute | solution.py:1085
  254.6 20.0 %collective-permute-start.53 = (bf16[2,232,768]{2,1,0:T(8,128)(2,1)S(1)}, bf16[2,232,768]{2,1,0:T(8,128)(2,1)S(1)}, u32[]{:S(2)}, u32[]{:S(2)}) collective-permute-start(bf16[2,232,768]{2,1,0:T(8,128)(2,1)S(1)} %add_convert_fusion.1.first_ref), channel_id=1, source_target_pairs={{0,2},{1,3},{2,0},{3,1},{4,6},{5,7},{6,4},{7,5},{8,10},{9,11},{10,... | collective-permute-start | bytes 2138120 | tf_op jit(solution)/shard_map/ppermute | solution.py:1085
  259.2 15.4 %collective-permute-start.56 = (bf16[2,2,96,768]{3,2,1,0:T(8,128)(2,1)}, bf16[2,2,96,768]{3,2,1,0:T(8,128)(2,1)S(1)}, u32[]{:S(2)}, u32[]{:S(2)}) collective-permute-start(bf16[2,2,96,768]{3,2,1,0:T(8,128)(2,1)} %get-tuple-element.419), channel_id=1, source_target_pairs={{0,8},{4,12},{8,0},{12,4},{16,24},{20,28},{24,16},{28,20},{1,9},{5... | collective-permute-start | bytes 1769480 | tf_op jit(solution)/shard_map/ppermute | solution.py:1085
  260.0 22.9 %collective-permute-start.57 = (bf16[4,1,96,768]{3,2,1,0:T(8,128)(2,1)S(1)}, bf16[4,1,96,768]{3,2,1,0:T(8,128)(2,1)S(1)}, u32[]{:S(2)}, u32[]{:S(2)}) collective-permute-start(bf16[4,1,96,768]{3,2,1,0:T(8,128)(2,1)S(1)} %copy-done.91), channel_id=1, source_target_pairs={{0,4},{4,0},{8,12},{12,8},{16,20},{20,16},{24,28},{28,24},{1,5},{5... | collective-permute-start | bytes 1769480 | tf_op jit(solution)/shard_map/ppermute | solution.py:1085
  287.9 21.6 %collective-permute-start.59 = (bf16[2,2,96,768]{3,2,1,0:T(8,128)(2,1)}, bf16[2,2,96,768]{3,2,1,0:T(8,128)(2,1)S(1)}, u32[]{:S(2)}, u32[]{:S(2)}) collective-permute-start(bf16[2,2,96,768]{3,2,1,0:T(8,128)(2,1)} %get-tuple-element.444), channel_id=1, source_target_pairs={{0,8},{4,12},{8,0},{12,4},{16,24},{20,28},{24,16},{28,20},{1,9},{5... | collective-permute-start | bytes 1769480 | tf_op jit(solution)/shard_map/ppermute | solution.py:1085
  288.6 19.1 %collective-permute-start.60 = (bf16[1,2,96,768]{3,2,1,0:T(8,128)(2,1)S(1)}, bf16[1,2,96,768]{3,2,1,0:T(8,128)(2,1)S(1)}, u32[]{:S(2)}, u32[]{:S(2)}) collective-permute-start(bf16[1,2,96,768]{3,2,1,0:T(8,128)(2,1)S(1)} %copy-done.93), channel_id=1, source_target_pairs={{0,16},{4,20},{8,24},{12,28},{16,0},{20,4},{24,8},{28,12},{1,17},{... | collective-permute-start | bytes 884744 | tf_op jit(solution)/shard_map/ppermute | solution.py:1085
  313.3 15.9 %collective-permute-start.63 = (bf16[4,1,96,768]{3,2,1,0:T(8,128)(2,1)}, bf16[4,1,96,768]{3,2,1,0:T(8,128)(2,1)S(1)}, u32[]{:S(2)}, u32[]{:S(2)}) collective-permute-start(bf16[4,1,96,768]{3,2,1,0:T(8,128)(2,1)} %get-tuple-element.454), channel_id=1, source_target_pairs={{0,4},{4,0},{8,12},{12,8},{16,20},{20,16},{24,28},{28,24},{1,5},{5... | collective-permute-start | bytes 1769480 | tf_op jit(solution)/shard_map/ppermute | solution.py:1085
  315.7 37.3 %collective-permute-start.62 = (bf16[2,232,768]{2,1,0:T(8,128)(2,1)S(1)}, bf16[2,232,768]{2,1,0:T(8,128)(2,1)S(1)}, u32[]{:S(2)}, u32[]{:S(2)}) collective-permute-start(bf16[2,232,768]{2,1,0:T(8,128)(2,1)S(1)} %add_convert_fusion.first_ref), channel_id=1, source_target_pairs={{0,2},{1,3},{2,0},{3,1},{4,6},{5,7},{6,4},{7,5},{8,10},{9,11},{10,... | collective-permute-start | bytes 2138120 | tf_op jit(solution)/shard_map/ppermute | solution.py:1085
  317.3 15.8 %collective-permute-start.64 = (bf16[1,2,96,768]{3,2,1,0:T(8,128)(2,1)S(1)}, bf16[1,2,96,768]{3,2,1,0:T(8,128)(2,1)S(1)}, u32[]{:S(2)}, u32[]{:S(2)}) collective-permute-start(bf16[1,2,96,768]{3,2,1,0:T(8,128)(2,1)S(1)} %copy-done.94), channel_id=1, source_target_pairs={{0,16},{4,20},{8,24},{12,28},{16,0},{20,4},{24,8},{28,12},{1,17},{... | collective-permute-start | bytes 884744 | tf_op jit(solution)/shard_map/ppermute | solution.py:1085
  358.6 39.0 %collective-permute-start.68 = (f32[2,232,768]{2,1,0:T(8,128)}, f32[2,232,768]{2,1,0:T(8,128)S(1)}, u32[]{:S(2)}, u32[]{:S(2)}) collective-permute-start(f32[2,232,768]{2,1,0:T(8,128)} %get-tuple-element.475), channel_id=1, source_target_pairs={{0,1},{1,0},{2,3},{3,2},{4,5},{5,4},{6,7},{7,6},{8,9},{9,8},{10,11... | collective-permute-start | bytes 4276232 | tf_op jit(solution)/shard_map/ppermute | solution.py:1085
  (147 other events, 1215.7 us)

commit v7 on v6

--- a/solution.py
+++ b/solution.py
@@ -155,8 +155,9 @@
     )(meta, *inputs)
 
 
-def key_mask(meta, pairs, slot):
-    place = lax.broadcasted_iota(jnp.int32, (1, ENC_LEN), 1)
+def key_mask(meta, pairs, slot, turned=False):
+    shape = (ENC_LEN, 1) if turned else (1, ENC_LEN)
+    place = lax.broadcasted_iota(jnp.int32, shape, 1 - turned)
     image, prefix = meta[1 + slot], meta[1 + pairs + slot]
     return (place < image * PATCHES) | ((place >= PATCHES) & (place < PATCHES + prefix))
 
@@ -185,6 +186,23 @@
     return tuple(jnp.concatenate(item, 1) for item in grads)
 
 
+def attend_heads_turned(plan, queries, keys, values, allowed, grad_mixed):
+    grads = ([], [], [])
+    for head in range(plan.heads):
+        cut = slice(head * HEAD_DIM, (head + 1) * HEAD_DIM)
+        query, key, value, grad = queries[:, cut], keys[:, cut], values[:, cut], grad_mixed[:, cut]
+        scores = jnp.where(allowed, mm_t(key, query) * 0.125, MASKED)
+        expons = jnp.exp(scores - jnp.max(scores, 0, keepdims=True))
+        probs = expons / jnp.sum(expons, 0, keepdims=True)
+        grad_probs = mm_t(value, grad)
+        inner = jnp.sum(grad_probs * probs, 0, keepdims=True)
+        grad_scores = (probs * (grad_probs - inner)).astype(LOW)
+        grads[0].append((t_mm(grad_scores, key) * 0.125).astype(LOW))
+        grads[1].append((mm(grad_scores, query) * 0.125).astype(LOW))
+        grads[2].append(mm(probs.astype(LOW), grad).astype(LOW))
+    return tuple(jnp.concatenate(item, 1) for item in grads)
+
+
 def slot_of(plan, count, base, step):
     return jnp.where(step < count, plan.half + base + step, base + step - count)
 
@@ -260,11 +278,11 @@
         value = pick(step, count, own_ref, oth_ref, ENC_LEN).astype(F32)
         normed = (value * rms_scale(value) * gain_ref[...]).astype(LOW)
         grad = pick(step, count, grad_own_ref, grad_oth_ref, ENC_LEN)
-        allowed = key_mask(meta, plan.pairs, slot_of(plan, count, 0, step))
+        allowed = key_mask(meta, plan.pairs, slot_of(plan, count, 0, step), True)
         grad_mixed = mm(grad, weight[0, :, w3:]).astype(LOW)
         acc[0, :, w3:] += t_mm(grad, kept_ref[0, :, w3:])
         joined = kept_ref[0, :, :w3]
-        grads = attend_heads_back(
+        grads = attend_heads_turned(
             plan, joined[:, :width], joined[:, width : 2 * width], joined[:, 2 * width :], allowed, grad_mixed
         )
         together = jnp.concatenate(grads, 1)
@@ -364,10 +382,10 @@
     )
 
 
-def self_mask(plan, meta):
+def self_mask(plan, meta, turned=False):
     rows = plan.pairs * SUFFIX
-    query = lax.broadcasted_iota(jnp.int32, (rows, rows), 0)
-    key = lax.broadcasted_iota(jnp.int32, (rows, rows), 1)
+    query = lax.broadcasted_iota(jnp.int32, (rows, rows), int(turned))
+    key = lax.broadcasted_iota(jnp.int32, (rows, rows), 1 - turned)
     pair = key // SUFFIX
     limit = jnp.zeros_like(key)
     for slot in range(plan.pairs):
@@ -425,12 +443,12 @@
         grad_mixed = mm(grad, weight[0, :, w3:]).astype(LOW)
         acc[0, :, w3:] = t_mm(grad, kept_ref[:, w3:])
         joined = kept_ref[:, :w3]
-        grads = attend_heads_back(
+        grads = attend_heads_turned(
             plan,
             joined[:, :width],
             joined[:, width : 2 * width],
             joined[:, 2 * width :],
-            self_mask(plan, meta),
+            self_mask(plan, meta, True),
             grad_mixed,
         )
         together = jnp.concatenate(grads, 1)
@@ -1259,13 +1277,12 @@
     own, oth = encoder_feed(plan, meta, norm_mid, norm_mid_oth, enc_feed, 0, half)
     own, oth = gather.step((own, oth), ("last", 3), ("far", 4), ("near", 4), later=(("four", 5),))
     sums = reduce_own(own, oth)
-    (dec_rel,) = gather.step((dec_rel,), ("last", 4), later=(("last", 3),))
+    (dec_rel,) = gather.step((dec_rel,), ("last", 4), ("far", 5), ("near", 5), later=(("last", 3),))
 
     self_att = [gather.take(3)]
     own, oth, kept_self = decoder_self(plan, meta, dec_rel, gains[2], self_att)
-    sums = gather.step(sums)
+    sums = gather.step(sums, later=(("far", 5), ("near", 5)))
     sums_self = reduce_own(own, oth, sums)
-    gather.step((sums_self[0],), ("far", 5), ("near", 5))
     cross_att = [gather.take(4)]
     memory = (enc_mid + (sums[0].astype(f32) + sums[1].astype(f32))).astype(low)
     dec_one, norm_cross = add_norm(meta, "add_norm_cross", dec_rel[:mid], *sums_self, gains[3])
@@ -1297,7 +1314,7 @@
         own, oth, own_long, oth_long, more_dec = hold((own, oth, own_long, oth_long, more_dec))
         more_cross = swap(grads_cross[0], "dp", 1)
     sums = reduce_own(own, oth)
-    sums_enc = reduce_own(own_long, oth_long, sums)
+    sums_enc = reduce_own(own_long, oth_long, sums[0])
     if direct:
         keep, more_dec, _ = hold((grads_dec[1], more_dec, sums[0]))
         keep_dec, away_dec = fold(plan, meta, [keep], [more_dec], halves)

time: 402 us -> 397 us (0.988)
  waiting for transfers between devices: 115 us -> 108 us
  starting transfers between devices: 68.5 us -> 72.6 us
    ppermute x74, waiting for transfers between devices: 115 us -> 108 us  [swap(): return lax.ppermute(value, axis, [(i, i ^ bit) for i in range(count)])]
    ppermute x74, starting transfers between devices: 68.5 us -> 72.6 us  [swap(): return lax.ppermute(value, axis, [(i, i ^ bit) for i in range(count)])]
  transfers between devices with their start and end apart: 74 -> 74, of which waited for: 43 -> 41; matrix products, arithmetic and copies ran while one was open for 7% -> 7% of each run, Pallas kernels for 37% -> 37%
where the time goes in v7:
time: 397 us; the launch traced here: 395 us
  Pallas kernels  164 us (41%)
  waiting for transfers between devices  108 us (27%)
  starting transfers between devices  72.6 us (18%)
  local copies, waits for them, and re-layouts  25.6 us (6%)
  other arithmetic  21.4 us (5%)
    pallas_call x30, Pallas kernels, call(): pl.pallas_call(body, name=name, out_shape=outs, grid_spec=pltpu.PrefetchS...  164 us
    ppermute x74, waiting for transfers between devices, swap(): return lax.ppermute(value, axis, [(i, i ^ bit) for i in range(count)])  108 us
    ppermute x74, starting transfers between devices, swap(): return lax.ppermute(value, axis, [(i, i ^ bit) for i in range(count)])  72.6 us
    unnamed x201, local copies, waits for them, and re-layouts  11.8 us
    convert_element_type x10, other arithmetic, reduce_own(): sent = (own.astype(f32) + swap(oth, 'mp', 1).astype(f32)).astype(low)  9.04 us
  transfers between devices with their start and end apart: 74, of which 41 were waited for; matrix products, arithmetic and copies ran while one was open for 7% of the time, Pallas kernels for 37%

profile of v7, /device:TPU:0, one launch (start us, length us, event | category | flops | bytes accessed | tf_op | source)
XLA Modules:
  0.0 395.1 jit_solution(6914298687187333825)
XLA Ops:
  2.7 4.0 %collective-permute-start = (bf16[104,768]{1,0:T(8,128)(2,1)}, bf16[104,768]{1,0:T(8,128)(2,1)}, u32[]{:S(2)}, u32[]{:S(2)}) collective-permute-start(bf16[104,768]{1,0:T(8,128)(2,1)} %pack_first.1), channel_id=1, source_target_pairs={{0,16},{4,20},{8,24},{12,28},{16,0},{20,4},{24,8},{28,12},{1,17},{... | collective-permute-start | bytes 479240 | tf_op jit(solution)/shard_map/ppermute | solution.py:1103
  25.4 4.4 %collective-permute-done.2.rest_1_ = bf16[208,768]{1,0:T(8,128)(2,1)S(1)} collective-permute-done((bf16[208,768]{1,0:T(8,128)(2,1)S(1)}, bf16[208,768]{1,0:T(8,128)(2,1)S(1)}, u32[]{:S(2)}, u32[]{:S(2)}) %collective-permute-start.2) | collective-permute-done | bytes 319520 | tf_op jit(solution)/shard_map/ppermute | solution.py:1103
  41.6 9.5 %encoder_attention.1 = (bf16[2,232,768]{2,1,0:T(8,128)(2,1)}, bf16[2,232,768]{2,1,0:T(8,128)(2,1)}, bf16[4,228,768]{2,1,0:T(8,128)(2,1)}) custom-call(s32[14]{0:T(128)} %concatenate.63.meta, bf16[2,232,768]{2,1,0:T(8,128)(2,1)} %get-tuple-element.533.own_ref.base_ref.in_ref, bf16[2,232,768]{2,1,0:T(8,128)(2,1)} %get-tuple-element.292.oth_ref, ...), custom_call_target="tpu_custom_call" | custom-call | flops 1 | bytes 1 | tf_op jit(solution)/shard_map/encoder_attention/pallas_call | solution.py:140
  62.5 10.1 %collective-permute-done.13 = bf16[192,768]{1,0:T(8,128)(2,1)S(1)} collective-permute-done((bf16[192,768]{1,0:T(8,128)(2,1)S(1)}, bf16[192,768]{1,0:T(8,128)(2,1)S(1)}, u32[]{:S(2)}, u32[]{:S(2)}) %collective-permute-start.13) | collective-permute-done | bytes 294944 | tf_op jit(solution)/shard_map/ppermute | solution.py:1103
  85.6 7.5 %encoder_feed.1 = (bf16[2,232,768]{2,1,0:T(8,128)(2,1)}, bf16[2,232,768]{2,1,0:T(8,128)(2,1)}) custom-call(s32[14]{0:T(128)} %concatenate.63.meta, bf16[2,232,768]{2,1,0:T(8,128)(2,1)} %get-tuple-element.319.own_ref, bf16[2,232,768]{2,1,0:T(8,128)(2,1)} %copy-done.8, bf16[192,768]{1,0:T(8,128)(2,1)} %copy-done.20, bf16[192,768]{1,0:T(8,128)(2,1)} %copy-done.37, ...), custom_call_target="tpu_custom_call" | custom-call | flops 1 | bytes 1 | tf_op jit(solution)/shard_map/encoder_feed/pallas_call | solution.py:140
  101.0 9.0 %collective-permute-done.21 = bf16[192,768]{1,0:T(8,128)(2,1)S(1)} collective-permute-done((bf16[192,768]{1,0:T(8,128)(2,1)S(1)}, bf16[192,768]{1,0:T(8,128)(2,1)S(1)}, u32[]{:S(2)}, u32[]{:S(2)}) %collective-permute-start.21) | collective-permute-done | bytes 294944 | tf_op jit(solution)/shard_map/ppermute | solution.py:1103
  111.5 4.1 %decoder_self.1 = (bf16[64,768]{1,0:T(8,128)(2,1)}, bf16[64,768]{1,0:T(8,128)(2,1)}, bf16[128,768]{1,0:T(8,128)(2,1)}) custom-call(s32[14]{0:T(128)} %concatenate.63.meta, bf16[128,768]{1,0:T(8,128)(2,1)} %bitcast.99, f32[1,768]{1,0:T(1,128)} %get-tuple-element.558.gain_ref, bf16[192,768]{1,0:T(8,128)(2,1)} %copy-done.18, bf16[192,768]{1,0:T(8,128)(2,1)} %copy-done.31, ...), custom_call_target="tpu_custom_call" | custom-call | flops 1 | bytes 1 | tf_op jit(solution)/shard_map/decoder_self/pallas_call | solution.py:140
  126.5 5.2 %collective-permute-done.28.rest_2_.rest_6_ = bf16[384,768]{1,0:T(8,128)(2,1)S(1)} collective-permute-done((bf16[384,768]{1,0:T(8,128)(2,1)S(1)}, bf16[384,768]{1,0:T(8,128)(2,1)S(1)}, u32[]{:S(2)}, u32[]{:S(2)}) %collective-permute-start.28) | collective-permute-done | bytes 589856 | tf_op jit(solution)/shard_map/ppermute | solution.py:1103
  136.4 8.1 %decoder_cross.1 = (bf16[2,32,768]{2,1,0:T(8,128)(2,1)}, bf16[2,32,768]{2,1,0:T(8,128)(2,1)}, bf16[4,32,384]{2,1,0:T(8,128)(2,1)}, bf16[4,228,384]{2,1,0:T(8,128)(2,1)}) custom-call(s32[14]{0:T(128)} %concatenate.63.meta, bf16[2,32,768]{2,1,0:T(8,128)(2,1)} %bitcast.107, bf16[2,32,768]{2,1,0:T(8,128)(2,1)} %bitcast.109, bf16[2,232,768]{2,1,0:T(8,128)(2,1)} %copy-done.1, ...), custom_call_target="tpu_custom_call" | custom-call | flops 1 | bytes 1 | tf_op jit(solution)/shard_map/decoder_cross/pallas_call | solution.py:140
  157.4 7.3 %decoder_feed.1 = (bf16[2,64,768]{2,1,0:T(8,128)(2,1)}, bf16[2,64,768]{2,1,0:T(8,128)(2,1)}, bf16[4,2,96,768]{3,2,1,0:T(8,128)(2,1)}, f32[4,2,96,768]{3,2,1,0:T(8,128)}) custom-call(s32[14]{0:T(128)} %concatenate.63.meta, bf16[64,768]{1,0:T(8,128)(2,1)} %get-tuple-element.358.own_ref, bf16[64,768]{1,0:T(8,128)(2,1)} %copy-done.83, ...), custom_call_target="tpu_custom_call" | custom-call | flops 1 | bytes 1 | tf_op jit(solution)/shard_map/decoder_feed/pallas_call | solution.py:140
  169.7 5.0 %collective-permute-done.36 = bf16[2,64,768]{2,1,0:T(8,128)(2,1)S(1)} collective-permute-done((bf16[2,64,768]{2,1,0:T(8,128)(2,1)S(1)}, bf16[2,64,768]{2,1,0:T(8,128)(2,1)S(1)}, u32[]{:S(2)}, u32[]{:S(2)}) %collective-permute-start.36) | collective-permute-done | bytes 196640 | tf_op jit(solution)/shard_map/ppermute | solution.py:1103
  180.2 14.8 %decoder_cross_back.1 = (bf16[2,32,768]{2,1,0:T(8,128)(2,1)}, bf16[2,32,768]{2,1,0:T(8,128)(2,1)}, bf16[2,232,768]{2,1,0:T(8,128)(2,1)}, bf16[2,232,768]{2,1,0:T...) custom-call(s32[14]{0:T(128)} %concatenate.63.meta, bf16[2,32,768]{2,1,0:T(8,128)(2,1)} %bitcast.108, ...), custom_call_target="tpu_custom_call" | custom-call | flops 1 | bytes 1 | tf_op jit(solution)/shard_map/decoder_cross_back/pallas_call | solution.py:140
  203.8 4.0 %fold.7 = (f32[2,2,96,768]{3,2,1,0:T(8,128)}, bf16[2,2,96,768]{3,2,1,0:T(8,128)(2,1)}) custom-call(s32[14]{0:T(128)} %concatenate.63.meta, f32[4,2,96,768]{3,2,1,0:T(8,128)} %get-tuple-element.379.rest_0_, bf16[4,2,96,768]{3,2,1,0:T(8,128)(2,1)} %copy-done.29), custom_call_target="tpu_custom_call" | custom-call | flops 1 | bytes 1 | tf_op jit(solution)/shard_map/fold/pallas_call | solution.py:140
  213.3 5.3 %decoder_self_back.1 = (bf16[64,768]{1,0:T(8,128)(2,1)}, bf16[64,768]{1,0:T(8,128)(2,1)}, bf16[4,1,96,768]{3,2,1,0:T(8,128)(2,1)}, f32[4,1,96,768]{3,2,1,0:T(8,128)}) custom-call(s32[14]{0:T(128)} %concatenate.63.meta, bf16[128,768]{1,0:T(8,128)(2,1)} %bitcast.100, f32[1,768]{1,0:T(1,128)} %get-tuple-element.558.gain_ref, ...), custom_call_target="tpu_custom_call" | custom-call | flops 1 | bytes 1 | tf_op jit(solution)/shard_map/decoder_self_back/pallas_call | solution.py:140
  229.5 14.8 %encoder_feed_back.1 = (bf16[2,232,768]{2,1,0:T(8,128)(2,1)}, bf16[2,232,768]{2,1,0:T(8,128)(2,1)}, bf16[4,1,96,768]{3,2,1,0:T(8,128)(2,1)}, f32[4,1,96,768]{3,2...) custom-call(s32[14]{0:T(128)} %concatenate.63.meta, ...), custom_call_target="tpu_custom_call" | custom-call | flops 1 | bytes 1 | tf_op jit(solution)/shard_map/encoder_feed_back/pallas_call | solution.py:140
  249.2 4.1 %fold.9 = (f32[2,2,96,768]{3,2,1,0:T(8,128)}, bf16[2,2,96,768]{3,2,1,0:T(8,128)(2,1)}) custom-call(s32[14]{0:T(128)} %concatenate.63.meta, f32[4,1,96,768]{3,2,1,0:T(8,128)} %get-tuple-element.413.rest_0_, f32[4,1,96,768]{3,2,1,0:T(8,128)} %get-tuple-element.414.rest_1_, bf16[4,1,96,768]{3,2,1,0:T(8,128)(2,1)} %copy-done.57, bf16[4,1,96,768]{3,2,1,0:T(8,128)(2,1)} %copy-done.60), custom_call_target="tpu_custom_call" | custom-call | flops 1 | bytes 1 | tf_op jit(solution)/shard_map/fold/pallas_call | solution.py:140
  256.7 4.2 %collective-permute-done.54.rest_2_ = bf16[4,1,96,768]{3,2,1,0:T(8,128)(2,1)S(1)} collective-permute-done((bf16[4,1,96,768]{3,2,1,0:T(8,128)(2,1)}, bf16[4,1,96,768]{3,2,1,0:T(8,128)(2,1)S(1)}, u32[]{:S(2)}, u32[]{:S(2)}) %collective-permute-start.54) | collective-permute-done | bytes 589856 | tf_op jit(solution)/shard_map/ppermute | solution.py:1103
  269.5 4.3 %norm_back_mid.1 = (f32[2,232,768]{2,1,0:T(8,128)}, bf16[2,232,768]{2,1,0:T(8,128)(2,1)}, f32[1,768]{1,0:T(1,128)}) custom-call(s32[14]{0:T(128)} %concatenate.63.meta, f32[2,232,768]{2,1,0:T(8,128)} %get-tuple-element.313.in_ref, f32[1,768]{1,0:T(1,128)} %get-tuple-element.559.gain_ref, f32[2,232,768]{2,1,0:T(8,128)} %get-tuple-element.531.grad_ref, ...), custom_call_target="tpu_custom_call" | custom-call | flops 1 | bytes 1 | tf_op jit(solution)/shard_map/norm_back_mid/pallas_call | solution.py:140
  277.8 4.1 %fold.11 = (f32[2,2,96,768]{3,2,1,0:T(8,128)}, bf16[2,2,96,768]{3,2,1,0:T(8,128)(2,1)}) custom-call(s32[14]{0:T(128)} %concatenate.63.meta, f32[4,1,96,768]{3,2,1,0:T(8,128)} %get-tuple-element.433.rest_0_, f32[4,1,96,768]{3,2,1,0:T(8,128)} %get-tuple-element.434.rest_1_, bf16[4,1,96,768]{3,2,1,0:T(8,128)(2,1)} %copy-done.58, bf16[4,1,96,768]{3,2,1,0:T(8,128)(2,1)} %copy-done.59), custom_call_target="tpu_custom_call" | custom-call | flops 1 | bytes 1 | tf_op jit(solution)/shard_map/fold/pallas_call | solution.py:140
  284.4 14.9 %encoder_attention_back.1 = (bf16[2,232,768]{2,1,0:T(8,128)(2,1)}, bf16[2,232,768]{2,1,0:T(8,128)(2,1)}, bf16[4,1,96,768]{3,2,1,0:T(8,128)(2,1)}, f32[4,1,96,768]{3,2,1,0:T(8,128)}) custom-call(s32[14]{0:T(128)} %concatenate.63.meta, bf16[2,232,768]{2,1,0:T(8,128)(2,1)} %get-tuple-element.533.own_ref.base_ref.in_ref, ...), custom_call_target="tpu_custom_call" | custom-call | flops 1 | bytes 1 | tf_op jit(solution)/shard_map/encoder_attention_back/pallas_call | solution.py:140
  313.4 9.8 %collective-permute-done.63.rest_1_ = bf16[4,1,96,768]{3,2,1,0:T(8,128)(2,1)S(1)} collective-permute-done((bf16[4,1,96,768]{3,2,1,0:T(8,128)(2,1)}, bf16[4,1,96,768]{3,2,1,0:T(8,128)(2,1)S(1)}, u32[]{:S(2)}, u32[]{:S(2)}) %collective-permute-start.63) | collective-permute-done | bytes 589856 | tf_op jit(solution)/shard_map/ppermute | solution.py:1103
  331.8 7.9 %collect.2 = (f32[6,96,768]{2,1,0:T(8,128)}, f32[6,8,768]{2,1,0:T(8,128)}) custom-call(s32[14]{0:T(128)} %concatenate.63.meta, f32[1,2,96,768]{3,2,1,0:T(8,128)} %get-tuple-element.463.rest_0_, bf16[1,2,96,768]{3,2,1,0:T(8,128)(2,1)} %copy-done.68, f32[1,2,96,768]{3,2,1,0:T(8,128)} %get-tuple-element.465.rest_2_, bf16[1,2,96,768]{3,2,1,0:T(8,128)(2,1)} %copy-done.69, ...), custom_call_target="tpu_custom_call" | custom-call | flops 1 | bytes 1 | tf_op jit(solution)/shard_map/collect/pallas_call | solution.py:140
  378.4 7.2 %update_attention.1 = (f32[3,3,96,192]{3,2,1,0:T(8,128)}, f32[3,3,96,192]{3,2,1,0:T(8,128)}, f32[3,3,96,192]{3,2,1,0:T(8,128)}, f32[3,3,96,192]{3,2,1,0:T(8,128)...) custom-call(s32[14]{0:T(128)} %concatenate.63.meta, ...), custom_call_target="tpu_custom_call" | custom-call | flops 1 | bytes 1 | tf_op jit(solution)/shard_map/update_attention/pallas_call | solution.py:140
  385.6 5.7 %update_feed.1 = (f32[2,96,768]{2,1,0:T(8,128)}, f32[2,96,768]{2,1,0:T(8,128)}, f32[2,96,768]{2,1,0:T(8,128)}, f32[2,96,768]{2,1,0:T(8,128)}, bf16[2,96,768]{2,1...) custom-call(s32[14]{0:T(128)} %concatenate.63.meta, ...), custom_call_target="tpu_custom_call" | custom-call | flops 1 | bytes 1 | tf_op jit(solution)/shard_map/update_feed/pallas_call | solution.py:140
  (435 shorter events, 216.5 us)
Async XLA Ops:
  31.0 20.0 %collective-permute-start.6 = (bf16[192,768]{1,0:T(8,128)(2,1)S(1)}, bf16[192,768]{1,0:T(8,128)(2,1)S(1)}, u32[]{:S(2)}, u32[]{:S(2)}) collective-permute-start(bf16[192,768]{1,0:T(8,128)(2,1)S(1)} %constant_dynamic-update-slice_fusion.2.rest_0_), channel_id=1, source_target_pairs={{0,4},{4,0},{8,12},{12,8},{16,20},{20,16},{24,28},{28,24},{1,5},{5... | collective-permute-start | bytes 884744 | tf_op jit(solution)/shard_map/ppermute | solution.py:1103
  32.6 18.5 %collective-permute-start.5 = (bf16[192,768]{1,0:T(8,128)(2,1)S(1)}, bf16[192,768]{1,0:T(8,128)(2,1)S(1)}, u32[]{:S(2)}, u32[]{:S(2)}) collective-permute-start(bf16[192,768]{1,0:T(8,128)(2,1)S(1)} %constant_dynamic-update-slice_fusion.2.rest_0_), channel_id=1, source_target_pairs={{0,8},{4,12},{8,0},{12,4},{16,24},{20,28},{24,16},{28,20},{1,9},{5... | collective-permute-start | bytes 884744 | tf_op jit(solution)/shard_map/ppermute | solution.py:1103
  32.6 18.5 %collective-permute-start.7 = (bf16[96,768]{1,0:T(8,128)(2,1)S(1)}, bf16[96,768]{1,0:T(8,128)(2,1)S(1)}, u32[]{:S(2)}, u32[]{:S(2)}) collective-permute-start(bf16[96,768]{1,0:T(8,128)(2,1)S(1)} %get-tuple-element.306), channel_id=1, source_target_pairs={{0,16},{4,20},{8,24},{12,28},{16,0},{20,4},{24,8},{28,12},{1,17},{... | collective-permute-start | bytes 442376 | tf_op jit(solution)/shard_map/ppermute | solution.py:1103
  54.9 20.2 %collective-permute-start.9 = (bf16[2,232,768]{2,1,0:T(8,128)(2,1)S(1)}, bf16[2,232,768]{2,1,0:T(8,128)(2,1)S(1)}, u32[]{:S(2)}, u32[]{:S(2)}) collective-permute-start(bf16[2,232,768]{2,1,0:T(8,128)(2,1)S(1)} %add_convert_fusion.5.first_ref), channel_id=1, source_target_pairs={{0,2},{1,3},{2,0},{3,1},{4,6},{5,7},{6,4},{7,5},{8,10},{9,11},{10,... | collective-permute-start | bytes 2138120 | tf_op jit(solution)/shard_map/ppermute | solution.py:1103
  56.5 16.2 %collective-permute-start.13 = (bf16[192,768]{1,0:T(8,128)(2,1)S(1)}, bf16[192,768]{1,0:T(8,128)(2,1)S(1)}, u32[]{:S(2)}, u32[]{:S(2)}) collective-permute-start(bf16[192,768]{1,0:T(8,128)(2,1)S(1)} %pad_maximum_fusion.5), channel_id=1, source_target_pairs={{0,16},{4,20},{8,24},{12,28},{16,0},{20,4},{24,8},{28,12},{1,17},{... | collective-permute-start | bytes 884744 | tf_op jit(solution)/shard_map/ppermute | solution.py:1103
  93.3 16.6 %collective-permute-start.21 = (bf16[192,768]{1,0:T(8,128)(2,1)S(1)}, bf16[192,768]{1,0:T(8,128)(2,1)S(1)}, u32[]{:S(2)}, u32[]{:S(2)}) collective-permute-start(bf16[192,768]{1,0:T(8,128)(2,1)S(1)} %copy-done.28), channel_id=1, source_target_pairs={{0,16},{4,20},{8,24},{12,28},{16,0},{20,4},{24,8},{28,12},{1,17},{... | collective-permute-start | bytes 884744 | tf_op jit(solution)/shard_map/ppermute | solution.py:1103
  99.4 19.4 %collective-permute-start.19 = (bf16[2,232,768]{2,1,0:T(8,128)(2,1)S(1)}, bf16[2,232,768]{2,1,0:T(8,128)(2,1)}, u32[]{:S(2)}, u32[]{:S(2)}) collective-permute-start(bf16[2,232,768]{2,1,0:T(8,128)(2,1)S(1)} %add_convert_fusion.4), channel_id=1, source_target_pairs={{0,2},{1,3},{2,0},{3,1},{4,6},{5,7},{6,4},{7,5},{8,10},{9,11},{10,... | collective-permute-start | bytes 2138120 | tf_op jit(solution)/shard_map/ppermute | solution.py:1103
  115.7 16.0 %collective-permute-start.28 = (bf16[384,768]{1,0:T(8,128)(2,1)S(1)}, bf16[384,768]{1,0:T(8,128)(2,1)S(1)}, u32[]{:S(2)}, u32[]{:S(2)}) collective-permute-start(bf16[384,768]{1,0:T(8,128)(2,1)S(1)} %constant_dynamic-update-slice_fusion.10.rest_0_.rest_4_), channel_id=1, source_target_pairs={{0,4},{4,0},{8,12},{12,8},{16,20},{20,16},{24,28},{28,24},{1,5},{5... | collective-permute-start | bytes 1769480 | tf_op jit(solution)/shard_map/ppermute | solution.py:1103
  133.7 21.5 %collective-permute-start.34 = (bf16[384,768]{1,0:T(8,128)(2,1)S(1)}, bf16[384,768]{1,0:T(8,128)(2,1)S(1)}, u32[]{:S(2)}, u32[]{:S(2)}) collective-permute-start(bf16[384,768]{1,0:T(8,128)(2,1)S(1)} %collective-permute-done.27.rest_1_.rest_5_), channel_id=1, source_target_pairs={{0,4},{4,0},{8,12},{12,8},{16,20},{20,16},{24,28},{28,24},{1,5},{5... | collective-permute-start | bytes 1769480 | tf_op jit(solution)/shard_map/ppermute | solution.py:1103
  164.7 30.3 %collective-permute-start.38 = (bf16[4,2,96,768]{3,2,1,0:T(8,128)(2,1)}, bf16[4,2,96,768]{3,2,1,0:T(8,128)(2,1)S(1)}, u32[]{:S(2)}, u32[]{:S(2)}) collective-permute-start(bf16[4,2,96,768]{3,2,1,0:T(8,128)(2,1)} %get-tuple-element.369), channel_id=1, source_target_pairs={{0,4},{4,0},{8,12},{12,8},{16,20},{20,16},{24,28},{28,24},{1,5},{5... | collective-permute-start | bytes 3538952 | tf_op jit(solution)/shard_map/ppermute | solution.py:1103
  201.4 21.3 %collective-permute-start.41 = (bf16[2,232,768]{2,1,0:T(8,128)(2,1)S(1)}, bf16[2,232,768]{2,1,0:T(8,128)(2,1)S(1)}, u32[]{:S(2)}, u32[]{:S(2)}) collective-permute-start(bf16[2,232,768]{2,1,0:T(8,128)(2,1)S(1)} %add_convert_fusion.2), channel_id=1, source_target_pairs={{0,2},{1,3},{2,0},{3,1},{4,6},{5,7},{6,4},{7,5},{8,10},{9,11},{10,... | collective-permute-start | bytes 2138120 | tf_op jit(solution)/shard_map/ppermute | solution.py:1103
  202.2 19.0 %collective-permute-start.46 = (bf16[4,1,96,768]{3,2,1,0:T(8,128)(2,1)S(1)}, bf16[4,1,96,768]{3,2,1,0:T(8,128)(2,1)S(1)}, u32[]{:S(2)}, u32[]{:S(2)}) collective-permute-start(bf16[4,1,96,768]{3,2,1,0:T(8,128)(2,1)S(1)} %copy-done.90), channel_id=1, source_target_pairs={{0,4},{4,0},{8,12},{12,8},{16,20},{20,16},{24,28},{28,24},{1,5},{5... | collective-permute-start | bytes 1769480 | tf_op jit(solution)/shard_map/ppermute | solution.py:1103
  227.2 17.1 %collective-permute-start.49 = (bf16[4,1,96,768]{3,2,1,0:T(8,128)(2,1)S(1)}, bf16[4,1,96,768]{3,2,1,0:T(8,128)(2,1)S(1)}, u32[]{:S(2)}, u32[]{:S(2)}) collective-permute-start(bf16[4,1,96,768]{3,2,1,0:T(8,128)(2,1)S(1)} %copy-done.92), channel_id=1, source_target_pairs={{0,4},{4,0},{8,12},{12,8},{16,20},{20,16},{24,28},{28,24},{1,5},{5... | collective-permute-start | bytes 1769480 | tf_op jit(solution)/shard_map/ppermute | solution.py:1103
  227.7 16.6 %collective-permute-start.50 = (bf16[1,2,96,768]{3,2,1,0:T(8,128)(2,1)}, bf16[1,2,96,768]{3,2,1,0:T(8,128)(2,1)S(1)}, u32[]{:S(2)}, u32[]{:S(2)}) collective-permute-start(bf16[1,2,96,768]{3,2,1,0:T(8,128)(2,1)} %get-tuple-element.403), channel_id=1, source_target_pairs={{0,16},{4,20},{8,24},{12,28},{16,0},{20,4},{24,8},{28,12},{1,17},{... | collective-permute-start | bytes 884744 | tf_op jit(solution)/shard_map/ppermute | solution.py:1103
  228.4 15.9 %collective-permute-start.51 = (bf16[64,768]{1,0:T(8,128)(2,1)S(1)}, bf16[64,768]{1,0:T(8,128)(2,1)S(1)}, u32[]{:S(2)}, u32[]{:S(2)}) collective-permute-start(bf16[64,768]{1,0:T(8,128)(2,1)S(1)} %add_convert_fusion.11.first_ref), channel_id=1, source_target_pairs={{0,2},{1,3},{2,0},{3,1},{4,6},{5,7},{6,4},{7,5},{8,10},{9,11},{10,... | collective-permute-start | bytes 294920 | tf_op jit(solution)/shard_map/ppermute | solution.py:1103
  244.4 16.4 %collective-permute-start.54 = (bf16[4,1,96,768]{3,2,1,0:T(8,128)(2,1)}, bf16[4,1,96,768]{3,2,1,0:T(8,128)(2,1)S(1)}, u32[]{:S(2)}, u32[]{:S(2)}) collective-permute-start(bf16[4,1,96,768]{3,2,1,0:T(8,128)(2,1)} %get-tuple-element.418), channel_id=1, source_target_pairs={{0,4},{4,0},{8,12},{12,8},{16,20},{20,16},{24,28},{28,24},{1,5},{5... | collective-permute-start | bytes 1769480 | tf_op jit(solution)/shard_map/ppermute | solution.py:1103
  248.1 20.6 %collective-permute-start.53 = (bf16[2,232,768]{2,1,0:T(8,128)(2,1)S(1)}, bf16[2,232,768]{2,1,0:T(8,128)(2,1)S(1)}, u32[]{:S(2)}, u32[]{:S(2)}) collective-permute-start(bf16[2,232,768]{2,1,0:T(8,128)(2,1)S(1)} %add_convert_fusion.1.first_ref), channel_id=1, source_target_pairs={{0,2},{1,3},{2,0},{3,1},{4,6},{5,7},{6,4},{7,5},{8,10},{9,11},{10,... | collective-permute-start | bytes 2138120 | tf_op jit(solution)/shard_map/ppermute | solution.py:1103
  255.0 22.0 %collective-permute-start.57 = (bf16[4,1,96,768]{3,2,1,0:T(8,128)(2,1)S(1)}, bf16[4,1,96,768]{3,2,1,0:T(8,128)(2,1)S(1)}, u32[]{:S(2)}, u32[]{:S(2)}) collective-permute-start(bf16[4,1,96,768]{3,2,1,0:T(8,128)(2,1)S(1)} %copy-done.91), channel_id=1, source_target_pairs={{0,4},{4,0},{8,12},{12,8},{16,20},{20,16},{24,28},{28,24},{1,5},{5... | collective-permute-start | bytes 1769480 | tf_op jit(solution)/shard_map/ppermute | solution.py:1103
  281.9 21.6 %collective-permute-start.59 = (bf16[2,2,96,768]{3,2,1,0:T(8,128)(2,1)}, bf16[2,2,96,768]{3,2,1,0:T(8,128)(2,1)S(1)}, u32[]{:S(2)}, u32[]{:S(2)}) collective-permute-start(bf16[2,2,96,768]{3,2,1,0:T(8,128)(2,1)} %get-tuple-element.442), channel_id=1, source_target_pairs={{0,8},{4,12},{8,0},{12,4},{16,24},{20,28},{24,16},{28,20},{1,9},{5... | collective-permute-start | bytes 1769480 | tf_op jit(solution)/shard_map/ppermute | solution.py:1103
  283.6 19.1 %collective-permute-start.60 = (bf16[1,2,96,768]{3,2,1,0:T(8,128)(2,1)S(1)}, bf16[1,2,96,768]{3,2,1,0:T(8,128)(2,1)S(1)}, u32[]{:S(2)}, u32[]{:S(2)}) collective-permute-start(bf16[1,2,96,768]{3,2,1,0:T(8,128)(2,1)S(1)} %copy-done.93), channel_id=1, source_target_pairs={{0,16},{4,20},{8,24},{12,28},{16,0},{20,4},{24,8},{28,12},{1,17},{... | collective-permute-start | bytes 884744 | tf_op jit(solution)/shard_map/ppermute | solution.py:1103
  307.3 15.9 %collective-permute-start.63 = (bf16[4,1,96,768]{3,2,1,0:T(8,128)(2,1)}, bf16[4,1,96,768]{3,2,1,0:T(8,128)(2,1)S(1)}, u32[]{:S(2)}, u32[]{:S(2)}) collective-permute-start(bf16[4,1,96,768]{3,2,1,0:T(8,128)(2,1)} %get-tuple-element.452), channel_id=1, source_target_pairs={{0,4},{4,0},{8,12},{12,8},{16,20},{20,16},{24,28},{28,24},{1,5},{5... | collective-permute-start | bytes 1769480 | tf_op jit(solution)/shard_map/ppermute | solution.py:1103
  309.7 38.2 %collective-permute-start.62 = (bf16[2,232,768]{2,1,0:T(8,128)(2,1)S(1)}, bf16[2,232,768]{2,1,0:T(8,128)(2,1)S(1)}, u32[]{:S(2)}, u32[]{:S(2)}) collective-permute-start(bf16[2,232,768]{2,1,0:T(8,128)(2,1)S(1)} %add_convert_fusion.first_ref), channel_id=1, source_target_pairs={{0,2},{1,3},{2,0},{3,1},{4,6},{5,7},{6,4},{7,5},{8,10},{9,11},{10,... | collective-permute-start | bytes 2138120 | tf_op jit(solution)/shard_map/ppermute | solution.py:1103
  310.8 16.3 %collective-permute-start.64 = (bf16[1,2,96,768]{3,2,1,0:T(8,128)(2,1)S(1)}, bf16[1,2,96,768]{3,2,1,0:T(8,128)(2,1)S(1)}, u32[]{:S(2)}, u32[]{:S(2)}) collective-permute-start(bf16[1,2,96,768]{3,2,1,0:T(8,128)(2,1)S(1)} %copy-done.94), channel_id=1, source_target_pairs={{0,16},{4,20},{8,24},{12,28},{16,0},{20,4},{24,8},{28,12},{1,17},{... | collective-permute-start | bytes 884744 | tf_op jit(solution)/shard_map/ppermute | solution.py:1103
  353.6 39.0 %collective-permute-start.68 = (f32[2,232,768]{2,1,0:T(8,128)}, f32[2,232,768]{2,1,0:T(8,128)S(1)}, u32[]{:S(2)}, u32[]{:S(2)}) collective-permute-start(f32[2,232,768]{2,1,0:T(8,128)} %get-tuple-element.473), channel_id=1, source_target_pairs={{0,1},{1,0},{2,3},{3,2},{4,5},{5,4},{6,7},{7,6},{8,9},{9,8},{10,11... | collective-permute-start | bytes 4276232 | tf_op jit(solution)/shard_map/ppermute | solution.py:1103
  (147 other events, 1198.8 us)

commit v8 on v7

--- a/solution.py
+++ b/solution.py
@@ -525,6 +525,14 @@
     )
 
 
+def pair_spec(shape):
+    return pl.BlockSpec((1,) + shape, lambda p, _: (p,) + (0,) * len(shape))
+
+
+def sides_spec(shape):
+    return pl.BlockSpec((2, 1) + shape, lambda p, _: (0, p) + (0,) * len(shape))
+
+
 def decoder_cross_back(
     plan, meta, own, oth, memory_own, memory_oth, pieces, kept_query, kept_key, grad_own, grad_oth
 ):
@@ -546,22 +554,25 @@
             plan.assemble(meta, pieces, refs, weight)
             grad = jnp.concatenate([grad_oth_ref[...], grad_own_ref[...]], 0).reshape(rows, D)
             grad_mixed[...] = mm(grad, weight[0, :, w3:]).astype(LOW)
-            acc[0, :, w3:] = t_mm(grad, query_ref[:, :, width:].reshape(rows, width))
+            acc[0, :, w3:] = t_mm(grad, query_ref[:, :, :, width:].reshape(rows, width))
             acc[0, :, width:w3] = jnp.zeros((D, w3 - width), F32)
 
-        memory = pick(step, count, memory_own_ref, memory_oth_ref, ENC_LEN)
-        allowed = key_mask(meta, plan.pairs, slot_of(plan, count, 0, step))
-        both = key_ref[0]
-        here = pl.ds(pl.multiple_of(step * SUFFIX, SUFFIX), SUFFIX)
-        query, grad_key, grad_value = attend_heads_back(
-            plan, query_ref[step, :, :width], both[:, :width], both[:, width:], allowed, grad_mixed[here, :]
-        )
-        grad_query[here, :] = query
-        together = jnp.concatenate([grad_key, grad_value], 1)
-        acc[0, :, width:w3] += t_mm(memory, together)
-        put(step, count, outs[2], outs[3], mm_t(together, weight[0, :, width:w3]).astype(LOW))
-
-        @pl.when(step == 2 * count - 1)
+        total = None
+        for side, (memory_ref, out) in enumerate(((memory_oth_ref, outs[3]), (memory_own_ref, outs[2]))):
+            allowed = key_mask(meta, plan.pairs, (1 - side) * plan.half + step)
+            both = key_ref[side, 0]
+            here = pl.ds(pl.multiple_of((side * count + step) * SUFFIX, SUFFIX), SUFFIX)
+            query, grad_key, grad_value = attend_heads_back(
+                plan, query_ref[side, step, :, :width], both[:, :width], both[:, width:], allowed, grad_mixed[here, :]
+            )
+            grad_query[here, :] = query
+            together = jnp.concatenate([grad_key, grad_value], 1)
+            product = t_mm(memory_ref[0, :ENC_LEN], together)
+            total = product if total is None else total + product
+            out[0, :ENC_LEN] = mm_t(together, weight[0, :, width:w3]).astype(LOW)
+        acc[0, :, width:w3] += total
+
+        @pl.when(step == count - 1)
         def _():
             normed = jnp.concatenate([oth_ref[...], own_ref[...]], 0).reshape(rows, D)
             queries = grad_query[...]
@@ -573,19 +584,19 @@
 
     part, long = (count, SUFFIX, D), (LONG, D)
     shapes = plan.grad_shapes(1)
-    long_specs = [own_spec(count, 0, long), oth_spec(count, 0, long)]
     return call(
         "decoder_cross_back",
         body,
-        (2 * count,),
+        (count,),
         meta,
         (own, oth, memory_own, memory_oth, kept_query, kept_key, grad_own, grad_oth, *flat(pieces)),
         [
             whole(part),
             whole(part),
-            *long_specs,
+            pair_spec(long),
+            pair_spec(long),
             whole(kept_query.shape),
-            step_spec(kept_key.shape[1:]),
+            sides_spec(kept_key.shape[2:]),
             whole(part),
             whole(part),
             *plan.weight_specs(pieces),
@@ -593,10 +604,9 @@
         [jax.ShapeDtypeStruct(part, LOW)] * 2
         + [jax.ShapeDtypeStruct((count,) + long, LOW)] * 2
         + shapes,
-        [whole(part), whole(part), *long_specs, *[whole(item.shape) for item in shapes]],
+        [whole(part), whole(part), pair_spec(long), pair_spec(long), *[whole(item.shape) for item in shapes]],
         plan.weight_scratch(pieces)
-        + [pltpu.VMEM((1, D, D), F32)]
-        + [pltpu.VMEM((rows, width), LOW), pltpu.VMEM((rows, width), LOW)],
+        + [pltpu.VMEM((1, D, D), F32), pltpu.VMEM((rows, width), LOW), pltpu.VMEM((rows, width), LOW)],
     )
 
 
@@ -1292,6 +1302,7 @@
 
     cross_in = (triple(norm_cross), triple(norm_cross_oth), memory, memory_oth, cross_att)
     own, oth, *kept_cross = decoder_cross(plan, meta, *cross_in)
+    kept_cross = [item.reshape((2, half) + item.shape[1:]) for item in kept_cross]
     sums = reduce_own(own, oth)
     dec_two, norm_last = add_norm(
         meta, "add_norm_last", dec_one, sums[0].reshape(mid, D), sums[1].reshape(mid, D), gains[4]
@@ -1341,13 +1352,11 @@
     enc_low_oth = core(enc_low)
 
     if direct:
-        keep_dec, away_dec = fold(plan, meta, [keep_dec], [more_dec], halves)
-        enc_low_oth, away_self, away_dec = hold((enc_low_oth, grads_self[0], away_dec))
+        enc_low_oth, away_self = hold((enc_low_oth, grads_self[0]))
         more_self = swap(away_self, "dp", 1)
-        more_dec = swap(away_dec, "dp", 4)
     own, oth, *grads_enc = encoder_feed_back(plan, meta, norm_mid, norm_mid_oth, enc_low, enc_low_oth, enc_feed)
     if direct:
-        own, oth, more_self, more_dec, *sums_self = hold((own, oth, more_self, more_dec, *sums_self))
+        own, oth, more_self, *sums_self = hold((own, oth, more_self, *sums_self))
         more_up, more_down = [swap(item, "dp", 1) for item in grads_enc[::2]]
     sums = reduce_own(own, oth)
     if direct:
@@ -1356,7 +1365,10 @@
         )
         keep_mid, away_mid = fold(plan, meta, [keep_cross, keep_self], [more_cross, more_self], halves)
         more_mid = swap(away_mid, "dp", 2)
-        sums_self, _, more_up = hold((sums_self, away_mid, more_up))
+        keep_dec, more_dec, _ = hold((keep_dec, more_dec, away_mid))
+        keep_dec, away_dec = fold(plan, meta, [keep_dec], [more_dec], halves)
+        more_dec = swap(away_dec, "dp", 4)
+        sums_self, _, more_up = hold((sums_self, away_dec, more_up))
     grad, gain_two = norm_back(meta, "norm_back_self", dec_rel[:mid], gains[2], grad, *sums_self, False)
     decoder_in_grad = absolute(triple(grad)).reshape(2 * mid, D)
     if direct:
@@ -1367,7 +1379,7 @@
     if direct:
         keep_mid, _ = hold((keep_mid, enc_low))
         keep_mid, away_mid = fold(plan, meta, [keep_mid], [more_mid], halves)
-        enc_low, more_down, away_mid = hold((enc_low, more_down, away_mid))
+        enc_low, more_down, away_mid, more_dec = hold((enc_low, more_down, away_mid, more_dec))
     enc_low_oth = core(enc_low)
 
     if direct:

time: 397 us -> 395 us (level)
  starting transfers between devices: 72.6 us -> 77.5 us
    ppermute x74, starting transfers between devices: 72.6 us -> 77.5 us  [swap(): return lax.ppermute(value, axis, [(i, i ^ bit) for i in range(count)])]
    unnamed x201 -> x197, local copies, waits for them, and re-layouts: 11.8 us -> 10.3 us
  transfers between devices with their start and end apart: 74 -> 74, of which waited for: 41 -> 42; matrix products, arithmetic and copies ran while one was open for 7% -> 7% of each run, Pallas kernels for 37% -> 37%
where the time goes in v8:
time: 395 us; the launch traced here: 393 us
  Pallas kernels  163 us (41%)
  waiting for transfers between devices  105 us (27%)
  starting transfers between devices  77.5 us (20%)
  local copies, waits for them, and re-layouts  23.4 us (6%)
  other arithmetic  21.4 us (5%)
    pallas_call x30, Pallas kernels, call(): pl.pallas_call(body, name=name, out_shape=outs, grid_spec=pltpu.PrefetchS...  163 us
    ppermute x74, waiting for transfers between devices, swap(): return lax.ppermute(value, axis, [(i, i ^ bit) for i in range(count)])  105 us
    ppermute x74, starting transfers between devices, swap(): return lax.ppermute(value, axis, [(i, i ^ bit) for i in range(count)])  77.5 us
    unnamed x197, local copies, waits for them, and re-layouts  10.3 us
    convert_element_type x10, other arithmetic, reduce_own(): sent = (own.astype(f32) + swap(oth, 'mp', 1).astype(f32)).astype(low)  9.04 us
  transfers between devices with their start and end apart: 74, of which 42 were waited for; matrix products, arithmetic and copies ran while one was open for 7% of the time, Pallas kernels for 37%

profile of v8, /device:TPU:0, one launch (start us, length us, event | category | flops | bytes accessed | tf_op | source)
XLA Modules:
  0.0 392.9 jit_solution(3214624617311865046)
XLA Ops:
  2.7 4.0 %collective-permute-start = (bf16[104,768]{1,0:T(8,128)(2,1)}, bf16[104,768]{1,0:T(8,128)(2,1)}, u32[]{:S(2)}, u32[]{:S(2)}) collective-permute-start(bf16[104,768]{1,0:T(8,128)(2,1)} %pack_first.1), channel_id=1, source_target_pairs={{0,16},{4,20},{8,24},{12,28},{16,0},{20,4},{24,8},{28,12},{1,17},{... | collective-permute-start | bytes 479240 | tf_op jit(solution)/shard_map/ppermute | solution.py:1113
  22.8 4.8 %collective-permute-done.2.rest_1_ = bf16[208,768]{1,0:T(8,128)(2,1)S(1)} collective-permute-done((bf16[208,768]{1,0:T(8,128)(2,1)S(1)}, bf16[208,768]{1,0:T(8,128)(2,1)S(1)}, u32[]{:S(2)}, u32[]{:S(2)}) %collective-permute-start.2) | collective-permute-done | bytes 319520 | tf_op jit(solution)/shard_map/ppermute | solution.py:1113
  39.5 9.5 %encoder_attention.1 = (bf16[2,232,768]{2,1,0:T(8,128)(2,1)}, bf16[2,232,768]{2,1,0:T(8,128)(2,1)}, bf16[4,228,768]{2,1,0:T(8,128)(2,1)}) custom-call(s32[14]{0:T(128)} %concatenate.63.meta, bf16[2,232,768]{2,1,0:T(8,128)(2,1)} %get-tuple-element.535.own_ref.base_ref.in_ref, bf16[2,232,768]{2,1,0:T(8,128)(2,1)} %get-tuple-element.293.oth_ref, ...), custom_call_target="tpu_custom_call" | custom-call | flops 1 | bytes 1 | tf_op jit(solution)/shard_map/encoder_attention/pallas_call | solution.py:140
  61.4 9.1 %collective-permute-done.13 = bf16[192,768]{1,0:T(8,128)(2,1)S(1)} collective-permute-done((bf16[192,768]{1,0:T(8,128)(2,1)S(1)}, bf16[192,768]{1,0:T(8,128)(2,1)S(1)}, u32[]{:S(2)}, u32[]{:S(2)}) %collective-permute-start.13) | collective-permute-done | bytes 294944 | tf_op jit(solution)/shard_map/ppermute | solution.py:1113
  84.2 7.4 %encoder_feed.1 = (bf16[2,232,768]{2,1,0:T(8,128)(2,1)}, bf16[2,232,768]{2,1,0:T(8,128)(2,1)}) custom-call(s32[14]{0:T(128)} %concatenate.63.meta, bf16[2,232,768]{2,1,0:T(8,128)(2,1)} %get-tuple-element.320.own_ref, bf16[2,232,768]{2,1,0:T(8,128)(2,1)} %copy-done.8, bf16[192,768]{1,0:T(8,128)(2,1)} %copy-done.20, bf16[192,768]{1,0:T(8,128)(2,1)} %copy-done.36, ...), custom_call_target="tpu_custom_call" | custom-call | flops 1 | bytes 1 | tf_op jit(solution)/shard_map/encoder_feed/pallas_call | solution.py:140
  99.8 8.7 %collective-permute-done.21 = bf16[192,768]{1,0:T(8,128)(2,1)S(1)} collective-permute-done((bf16[192,768]{1,0:T(8,128)(2,1)S(1)}, bf16[192,768]{1,0:T(8,128)(2,1)S(1)}, u32[]{:S(2)}, u32[]{:S(2)}) %collective-permute-start.21) | collective-permute-done | bytes 294944 | tf_op jit(solution)/shard_map/ppermute | solution.py:1113
  110.7 4.1 %decoder_self.1 = (bf16[64,768]{1,0:T(8,128)(2,1)}, bf16[64,768]{1,0:T(8,128)(2,1)}, bf16[128,768]{1,0:T(8,128)(2,1)}) custom-call(s32[14]{0:T(128)} %concatenate.63.meta, bf16[128,768]{1,0:T(8,128)(2,1)} %bitcast.101, f32[1,768]{1,0:T(1,128)} %get-tuple-element.560.gain_ref, bf16[192,768]{1,0:T(8,128)(2,1)} %copy-done.18, bf16[192,768]{1,0:T(8,128)(2,1)} %copy-done.30, ...), custom_call_target="tpu_custom_call" | custom-call | flops 1 | bytes 1 | tf_op jit(solution)/shard_map/decoder_self/pallas_call | solution.py:140
  125.4 5.3 %collective-permute-done.27.rest_1_.rest_5_ = bf16[384,768]{1,0:T(8,128)(2,1)S(1)} collective-permute-done((bf16[384,768]{1,0:T(8,128)(2,1)S(1)}, bf16[384,768]{1,0:T(8,128)(2,1)S(1)}, u32[]{:S(2)}, u32[]{:S(2)}) %collective-permute-start.27) | collective-permute-done | bytes 589856 | tf_op jit(solution)/shard_map/ppermute | solution.py:1113
  134.9 8.1 %decoder_cross.1 = (bf16[2,32,768]{2,1,0:T(8,128)(2,1)}, bf16[2,32,768]{2,1,0:T(8,128)(2,1)}, bf16[4,32,384]{2,1,0:T(8,128)(2,1)}, bf16[4,228,384]{2,1,0:T(8,128)(2,1)}) custom-call(s32[14]{0:T(128)} %concatenate.63.meta, bf16[2,32,768]{2,1,0:T(8,128)(2,1)} %bitcast.110, bf16[2,32,768]{2,1,0:T(8,128)(2,1)} %bitcast.112, bf16[2,232,768]{2,1,0:T(8,128)(2,1)} %copy-done.1, ...), custom_call_target="tpu_custom_call" | custom-call | flops 1 | bytes 1 | tf_op jit(solution)/shard_map/decoder_cross/pallas_call | solution.py:140
  155.8 7.3 %decoder_feed.1 = (bf16[2,64,768]{2,1,0:T(8,128)(2,1)}, bf16[2,64,768]{2,1,0:T(8,128)(2,1)}, bf16[4,2,96,768]{3,2,1,0:T(8,128)(2,1)}, f32[4,2,96,768]{3,2,1,0:T(8,128)}) custom-call(s32[14]{0:T(128)} %concatenate.63.meta, bf16[64,768]{1,0:T(8,128)(2,1)} %get-tuple-element.359.own_ref, bf16[64,768]{1,0:T(8,128)(2,1)} %copy-done.81, ...), custom_call_target="tpu_custom_call" | custom-call | flops 1 | bytes 1 | tf_op jit(solution)/shard_map/decoder_feed/pallas_call | solution.py:140
  168.7 4.8 %collective-permute-done.36 = bf16[2,64,768]{2,1,0:T(8,128)(2,1)S(1)} collective-permute-done((bf16[2,64,768]{2,1,0:T(8,128)(2,1)S(1)}, bf16[2,64,768]{2,1,0:T(8,128)(2,1)S(1)}, u32[]{:S(2)}, u32[]{:S(2)}) %collective-permute-start.36) | collective-permute-done | bytes 196640 | tf_op jit(solution)/shard_map/ppermute | solution.py:1113
  179.0 13.6 %decoder_cross_back.1 = (bf16[2,32,768]{2,1,0:T(8,128)(2,1)}, bf16[2,32,768]{2,1,0:T(8,128)(2,1)}, bf16[2,232,768]{2,1,0:T(8,128)(2,1)}, bf16[2,232,768]{2,1,0:T...) custom-call(s32[14]{0:T(128)} %concatenate.63.meta, bf16[2,32,768]{2,1,0:T(8,128)(2,1)} %bitcast.111, ...), custom_call_target="tpu_custom_call" | custom-call | flops 1 | bytes 1 | tf_op jit(solution)/shard_map/decoder_cross_back/pallas_call | solution.py:140
  201.1 4.0 %fold.7 = (f32[2,2,96,768]{3,2,1,0:T(8,128)}, bf16[2,2,96,768]{3,2,1,0:T(8,128)(2,1)}) custom-call(s32[14]{0:T(128)} %concatenate.63.meta, f32[4,2,96,768]{3,2,1,0:T(8,128)} %get-tuple-element.380.rest_0_, bf16[4,2,96,768]{3,2,1,0:T(8,128)(2,1)} %copy-done.29), custom_call_target="tpu_custom_call" | custom-call | flops 1 | bytes 1 | tf_op jit(solution)/shard_map/fold/pallas_call | solution.py:140
  210.9 5.3 %decoder_self_back.1 = (bf16[64,768]{1,0:T(8,128)(2,1)}, bf16[64,768]{1,0:T(8,128)(2,1)}, bf16[4,1,96,768]{3,2,1,0:T(8,128)(2,1)}, f32[4,1,96,768]{3,2,1,0:T(8,128)}) custom-call(s32[14]{0:T(128)} %concatenate.63.meta, bf16[128,768]{1,0:T(8,128)(2,1)} %bitcast.102, f32[1,768]{1,0:T(1,128)} %get-tuple-element.560.gain_ref, ...), custom_call_target="tpu_custom_call" | custom-call | flops 1 | bytes 1 | tf_op jit(solution)/shard_map/decoder_self_back/pallas_call | solution.py:140
  225.6 14.8 %encoder_feed_back.1 = (bf16[2,232,768]{2,1,0:T(8,128)(2,1)}, bf16[2,232,768]{2,1,0:T(8,128)(2,1)}, bf16[4,1,96,768]{3,2,1,0:T(8,128)(2,1)}, f32[4,1,96,768]{3,2...) custom-call(s32[14]{0:T(128)} %concatenate.63.meta, ...), custom_call_target="tpu_custom_call" | custom-call | flops 1 | bytes 1 | tf_op jit(solution)/shard_map/encoder_feed_back/pallas_call | solution.py:140
  244.8 4.1 %fold.8 = (f32[2,2,96,768]{3,2,1,0:T(8,128)}, bf16[2,2,96,768]{3,2,1,0:T(8,128)(2,1)}) custom-call(s32[14]{0:T(128)} %concatenate.63.meta, f32[4,1,96,768]{3,2,1,0:T(8,128)} %get-tuple-element.412.rest_0_, f32[4,1,96,768]{3,2,1,0:T(8,128)} %get-tuple-element.413.rest_1_, bf16[4,1,96,768]{3,2,1,0:T(8,128)(2,1)} %copy-done.57, bf16[4,1,96,768]{3,2,1,0:T(8,128)(2,1)} %copy-done.60), custom_call_target="tpu_custom_call" | custom-call | flops 1 | bytes 1 | tf_op jit(solution)/shard_map/fold/pallas_call | solution.py:140
  266.5 4.3 %norm_back_mid.1 = (f32[2,232,768]{2,1,0:T(8,128)}, bf16[2,232,768]{2,1,0:T(8,128)(2,1)}, f32[1,768]{1,0:T(1,128)}) custom-call(s32[14]{0:T(128)} %concatenate.63.meta, f32[2,232,768]{2,1,0:T(8,128)} %get-tuple-element.314.in_ref, f32[1,768]{1,0:T(1,128)} %get-tuple-element.561.gain_ref, f32[2,232,768]{2,1,0:T(8,128)} %get-tuple-element.533.grad_ref, ...), custom_call_target="tpu_custom_call" | custom-call | flops 1 | bytes 1 | tf_op jit(solution)/shard_map/norm_back_mid/pallas_call | solution.py:140
  276.6 4.1 %fold.11 = (f32[2,2,96,768]{3,2,1,0:T(8,128)}, bf16[2,2,96,768]{3,2,1,0:T(8,128)(2,1)}) custom-call(s32[14]{0:T(128)} %concatenate.63.meta, f32[4,1,96,768]{3,2,1,0:T(8,128)} %get-tuple-element.435.rest_0_, f32[4,1,96,768]{3,2,1,0:T(8,128)} %get-tuple-element.436.rest_1_, bf16[4,1,96,768]{3,2,1,0:T(8,128)(2,1)} %copy-done.58, bf16[4,1,96,768]{3,2,1,0:T(8,128)(2,1)} %copy-done.59), custom_call_target="tpu_custom_call" | custom-call | flops 1 | bytes 1 | tf_op jit(solution)/shard_map/fold/pallas_call | solution.py:140
  282.8 14.9 %encoder_attention_back.1 = (bf16[2,232,768]{2,1,0:T(8,128)(2,1)}, bf16[2,232,768]{2,1,0:T(8,128)(2,1)}, bf16[4,1,96,768]{3,2,1,0:T(8,128)(2,1)}, f32[4,1,96,768]{3,2,1,0:T(8,128)}) custom-call(s32[14]{0:T(128)} %concatenate.63.meta, bf16[2,232,768]{2,1,0:T(8,128)(2,1)} %get-tuple-element.535.own_ref.base_ref.in_ref, ...), custom_call_target="tpu_custom_call" | custom-call | flops 1 | bytes 1 | tf_op jit(solution)/shard_map/encoder_attention_back/pallas_call | solution.py:140
  311.0 11.8 %collective-permute-done.63.rest_1_ = bf16[4,1,96,768]{3,2,1,0:T(8,128)(2,1)S(1)} collective-permute-done((bf16[4,1,96,768]{3,2,1,0:T(8,128)(2,1)}, bf16[4,1,96,768]{3,2,1,0:T(8,128)(2,1)S(1)}, u32[]{:S(2)}, u32[]{:S(2)}) %collective-permute-start.63) | collective-permute-done | bytes 589856 | tf_op jit(solution)/shard_map/ppermute | solution.py:1113
  331.1 7.9 %collect.2 = (f32[6,96,768]{2,1,0:T(8,128)}, f32[6,8,768]{2,1,0:T(8,128)}) custom-call(s32[14]{0:T(128)} %concatenate.63.meta, f32[1,2,96,768]{3,2,1,0:T(8,128)} %get-tuple-element.465.rest_0_, bf16[1,2,96,768]{3,2,1,0:T(8,128)(2,1)} %copy-done.68, f32[1,2,96,768]{3,2,1,0:T(8,128)} %get-tuple-element.467.rest_2_, bf16[1,2,96,768]{3,2,1,0:T(8,128)(2,1)} %copy-done.69, ...), custom_call_target="tpu_custom_call" | custom-call | flops 1 | bytes 1 | tf_op jit(solution)/shard_map/collect/pallas_call | solution.py:140
  353.5 4.2 %collective-permute-done.70 = bf16[8,8,768]{2,1,0:T(8,128)(2,1)S(1)} collective-permute-done((bf16[8,8,768]{2,1,0:T(8,128)(2,1)S(1)}, bf16[8,8,768]{2,1,0:T(8,128)(2,1)S(1)}, u32[]{:S(2)}, u32[]{:S(2)}) %collective-permute-start.70) | collective-permute-done | bytes 98336 | tf_op jit(solution)/shard_map/ppermute | solution.py:1113
  376.3 7.2 %update_attention.1 = (f32[3,3,96,192]{3,2,1,0:T(8,128)}, f32[3,3,96,192]{3,2,1,0:T(8,128)}, f32[3,3,96,192]{3,2,1,0:T(8,128)}, f32[3,3,96,192]{3,2,1,0:T(8,128)...) custom-call(s32[14]{0:T(128)} %concatenate.63.meta, ...), custom_call_target="tpu_custom_call" | custom-call | flops 1 | bytes 1 | tf_op jit(solution)/shard_map/update_attention/pallas_call | solution.py:140
  383.5 5.7 %update_feed.1 = (f32[2,96,768]{2,1,0:T(8,128)}, f32[2,96,768]{2,1,0:T(8,128)}, f32[2,96,768]{2,1,0:T(8,128)}, f32[2,96,768]{2,1,0:T(8,128)}, bf16[2,96,768]{2,1...) custom-call(s32[14]{0:T(128)} %concatenate.63.meta, ...), custom_call_target="tpu_custom_call" | custom-call | flops 1 | bytes 1 | tf_op jit(solution)/shard_map/update_feed/pallas_call | solution.py:140
  (431 shorter events, 214.7 us)
Async XLA Ops:
  29.9 19.1 %collective-permute-start.5 = (bf16[192,768]{1,0:T(8,128)(2,1)S(1)}, bf16[192,768]{1,0:T(8,128)(2,1)S(1)}, u32[]{:S(2)}, u32[]{:S(2)}) collective-permute-start(bf16[192,768]{1,0:T(8,128)(2,1)S(1)} %constant_dynamic-update-slice_fusion.2.rest_0_), channel_id=1, source_target_pairs={{0,8},{4,12},{8,0},{12,4},{16,24},{20,28},{24,16},{28,20},{1,9},{5... | collective-permute-start | bytes 884744 | tf_op jit(solution)/shard_map/ppermute | solution.py:1113
  30.7 18.3 %collective-permute-start.6 = (bf16[192,768]{1,0:T(8,128)(2,1)S(1)}, bf16[192,768]{1,0:T(8,128)(2,1)S(1)}, u32[]{:S(2)}, u32[]{:S(2)}) collective-permute-start(bf16[192,768]{1,0:T(8,128)(2,1)S(1)} %constant_dynamic-update-slice_fusion.2.rest_0_), channel_id=1, source_target_pairs={{0,4},{4,0},{8,12},{12,8},{16,20},{20,16},{24,28},{28,24},{1,5},{5... | collective-permute-start | bytes 884744 | tf_op jit(solution)/shard_map/ppermute | solution.py:1113
  32.2 16.7 %collective-permute-start.7 = (bf16[96,768]{1,0:T(8,128)(2,1)S(1)}, bf16[96,768]{1,0:T(8,128)(2,1)S(1)}, u32[]{:S(2)}, u32[]{:S(2)}) collective-permute-start(bf16[96,768]{1,0:T(8,128)(2,1)S(1)} %get-tuple-element.307), channel_id=1, source_target_pairs={{0,16},{4,20},{8,24},{12,28},{16,0},{20,4},{24,8},{28,12},{1,17},{... | collective-permute-start | bytes 442376 | tf_op jit(solution)/shard_map/ppermute | solution.py:1113
  52.7 19.5 %collective-permute-start.9 = (bf16[2,232,768]{2,1,0:T(8,128)(2,1)S(1)}, bf16[2,232,768]{2,1,0:T(8,128)(2,1)S(1)}, u32[]{:S(2)}, u32[]{:S(2)}) collective-permute-start(bf16[2,232,768]{2,1,0:T(8,128)(2,1)S(1)} %add_convert_fusion.5.first_ref), channel_id=1, source_target_pairs={{0,2},{1,3},{2,0},{3,1},{4,6},{5,7},{6,4},{7,5},{8,10},{9,11},{10,... | collective-permute-start | bytes 2138120 | tf_op jit(solution)/shard_map/ppermute | solution.py:1113
  54.4 16.2 %collective-permute-start.13 = (bf16[192,768]{1,0:T(8,128)(2,1)S(1)}, bf16[192,768]{1,0:T(8,128)(2,1)S(1)}, u32[]{:S(2)}, u32[]{:S(2)}) collective-permute-start(bf16[192,768]{1,0:T(8,128)(2,1)S(1)} %pad_maximum_fusion.5), channel_id=1, source_target_pairs={{0,16},{4,20},{8,24},{12,28},{16,0},{20,4},{24,8},{28,12},{1,17},{... | collective-permute-start | bytes 884744 | tf_op jit(solution)/shard_map/ppermute | solution.py:1113
  91.8 16.7 %collective-permute-start.21 = (bf16[192,768]{1,0:T(8,128)(2,1)S(1)}, bf16[192,768]{1,0:T(8,128)(2,1)S(1)}, u32[]{:S(2)}, u32[]{:S(2)}) collective-permute-start(bf16[192,768]{1,0:T(8,128)(2,1)S(1)} %copy-done.28), channel_id=1, source_target_pairs={{0,16},{4,20},{8,24},{12,28},{16,0},{20,4},{24,8},{28,12},{1,17},{... | collective-permute-start | bytes 884744 | tf_op jit(solution)/shard_map/ppermute | solution.py:1113
  98.2 19.4 %collective-permute-start.19 = (bf16[2,232,768]{2,1,0:T(8,128)(2,1)S(1)}, bf16[2,232,768]{2,1,0:T(8,128)(2,1)}, u32[]{:S(2)}, u32[]{:S(2)}) collective-permute-start(bf16[2,232,768]{2,1,0:T(8,128)(2,1)S(1)} %add_convert_fusion.4), channel_id=1, source_target_pairs={{0,2},{1,3},{2,0},{3,1},{4,6},{5,7},{6,4},{7,5},{8,10},{9,11},{10,... | collective-permute-start | bytes 2138120 | tf_op jit(solution)/shard_map/ppermute | solution.py:1113
  132.2 21.5 %collective-permute-start.34 = (bf16[384,768]{1,0:T(8,128)(2,1)S(1)}, bf16[384,768]{1,0:T(8,128)(2,1)S(1)}, u32[]{:S(2)}, u32[]{:S(2)}) collective-permute-start(bf16[384,768]{1,0:T(8,128)(2,1)S(1)} %collective-permute-done.27.rest_1_.rest_5_), channel_id=1, source_target_pairs={{0,4},{4,0},{8,12},{12,8},{16,20},{20,16},{24,28},{28,24},{1,5},{5... | collective-permute-start | bytes 1769480 | tf_op jit(solution)/shard_map/ppermute | solution.py:1113
  163.1 29.5 %collective-permute-start.38 = (bf16[4,2,96,768]{3,2,1,0:T(8,128)(2,1)}, bf16[4,2,96,768]{3,2,1,0:T(8,128)(2,1)S(1)}, u32[]{:S(2)}, u32[]{:S(2)}) collective-permute-start(bf16[4,2,96,768]{3,2,1,0:T(8,128)(2,1)} %get-tuple-element.370), channel_id=1, source_target_pairs={{0,4},{4,0},{8,12},{12,8},{16,20},{20,16},{24,28},{28,24},{1,5},{5... | collective-permute-start | bytes 3538952 | tf_op jit(solution)/shard_map/ppermute | solution.py:1113
  199.2 20.7 %collective-permute-start.41 = (bf16[2,232,768]{2,1,0:T(8,128)(2,1)S(1)}, bf16[2,232,768]{2,1,0:T(8,128)(2,1)S(1)}, u32[]{:S(2)}, u32[]{:S(2)}) collective-permute-start(bf16[2,232,768]{2,1,0:T(8,128)(2,1)S(1)} %add_convert_fusion.2), channel_id=1, source_target_pairs={{0,2},{1,3},{2,0},{3,1},{4,6},{5,7},{6,4},{7,5},{8,10},{9,11},{10,... | collective-permute-start | bytes 2138120 | tf_op jit(solution)/shard_map/ppermute | solution.py:1113
  199.8 18.9 %collective-permute-start.46 = (bf16[4,1,96,768]{3,2,1,0:T(8,128)(2,1)S(1)}, bf16[4,1,96,768]{3,2,1,0:T(8,128)(2,1)S(1)}, u32[]{:S(2)}, u32[]{:S(2)}) collective-permute-start(bf16[4,1,96,768]{3,2,1,0:T(8,128)(2,1)S(1)} %copy-done.88), channel_id=1, source_target_pairs={{0,4},{4,0},{8,12},{12,8},{16,20},{20,16},{24,28},{28,24},{1,5},{5... | collective-permute-start | bytes 1769480 | tf_op jit(solution)/shard_map/ppermute | solution.py:1113
  223.4 17.0 %collective-permute-start.49 = (bf16[4,1,96,768]{3,2,1,0:T(8,128)(2,1)S(1)}, bf16[4,1,96,768]{3,2,1,0:T(8,128)(2,1)S(1)}, u32[]{:S(2)}, u32[]{:S(2)}) collective-permute-start(bf16[4,1,96,768]{3,2,1,0:T(8,128)(2,1)S(1)} %copy-done.90), channel_id=1, source_target_pairs={{0,4},{4,0},{8,12},{12,8},{16,20},{20,16},{24,28},{28,24},{1,5},{5... | collective-permute-start | bytes 1769480 | tf_op jit(solution)/shard_map/ppermute | solution.py:1113
  224.1 16.3 %collective-permute-start.50 = (bf16[64,768]{1,0:T(8,128)(2,1)S(1)}, bf16[64,768]{1,0:T(8,128)(2,1)S(1)}, u32[]{:S(2)}, u32[]{:S(2)}) collective-permute-start(bf16[64,768]{1,0:T(8,128)(2,1)S(1)} %add_convert_fusion.11.first_ref), channel_id=1, source_target_pairs={{0,2},{1,3},{2,0},{3,1},{4,6},{5,7},{6,4},{7,5},{8,10},{9,11},{10,... | collective-permute-start | bytes 294920 | tf_op jit(solution)/shard_map/ppermute | solution.py:1113
  240.6 16.4 %collective-permute-start.53 = (bf16[4,1,96,768]{3,2,1,0:T(8,128)(2,1)}, bf16[4,1,96,768]{3,2,1,0:T(8,128)(2,1)S(1)}, u32[]{:S(2)}, u32[]{:S(2)}) collective-permute-start(bf16[4,1,96,768]{3,2,1,0:T(8,128)(2,1)} %get-tuple-element.420), channel_id=1, source_target_pairs={{0,4},{4,0},{8,12},{12,8},{16,20},{20,16},{24,28},{28,24},{1,5},{5... | collective-permute-start | bytes 1769480 | tf_op jit(solution)/shard_map/ppermute | solution.py:1113
  244.2 21.4 %collective-permute-start.52 = (bf16[2,232,768]{2,1,0:T(8,128)(2,1)S(1)}, bf16[2,232,768]{2,1,0:T(8,128)(2,1)S(1)}, u32[]{:S(2)}, u32[]{:S(2)}) collective-permute-start(bf16[2,232,768]{2,1,0:T(8,128)(2,1)S(1)} %add_convert_fusion.1.first_ref), channel_id=1, source_target_pairs={{0,2},{1,3},{2,0},{3,1},{4,6},{5,7},{6,4},{7,5},{8,10},{9,11},{10,... | collective-permute-start | bytes 2138120 | tf_op jit(solution)/shard_map/ppermute | solution.py:1113
  248.9 16.7 %collective-permute-start.55 = (bf16[2,2,96,768]{3,2,1,0:T(8,128)(2,1)}, bf16[2,2,96,768]{3,2,1,0:T(8,128)(2,1)S(1)}, u32[]{:S(2)}, u32[]{:S(2)}) collective-permute-start(bf16[2,2,96,768]{3,2,1,0:T(8,128)(2,1)} %get-tuple-element.416), channel_id=1, source_target_pairs={{0,8},{4,12},{8,0},{12,4},{16,24},{20,28},{24,16},{28,20},{1,9},{5... | collective-permute-start | bytes 1769480 | tf_op jit(solution)/shard_map/ppermute | solution.py:1113
  250.5 23.4 %collective-permute-start.56 = (bf16[4,1,96,768]{3,2,1,0:T(8,128)(2,1)S(1)}, bf16[4,1,96,768]{3,2,1,0:T(8,128)(2,1)S(1)}, u32[]{:S(2)}, u32[]{:S(2)}) collective-permute-start(bf16[4,1,96,768]{3,2,1,0:T(8,128)(2,1)S(1)} %copy-done.89), channel_id=1, source_target_pairs={{0,4},{4,0},{8,12},{12,8},{16,20},{20,16},{24,28},{28,24},{1,5},{5... | collective-permute-start | bytes 1769480 | tf_op jit(solution)/shard_map/ppermute | solution.py:1113
  259.6 16.9 %collective-permute-start.57 = (bf16[1,2,96,768]{3,2,1,0:T(8,128)(2,1)}, bf16[1,2,96,768]{3,2,1,0:T(8,128)(2,1)S(1)}, u32[]{:S(2)}, u32[]{:S(2)}) collective-permute-start(bf16[1,2,96,768]{3,2,1,0:T(8,128)(2,1)} %get-tuple-element.419), channel_id=1, source_target_pairs={{0,16},{4,20},{8,24},{12,28},{16,0},{20,4},{24,8},{28,12},{1,17},{... | collective-permute-start | bytes 884744 | tf_op jit(solution)/shard_map/ppermute | solution.py:1113
  280.7 22.3 %collective-permute-start.59 = (bf16[2,2,96,768]{3,2,1,0:T(8,128)(2,1)}, bf16[2,2,96,768]{3,2,1,0:T(8,128)(2,1)S(1)}, u32[]{:S(2)}, u32[]{:S(2)}) collective-permute-start(bf16[2,2,96,768]{3,2,1,0:T(8,128)(2,1)} %get-tuple-element.444), channel_id=1, source_target_pairs={{0,8},{4,12},{8,0},{12,4},{16,24},{20,28},{24,16},{28,20},{1,9},{5... | collective-permute-start | bytes 1769480 | tf_op jit(solution)/shard_map/ppermute | solution.py:1113
  280.7 20.0 %collective-permute-start.60 = (bf16[1,2,96,768]{3,2,1,0:T(8,128)(2,1)S(1)}, bf16[1,2,96,768]{3,2,1,0:T(8,128)(2,1)S(1)}, u32[]{:S(2)}, u32[]{:S(2)}) collective-permute-start(bf16[1,2,96,768]{3,2,1,0:T(8,128)(2,1)S(1)} %copy-done.91), channel_id=1, source_target_pairs={{0,16},{4,20},{8,24},{12,28},{16,0},{20,4},{24,8},{28,12},{1,17},{... | collective-permute-start | bytes 884744 | tf_op jit(solution)/shard_map/ppermute | solution.py:1113
  306.9 15.9 %collective-permute-start.63 = (bf16[4,1,96,768]{3,2,1,0:T(8,128)(2,1)}, bf16[4,1,96,768]{3,2,1,0:T(8,128)(2,1)S(1)}, u32[]{:S(2)}, u32[]{:S(2)}) collective-permute-start(bf16[4,1,96,768]{3,2,1,0:T(8,128)(2,1)} %get-tuple-element.454), channel_id=1, source_target_pairs={{0,4},{4,0},{8,12},{12,8},{16,20},{20,16},{24,28},{28,24},{1,5},{5... | collective-permute-start | bytes 1769480 | tf_op jit(solution)/shard_map/ppermute | solution.py:1113
  309.2 36.6 %collective-permute-start.62 = (bf16[2,232,768]{2,1,0:T(8,128)(2,1)S(1)}, bf16[2,232,768]{2,1,0:T(8,128)(2,1)S(1)}, u32[]{:S(2)}, u32[]{:S(2)}) collective-permute-start(bf16[2,232,768]{2,1,0:T(8,128)(2,1)S(1)} %add_convert_fusion.first_ref), channel_id=1, source_target_pairs={{0,2},{1,3},{2,0},{3,1},{4,6},{5,7},{6,4},{7,5},{8,10},{9,11},{10,... | collective-permute-start | bytes 2138120 | tf_op jit(solution)/shard_map/ppermute | solution.py:1113
  309.8 16.8 %collective-permute-start.64 = (bf16[1,2,96,768]{3,2,1,0:T(8,128)(2,1)S(1)}, bf16[1,2,96,768]{3,2,1,0:T(8,128)(2,1)S(1)}, u32[]{:S(2)}, u32[]{:S(2)}) collective-permute-start(bf16[1,2,96,768]{3,2,1,0:T(8,128)(2,1)S(1)} %copy-done.92), channel_id=1, source_target_pairs={{0,16},{4,20},{8,24},{12,28},{16,0},{20,4},{24,8},{28,12},{1,17},{... | collective-permute-start | bytes 884744 | tf_op jit(solution)/shard_map/ppermute | solution.py:1113
  351.5 38.9 %collective-permute-start.68 = (f32[2,232,768]{2,1,0:T(8,128)}, f32[2,232,768]{2,1,0:T(8,128)S(1)}, u32[]{:S(2)}, u32[]{:S(2)}) collective-permute-start(f32[2,232,768]{2,1,0:T(8,128)} %get-tuple-element.475), channel_id=1, source_target_pairs={{0,1},{1,0},{2,3},{3,2},{4,5},{5,4},{6,7},{7,6},{8,9},{9,8},{10,11... | collective-permute-start | bytes 4276232 | tf_op jit(solution)/shard_map/ppermute | solution.py:1113
  (145 other events, 1185.3 us)

commit v9 on v8

--- a/solution.py
+++ b/solution.py
@@ -1417,7 +1417,17 @@
     gain_tile = jnp.concatenate(
         [gain_zero, gain_one, gain_two, gain_three, gain_four, jnp.zeros((3, D), f32)]
     )[None]
-    tiles = total_all(jnp.concatenate([tiles, tile_att, gain_tile]))
+    tiles = total(jnp.concatenate([tiles, tile_att, gain_tile]), [("mp", mp_n)])
+    if direct:
+        sent = tiles.astype(low)
+        other = swap(sent, "dp", 1)
+        sent, encoder_in_grad = hold((sent, encoder_in_grad))
+        tiles = sent.astype(f32) + other.astype(f32)
+        for bit in bits(dp_n)[1:]:
+            sent = tiles.astype(low)
+            tiles = sent.astype(f32) + swap(sent, "dp", bit).astype(f32)
+    else:
+        tiles = total_dp(tiles)
     done = finish(
         plan,
         meta,

time: 395 us -> 392 us (level)
    unnamed x197 -> x199, local copies, waits for them, and re-layouts: 10.3 us -> 9.67 us
  transfers between devices with their start and end apart: 74 -> 74, of which waited for: 42 -> 42; matrix products, arithmetic and copies ran while one was open for 7% -> 7% of each run, Pallas kernels for 37% -> 34%
where the time goes in v9:
time: 392 us; the launch traced here: 390 us
  Pallas kernels  163 us (42%)
  waiting for transfers between devices  104 us (27%)
  starting transfers between devices  77.2 us (20%)
  local copies, waits for them, and re-layouts  22.8 us (6%)
  other arithmetic  20.5 us (5%)
    pallas_call x30, Pallas kernels, call(): pl.pallas_call(body, name=name, out_shape=outs, grid_spec=pltpu.PrefetchS...  163 us
    ppermute x74, waiting for transfers between devices, swap(): return lax.ppermute(value, axis, [(i, i ^ bit) for i in range(count)])  104 us
    ppermute x74, starting transfers between devices, swap(): return lax.ppermute(value, axis, [(i, i ^ bit) for i in range(count)])  77.2 us
    unnamed x199, local copies, waits for them, and re-layouts  9.67 us
    convert_element_type x10, other arithmetic, reduce_own(): sent = (own.astype(f32) + swap(oth, 'mp', 1).astype(f32)).astype(low)  9.04 us
  transfers between devices with their start and end apart: 74, of which 42 were waited for; matrix products, arithmetic and copies ran while one was open for 7% of the time, Pallas kernels for 34%

profile of v9, /device:TPU:0, one launch (start us, length us, event | category | flops | bytes accessed | tf_op | source)
XLA Modules:
  0.0 390.3 jit_solution(17321915464672170271)
XLA Ops:
  2.7 4.0 %collective-permute-start = (bf16[104,768]{1,0:T(8,128)(2,1)}, bf16[104,768]{1,0:T(8,128)(2,1)}, u32[]{:S(2)}, u32[]{:S(2)}) collective-permute-start(bf16[104,768]{1,0:T(8,128)(2,1)} %pack_first.1), channel_id=1, source_target_pairs={{0,16},{4,20},{8,24},{12,28},{16,0},{20,4},{24,8},{28,12},{1,17},{... | collective-permute-start | bytes 479240 | tf_op jit(solution)/shard_map/ppermute | solution.py:1113
  22.8 4.8 %collective-permute-done.2.rest_1_ = bf16[208,768]{1,0:T(8,128)(2,1)S(1)} collective-permute-done((bf16[208,768]{1,0:T(8,128)(2,1)S(1)}, bf16[208,768]{1,0:T(8,128)(2,1)S(1)}, u32[]{:S(2)}, u32[]{:S(2)}) %collective-permute-start.2) | collective-permute-done | bytes 319520 | tf_op jit(solution)/shard_map/ppermute | solution.py:1113
  39.5 9.5 %encoder_attention.1 = (bf16[2,232,768]{2,1,0:T(8,128)(2,1)}, bf16[2,232,768]{2,1,0:T(8,128)(2,1)}, bf16[4,228,768]{2,1,0:T(8,128)(2,1)}) custom-call(s32[14]{0:T(128)} %concatenate.63.meta, bf16[2,232,768]{2,1,0:T(8,128)(2,1)} %get-tuple-element.539.own_ref.base_ref.in_ref, bf16[2,232,768]{2,1,0:T(8,128)(2,1)} %get-tuple-element.295.oth_ref, ...), custom_call_target="tpu_custom_call" | custom-call | flops 1 | bytes 1 | tf_op jit(solution)/shard_map/encoder_attention/pallas_call | solution.py:140
  61.4 9.1 %collective-permute-done.13 = bf16[192,768]{1,0:T(8,128)(2,1)S(1)} collective-permute-done((bf16[192,768]{1,0:T(8,128)(2,1)S(1)}, bf16[192,768]{1,0:T(8,128)(2,1)S(1)}, u32[]{:S(2)}, u32[]{:S(2)}) %collective-permute-start.13) | collective-permute-done | bytes 294944 | tf_op jit(solution)/shard_map/ppermute | solution.py:1113
  84.2 7.5 %encoder_feed.1 = (bf16[2,232,768]{2,1,0:T(8,128)(2,1)}, bf16[2,232,768]{2,1,0:T(8,128)(2,1)}) custom-call(s32[14]{0:T(128)} %concatenate.63.meta, bf16[2,232,768]{2,1,0:T(8,128)(2,1)} %get-tuple-element.322.own_ref, bf16[2,232,768]{2,1,0:T(8,128)(2,1)} %copy-done.8, bf16[192,768]{1,0:T(8,128)(2,1)} %copy-done.20, bf16[192,768]{1,0:T(8,128)(2,1)} %copy-done.36, ...), custom_call_target="tpu_custom_call" | custom-call | flops 1 | bytes 1 | tf_op jit(solution)/shard_map/encoder_feed/pallas_call | solution.py:140
  99.8 8.7 %collective-permute-done.21 = bf16[192,768]{1,0:T(8,128)(2,1)S(1)} collective-permute-done((bf16[192,768]{1,0:T(8,128)(2,1)S(1)}, bf16[192,768]{1,0:T(8,128)(2,1)S(1)}, u32[]{:S(2)}, u32[]{:S(2)}) %collective-permute-start.21) | collective-permute-done | bytes 294944 | tf_op jit(solution)/shard_map/ppermute | solution.py:1113
  110.7 4.1 %decoder_self.1 = (bf16[64,768]{1,0:T(8,128)(2,1)}, bf16[64,768]{1,0:T(8,128)(2,1)}, bf16[128,768]{1,0:T(8,128)(2,1)}) custom-call(s32[14]{0:T(128)} %concatenate.63.meta, bf16[128,768]{1,0:T(8,128)(2,1)} %bitcast.101, f32[1,768]{1,0:T(1,128)} %get-tuple-element.564.gain_ref, bf16[192,768]{1,0:T(8,128)(2,1)} %copy-done.18, bf16[192,768]{1,0:T(8,128)(2,1)} %copy-done.30, ...), custom_call_target="tpu_custom_call" | custom-call | flops 1 | bytes 1 | tf_op jit(solution)/shard_map/decoder_self/pallas_call | solution.py:140
  125.4 5.3 %collective-permute-done.27.rest_1_.rest_5_ = bf16[384,768]{1,0:T(8,128)(2,1)S(1)} collective-permute-done((bf16[384,768]{1,0:T(8,128)(2,1)S(1)}, bf16[384,768]{1,0:T(8,128)(2,1)S(1)}, u32[]{:S(2)}, u32[]{:S(2)}) %collective-permute-start.27) | collective-permute-done | bytes 589856 | tf_op jit(solution)/shard_map/ppermute | solution.py:1113
  134.9 8.1 %decoder_cross.1 = (bf16[2,32,768]{2,1,0:T(8,128)(2,1)}, bf16[2,32,768]{2,1,0:T(8,128)(2,1)}, bf16[4,32,384]{2,1,0:T(8,128)(2,1)}, bf16[4,228,384]{2,1,0:T(8,128)(2,1)}) custom-call(s32[14]{0:T(128)} %concatenate.63.meta, bf16[2,32,768]{2,1,0:T(8,128)(2,1)} %bitcast.110, bf16[2,32,768]{2,1,0:T(8,128)(2,1)} %bitcast.112, bf16[2,232,768]{2,1,0:T(8,128)(2,1)} %copy-done.1, ...), custom_call_target="tpu_custom_call" | custom-call | flops 1 | bytes 1 | tf_op jit(solution)/shard_map/decoder_cross/pallas_call | solution.py:140
  155.8 7.3 %decoder_feed.1 = (bf16[2,64,768]{2,1,0:T(8,128)(2,1)}, bf16[2,64,768]{2,1,0:T(8,128)(2,1)}, bf16[4,2,96,768]{3,2,1,0:T(8,128)(2,1)}, f32[4,2,96,768]{3,2,1,0:T(8,128)}) custom-call(s32[14]{0:T(128)} %concatenate.63.meta, bf16[64,768]{1,0:T(8,128)(2,1)} %get-tuple-element.361.own_ref, bf16[64,768]{1,0:T(8,128)(2,1)} %copy-done.82, ...), custom_call_target="tpu_custom_call" | custom-call | flops 1 | bytes 1 | tf_op jit(solution)/shard_map/decoder_feed/pallas_call | solution.py:140
  168.7 4.8 %collective-permute-done.36 = bf16[2,64,768]{2,1,0:T(8,128)(2,1)S(1)} collective-permute-done((bf16[2,64,768]{2,1,0:T(8,128)(2,1)S(1)}, bf16[2,64,768]{2,1,0:T(8,128)(2,1)S(1)}, u32[]{:S(2)}, u32[]{:S(2)}) %collective-permute-start.36) | collective-permute-done | bytes 196640 | tf_op jit(solution)/shard_map/ppermute | solution.py:1113
  179.0 13.6 %decoder_cross_back.1 = (bf16[2,32,768]{2,1,0:T(8,128)(2,1)}, bf16[2,32,768]{2,1,0:T(8,128)(2,1)}, bf16[2,232,768]{2,1,0:T(8,128)(2,1)}, bf16[2,232,768]{2,1,0:T...) custom-call(s32[14]{0:T(128)} %concatenate.63.meta, bf16[2,32,768]{2,1,0:T(8,128)(2,1)} %bitcast.111, ...), custom_call_target="tpu_custom_call" | custom-call | flops 1 | bytes 1 | tf_op jit(solution)/shard_map/decoder_cross_back/pallas_call | solution.py:140
  210.9 5.3 %decoder_self_back.1 = (bf16[64,768]{1,0:T(8,128)(2,1)}, bf16[64,768]{1,0:T(8,128)(2,1)}, bf16[4,1,96,768]{3,2,1,0:T(8,128)(2,1)}, f32[4,1,96,768]{3,2,1,0:T(8,128)}) custom-call(s32[14]{0:T(128)} %concatenate.63.meta, bf16[128,768]{1,0:T(8,128)(2,1)} %bitcast.102, f32[1,768]{1,0:T(1,128)} %get-tuple-element.564.gain_ref, ...), custom_call_target="tpu_custom_call" | custom-call | flops 1 | bytes 1 | tf_op jit(solution)/shard_map/decoder_self_back/pallas_call | solution.py:140
  225.7 14.8 %encoder_feed_back.1 = (bf16[2,232,768]{2,1,0:T(8,128)(2,1)}, bf16[2,232,768]{2,1,0:T(8,128)(2,1)}, bf16[4,1,96,768]{3,2,1,0:T(8,128)(2,1)}, f32[4,1,96,768]{3,2...) custom-call(s32[14]{0:T(128)} %concatenate.63.meta, ...), custom_call_target="tpu_custom_call" | custom-call | flops 1 | bytes 1 | tf_op jit(solution)/shard_map/encoder_feed_back/pallas_call | solution.py:140
  244.8 4.1 %fold.8 = (f32[2,2,96,768]{3,2,1,0:T(8,128)}, bf16[2,2,96,768]{3,2,1,0:T(8,128)(2,1)}) custom-call(s32[14]{0:T(128)} %concatenate.63.meta, f32[4,1,96,768]{3,2,1,0:T(8,128)} %get-tuple-element.415.rest_0_, f32[4,1,96,768]{3,2,1,0:T(8,128)} %get-tuple-element.416.rest_1_, bf16[4,1,96,768]{3,2,1,0:T(8,128)(2,1)} %copy-done.57, bf16[4,1,96,768]{3,2,1,0:T(8,128)(2,1)} %copy-done.60), custom_call_target="tpu_custom_call" | custom-call | flops 1 | bytes 1 | tf_op jit(solution)/shard_map/fold/pallas_call | solution.py:140
  266.5 4.2 %norm_back_mid.1 = (f32[2,232,768]{2,1,0:T(8,128)}, bf16[2,232,768]{2,1,0:T(8,128)(2,1)}, f32[1,768]{1,0:T(1,128)}) custom-call(s32[14]{0:T(128)} %concatenate.63.meta, f32[2,232,768]{2,1,0:T(8,128)} %get-tuple-element.316.in_ref, f32[1,768]{1,0:T(1,128)} %get-tuple-element.565.gain_ref, f32[2,232,768]{2,1,0:T(8,128)} %get-tuple-element.537.grad_ref, ...), custom_call_target="tpu_custom_call" | custom-call | flops 1 | bytes 1 | tf_op jit(solution)/shard_map/norm_back_mid/pallas_call | solution.py:140
  276.6 4.1 %fold.11 = (f32[2,2,96,768]{3,2,1,0:T(8,128)}, bf16[2,2,96,768]{3,2,1,0:T(8,128)(2,1)}) custom-call(s32[14]{0:T(128)} %concatenate.63.meta, f32[4,1,96,768]{3,2,1,0:T(8,128)} %get-tuple-element.436.rest_0_, f32[4,1,96,768]{3,2,1,0:T(8,128)} %get-tuple-element.437.rest_1_, bf16[4,1,96,768]{3,2,1,0:T(8,128)(2,1)} %copy-done.58, bf16[4,1,96,768]{3,2,1,0:T(8,128)(2,1)} %copy-done.59), custom_call_target="tpu_custom_call" | custom-call | flops 1 | bytes 1 | tf_op jit(solution)/shard_map/fold/pallas_call | solution.py:140
  282.8 14.9 %encoder_attention_back.1 = (bf16[2,232,768]{2,1,0:T(8,128)(2,1)}, bf16[2,232,768]{2,1,0:T(8,128)(2,1)}, bf16[4,1,96,768]{3,2,1,0:T(8,128)(2,1)}, f32[4,1,96,768]{3,2,1,0:T(8,128)}) custom-call(s32[14]{0:T(128)} %concatenate.63.meta, bf16[2,232,768]{2,1,0:T(8,128)(2,1)} %get-tuple-element.539.own_ref.base_ref.in_ref, ...), custom_call_target="tpu_custom_call" | custom-call | flops 1 | bytes 1 | tf_op jit(solution)/shard_map/encoder_attention_back/pallas_call | solution.py:140
  311.0 11.8 %collective-permute-done.59.rest_1_ = bf16[4,1,96,768]{3,2,1,0:T(8,128)(2,1)S(1)} collective-permute-done((bf16[4,1,96,768]{3,2,1,0:T(8,128)(2,1)}, bf16[4,1,96,768]{3,2,1,0:T(8,128)(2,1)S(1)}, u32[]{:S(2)}, u32[]{:S(2)}) %collective-permute-start.59) | collective-permute-done | bytes 589856 | tf_op jit(solution)/shard_map/ppermute | solution.py:1113
  331.0 7.9 %collect.2 = (f32[6,96,768]{2,1,0:T(8,128)}, f32[6,8,768]{2,1,0:T(8,128)}) custom-call(s32[14]{0:T(128)} %concatenate.63.meta, f32[1,2,96,768]{3,2,1,0:T(8,128)} %get-tuple-element.462.rest_0_, bf16[1,2,96,768]{3,2,1,0:T(8,128)(2,1)} %copy-done.68, f32[1,2,96,768]{3,2,1,0:T(8,128)} %get-tuple-element.464.rest_2_, bf16[1,2,96,768]{3,2,1,0:T(8,128)(2,1)} %copy-done.69, ...), custom_call_target="tpu_custom_call" | custom-call | flops 1 | bytes 1 | tf_op jit(solution)/shard_map/collect/pallas_call | solution.py:140
  342.1 4.1 %norm_back_enc.1 = (f32[2,232,768]{2,1,0:T(8,128)}, f32[1,768]{1,0:T(1,128)}) custom-call(s32[14]{0:T(128)} %concatenate.63.meta, bf16[2,232,768]{2,1,0:T(8,128)(2,1)} %get-tuple-element.539.own_ref.base_ref.in_ref, f32[1,768]{1,0:T(1,128)} %get-tuple-element.566.gain_ref, f32[2,232,768]{2,1,0:T(8,128)} %get-tuple-element.478.grad_ref, ...), custom_call_target="tpu_custom_call" | custom-call | flops 1 | bytes 1 | tf_op jit(solution)/shard_map/norm_back_enc/pallas_call | solution.py:140
  353.4 4.4 %collective-permute-done.69 = bf16[8,8,768]{2,1,0:T(8,128)(2,1)S(1)} collective-permute-done((bf16[8,8,768]{2,1,0:T(8,128)(2,1)S(1)}, bf16[8,8,768]{2,1,0:T(8,128)(2,1)S(1)}, u32[]{:S(2)}, u32[]{:S(2)}) %collective-permute-start.69) | collective-permute-done | bytes 98336 | tf_op jit(solution)/shard_map/ppermute | solution.py:1113
  377.4 7.2 %update_attention.1 = (f32[3,3,96,192]{3,2,1,0:T(8,128)}, f32[3,3,96,192]{3,2,1,0:T(8,128)}, f32[3,3,96,192]{3,2,1,0:T(8,128)}, f32[3,3,96,192]{3,2,1,0:T(8,128)...) custom-call(s32[14]{0:T(128)} %concatenate.63.meta, ...), custom_call_target="tpu_custom_call" | custom-call | flops 1 | bytes 1 | tf_op jit(solution)/shard_map/update_attention/pallas_call | solution.py:140
  384.6 5.6 %update_feed.1 = (f32[2,96,768]{2,1,0:T(8,128)}, f32[2,96,768]{2,1,0:T(8,128)}, f32[2,96,768]{2,1,0:T(8,128)}, f32[2,96,768]{2,1,0:T(8,128)}, bf16[2,96,768]{2,1...) custom-call(s32[14]{0:T(128)} %concatenate.63.meta, ...), custom_call_target="tpu_custom_call" | custom-call | flops 1 | bytes 1 | tf_op jit(solution)/shard_map/update_feed/pallas_call | solution.py:140
  (433 shorter events, 211.8 us)
Async XLA Ops:
  29.9 19.1 %collective-permute-start.5 = (bf16[192,768]{1,0:T(8,128)(2,1)S(1)}, bf16[192,768]{1,0:T(8,128)(2,1)S(1)}, u32[]{:S(2)}, u32[]{:S(2)}) collective-permute-start(bf16[192,768]{1,0:T(8,128)(2,1)S(1)} %constant_dynamic-update-slice_fusion.2.rest_0_), channel_id=1, source_target_pairs={{0,8},{4,12},{8,0},{12,4},{16,24},{20,28},{24,16},{28,20},{1,9},{5... | collective-permute-start | bytes 884744 | tf_op jit(solution)/shard_map/ppermute | solution.py:1113
  30.7 18.3 %collective-permute-start.6 = (bf16[192,768]{1,0:T(8,128)(2,1)S(1)}, bf16[192,768]{1,0:T(8,128)(2,1)S(1)}, u32[]{:S(2)}, u32[]{:S(2)}) collective-permute-start(bf16[192,768]{1,0:T(8,128)(2,1)S(1)} %constant_dynamic-update-slice_fusion.2.rest_0_), channel_id=1, source_target_pairs={{0,4},{4,0},{8,12},{12,8},{16,20},{20,16},{24,28},{28,24},{1,5},{5... | collective-permute-start | bytes 884744 | tf_op jit(solution)/shard_map/ppermute | solution.py:1113
  32.2 16.7 %collective-permute-start.7 = (bf16[96,768]{1,0:T(8,128)(2,1)S(1)}, bf16[96,768]{1,0:T(8,128)(2,1)S(1)}, u32[]{:S(2)}, u32[]{:S(2)}) collective-permute-start(bf16[96,768]{1,0:T(8,128)(2,1)S(1)} %get-tuple-element.309), channel_id=1, source_target_pairs={{0,16},{4,20},{8,24},{12,28},{16,0},{20,4},{24,8},{28,12},{1,17},{... | collective-permute-start | bytes 442376 | tf_op jit(solution)/shard_map/ppermute | solution.py:1113
  52.7 19.5 %collective-permute-start.9 = (bf16[2,232,768]{2,1,0:T(8,128)(2,1)S(1)}, bf16[2,232,768]{2,1,0:T(8,128)(2,1)S(1)}, u32[]{:S(2)}, u32[]{:S(2)}) collective-permute-start(bf16[2,232,768]{2,1,0:T(8,128)(2,1)S(1)} %add_convert_fusion.5.first_ref), channel_id=1, source_target_pairs={{0,2},{1,3},{2,0},{3,1},{4,6},{5,7},{6,4},{7,5},{8,10},{9,11},{10,... | collective-permute-start | bytes 2138120 | tf_op jit(solution)/shard_map/ppermute | solution.py:1113
  54.4 16.2 %collective-permute-start.13 = (bf16[192,768]{1,0:T(8,128)(2,1)S(1)}, bf16[192,768]{1,0:T(8,128)(2,1)S(1)}, u32[]{:S(2)}, u32[]{:S(2)}) collective-permute-start(bf16[192,768]{1,0:T(8,128)(2,1)S(1)} %pad_maximum_fusion.5), channel_id=1, source_target_pairs={{0,16},{4,20},{8,24},{12,28},{16,0},{20,4},{24,8},{28,12},{1,17},{... | collective-permute-start | bytes 884744 | tf_op jit(solution)/shard_map/ppermute | solution.py:1113
  91.8 16.7 %collective-permute-start.21 = (bf16[192,768]{1,0:T(8,128)(2,1)S(1)}, bf16[192,768]{1,0:T(8,128)(2,1)S(1)}, u32[]{:S(2)}, u32[]{:S(2)}) collective-permute-start(bf16[192,768]{1,0:T(8,128)(2,1)S(1)} %copy-done.28), channel_id=1, source_target_pairs={{0,16},{4,20},{8,24},{12,28},{16,0},{20,4},{24,8},{28,12},{1,17},{... | collective-permute-start | bytes 884744 | tf_op jit(solution)/shard_map/ppermute | solution.py:1113
  98.2 19.4 %collective-permute-start.19 = (bf16[2,232,768]{2,1,0:T(8,128)(2,1)S(1)}, bf16[2,232,768]{2,1,0:T(8,128)(2,1)}, u32[]{:S(2)}, u32[]{:S(2)}) collective-permute-start(bf16[2,232,768]{2,1,0:T(8,128)(2,1)S(1)} %add_convert_fusion.4), channel_id=1, source_target_pairs={{0,2},{1,3},{2,0},{3,1},{4,6},{5,7},{6,4},{7,5},{8,10},{9,11},{10,... | collective-permute-start | bytes 2138120 | tf_op jit(solution)/shard_map/ppermute | solution.py:1113
  114.9 15.8 %collective-permute-start.27 = (bf16[384,768]{1,0:T(8,128)(2,1)S(1)}, bf16[384,768]{1,0:T(8,128)(2,1)S(1)}, u32[]{:S(2)}, u32[]{:S(2)}) collective-permute-start(bf16[384,768]{1,0:T(8,128)(2,1)S(1)} %constant_dynamic-update-slice_fusion.10.rest_0_.rest_4_), channel_id=1, source_target_pairs={{0,8},{4,12},{8,0},{12,4},{16,24},{20,28},{24,16},{28,20},{1,9},{5... | collective-permute-start | bytes 1769480 | tf_op jit(solution)/shard_map/ppermute | solution.py:1113
  132.2 21.5 %collective-permute-start.34 = (bf16[384,768]{1,0:T(8,128)(2,1)S(1)}, bf16[384,768]{1,0:T(8,128)(2,1)S(1)}, u32[]{:S(2)}, u32[]{:S(2)}) collective-permute-start(bf16[384,768]{1,0:T(8,128)(2,1)S(1)} %collective-permute-done.27.rest_1_.rest_5_), channel_id=1, source_target_pairs={{0,4},{4,0},{8,12},{12,8},{16,20},{20,16},{24,28},{28,24},{1,5},{5... | collective-permute-start | bytes 1769480 | tf_op jit(solution)/shard_map/ppermute | solution.py:1113
  163.1 29.5 %collective-permute-start.38 = (bf16[4,2,96,768]{3,2,1,0:T(8,128)(2,1)}, bf16[4,2,96,768]{3,2,1,0:T(8,128)(2,1)S(1)}, u32[]{:S(2)}, u32[]{:S(2)}) collective-permute-start(bf16[4,2,96,768]{3,2,1,0:T(8,128)(2,1)} %get-tuple-element.372), channel_id=1, source_target_pairs={{0,4},{4,0},{8,12},{12,8},{16,20},{20,16},{24,28},{28,24},{1,5},{5... | collective-permute-start | bytes 3538952 | tf_op jit(solution)/shard_map/ppermute | solution.py:1113
  199.2 20.7 %collective-permute-start.41 = (bf16[2,232,768]{2,1,0:T(8,128)(2,1)S(1)}, bf16[2,232,768]{2,1,0:T(8,128)(2,1)S(1)}, u32[]{:S(2)}, u32[]{:S(2)}) collective-permute-start(bf16[2,232,768]{2,1,0:T(8,128)(2,1)S(1)} %add_convert_fusion.2), channel_id=1, source_target_pairs={{0,2},{1,3},{2,0},{3,1},{4,6},{5,7},{6,4},{7,5},{8,10},{9,11},{10,... | collective-permute-start | bytes 2138120 | tf_op jit(solution)/shard_map/ppermute | solution.py:1113
  199.8 18.9 %collective-permute-start.46 = (bf16[4,1,96,768]{3,2,1,0:T(8,128)(2,1)S(1)}, bf16[4,1,96,768]{3,2,1,0:T(8,128)(2,1)S(1)}, u32[]{:S(2)}, u32[]{:S(2)}) collective-permute-start(bf16[4,1,96,768]{3,2,1,0:T(8,128)(2,1)S(1)} %copy-done.89), channel_id=1, source_target_pairs={{0,4},{4,0},{8,12},{12,8},{16,20},{20,16},{24,28},{28,24},{1,5},{5... | collective-permute-start | bytes 1769480 | tf_op jit(solution)/shard_map/ppermute | solution.py:1113
  223.4 17.1 %collective-permute-start.49 = (bf16[4,1,96,768]{3,2,1,0:T(8,128)(2,1)S(1)}, bf16[4,1,96,768]{3,2,1,0:T(8,128)(2,1)S(1)}, u32[]{:S(2)}, u32[]{:S(2)}) collective-permute-start(bf16[4,1,96,768]{3,2,1,0:T(8,128)(2,1)S(1)} %copy-done.91), channel_id=1, source_target_pairs={{0,4},{4,0},{8,12},{12,8},{16,20},{20,16},{24,28},{28,24},{1,5},{5... | collective-permute-start | bytes 1769480 | tf_op jit(solution)/shard_map/ppermute | solution.py:1113
  224.1 16.3 %collective-permute-start.50 = (bf16[64,768]{1,0:T(8,128)(2,1)S(1)}, bf16[64,768]{1,0:T(8,128)(2,1)S(1)}, u32[]{:S(2)}, u32[]{:S(2)}) collective-permute-start(bf16[64,768]{1,0:T(8,128)(2,1)S(1)} %add_convert_fusion.11.first_ref), channel_id=1, source_target_pairs={{0,2},{1,3},{2,0},{3,1},{4,6},{5,7},{6,4},{7,5},{8,10},{9,11},{10,... | collective-permute-start | bytes 294920 | tf_op jit(solution)/shard_map/ppermute | solution.py:1113
  240.6 16.4 %collective-permute-start.53 = (bf16[4,1,96,768]{3,2,1,0:T(8,128)(2,1)}, bf16[4,1,96,768]{3,2,1,0:T(8,128)(2,1)S(1)}, u32[]{:S(2)}, u32[]{:S(2)}) collective-permute-start(bf16[4,1,96,768]{3,2,1,0:T(8,128)(2,1)} %get-tuple-element.423), channel_id=1, source_target_pairs={{0,4},{4,0},{8,12},{12,8},{16,20},{20,16},{24,28},{28,24},{1,5},{5... | collective-permute-start | bytes 1769480 | tf_op jit(solution)/shard_map/ppermute | solution.py:1113
  244.3 21.4 %collective-permute-start.52 = (bf16[2,232,768]{2,1,0:T(8,128)(2,1)S(1)}, bf16[2,232,768]{2,1,0:T(8,128)(2,1)S(1)}, u32[]{:S(2)}, u32[]{:S(2)}) collective-permute-start(bf16[2,232,768]{2,1,0:T(8,128)(2,1)S(1)} %add_convert_fusion.1.first_ref), channel_id=1, source_target_pairs={{0,2},{1,3},{2,0},{3,1},{4,6},{5,7},{6,4},{7,5},{8,10},{9,11},{10,... | collective-permute-start | bytes 2138120 | tf_op jit(solution)/shard_map/ppermute | solution.py:1113
  248.9 16.7 %collective-permute-start.55 = (bf16[2,2,96,768]{3,2,1,0:T(8,128)(2,1)}, bf16[2,2,96,768]{3,2,1,0:T(8,128)(2,1)S(1)}, u32[]{:S(2)}, u32[]{:S(2)}) collective-permute-start(bf16[2,2,96,768]{3,2,1,0:T(8,128)(2,1)} %get-tuple-element.419), channel_id=1, source_target_pairs={{0,8},{4,12},{8,0},{12,4},{16,24},{20,28},{24,16},{28,20},{1,9},{5... | collective-permute-start | bytes 1769480 | tf_op jit(solution)/shard_map/ppermute | solution.py:1113
  250.5 23.4 %collective-permute-start.56 = (bf16[4,1,96,768]{3,2,1,0:T(8,128)(2,1)S(1)}, bf16[4,1,96,768]{3,2,1,0:T(8,128)(2,1)S(1)}, u32[]{:S(2)}, u32[]{:S(2)}) collective-permute-start(bf16[4,1,96,768]{3,2,1,0:T(8,128)(2,1)S(1)} %copy-done.90), channel_id=1, source_target_pairs={{0,4},{4,0},{8,12},{12,8},{16,20},{20,16},{24,28},{28,24},{1,5},{5... | collective-permute-start | bytes 1769480 | tf_op jit(solution)/shard_map/ppermute | solution.py:1113
  259.6 16.9 %collective-permute-start.57 = (bf16[1,2,96,768]{3,2,1,0:T(8,128)(2,1)}, bf16[1,2,96,768]{3,2,1,0:T(8,128)(2,1)S(1)}, u32[]{:S(2)}, u32[]{:S(2)}) collective-permute-start(bf16[1,2,96,768]{3,2,1,0:T(8,128)(2,1)} %get-tuple-element.422), channel_id=1, source_target_pairs={{0,16},{4,20},{8,24},{12,28},{16,0},{20,4},{24,8},{28,12},{1,17},{... | collective-permute-start | bytes 884744 | tf_op jit(solution)/shard_map/ppermute | solution.py:1113
  280.7 22.3 %collective-permute-start.60 = (bf16[2,2,96,768]{3,2,1,0:T(8,128)(2,1)}, bf16[2,2,96,768]{3,2,1,0:T(8,128)(2,1)S(1)}, u32[]{:S(2)}, u32[]{:S(2)}) collective-permute-start(bf16[2,2,96,768]{3,2,1,0:T(8,128)(2,1)} %get-tuple-element.447), channel_id=1, source_target_pairs={{0,8},{4,12},{8,0},{12,4},{16,24},{20,28},{24,16},{28,20},{1,9},{5... | collective-permute-start | bytes 1769480 | tf_op jit(solution)/shard_map/ppermute | solution.py:1113
  280.8 20.0 %collective-permute-start.61 = (bf16[1,2,96,768]{3,2,1,0:T(8,128)(2,1)S(1)}, bf16[1,2,96,768]{3,2,1,0:T(8,128)(2,1)S(1)}, u32[]{:S(2)}, u32[]{:S(2)}) collective-permute-start(bf16[1,2,96,768]{3,2,1,0:T(8,128)(2,1)S(1)} %copy-done.92), channel_id=1, source_target_pairs={{0,16},{4,20},{8,24},{12,28},{16,0},{20,4},{24,8},{28,12},{1,17},{... | collective-permute-start | bytes 884744 | tf_op jit(solution)/shard_map/ppermute | solution.py:1113
  306.9 15.9 %collective-permute-start.59 = (bf16[4,1,96,768]{3,2,1,0:T(8,128)(2,1)}, bf16[4,1,96,768]{3,2,1,0:T(8,128)(2,1)S(1)}, u32[]{:S(2)}, u32[]{:S(2)}) collective-permute-start(bf16[4,1,96,768]{3,2,1,0:T(8,128)(2,1)} %get-tuple-element.444), channel_id=1, source_target_pairs={{0,4},{4,0},{8,12},{12,8},{16,20},{20,16},{24,28},{28,24},{1,5},{5... | collective-permute-start | bytes 1769480 | tf_op jit(solution)/shard_map/ppermute | solution.py:1113
  309.2 31.9 %collective-permute-start.67 = (bf16[2,232,768]{2,1,0:T(8,128)(2,1)S(1)}, bf16[2,232,768]{2,1,0:T(8,128)(2,1)S(1)}, u32[]{:S(2)}, u32[]{:S(2)}) collective-permute-start(bf16[2,232,768]{2,1,0:T(8,128)(2,1)S(1)} %add_convert_fusion.first_ref), channel_id=1, source_target_pairs={{0,2},{1,3},{2,0},{3,1},{4,6},{5,7},{6,4},{7,5},{8,10},{9,11},{10,... | collective-permute-start | bytes 2138120 | tf_op jit(solution)/shard_map/ppermute | solution.py:1113
  309.8 16.8 %collective-permute-start.63 = (bf16[1,2,96,768]{3,2,1,0:T(8,128)(2,1)S(1)}, bf16[1,2,96,768]{3,2,1,0:T(8,128)(2,1)S(1)}, u32[]{:S(2)}, u32[]{:S(2)}) collective-permute-start(bf16[1,2,96,768]{3,2,1,0:T(8,128)(2,1)S(1)} %copy-done.93), channel_id=1, source_target_pairs={{0,16},{4,20},{8,24},{12,28},{16,0},{20,4},{24,8},{28,12},{1,17},{... | collective-permute-start | bytes 884744 | tf_op jit(solution)/shard_map/ppermute | solution.py:1113
  (146 other events, 1134.0 us)
